TPU v7x, 32 devices: a whole 2x2x4 slice. The times are simulated.
32 devices in a mesh: row: 4 (over y, x), col: 8 (over z, core).
Axes of the slice: x: 2, y: 2, z: 4, core: 2. Of those that a mesh axis runs over, the one named last changes fastest.
Arguments:
- hidden_states: bfloat16 [1536, 4096], P('col', 'row'), may hold values from -50 to 50
- out_grad: bfloat16 [1536, 4096], P('col', 'row'), may hold values from -6 to 6
- lengths: int32 [4, 4], P('row'), may hold values from 1 to 512, 1024 in all within a row
- norm_gains: bfloat16 [2, 2, 1536], P(None, None, 'col'), may hold values from 0.099609375 to 1.8984375
- qkv_weight: bfloat16 [2, 1536, 2048], P(None, 'row', 'col'), may hold values from -0.15625 to 0.15625
- qkv_bias: bfloat16 [2, 16, 128], P(None, 'col', 'row'), may hold values from -2 to 2
- out_weight: bfloat16 [2, 1536, 1536], P(None, 'col', 'row'), may hold values from -0.625 to 0.625
- gate_weight: bfloat16 [2, 1536, 8960], P(None, 'row', 'col'), may hold values from -0.15625 to 0.15625
- up_weight: bfloat16 [2, 1536, 8960], P(None, 'row', 'col'), may hold values from -0.15625 to 0.15625
- down_weight: bfloat16 [2, 8960, 1536], P(None, 'col', 'row'), may hold values from -0.0625 to 0.0625
Outputs:
- out_states: bfloat16 [1536, 4096], P('col', 'row')
- input_grad: float32 [1536, 4096], P('col', 'row')
- norm_gains_grad: float32 [2, 2, 1536], P(None, None, 'col')
- qkv_weight_grad: float32 [2, 1536, 2048], P(None, 'row', 'col')
- qkv_bias_grad: float32 [2, 16, 128], P(None, 'col', 'row')
- out_weight_grad: float32 [2, 1536, 1536], P(None, 'col', 'row')
- gate_weight_grad: float32 [2, 1536, 8960], P(None, 'row', 'col')
- up_weight_grad: float32 [2, 1536, 8960], P(None, 'row', 'col')
- down_weight_grad: float32 [2, 8960, 1536], P(None, 'col', 'row')
Inputs may be any that keep to these rules, and one draw needn't show every extreme that they name: Row g lists, in order, the lengths of the sequences packed into row group g; each row sums to 1024 and holds one length of exactly 512.
All inputs are finite; a program needn't handle non-finite values.
Results may differ from a plain program's by a relative error of at most 0.017.
Values may be sent and summed in bfloat16 or wider, within the bound.
A program may use at most 256 MiB of HBM per device.

v0:
```python
from functools import partial

import jax
import jax.numpy as jnp
from jax import lax
from jax.sharding import PartitionSpec as P

D = 1536
HEADS = 12
KV_HEADS = 2
HD = 128
LAYERS = 2
SEQ_MAX = 512
QB = 128


eps_norm = 1e-06
rope_base = 1000000.0
neg_fill = -1e30


def row_starts(sizes, count):
    ends = jnp.cumsum(sizes)
    firsts = ends - sizes
    places = jnp.arange(count, dtype=jnp.int32)
    inside = (places[None, :] >= firsts[:, None]) & (places[None, :] < ends[:, None])
    return jnp.sum(jnp.where(inside, firsts[:, None], 0), axis=0)


def rope_tables(positions):
    half = HD // 2
    freq = rope_base ** (-(jnp.arange(half, dtype=jnp.float32) * (2.0 / HD)))
    angle = freq[:, None] * positions.astype(jnp.float32)[None, :]
    cosine = jnp.concatenate([jnp.cos(angle), jnp.cos(angle)], axis=0)
    sine = jnp.concatenate([jnp.sin(angle), jnp.sin(angle)], axis=0)
    return (cosine, sine)


def rotate(values, cosine, sine):
    half = HD // 2
    turned = jnp.concatenate([-values[:, half:], values[:, :half]], axis=1)
    return values * cosine + turned * sine


def rotate_back(grads, cosine, sine):
    half = HD // 2
    lifted = grads * sine
    turned = jnp.concatenate([lifted[:, half:], -lifted[:, :half]], axis=1)
    return grads * cosine + turned


def contract_first(left, right):
    return lax.dot_general(
        left, right, (((0,), (0,)), ((), ())), preferred_element_type=jnp.float32
    )


def contract_last(left, right):
    return lax.dot_general(
        left, right, (((1,), (1,)), ((), ())), preferred_element_type=jnp.float32
    )


def feature_total(values):
    return lax.psum(jnp.sum(values, axis=0), "col")


def spread(values):
    return lax.all_gather(values, "col", axis=0, tiled=True)


def summed_rows(make_term, rows):
    return lax.psum_scatter(
        make_term(jnp.int32(0), lax.axis_size("col") * rows), "col", scatter_dimension=0, tiled=True
    )


def to_blocks(values):
    return lax.all_to_all(values, "col", split_axis=1, concat_axis=0, tiled=True)


def to_tokens(values):
    return lax.all_to_all(values, "col", split_axis=0, concat_axis=1, tiled=True)


def by_columns(weight, acts, start, count):
    return contract_first(weight, acts)


def by_rows(weight, grads, start, count):
    return jnp.dot(weight, grads, preferred_element_type=jnp.float32)


def by_rows_pair(first_weight, first_grads, second_weight, second_grads, start, count):
    return by_rows(first_weight, first_grads, start, count) + by_rows(
        second_weight, second_grads, start, count
    )


def norm_forward(residual, gain):
    totals = feature_total(residual * residual)
    scale = lax.rsqrt(totals / D + eps_norm)
    return (scale, (residual * scale * gain[:, None]).astype(jnp.bfloat16))


def norm_backward(d_normed, residual, scale, gain):
    weighted = d_normed * gain[:, None]
    inner = feature_total(weighted * residual)
    d_residual = weighted * scale - residual * (scale * scale * scale) * inner / D
    d_gain = jnp.sum(d_normed * residual * scale, axis=1)
    return (d_residual, d_gain)


def attend_scores(queries, keys, mask):
    scores = jnp.einsum(
        "kghq,khj->kgqj", queries, keys, preferred_element_type=jnp.float32
    ) * HD ** (-0.5)
    return jnp.where(mask[None, None], scores, neg_fill)


def per_device(
    hidden_states,
    out_grad,
    lengths,
    norm_gains,
    qkv_weight,
    qkv_bias,
    out_weight,
    gate_weight,
    up_weight,
    down_weight,
):
    feat_rows, tok_row = hidden_states.shape
    col_at = lax.axis_index("col")
    starts = row_starts(lengths[0], tok_row)
    positions = jnp.arange(tok_row, dtype=jnp.int32) - starts
    cosine, sine = rope_tables(positions)
    first = col_at * QB
    block_starts = lax.dynamic_slice_in_dim(starts, first, QB)
    cos_block = lax.dynamic_slice_in_dim(cosine, first, QB, 1)
    sin_block = lax.dynamic_slice_in_dim(sine, first, QB, 1)
    reach = QB + SEQ_MAX
    window = jnp.maximum(first - SEQ_MAX, 0)
    key_places = window + jnp.arange(reach, dtype=jnp.int32)
    query_places = first + jnp.arange(QB, dtype=jnp.int32)
    mask = (key_places[None, :] >= block_starts[:, None]) & (
        key_places[None, :] <= query_places[:, None]
    )
    group = HEADS // KV_HEADS
    rotary = HEADS + KV_HEADS
    query_rows = HEADS * HD
    kv_rows = KV_HEADS * HD
    gains = norm_gains.astype(jnp.float32)
    residual = hidden_states.astype(jnp.float32)
    saved = []
    for layer in range(LAYERS):
        w_qkv, b_qkv, w_out, w_gate, w_up, w_down = (
            lax.all_gather(qkv_weight[layer], "row", axis=0, tiled=True),
            lax.all_gather(qkv_bias[layer], "row", axis=1, tiled=True),
            lax.all_gather(out_weight[layer], "row", axis=1, tiled=True),
            lax.all_gather(gate_weight[layer], "row", axis=0, tiled=True),
            lax.all_gather(up_weight[layer], "row", axis=0, tiled=True),
            lax.all_gather(down_weight[layer], "row", axis=1, tiled=True),
        )
        scale_one, normed_one = norm_forward(residual, gains[layer, 0])
        full_one = spread(normed_one)
        raw = contract_first(w_qkv, full_one) + b_qkv.reshape(-1).astype(jnp.float32)[:, None]
        local_heads = raw.shape[0] // HD
        shaped = raw.reshape(local_heads, HD, tok_row)
        head_ids = col_at * local_heads + jnp.arange(local_heads)
        turned = jnp.where((head_ids < rotary)[:, None, None], rotate(shaped, cosine, sine), shaped)
        blocked = to_blocks(turned.reshape(raw.shape).astype(jnp.bfloat16))
        kv_full = lax.all_gather(blocked[query_rows:], "col", axis=1, tiled=True)
        kv_window = lax.dynamic_slice_in_dim(kv_full, window, reach, 1)
        queries = blocked[:query_rows].reshape(KV_HEADS, group, HD, QB)
        keys = kv_window[:kv_rows].reshape(KV_HEADS, HD, reach)
        values = kv_window[kv_rows:].reshape(KV_HEADS, HD, reach)
        masked = attend_scores(queries, keys, mask)
        row_top = jnp.max(masked, axis=-1, keepdims=True)
        lifted = jnp.exp(masked - row_top)
        row_mass = jnp.sum(lifted, axis=-1, keepdims=True)
        probs = lifted / row_mass
        log_mass = row_top + jnp.log(row_mass)
        mixed = (
            jnp.einsum(
                "kgqj,khj->kghq",
                probs.astype(jnp.bfloat16),
                values,
                preferred_element_type=jnp.float32,
            )
            .reshape(query_rows, QB)
            .astype(jnp.bfloat16)
        )
        carried = to_tokens(mixed)
        attention = summed_rows(partial(by_columns, w_out, carried), feat_rows)
        residual_mid = residual + attention
        scale_two, normed_two = norm_forward(residual_mid, gains[layer, 1])
        full_two = spread(normed_two)
        gate = contract_first(w_gate, full_two)
        up = contract_first(w_up, full_two)
        hidden = (gate * jax.nn.sigmoid(gate) * up).astype(jnp.bfloat16)
        feed = summed_rows(partial(by_columns, w_down, hidden), feat_rows)
        saved.append(
            (
                residual,
                scale_one,
                full_one,
                blocked,
                kv_window,
                log_mass,
                mixed,
                carried,
                residual_mid,
                scale_two,
                full_two,
                gate,
                up,
                hidden,
                (w_qkv, w_out, w_gate, w_up, w_down),
                local_heads,
            )
        )
        residual = residual_mid + feed
    out_states = residual.astype(jnp.bfloat16)
    grad = out_grad.astype(jnp.float32)
    layer_grads = [None] * LAYERS
    gain_terms = [None] * LAYERS
    for layer in reversed(range(LAYERS)):
        (
            residual_in,
            scale_one,
            full_one,
            blocked,
            kv_window,
            log_mass,
            mixed,
            carried,
            residual_mid,
            scale_two,
            full_two,
            gate,
            up,
            hidden,
            weights_full,
            local_heads,
        ) = saved[layer]
        w_qkv, w_out, w_gate, w_up, w_down = weights_full
        grad_full = spread(grad.astype(jnp.bfloat16))
        d_down = contract_last(hidden, grad_full)
        d_hidden = jnp.dot(w_down, grad_full, preferred_element_type=jnp.float32)
        squash = jax.nn.sigmoid(gate)
        d_gate = (d_hidden * up * squash * (1.0 + gate * (1.0 - squash))).astype(jnp.bfloat16)
        d_up = (d_hidden * gate * squash).astype(jnp.bfloat16)
        d_gate_w = contract_last(full_two, d_gate)
        d_up_w = contract_last(full_two, d_up)
        d_normed_two = summed_rows(partial(by_rows_pair, w_gate, d_gate, w_up, d_up), feat_rows)
        d_residual, d_gain_two = norm_backward(
            d_normed_two, residual_mid, scale_two, gains[layer, 1]
        )
        grad = grad + d_residual
        grad_full = spread(grad.astype(jnp.bfloat16))
        d_out_w = contract_last(carried, grad_full)
        d_mixed = to_blocks(
            jnp.dot(w_out, grad_full, preferred_element_type=jnp.float32).astype(jnp.bfloat16)
        )
        queries = blocked[:query_rows].reshape(KV_HEADS, group, HD, QB)
        keys = kv_window[:kv_rows].reshape(KV_HEADS, HD, reach)
        values = kv_window[kv_rows:].reshape(KV_HEADS, HD, reach)
        masked = attend_scores(queries, keys, mask)
        probs = jnp.exp(masked - log_mass)
        low_probs = probs.astype(jnp.bfloat16)
        d_heads_mix = d_mixed.reshape(KV_HEADS, group, HD, QB)
        d_probs = jnp.einsum(
            "kghq,khj->kgqj", d_heads_mix, values, preferred_element_type=jnp.float32
        )
        inner = jnp.sum(probs * d_probs, axis=-1, keepdims=True)
        d_scores = (probs * (d_probs - inner)).astype(jnp.bfloat16)
        d_queries = (
            jnp.einsum("kgqj,khj->kghq", d_scores, keys, preferred_element_type=jnp.float32)
            * HD ** (-0.5)
        ).reshape(query_rows, QB)
        d_keys = (
            jnp.einsum("kgqj,kghq->khj", d_scores, queries, preferred_element_type=jnp.float32)
            * HD ** (-0.5)
        ).reshape(kv_rows, reach)
        d_values = jnp.einsum(
            "kgqj,kghq->khj", low_probs, d_heads_mix, preferred_element_type=jnp.float32
        ).reshape(kv_rows, reach)
        d_window = jnp.concatenate([d_keys, d_values], axis=0)
        d_placed = lax.dynamic_update_slice_in_dim(
            jnp.zeros((2 * kv_rows, tok_row), jnp.float32), d_window, window, 1
        )
        d_kv = lax.psum_scatter(d_placed, "col", scatter_dimension=1, tiled=True)
        d_heads = jnp.concatenate([d_queries, d_kv], axis=0).reshape(HEADS + 2 * KV_HEADS, HD, QB)
        d_turned = jnp.concatenate(
            [rotate_back(d_heads[:rotary], cos_block, sin_block), d_heads[rotary:]], axis=0
        )
        d_raw = to_tokens(d_turned.reshape((HEADS + 2 * KV_HEADS) * HD, QB).astype(jnp.bfloat16))
        d_bias = jnp.sum(d_raw, axis=1, dtype=jnp.float32).reshape(local_heads, HD)
        d_qkv_w = contract_last(full_one, d_raw)
        d_normed_one = summed_rows(partial(by_rows, w_qkv, d_raw), feat_rows)
        d_residual, d_gain_one = norm_backward(
            d_normed_one, residual_in, scale_one, gains[layer, 0]
        )
        grad = grad + d_residual
        layer_grads[layer] = (
            lax.psum_scatter(d_qkv_w, "row", scatter_dimension=0, tiled=True),
            lax.psum_scatter(d_bias, "row", scatter_dimension=1, tiled=True),
            lax.psum_scatter(d_out_w, "row", scatter_dimension=1, tiled=True),
            lax.psum_scatter(d_gate_w, "row", scatter_dimension=0, tiled=True),
            lax.psum_scatter(d_up_w, "row", scatter_dimension=0, tiled=True),
            lax.psum_scatter(d_down, "row", scatter_dimension=1, tiled=True),
        )
        gain_terms[layer] = jnp.stack([d_gain_one, d_gain_two])
    gain_grads = lax.psum(jnp.stack(gain_terms), "row")
    stacked = [jnp.stack([entry[member] for entry in layer_grads]) for member in range(6)]
    return (
        out_states,
        grad,
        gain_grads,
        stacked[0],
        stacked[1],
        stacked[2],
        stacked[3],
        stacked[4],
        stacked[5],
    )


def solution(mesh):
    placed = (
        P("col", "row"),
        P("col", "row"),
        P("row", None),
        P(None, None, "col"),
        P(None, "row", "col"),
        P(None, "col", "row"),
        P(None, "col", "row"),
        P(None, "row", "col"),
        P(None, "row", "col"),
        P(None, "col", "row"),
    )
    return jax.shard_map(
        per_device,
        mesh=mesh,
        in_specs=placed,
        out_specs=(
            P("col", "row"),
            P("col", "row"),
            P(None, None, "col"),
            P(None, "row", "col"),
            P(None, "col", "row"),
            P(None, "col", "row"),
            P(None, "row", "col"),
            P(None, "row", "col"),
            P(None, "col", "row"),
        ),
        check_vma=False,
    )
```

profile of v0, /device:TPU:31, one launch (start us, length us, event | category | flops | bytes accessed | tf_op | source)
XLA Modules:
  0.0 2284.9 jit_solution(13109288929776706779)
XLA Ops:
  10.0 13.1 psum.63
  47.4 16.9 all-gather.29.cloned.1.call-done
  73.1 17.5 all_to_all.128
  91.6 22.6 all-gather.31.cloned.1.call-done
  149.1 66.5 %reduce-scatter.67.cloned.1.call-done = f32[192,1024]{1,0:T(8,128)} async-done(((f32[1536,1024]{1,0:T(8,128)}), f32[192,1024]{1,0:T(8,128)}) %reduce-scatter.67.cloned.1.call-update) | async-done | bytes 786448 | tf_op jit(solution)/shard_map/reduce_scatter | solution.py:73
  216.9 13.2 psum.64
  235.9 33.6 %all-gather.33.cloned.1.call-done = bf16[1536,1024]{1,0:T(8,128)(2,1)} async-done(((bf16[192,1024]{1,0:T(8,128)(2,1)}), bf16[1536,1024]{1,0:T(8,128)(2,1)}) %all-gather.33.cloned.1.call-update) | async-done | bytes 3145744 | tf_op jit(solution)/shard_map/all_gather | solution.py:69
  278.3 39.0 %all-gather.51.cloned.1.call-done = bf16[1,1536,1120]{1,2,0:T(8,128)(2,1)} async-done(((bf16[1,384,1120]{1,2,0:T(8,128)(2,1)}), bf16[1,1536,1120]{1,2,0:T(8,128)(2,1)}) %all-gather.51.cloned.1.call-update) | async-done | bytes 3440656 | tf_op jit(solution)/shard_map/all_gather | solution.py:162
  328.5 36.8 %all-gather.53.cloned.1.call-done = bf16[1,1120,1536]{2,1,0:T(8,128)(2,1)} async-done(((bf16[1,1120,384]{2,1,0:T(8,128)(2,1)}), bf16[1,1120,1536]{2,1,0:T(8,128)(2,1)}) %all-gather.53.cloned.1.call-update) | async-done | bytes 3440656 | tf_op jit(solution)/shard_map/all_gather | solution.py:163
  381.6 68.5 %reduce-scatter.69.cloned.1.call-done = f32[192,1024]{1,0:T(8,128)} async-done(((f32[1536,1024]{1,0:T(8,128)}), f32[192,1024]{1,0:T(8,128)}) %reduce-scatter.69.cloned.1.call-update) | async-done | bytes 786448 | tf_op jit(solution)/shard_map/reduce_scatter | solution.py:73
  451.3 13.1 psum.65
  481.6 22.3 all-gather.35.cloned.1.call-done
  512.5 17.5 all_to_all.129
  530.8 22.6 all-gather.37.cloned.1.call-done
  585.4 68.4 %reduce-scatter.71.cloned.1.call-done = f32[192,1024]{1,0:T(8,128)} async-done(((f32[1536,1024]{1,0:T(8,128)}), f32[192,1024]{1,0:T(8,128)}) %reduce-scatter.71.cloned.1.call-update) | async-done | bytes 786448 | tf_op jit(solution)/shard_map/reduce_scatter | solution.py:73
  655.1 13.1 psum.66
  671.3 30.1 %all-gather.57.cloned.1.call-done = bf16[1,1536,1120]{1,2,0:T(8,128)(2,1)} async-done(((bf16[1,384,1120]{1,2,0:T(8,128)(2,1)}), bf16[1,1536,1120]{1,2,0:T(8,128)(2,1)}) %all-gather.57.cloned.1.call-update) | async-done | bytes 3440656 | tf_op jit(solution)/shard_map/all_gather | solution.py:162
  701.4 39.7 %all-gather.39.cloned.1.call-done = bf16[1536,1024]{1,0:T(8,128)(2,1)} async-done(((bf16[192,1024]{1,0:T(8,128)(2,1)}), bf16[1536,1024]{1,0:T(8,128)(2,1)}) %all-gather.39.cloned.1.call-update) | async-done | bytes 3145744 | tf_op jit(solution)/shard_map/all_gather | solution.py:69
  750.0 38.5 %all-gather.55.cloned.1.call-done = bf16[1,1536,1120]{1,2,0:T(8,128)(2,1)} async-done(((bf16[1,384,1120]{1,2,0:T(8,128)(2,1)}), bf16[1,1536,1120]{1,2,0:T(8,128)(2,1)}) %all-gather.55.cloned.1.call-update) | async-done | bytes 3440656 | tf_op jit(solution)/shard_map/all_gather | solution.py:161
  797.3 38.9 %all-gather.59.cloned.1.call-done = bf16[1,1120,1536]{2,1,0:T(8,128)(2,1)} async-done(((bf16[1,1120,384]{2,1,0:T(8,128)(2,1)}), bf16[1,1120,1536]{2,1,0:T(8,128)(2,1)}) %all-gather.59.cloned.1.call-update) | async-done | bytes 3440656 | tf_op jit(solution)/shard_map/all_gather | solution.py:163
  836.2 39.3 %all-gather.41.cloned.1.call-done = bf16[1536,1024]{1,0:T(8,128)(2,1)} async-done(((bf16[192,1024]{1,0:T(8,128)(2,1)}), bf16[1536,1024]{1,0:T(8,128)(2,1)}) %all-gather.41.cloned.1.call-update) | async-done | bytes 3145744 | tf_op jit(solution)/shard_map/all_gather | solution.py:69
  875.5 12.5 fusion.14
  905.9 67.8 %reduce-scatter.75.cloned.1.call-done = f32[192,1024]{1,0:T(8,128)} async-done(((f32[1536,1024]{1,0:T(8,128)}), f32[192,1024]{1,0:T(8,128)}) %reduce-scatter.75.cloned.1.call-update) | async-done | bytes 786448 | tf_op jit(solution)/shard_map/reduce_scatter | solution.py:73
  975.6 13.0 psum.67
  990.9 38.2 %all-gather.43.cloned.1.call-done = bf16[1536,1024]{1,0:T(8,128)(2,1)} async-done(((bf16[192,1024]{1,0:T(8,128)(2,1)}), bf16[1536,1024]{1,0:T(8,128)(2,1)}) %all-gather.43.cloned.1.call-update) | async-done | bytes 3145744 | tf_op jit(solution)/shard_map/all_gather | solution.py:69
  1067.9 31.2 %reduce-scatter.43.cloned.1.call-done = f32[512,128]{1,0:T(8,128)} async-done(((f32[512,1024]{1,0:T(8,128)}), f32[512,128]{1,0:T(8,128)}) %reduce-scatter.43.cloned.1.call-update) | async-done | bytes 262160 | tf_op jit(solution)/shard_map/reduce_scatter | solution.py:293
  1102.6 17.7 all_to_all.130
  1147.2 51.7 %reduce-scatter.77.cloned.1.call-done = f32[192,1024]{1,0:T(8,128)} async-done(((f32[1536,1024]{1,0:T(8,128)}), f32[192,1024]{1,0:T(8,128)}) %reduce-scatter.77.cloned.1.call-update) | async-done | bytes 786448 | tf_op jit(solution)/shard_map/reduce_scatter | solution.py:73
  1200.8 14.1 psum.68
  1214.9 54.7 %reduce-scatter.73.cloned.1.call-done = f32[192,1024]{1,0:T(8,128)} async-done(((f32[1536,1024]{1,0:T(8,128)}), f32[192,1024]{1,0:T(8,128)}) %reduce-scatter.73.cloned.1.call-update) | async-done | bytes 786448 | tf_op jit(solution)/shard_map/reduce_scatter | solution.py:73
  1272.5 37.4 %all-gather.45.cloned.1.call-done = bf16[1536,1024]{1,0:T(8,128)(2,1)} async-done(((bf16[192,1024]{1,0:T(8,128)(2,1)}), bf16[1536,1024]{1,0:T(8,128)(2,1)}) %all-gather.45.cloned.1.call-update) | async-done | bytes 3145744 | tf_op jit(solution)/shard_map/all_gather | solution.py:69
  1338.3 67.7 %reduce-scatter.79.cloned.1.call-done = f32[192,1024]{1,0:T(8,128)} async-done(((f32[1536,1024]{1,0:T(8,128)}), f32[192,1024]{1,0:T(8,128)}) %reduce-scatter.79.cloned.1.call-update) | async-done | bytes 786448 | tf_op jit(solution)/shard_map/reduce_scatter | solution.py:73
  1407.3 13.1 psum.69
  1422.8 38.2 %all-gather.47.cloned.1.call-done = bf16[1536,1024]{1,0:T(8,128)(2,1)} async-done(((bf16[192,1024]{1,0:T(8,128)(2,1)}), bf16[1536,1024]{1,0:T(8,128)(2,1)}) %all-gather.47.cloned.1.call-update) | async-done | bytes 3145744 | tf_op jit(solution)/shard_map/all_gather | solution.py:69
  1565.1 18.5 all_to_all.131
  1604.3 29.9 %reduce-scatter.65.cloned.1.call-done = f32[1120,384]{1,0:T(8,128)} async-done(((f32[1120,1536]{1,0:T(8,128)}), f32[1120,384]{1,0:T(8,128)}) %reduce-scatter.65.cloned.1.call-update) | async-done | bytes 1720336 | tf_op jit(solution)/shard_map/reduce_scatter | solution.py:312
  1634.2 77.8 %reduce-scatter.63.cloned.1.call-done = f32[1120,384]{1,0:T(8,128)} async-done(((f32[1120,1536]{1,0:T(8,128)}), f32[1120,384]{1,0:T(8,128)}) %reduce-scatter.63.cloned.1.call-update) | async-done | bytes 1720336 | tf_op jit(solution)/shard_map/reduce_scatter | solution.py:312
  1716.0 73.9 %reduce-scatter.61.cloned.1.call-done = f32[384,1120]{0,1:T(8,128)} async-done(((f32[1536,1120]{0,1:T(8,128)}), f32[384,1120]{0,1:T(8,128)}) %reduce-scatter.61.cloned.1.call-update) | async-done | bytes 1720336 | tf_op jit(solution)/shard_map/reduce_scatter | solution.py:311
  1789.8 77.8 %reduce-scatter.59.cloned.1.call-done = f32[384,1120]{0,1:T(8,128)} async-done(((f32[1536,1120]{0,1:T(8,128)}), f32[384,1120]{0,1:T(8,128)}) %reduce-scatter.59.cloned.1.call-update) | async-done | bytes 1720336 | tf_op jit(solution)/shard_map/reduce_scatter | solution.py:311
  1871.6 73.9 %reduce-scatter.57.cloned.1.call-done = f32[384,1120]{0,1:T(8,128)} async-done(((f32[1536,1120]{0,1:T(8,128)}), f32[384,1120]{0,1:T(8,128)}) %reduce-scatter.57.cloned.1.call-update) | async-done | bytes 1720336 | tf_op jit(solution)/shard_map/reduce_scatter | solution.py:310
  1945.4 77.8 %reduce-scatter.55.cloned.1.call-done = f32[384,1120]{0,1:T(8,128)} async-done(((f32[1536,1120]{0,1:T(8,128)}), f32[384,1120]{0,1:T(8,128)}) %reduce-scatter.55.cloned.1.call-update) | async-done | bytes 1720336 | tf_op jit(solution)/shard_map/reduce_scatter | solution.py:310
  2027.3 27.6 %reduce-scatter.53.cloned.1.call-done = f32[192,384]{1,0:T(8,128)} async-done(((f32[192,1536]{1,0:T(8,128)}), f32[192,384]{1,0:T(8,128)}) %reduce-scatter.53.cloned.1.call-update) | async-done | bytes 294928 | tf_op jit(solution)/shard_map/reduce_scatter | solution.py:309
  2054.9 31.5 %reduce-scatter.51.cloned.1.call-done = f32[192,384]{1,0:T(8,128)} async-done(((f32[192,1536]{1,0:T(8,128)}), f32[192,384]{1,0:T(8,128)}) %reduce-scatter.51.cloned.1.call-update) | async-done | bytes 294928 | tf_op jit(solution)/shard_map/reduce_scatter | solution.py:309
  2088.3 24.6 %reduce-scatter.83.cloned.1.call-done = f32[32,2]{1,0:T(8,128)} async-done(((f32[128,2]{1,0:T(8,128)}), f32[32,2]{1,0:T(8,128)}) %reduce-scatter.83.cloned.1.call-update) | async-done | bytes 272
  2114.3 33.1 %reduce-scatter.49.cloned.1.call-done = f32[384,256]{1,0:T(8,128)} async-done(((f32[1536,256]{1,0:T(8,128)}), f32[384,256]{1,0:T(8,128)}) %reduce-scatter.49.cloned.1.call-update) | async-done | bytes 393232 | tf_op jit(solution)/shard_map/reduce_scatter | solution.py:307
  2147.4 34.2 %reduce-scatter.47.cloned.1.call-done = f32[384,256]{1,0:T(8,128)} async-done(((f32[1536,256]{1,0:T(8,128)}), f32[384,256]{1,0:T(8,128)}) %reduce-scatter.47.cloned.1.call-update) | async-done | bytes 393232 | tf_op jit(solution)/shard_map/reduce_scatter | solution.py:307
  2183.6 68.5 %reduce-scatter.81.cloned.1.call-done = f32[192,1024]{1,0:T(8,128)} async-done(((f32[1536,1024]{1,0:T(8,128)}), f32[192,1024]{1,0:T(8,128)}) %reduce-scatter.81.cloned.1.call-update) | async-done | bytes 786448 | tf_op jit(solution)/shard_map/reduce_scatter | solution.py:73
  2260.3 14.5 psum.70
  (410 shorter events, 475.6 us)
Async XLA Ops:
  8.0 56.3 %all-gather.29.cloned.1.call-start = ((), (), s32[]{:S(2)}) async-start(), calls=%async_computation.30 | async-start | bytes 3538944 | tf_op jit(solution)/shard_map/all_gather | solution.py:69
  8.8 456.1 %copy-start.67 = (f32[1,1,192]{2,1,0:T(1,128)}, f32[1,1,192]{2,1,0:T(1,128)S(1)}, u32[]{:S(2)}) copy-start(f32[1,1,192]{2,1,0:T(1,128)S(1)} %get-tuple-element.93) | copy-start | bytes 2308
  8.9 979.8 %copy-start.60 = (f32[1,1,192]{2,1,0:T(1,128)}, f32[1,1,192]{2,1,0:T(1,128)S(1)}, u32[]{:S(2)}) copy-start(f32[1,1,192]{2,1,0:T(1,128)S(1)} %get-tuple-element.92) | copy-start | bytes 2308
  26.1 88.1 %all-gather.31.cloned.1.call-start = ((), (), s32[]{:S(2)}) async-start(), calls=%async_computation.31 | async-start | bytes 1179648 | tf_op jit(solution)/shard_map/all_gather | solution.py:173
  119.9 15.8 all-to-all-start.1
  125.2 90.4 %reduce-scatter.67.cloned.1.call-start = ((), (), s32[]{:S(2)}) async-start(), calls=%async_computation.58 | async-start | bytes 7077888 | tf_op jit(solution)/shard_map/reduce_scatter | solution.py:73
  146.1 89.8 %all-gather.49.cloned.1.call-start = ((), (), s32[]{:S(2)}) async-start(), calls=%async_computation.52 | async-start | bytes 4300800 | tf_op jit(solution)/shard_map/all_gather | solution.py:161
  149.0 120.6 %all-gather.33.cloned.1.call-start = ((), (), s32[]{:S(2)}) async-start(), calls=%async_computation.32 | async-start | bytes 3538944 | tf_op jit(solution)/shard_map/all_gather | solution.py:69
  216.9 233.2 %copy-start.4 = (f32[192,1024]{1,0:T(8,128)}, f32[192,1024]{1,0:T(8,128)S(1)}, u32[]{:S(2)}) copy-start(f32[192,1024]{1,0:T(8,128)S(1)} %get-tuple-element.53) | copy-start | bytes 2359300
  231.6 85.7 %all-gather.51.cloned.1.call-start = ((), (), s32[]{:S(2)}) async-start(), calls=%async_computation.53 | async-start | bytes 4300800 | tf_op jit(solution)/shard_map/all_gather | solution.py:162
  234.4 130.8 %all-gather.53.cloned.1.call-start = ((), (), s32[]{:S(2)}) async-start(), calls=%async_computation.54 | async-start | bytes 4300800 | tf_op jit(solution)/shard_map/all_gather | solution.py:163
  235.9 214.2 %reduce-scatter.69.cloned.1.call-start = ((), (), s32[]{:S(2)}) async-start(), calls=%async_computation.59 | async-start | bytes 7077888 | tf_op jit(solution)/shard_map/reduce_scatter | solution.py:73
  381.5 122.3 %all-gather.35.cloned.1.call-start = ((), (), s32[]{:S(2)}) async-start(), calls=%async_computation.33 | async-start | bytes 3538944 | tf_op jit(solution)/shard_map/all_gather | solution.py:69
  465.8 87.6 %all-gather.37.cloned.1.call-start = ((), (), s32[]{:S(2)}) async-start(), calls=%async_computation.34 | async-start | bytes 1179648 | tf_op jit(solution)/shard_map/all_gather | solution.py:173
  559.0 15.4 all-to-all-start.3
  564.5 89.3 %reduce-scatter.71.cloned.1.call-start = ((), (), s32[]{:S(2)}) async-start(), calls=%async_computation.60 | async-start | bytes 7077888 | tf_op jit(solution)/shard_map/reduce_scatter | solution.py:73
  584.8 116.6 %all-gather.57.cloned.1.call-start = ((), (), s32[]{:S(2)}) async-start(), calls=%async_computation.56 | async-start | bytes 4300800 | tf_op jit(solution)/shard_map/all_gather | solution.py:162
  585.4 155.8 %all-gather.39.cloned.1.call-start = ((), (), s32[]{:S(2)}) async-start(), calls=%async_computation.35 | async-start | bytes 3538944 | tf_op jit(solution)/shard_map/all_gather | solution.py:69
  668.1 320.6 %copy-start.54 = (f32[1024]{0:T(1024)}, f32[1024]{0:T(1024)S(1)}, u32[]{:S(2)}) copy-start(f32[1024]{0:T(1024)S(1)} %get-tuple-element.90) | copy-start | bytes 12292
  669.0 119.4 %all-gather.55.cloned.1.call-start = ((), (), s32[]{:S(2)}) async-start(), calls=%async_computation.55 | async-start | bytes 4300800 | tf_op jit(solution)/shard_map/all_gather | solution.py:161
  669.8 166.4 %all-gather.59.cloned.1.call-start = ((), (), s32[]{:S(2)}) async-start(), calls=%async_computation.57 | async-start | bytes 4300800 | tf_op jit(solution)/shard_map/all_gather | solution.py:163
  670.4 205.2 %all-gather.41.cloned.1.call-start = ((), (), s32[]{:S(2)}) async-start(), calls=%async_computation.36 | async-start | bytes 3538944 | tf_op jit(solution)/shard_map/all_gather | solution.py:69
  671.1 302.7 %reduce-scatter.75.cloned.1.call-start = ((), (), s32[]{:S(2)}) async-start(), calls=%async_computation.62 | async-start | bytes 7077888 | tf_op jit(solution)/shard_map/reduce_scatter | solution.py:73
  905.9 123.2 %all-gather.43.cloned.1.call-start = ((), (), s32[]{:S(2)}) async-start(), calls=%async_computation.37 | async-start | bytes 3538944 | tf_op jit(solution)/shard_map/all_gather | solution.py:69
  1032.6 15.7 all-to-all-start.4
  1038.4 60.8 %reduce-scatter.43.cloned.1.call-start = ((), (), s32[]{:S(2)}) async-start(), calls=%async_computation.38 | async-start | bytes 2359296 | tf_op jit(solution)/shard_map/reduce_scatter | solution.py:293
  1063.7 135.3 %reduce-scatter.77.cloned.1.call-start = ((), (), s32[]{:S(2)}) async-start(), calls=%async_computation.63 | async-start | bytes 7077888 | tf_op jit(solution)/shard_map/reduce_scatter | solution.py:73
  1130.9 138.7 %reduce-scatter.73.cloned.1.call-start = ((), (), s32[]{:S(2)}) async-start(), calls=%async_computation.61 | async-start | bytes 7077888 | tf_op jit(solution)/shard_map/reduce_scatter | solution.py:73
  1147.2 162.7 %all-gather.45.cloned.1.call-start = ((), (), s32[]{:S(2)}) async-start(), calls=%async_computation.39 | async-start | bytes 3538944 | tf_op jit(solution)/shard_map/all_gather | solution.py:69
  1272.3 133.7 %reduce-scatter.79.cloned.1.call-start = ((), (), s32[]{:S(2)}) async-start(), calls=%async_computation.64 | async-start | bytes 7077888 | tf_op jit(solution)/shard_map/reduce_scatter | solution.py:73
  1338.2 122.7 %all-gather.47.cloned.1.call-start = ((), (), s32[]{:S(2)}) async-start(), calls=%async_computation.40 | async-start | bytes 3538944 | tf_op jit(solution)/shard_map/all_gather | solution.py:69
  1464.5 15.9 all-to-all-start.6
  1470.5 92.3 %reduce-scatter.45.cloned.1.call-start = ((), (), s32[]{:S(2)}) async-start(), calls=%async_computation.41 | async-start | bytes 2359296 | tf_op jit(solution)/shard_map/reduce_scatter | solution.py:293
  1494.3 109.1 %reduce-scatter.85.cloned.1.call-start = ((), (), s32[]{:S(2)}) async-start(), calls=%async_computation.67 | async-start | bytes 81920
  1496.4 137.8 %reduce-scatter.65.cloned.1.call-start = ((), (), s32[]{:S(2)}) async-start(), calls=%async_computation.51 | async-start | bytes 8601600 | tf_op jit(solution)/shard_map/reduce_scatter | solution.py:312
  1505.5 206.4 %reduce-scatter.63.cloned.1.call-start = ((), (), s32[]{:S(2)}) async-start(), calls=%async_computation.50 | async-start | bytes 8601600 | tf_op jit(solution)/shard_map/reduce_scatter | solution.py:312
  1514.8 275.0 %reduce-scatter.61.cloned.1.call-start = ((), (), s32[]{:S(2)}) async-start(), calls=%async_computation.49 | async-start | bytes 8601600 | tf_op jit(solution)/shard_map/reduce_scatter | solution.py:311
  1524.6 343.0 %reduce-scatter.59.cloned.1.call-start = ((), (), s32[]{:S(2)}) async-start(), calls=%async_computation.48 | async-start | bytes 8601600 | tf_op jit(solution)/shard_map/reduce_scatter | solution.py:311
  1533.9 411.6 %reduce-scatter.57.cloned.1.call-start = ((), (), s32[]{:S(2)}) async-start(), calls=%async_computation.47 | async-start | bytes 8601600 | tf_op jit(solution)/shard_map/reduce_scatter | solution.py:310
  1543.2 480.1 %reduce-scatter.55.cloned.1.call-start = ((), (), s32[]{:S(2)}) async-start(), calls=%async_computation.46 | async-start | bytes 8601600 | tf_op jit(solution)/shard_map/reduce_scatter | solution.py:310
  1552.7 502.2 %reduce-scatter.53.cloned.1.call-start = ((), (), s32[]{:S(2)}) async-start(), calls=%async_computation.45 | async-start | bytes 1474560 | tf_op jit(solution)/shard_map/reduce_scatter | solution.py:309
  1557.8 528.6 %reduce-scatter.51.cloned.1.call-start = ((), (), s32[]{:S(2)}) async-start(), calls=%async_computation.44 | async-start | bytes 1474560 | tf_op jit(solution)/shard_map/reduce_scatter | solution.py:309
  1562.0 550.9 %reduce-scatter.83.cloned.1.call-start = ((), (), s32[]{:S(2)}) async-start(), calls=%async_computation.66 | async-start | bytes 81920
  1584.6 562.8 %reduce-scatter.49.cloned.1.call-start = ((), (), s32[]{:S(2)}) async-start(), calls=%async_computation.43 | async-start | bytes 1966080 | tf_op jit(solution)/shard_map/reduce_scatter | solution.py:307
  1588.7 592.9 %reduce-scatter.47.cloned.1.call-start = ((), (), s32[]{:S(2)}) async-start(), calls=%async_computation.42 | async-start | bytes 1966080 | tf_op jit(solution)/shard_map/reduce_scatter | solution.py:307
  1593.0 659.0 %reduce-scatter.81.cloned.1.call-start = ((), (), s32[]{:S(2)}) async-start(), calls=%async_computation.65 | async-start | bytes 7077888 | tf_op jit(solution)/shard_map/reduce_scatter | solution.py:73
  2027.3 247.6 %copy-start.29 = (f32[192,1024]{1,0:T(8,128)S(1)}, f32[192,1024]{1,0:T(8,128)}, u32[]{:S(2)}) copy-start(f32[192,1024]{1,0:T(8,128)} %get-tuple-element.45) | copy-start | bytes 2359300
  2027.3 247.6 %copy-start.63 = (f32[1024]{0:T(1024)S(1)}, f32[1024]{0:T(1024)}, u32[]{:S(2)}) copy-start(f32[1024]{0:T(1024)} %get-tuple-element.84) | copy-start | bytes 12292
  (73 other events, 2589.0 us)
Sparse Core Ops, SparseCore 0:
  26.2 38.0 all-gather.28
  91.4 22.6 all-gather.30
  146.2 69.3 reduce-scatter.66
  381.6 68.3 reduce-scatter.68
  906.0 67.7 reduce-scatter.74
  991.0 38.0 all-gather.42
  1063.8 35.3 reduce-scatter.42
  1131.0 67.8 reduce-scatter.76
  1201.2 68.3 reduce-scatter.72
  1422.9 38.0 all-gather.46
  1494.5 35.1 reduce-scatter.44
  1532.8 22.9 reduce-scatter.84
  1558.8 75.3 reduce-scatter.64
  1637.0 74.9 reduce-scatter.62
  1714.8 74.9 reduce-scatter.60
  1792.7 74.8 reduce-scatter.58
  1870.4 74.9 reduce-scatter.56
  1948.3 74.9 reduce-scatter.54
  2026.2 28.6 reduce-scatter.52
  2057.6 28.6 reduce-scatter.50
  2089.1 23.7 reduce-scatter.82
  2115.9 31.4 reduce-scatter.48
  2150.4 31.1 reduce-scatter.46
  2183.7 68.3 reduce-scatter.80
Sparse Core Ops, SparseCore 1:
  149.1 47.0 all-gather.48
  231.6 37.9 all-gather.32
  271.9 45.4 all-gather.50
  319.1 46.0 all-gather.52
  465.9 37.9 all-gather.34
  530.8 22.5 all-gather.36
  584.9 68.9 reduce-scatter.70
  655.5 45.9 all-gather.56
  703.5 37.6 all-gather.38
  743.0 45.4 all-gather.54
  790.1 46.0 all-gather.58
  837.9 37.6 all-gather.40
  1272.4 37.4 all-gather.44
  1338.3 67.6 reduce-scatter.78
where the time goes:
time: 2300 us; the launch traced here: 2280 us
  waiting for transfers between devices  1620 us (70%)
  blocking collectives  236 us (10%)
  matrix products  220 us (10%)
  local copies, waits for them, and re-layouts  97.7 us (4%)
  other arithmetic  63.8 us (3%)
  starting transfers between devices  25 us (1%)
    reduce_scatter x8, waiting for transfers between devices, summed_rows(): lax.psum_scatter(make_term(jnp.int32(0), lax.axis_size('col') * rows), 'c...  514 us
    all_gather x8, waiting for transfers between devices, spread(): return lax.all_gather(values, 'col', axis=0, tiled=True)  266 us
    reduce_scatter x2, waiting for transfers between devices, per_device(): lax.psum_scatter(d_gate_w, 'row', scatter_dimension=0, tiled=True)  152 us
    reduce_scatter x2, waiting for transfers between devices, per_device(): lax.psum_scatter(d_up_w, 'row', scatter_dimension=0, tiled=True)  152 us
    reduce_scatter x2, waiting for transfers between devices, per_device(): lax.psum_scatter(d_down, 'row', scatter_dimension=1, tiled=True)  108 us
    psum x8, blocking collectives, feature_total(): return lax.psum(jnp.sum(values, axis=0), 'col')  107 us
    all_gather x2, waiting for transfers between devices, per_device(): lax.all_gather(down_weight[layer], 'row', axis=1, tiled=True)  75.7 us
    dot_general x10, matrix products, contract_last(): lax.dot_general(left, right, (((1,), (1,)), ((), ())), preferred_element_...  71.6 us
  transfers between devices with their start and end apart: 42, of which 38 were waited for; matrix products, arithmetic and copies ran while one was open for 8% of the time, Pallas kernels for 0%

commit v1 on v0

--- a/solution.py
+++ b/solution.py
@@ -3,6 +3,8 @@
 import jax
 import jax.numpy as jnp
 from jax import lax
+from jax.experimental import pallas as pl
+from jax.experimental.pallas import tpu as pltpu
 from jax.sharding import PartitionSpec as P
 
 D = 1536
@@ -12,6 +14,679 @@
 LAYERS = 2
 SEQ_MAX = 512
 QB = 128
+MESH = pl.DeviceIdType.MESH
+LOW = jnp.bfloat16
+F32 = jnp.float32
+ANY = pl.BlockSpec(memory_space=pl.ANY)
+ONCHIP = pl.BlockSpec(memory_space=pltpu.VMEM)
+HALF = 208
+
+
+class Place:
+    def __init__(self):
+        self.r = lax.axis_index("row")
+        self.k = lax.axis_index("col")
+        self.z = self.k // 2
+        self.c = self.k % 2
+
+    def at(self, z, c):
+        return (self.r, 2 * z + c)
+
+    def rows(self):
+        x, y = self.r % 2, self.r // 2
+        return (2 * y + (1 - x), 2 * (1 - y) + x, 2 * (1 - y) + (1 - x))
+
+
+def remote(src, dst, send, recv, device):
+    return pltpu.make_async_remote_copy(
+        src_ref=src, dst_ref=dst, send_sem=send, recv_sem=recv, device_id=device, device_id_type=MESH
+    )
+
+
+class Later:
+    def __init__(self):
+        self.todo = []
+
+    def add(self, wait, cond=None):
+        self.todo.append((wait, cond))
+
+    def run(self):
+        for wait, cond in self.todo:
+            if cond is None:
+                wait()
+            else:
+                pl.when(cond)(wait)
+
+
+def greet(place, reach):
+    barrier = pltpu.get_barrier_semaphore()
+
+    def hail(device):
+        pl.semaphore_signal(barrier, inc=1, device_id=device, device_id_type=MESH)
+
+    if "all" in reach:
+        for rr in range(4):
+            for kk in range(8):
+                pl.when((place.r != rr) | (place.k != kk))(partial(hail, (rr, kk)))
+        pl.semaphore_wait(barrier, 31)
+        return
+    count = 0
+    if "rows" in reach:
+        for row in place.rows():
+            hail((row, place.k))
+        count += 3
+    if "col" in reach:
+        for kk in range(8):
+            pl.when(place.k != kk)(partial(hail, (place.r, kk)))
+        pl.semaphore_wait(barrier, count + 7)
+        return
+    hail(place.at(place.z, 1 - place.c))
+    count += 1
+    if "line" not in reach:
+        pl.semaphore_wait(barrier, count)
+        return
+    pl.when(place.z < 3)(partial(hail, place.at(jnp.minimum(place.z + 1, 3), place.c)))
+    pl.when(place.z > 0)(partial(hail, place.at(jnp.maximum(place.z - 1, 0), place.c)))
+    edge = (place.z == 0) | (place.z == 3)
+    pl.when(edge)(lambda: pl.semaphore_wait(barrier, count + 1))
+    pl.when(jnp.logical_not(edge))(lambda: pl.semaphore_wait(barrier, count + 2))
+
+
+class Cargo:
+    arrays = ()
+    outs = ()
+    scratch = ()
+    reach = "rows"
+    slow = False
+
+    def middle(self, place, ins, outs, scratch, later):
+        pass
+
+
+def part_of(ref, dim, row, size):
+    cut = pl.ds(pl.multiple_of(row * size, 128 if dim else 16), size)
+    return ref.at[:, cut] if dim else ref.at[cut, :]
+
+
+class GatherRows(Cargo):
+    def __init__(self, block, dim):
+        self.dim = dim
+        self.arrays = (block,)
+        full = list(block.shape)
+        full[dim] *= 4
+        self.size = block.shape[dim]
+        self.half = block.shape[0] // 32 * 16
+        self.rest = block.shape[0] - self.half
+        self.outs = (jax.ShapeDtypeStruct(tuple(full), block.dtype),)
+        self.scratch = (pltpu.SemaphoreType.DMA((6,)), pltpu.SemaphoreType.DMA((6,)), pltpu.SemaphoreType.DMA((1,)))
+
+    def halves(self, ref):
+        return ref.at[0 : self.half, :], ref.at[self.half :, :]
+
+    def spots(self, full, row):
+        if self.dim:
+            cut = pl.ds(pl.multiple_of(row * self.size, 128), self.size)
+            return full.at[0 : self.half, cut], full.at[self.half :, cut]
+        first = pl.multiple_of(row * self.size, 16)
+        return full.at[pl.ds(first, self.half), :], full.at[pl.ds(first + self.half, self.rest), :]
+
+    def copies(self, place, ins, outs, scratch):
+        (src,), (dst,), (send, recv, _) = ins, outs, scratch
+        x, y, d = place.rows()
+        block, mine = self.halves(src), self.spots(dst, place.r)
+        from_x, from_y = self.spots(dst, x), self.spots(dst, y)
+        out = [
+            remote(block[0], mine[0], send.at[0], recv.at[0], (x, place.k)),
+            remote(block[1], mine[1], send.at[1], recv.at[3], (y, place.k)),
+            remote(block[1], mine[1], send.at[2], recv.at[1], (x, place.k)),
+            remote(block[0], mine[0], send.at[3], recv.at[2], (y, place.k)),
+        ]
+        onward = [
+            remote(from_x[0], from_x[0], send.at[4], recv.at[4], (y, place.k)),
+            remote(from_y[1], from_y[1], send.at[5], recv.at[5], (x, place.k)),
+        ]
+        return out, onward
+
+    def start(self, place, ins, outs, scratch, later):
+        (src,), (dst,), (_, _, keep_sem) = ins, outs, scratch
+        for copy in self.copies(place, ins, outs, scratch)[0]:
+            copy.start()
+        keep = pltpu.make_async_copy(src, part_of(dst, self.dim, place.r, self.size), keep_sem.at[0])
+        keep.start()
+        later.add(keep.wait)
+
+    def middle(self, place, ins, outs, scratch, later):
+        (src,), (dst,), (send, recv, _) = ins, outs, scratch
+        x, y, d = place.rows()
+        from_x, from_y, from_d = self.spots(dst, x), self.spots(dst, y), self.spots(dst, d)
+        block = self.halves(src)
+
+        def arrived(view, sem, device):
+            return remote(view, view, send.at[0], recv.at[sem], device)
+
+        out, onward = self.copies(place, ins, outs, scratch)
+        arrived(from_x[0], 0, (x, place.k)).wait_recv()
+        onward[0].start()
+        arrived(from_y[1], 3, (y, place.k)).wait_recv()
+        onward[1].start()
+        for view, sem, row in ((from_x[1], 1, x), (from_y[0], 2, y), (from_d[0], 4, y), (from_d[1], 5, x)):
+            later.add(arrived(view, sem, (row, place.k)).wait_recv)
+        for copy in (*out, *onward):
+            later.add(copy.wait_send)
+
+
+class ScatterRows(Cargo):
+    def __init__(self, grad, dim):
+        self.dim = dim
+        self.arrays = (grad,)
+        part = list(grad.shape)
+        part[dim] //= 4
+        self.size = part[dim]
+        self.half = part[0] // 32 * 16
+        self.rest = part[0] - self.half
+        self.outs = (jax.ShapeDtypeStruct((2, *part), grad.dtype),)
+        upper, lower = pltpu.VMEM((self.half, part[1]), grad.dtype), pltpu.VMEM((self.rest, part[1]), grad.dtype)
+        self.scratch = (
+            *(upper, lower, lower, upper, lower, upper),
+            pltpu.SemaphoreType.DMA((6,)),
+            pltpu.SemaphoreType.DMA((6,)),
+            pltpu.SemaphoreType.DMA((2,)),
+        )
+
+    def spots(self, full, row):
+        if self.dim:
+            cut = pl.ds(pl.multiple_of(row * self.size, 128), self.size)
+            return full.at[0 : self.half, cut], full.at[self.half :, cut]
+        first = pl.multiple_of(row * self.size, 16)
+        return full.at[pl.ds(first, self.half), :], full.at[pl.ds(first + self.half, self.rest), :]
+
+    def copies(self, place, ins, outs, scratch):
+        (src,), (dst,) = ins, outs
+        via_x, via_y, own_x, own_y, sum_x, sum_y, send, recv, keep = scratch
+        x, y, d = place.rows()
+        for_x, for_y, for_d = self.spots(src, x), self.spots(src, y), self.spots(src, d)
+        slot_x = dst.at[0, 0 : self.half, :], dst.at[0, self.half :, :]
+        slot_y = dst.at[1, 0 : self.half, :], dst.at[1, self.half :, :]
+        first = [
+            remote(for_d[0], via_x, send.at[0], recv.at[0], (x, place.k)),
+            remote(for_d[1], via_y, send.at[1], recv.at[1], (y, place.k)),
+            remote(for_x[0], slot_x[0], send.at[2], recv.at[2], (x, place.k)),
+            remote(for_y[1], slot_y[1], send.at[3], recv.at[3], (y, place.k)),
+        ]
+        held = [
+            pltpu.make_async_copy(for_x[1], own_x, keep.at[0]),
+            pltpu.make_async_copy(for_y[0], own_y, keep.at[1]),
+        ]
+        last = [
+            remote(sum_x, slot_x[1], send.at[4], recv.at[4], (x, place.k)),
+            remote(sum_y, slot_y[0], send.at[5], recv.at[5], (y, place.k)),
+        ]
+        return first, held, last
+
+    def start(self, place, ins, outs, scratch, later):
+        first, held, _ = self.copies(place, ins, outs, scratch)
+        for copy in (*first, *held):
+            copy.start()
+
+    def middle(self, place, ins, outs, scratch, later):
+        via_x, via_y, own_x, own_y, sum_x, sum_y, *_ = scratch
+        first, held, last = self.copies(place, ins, outs, scratch)
+        held[0].wait()
+        first[1].wait_recv()
+        add_into(sum_x, [own_x, via_y])
+        last[0].start()
+        held[1].wait()
+        first[0].wait_recv()
+        add_into(sum_y, [own_y, via_x])
+        last[1].start()
+        for copy in (*first, *last):
+            later.add(copy.wait_send)
+        for copy in (*first[2:], *last):
+            later.add(copy.wait_recv)
+
+
+class Swap(Cargo):
+    reach = "line"
+
+    def __init__(self, *arrays):
+        self.arrays = arrays
+        self.outs = tuple(jax.ShapeDtypeStruct(a.shape, a.dtype) for a in arrays)
+        self.scratch = (pltpu.SemaphoreType.DMA((len(arrays),)), pltpu.SemaphoreType.DMA((len(arrays),)))
+
+    def start(self, place, ins, outs, scratch, later):
+        send, recv = scratch
+        for i, (src, dst) in enumerate(zip(ins, outs)):
+            copy = remote(src, dst, send.at[i], recv.at[i], place.at(place.z, 1 - place.c))
+            copy.start()
+            later.add(copy.wait)
+
+
+def tile_owner(z, t):
+    if t < 3:
+        head = 3 * z + t
+        return head // 2, head % 2
+    return 3 + t, z // 2
+
+
+class HeadsToChips(Cargo):
+    reach = "col"
+
+    def __init__(self, tiles):
+        self.arrays = (tiles,)
+        self.outs = (jax.ShapeDtypeStruct((HALF, 5 * HD), LOW),)
+        self.scratch = (pltpu.SemaphoreType.DMA((2, 2, 2)), pltpu.SemaphoreType.DMA((5,)))
+
+    def start(self, place, ins, outs, scratch, later):
+        (tiles,), (slab,), (send, recv) = ins, outs, scratch
+        r, k, z, c = place.r, place.k, place.z, place.c
+        query = k < 6
+        for second in range(2):
+            for i in range(2):
+                head = 2 * k + i
+                chip = jnp.where(query, head // 3, 2 * i + second)
+                t = jnp.where(query, head % 3, k - 3)
+                spot = slab.at[:, pl.ds(pl.multiple_of(t * HD, HD), HD)]
+                for core in range(2):
+                    here = k == 2 * chip + core
+                    away = jnp.logical_not(here)
+                    if second == 1:
+                        here, away = here & (k >= 6), away & (k >= 6)
+                    sem = send.at[i, second, core]
+                    copy = remote(tiles.at[i, core], spot, sem, recv.at[t], (r, 2 * chip + core))
+                    pl.when(away)(copy.start)
+                    later.add(copy.wait_send, away)
+                    keep = pltpu.make_async_copy(tiles.at[i, core], spot, sem)
+                    pl.when(here)(keep.start)
+                    later.add(keep.wait, here)
+        for t in range(5):
+            owner, _ = tile_owner(z, t)
+            came = remote(
+                tiles.at[0, 0], slab.at[:, t * HD : (t + 1) * HD], send.at[0, 0, 0], recv.at[t], (r, owner)
+            )
+            later.add(came.wait_recv, k != owner)
+
+
+class HeadsToOwners(Cargo):
+    reach = "col"
+
+    def __init__(self, slab):
+        self.arrays = (slab,)
+        self.outs = (jax.ShapeDtypeStruct((2, 2, 2, HALF, HD), LOW),)
+        self.scratch = (pltpu.SemaphoreType.DMA((5,)), pltpu.SemaphoreType.DMA((2, 2, 2)))
+
+    def start(self, place, ins, outs, scratch, later):
+        (slab,), (tiles,), (send, recv) = ins, outs, scratch
+        r, k, z, c = place.r, place.k, place.z, place.c
+        for t in range(5):
+            owner, i = tile_owner(z, t)
+            which = z % 2 if t >= 3 else 0
+            view, spot = slab.at[:, t * HD : (t + 1) * HD], tiles.at[i, c, which]
+            here = k == owner
+            copy = remote(view, spot, send.at[t], recv.at[i, c, which], (r, owner))
+            pl.when(jnp.logical_not(here))(copy.start)
+            later.add(copy.wait_send, jnp.logical_not(here))
+            keep = pltpu.make_async_copy(view, spot, send.at[t])
+            pl.when(here)(keep.start)
+            later.add(keep.wait, here)
+        for i in range(2):
+            for which in range(2):
+                chip = jnp.where(k < 6, (2 * k + i) // 3, 2 * i + which)
+                for core in range(2):
+                    wanted = k != 2 * chip + core
+                    if which == 1:
+                        wanted = wanted & (k >= 6)
+                    came = remote(
+                        slab.at[:, 0:HD],
+                        tiles.at[i, core, which],
+                        send.at[0],
+                        recv.at[i, core, which],
+                        (r, 2 * chip + core),
+                    )
+                    later.add(came.wait_recv, wanted)
+
+
+class Exchange(Cargo):
+    def __init__(self, chunks, every_row=False):
+        self.arrays = (chunks,)
+        self.rows_too = every_row
+        self.reach = "all" if every_row else "col"
+        lead = (4,) if every_row else ()
+        self.outs = (jax.ShapeDtypeStruct((*lead, *chunks.shape), chunks.dtype),)
+        self.scratch = (pltpu.SemaphoreType.DMA((4, 8)), pltpu.SemaphoreType.DMA((4, 8)))
+
+    def start(self, place, ins, outs, sems, later):
+        (src,), (dst,), (send, recv) = ins, outs, sems
+        r, k = place.r, place.k
+        for rr in range(4) if self.rows_too else (None,):
+            to_row = r if rr is None else rr
+            for kk in range(8):
+                here = (k == kk) if rr is None else (k == kk) & (r == rr)
+                mine = dst.at[k] if rr is None else dst.at[r, k]
+                theirs = dst.at[kk] if rr is None else dst.at[rr, kk]
+                at = 0 if rr is None else rr
+                my_at = 0 if rr is None else r
+                copy = remote(src.at[kk], mine, send.at[at, kk], recv.at[my_at, k], (to_row, kk))
+                pl.when(jnp.logical_not(here))(copy.start)
+                later.add(copy.wait_send, jnp.logical_not(here))
+                came = remote(src.at[kk], theirs, send.at[at, kk], recv.at[at, kk], (to_row, kk))
+                later.add(came.wait_recv, jnp.logical_not(here))
+                keep = pltpu.make_async_copy(src.at[kk], mine, send.at[at, kk])
+                pl.when(here)(keep.start)
+                later.add(keep.wait, here)
+
+
+def add_into(dst, views):
+    rows = dst.shape[0]
+
+    def step(i, carry):
+        cut = pl.ds(pl.multiple_of(i * 16, 16), 16)
+        total = views[0][cut, :].astype(F32)
+        for view in views[1:]:
+            total = total + view[cut, :].astype(F32)
+        dst[cut, :] = total.astype(dst.dtype)
+        return carry
+
+    lax.fori_loop(0, rows // 16, step, 0)
+
+
+def gather_line(place, block, full, sems, later, both, middle):
+    send_r, send_l, send_p, recv, keep_sem = sems
+    z, c = place.z, place.c
+
+    def spot(zz, cc):
+        return full.at[2 * zz + cc] if both else full.at[zz]
+
+    def arrival(zz, cc):
+        return recv.at[2 * zz + cc]
+
+    def pass_on(src, zz, slot):
+        dst, sem = spot(zz, c), arrival(zz, c)
+
+        def go(send, device):
+            return remote(src, dst, send.at[slot], sem, device)
+
+        return (
+            go(send_r, place.at(jnp.minimum(z + 1, 3), c)),
+            go(send_l, place.at(jnp.maximum(z - 1, 0), c)),
+            go(send_p, place.at(z, 1 - c)),
+        )
+
+    right, left, partner = pass_on(block, z, 0)
+    pl.when(z < 3)(right.start)
+    pl.when(z > 0)(left.start)
+    later.add(right.wait_send, z < 3)
+    later.add(left.wait_send, z > 0)
+    if both:
+        partner.start()
+        later.add(partner.wait_send)
+    keep = pltpu.make_async_copy(block, spot(z, c), keep_sem.at[0])
+    keep.start()
+    later.add(keep.wait)
+    for t in range(1, 4):
+        if t == 2:
+            middle()
+        for way in (-1, 1):
+            there = z + way * t
+            valid = (there >= 0) & (there <= 3)
+            zz = jnp.clip(there, 0, 3)
+            right, left, partner = pass_on(spot(zz, c), zz, t if way == -1 else 3 + t)
+            onward, may = (right, z < 3) if way == -1 else (left, z > 0)
+
+            @pl.when(valid)
+            def _(onward=onward, may=may, partner=partner):
+                onward.wait_recv()
+                pl.when(may)(onward.start)
+                if both:
+                    partner.start()
+
+            later.add(onward.wait_send, valid & may)
+            if both:
+                later.add(partner.wait_send, valid)
+    if both:
+        for zz in range(4):
+            came = remote(block, spot(zz, 1 - c), send_p.at[0], arrival(zz, 1 - c), place.at(z, 1 - c))
+            later.add(came.wait_recv)
+
+
+def reduce_line(place, part, out, from_p, from_r, from_l, held, sems, later, both, middle):
+    send_p, recv_p, send, recv_r, recv_l = sems
+    z, c = place.z, place.c
+    right_at, left_at = place.at(jnp.minimum(z + 1, 3), c), place.at(jnp.maximum(z - 1, 0), c)
+
+    def own(j):
+        return part.at[2 * j + c] if both else part.at[j]
+
+    def partner(j):
+        return remote(part.at[2 * j + 1 - c], from_p.at[j], send_p.at[j], recv_p.at[j], place.at(z, 1 - c))
+
+    def moving(j, buffer, sem, device):
+        return remote(held.at[j], buffer.at[j], send.at[j], sem.at[j], device)
+
+    if both:
+        for j in (3, 0, 2, 1):
+            copy = partner(j)
+            copy.start()
+            later.add(copy.wait_send)
+
+    def terms(j):
+        if both:
+            partner(j).wait_recv()
+            return [own(j), from_p.at[j]]
+        return [own(j)]
+
+    for s in range(3):
+        if s == 2:
+            middle()
+        for go_right in (True, False):
+            if go_right:
+                j, valid, first = 3 - s + z, z <= s, z == 0
+                buffer, sem, device = from_r, recv_r, right_at
+            else:
+                j, valid, first = s - 3 + z, z >= 3 - s, z == 3
+                buffer, sem, device = from_l, recv_l, left_at
+            j = jnp.clip(j, 0, 3)
+            copy = moving(j, buffer, sem, device)
+
+            @pl.when(valid & first)
+            def _(j=j, copy=copy):
+                add_into(held.at[j], terms(j))
+                copy.start()
+
+            @pl.when(valid & jnp.logical_not(first))
+            def _(j=j, copy=copy, buffer=buffer):
+                views = terms(j)
+                copy.wait_recv()
+                add_into(held.at[j], [*views, buffer.at[j]])
+                copy.start()
+
+            later.add(copy.wait_send, valid)
+    views = terms(z)
+    last_r, last_l = moving(z, from_r, recv_r, right_at), moving(z, from_l, recv_l, left_at)
+
+    @pl.when(z == 0)
+    def _():
+        last_l.wait_recv()
+        add_into(out, [*views, from_l.at[z]])
+
+    @pl.when(z == 3)
+    def _():
+        last_r.wait_recv()
+        add_into(out, [*views, from_r.at[z]])
+
+    @pl.when((z > 0) & (z < 3))
+    def _():
+        last_r.wait_recv()
+        last_l.wait_recv()
+        add_into(out, [*views, from_r.at[z], from_l.at[z]])
+
+
+class Names:
+    def __init__(self):
+        self.next = 0
+
+    def take(self):
+        self.next += 1
+        return self.next - 1
+
+
+def carry_kernel(body, reach, n_in, n_out, n_scratch, cargo, *refs):
+    refs = list(refs)
+
+    def pop(n):
+        taken = refs[:n]
+        del refs[:n]
+        return taken
+
+    ins = pop(n_in)
+    cargo_ins = [pop(len(item.arrays)) for item in cargo]
+    outs = pop(n_out)
+    cargo_outs = [pop(len(item.outs)) for item in cargo]
+    scratch = pop(n_scratch)
+    cargo_scratch = [pop(len(item.scratch)) for item in cargo]
+    place = Place()
+    later = Later()
+    loads = list(zip(cargo, cargo_ins, cargo_outs, cargo_scratch))
+    greet(place, {reach, *(item.reach for item in cargo)})
+    for item, *theirs in loads:
+        item.start(place, *theirs, later)
+
+    def middle():
+        for item, *theirs in loads:
+            item.middle(place, *theirs, later)
+
+    body(place, ins, outs, scratch, later, middle)
+    later.run()
+
+
+def carry_call(names, body, reach, arrays, in_specs, outs, out_specs, scratch, cargo, name=None):
+    call = pl.pallas_call(
+        partial(carry_kernel, body, reach, len(arrays), len(outs), len(scratch), cargo),
+        out_shape=[*outs, *(o for item in cargo for o in item.outs)],
+        in_specs=[*in_specs, *(ANY for item in cargo for _ in item.arrays)],
+        out_specs=[*out_specs, *(ANY for item in cargo for _ in item.outs)],
+        scratch_shapes=[*scratch, *(s for item in cargo for s in item.scratch)],
+        compiler_params=pltpu.CompilerParams(
+            collective_id=names.take(), has_side_effects=True, vmem_limit_bytes=40 * 2**20
+        ),
+        name=name,
+    )
+    results = list(call(*arrays, *(a for item in cargo for a in item.arrays)))
+    main = results[: len(outs)]
+    rest = results[len(outs) :]
+    loads = []
+    for item in cargo:
+        loads.append(rest[: len(item.outs)])
+        rest = rest[len(item.outs) :]
+    return main, loads
+
+
+def gather_tokens(names, block, cargo, both=True, name=None):
+    tokens, width = block.shape
+    blocks = 8 if both else 4
+
+    def body(place, ins, outs, scratch, later, middle):
+        gather_line(place, ins[0], outs[0], scratch, later, both, middle)
+
+    (full,), loads = carry_call(
+        names,
+        body,
+        "line",
+        [block],
+        [ONCHIP],
+        [jax.ShapeDtypeStruct((blocks, tokens, width), block.dtype)],
+        [ANY],
+        [
+            pltpu.SemaphoreType.DMA((7,)),
+            pltpu.SemaphoreType.DMA((7,)),
+            pltpu.SemaphoreType.DMA((7,)),
+            pltpu.SemaphoreType.DMA((8,)),
+            pltpu.SemaphoreType.DMA((1,)),
+        ],
+        cargo,
+        name=name,
+    )
+    return full.reshape(blocks * tokens, width), loads
+
+
+def reduce_tokens(names, part, cargo, both=True, name=None):
+    blocks = 8 if both else 4
+    tokens, width = part.shape[0] // blocks, part.shape[1]
+
+    def body(place, ins, outs, scratch, later, middle):
+        from_p, from_r, from_l, held, *sems = scratch
+        reduce_line(place, ins[0], outs[0], from_p, from_r, from_l, held, sems, later, both, middle)
+
+    (total,), loads = carry_call(
+        names,
+        body,
+        "line",
+        [part.reshape(blocks, tokens, width)],
+        [ONCHIP],
+        [jax.ShapeDtypeStruct((tokens, width), F32)],
+        [ONCHIP],
+        [
+            *[pltpu.VMEM((4, tokens, width), LOW)] * 4,
+            *[pltpu.SemaphoreType.DMA((4,))] * 5,
+        ],
+        cargo,
+        name=name,
+    )
+    return total, loads
+
+
+def stages_call(names, stages, name=None):
+    cargo = [item for stage in stages for item in stage]
+    arrays, outs, scratch = [], [], []
+    for item in cargo:
+        arrays += [a for a in item.arrays if not isinstance(a, From)]
+        outs += item.outs
+        scratch += item.scratch
+    n_in, n_out = len(arrays), len(outs)
+
+    def kernel(*refs):
+        ins, made, held = list(refs[:n_in]), list(refs[n_in : n_in + n_out]), list(refs[n_in + n_out :])
+        place = Place()
+        greet(place, {item.reach for item in cargo})
+        out_refs = {}
+        last = Later()
+        for stage in stages:
+            later = Later()
+            begun = []
+            for item in stage:
+                mine = [out_refs[a.item][a.at] if isinstance(a, From) else ins.pop(0) for a in item.arrays]
+                out_refs[item] = [made.pop(0) for _ in item.outs]
+                kept = [held.pop(0) for _ in item.scratch]
+                begun.append((item, mine, out_refs[item], kept, last if item.slow else later))
+            for item, *theirs in begun:
+                item.start(place, *theirs)
+            for item, *theirs in begun:
+                item.middle(place, *theirs)
+            later.run()
+        last.run()
+
+    results = list(
+        pl.pallas_call(
+            kernel,
+            out_shape=outs,
+            in_specs=[ANY] * n_in,
+            out_specs=[ANY] * n_out,
+            scratch_shapes=scratch,
+            compiler_params=pltpu.CompilerParams(
+                collective_id=names.take(), has_side_effects=True, vmem_limit_bytes=40 * 2**20
+            ),
+            name=name,
+        )(*arrays)
+    )
+    loads = []
+    for item in cargo:
+        loads.append([results.pop(0) for _ in item.outs])
+    return loads
+
+
+class From:
+    def __init__(self, item, at=0):
+        self.item, self.at = item, at
+        self.shape, self.dtype = item.outs[at].shape, item.outs[at].dtype
 
 
 eps_norm = 1e-06
@@ -327,6 +1002,329 @@
     )
 
 
+def softmax_scores(queries, keys, mask):
+    scores = jnp.einsum("htd,ud->htu", queries, keys, preferred_element_type=F32) * HD ** (-0.5)
+    return jnp.where(mask[None], scores, neg_fill)
+
+
+def dot(a, b):
+    return jnp.dot(a, b, preferred_element_type=F32)
+
+
+def dot_t(a, b):
+    return lax.dot_general(a, b, (((1,), (1,)), ((), ())), preferred_element_type=F32)
+
+
+def t_dot(a, b):
+    return lax.dot_general(a, b, (((0,), (0,)), ((), ())), preferred_element_type=F32)
+
+
+def turn(values, cosine, sine):
+    half = HD // 2
+    turned = jnp.concatenate([-values[..., half:], values[..., :half]], axis=-1)
+    return values * cosine + turned * sine
+
+
+def turn_back(grads, cosine, sine):
+    half = HD // 2
+    lifted = grads * sine
+    turned = jnp.concatenate([lifted[..., half:], -lifted[..., :half]], axis=-1)
+    return grads * cosine + turned
+
+
+def norm_on(residual, gain):
+    scale = lax.rsqrt(jnp.mean(residual * residual, axis=1, keepdims=True) + eps_norm)
+    return scale, (residual * scale * gain[None, :]).astype(LOW)
+
+
+def norm_back(d_normed, residual, scale, gain):
+    weighted = d_normed * gain[None, :]
+    inner = jnp.sum(weighted * residual, axis=1, keepdims=True)
+    d_residual = weighted * scale - residual * (scale * scale * scale) * inner / D
+    d_gain = jnp.sum(d_normed * residual * scale, axis=0)
+    return d_residual, d_gain
+
+
+def per_device_line(
+    hidden_states,
+    out_grad,
+    lengths,
+    norm_gains,
+    qkv_weight,
+    qkv_bias,
+    out_weight,
+    gate_weight,
+    up_weight,
+    down_weight,
+):
+    names = Names()
+    tok_row = hidden_states.shape[1]
+    row_at = lax.axis_index("row")
+    col_at = lax.axis_index("col")
+    core = col_at % 2
+    starts = row_starts(lengths[0], tok_row)
+    places = jnp.arange(tok_row, dtype=jnp.int32)
+    cosine, sine = rope_tables(places - starts)
+    cosine, sine = cosine.T[:, None], sine.T[:, None]
+
+    def own(values):
+        cut = values.reshape(4, 2, QB, *values.shape[1:])
+        return lax.dynamic_index_in_dim(cut, core, 1, keepdims=False).reshape(4 * QB, *values.shape[1:])
+
+    mask = (places[None, :] >= own(starts)[:, None]) & (places[None, :] <= own(places)[:, None])
+
+    def head_tiles(layer):
+        biases = jnp.zeros((2, 1, 16, HD), LOW)
+        biases = lax.dynamic_update_slice(biases, qkv_bias[layer][:, None, None], (0, 0, 0, row_at * (HD // 4)))
+        tiles = qkv_weight[layer].reshape(2, D // 8, 2, HD).transpose(2, 0, 1, 3)
+        return jnp.concatenate([tiles, jnp.broadcast_to(biases, (2, 2, 16, HD))], axis=2)
+
+    def slab_of(mine, theirs, out_mine, out_theirs):
+        first, second = jnp.where(core == 0, mine, theirs), jnp.where(core == 0, theirs, mine)
+        both = jnp.stack([first.reshape(4, HALF, 5 * HD), second.reshape(4, HALF, 5 * HD)], axis=1)
+        w_qkv = both[:, :, : D // 8].reshape(D, 5 * HD)
+        bias = jnp.sum(both[:, 0, D // 8].astype(F32), axis=0)
+        w_out = jnp.concatenate(
+            [jnp.where(core == 0, out_mine, out_theirs), jnp.where(core == 0, out_theirs, out_mine)], axis=0
+        )
+        return w_qkv, bias, w_out
+
+    arrivals = jnp.concatenate(
+        [
+            hidden_states.T.reshape(8, QB, D // 8),
+            out_grad.T.reshape(8, QB, D // 8),
+            jnp.broadcast_to(
+                jnp.pad(norm_gains.reshape(2 * LAYERS, D // 8), ((0, 16 - 2 * LAYERS), (0, 0))), (8, 16, D // 8)
+            ),
+        ],
+        axis=1,
+    )
+    spread = Exchange(arrivals)
+    spread.slow = True
+    to_chips = [HeadsToChips(head_tiles(layer)) for layer in range(LAYERS)]
+    to_chips[1].slow = True
+    slab_rows, out_rows = GatherRows(From(to_chips[0]), 0), GatherRows(out_weight[0], 1)
+    swap = Swap(From(slab_rows), From(out_rows))
+    loads = stages_call(
+        names, [[to_chips[0]], [slab_rows, out_rows, spread, to_chips[1]], [swap]], name="open"
+    )
+    (_,), (mine,), (out_mine,), (came,), (slab_next,), (theirs, out_theirs) = loads
+    load = (mine, theirs, out_mine, out_theirs)
+    came = came.transpose(1, 0, 2).reshape(2 * QB + 16, D)
+    residual = came[:QB].astype(F32)
+    grad = came[QB : 2 * QB].astype(F32)
+    gains = came[2 * QB : 2 * QB + 2 * LAYERS].astype(F32).reshape(LAYERS, 2, D)
+
+    def weights_in(layer):
+        return [GatherRows(gate_weight[layer], 0), GatherRows(up_weight[layer], 0), GatherRows(down_weight[layer], 1)]
+
+    sent = weights_in(0)
+    grad_full_last, ((w_gate,),) = gather_tokens(names, grad.astype(LOW), sent[:1], name="gather_three_1")
+    saved = []
+    for layer in range(LAYERS):
+        if layer == 1:
+            mine, out_mine, (w_gate,) = load
+        scale_one, normed_one = norm_on(residual, gains[layer, 0])
+        if layer == 0:
+            normed_one, _ = lax.optimization_barrier((normed_one, grad_full_last))
+        cargo = [sent[1]] if layer == 0 else [sent[1], Swap(mine, out_mine)]
+        full_one, loads = gather_tokens(names, normed_one, cargo, name=f"gather_one_{layer}")
+        w_up = loads[0][0]
+        if layer == 1:
+            load = (mine, loads[1][0], out_mine, loads[1][1])
+        w_qkv, bias, w_out = slab_of(*load)
+        raw = (dot(full_one, w_qkv) + bias[None]).reshape(tok_row, 5, HD)
+        turned = jnp.concatenate([turn(raw[:, :4], cosine, sine), raw[:, 4:]], axis=1).astype(LOW)
+        queries = own(turned[:, :3]).transpose(1, 0, 2)
+        keys, values = turned[:, 3], turned[:, 4]
+        masked = softmax_scores(queries, keys, mask)
+        row_top = jnp.max(masked, axis=-1, keepdims=True)
+        lifted = jnp.exp(masked - row_top)
+        row_mass = jnp.sum(lifted, axis=-1, keepdims=True)
+        probs = (lifted / row_mass).astype(LOW)
+        log_mass = row_top + jnp.log(row_mass)
+        mixed = jnp.einsum("htu,ud->thd", probs, values, preferred_element_type=F32)
+        mixed = mixed.astype(LOW).reshape(4 * QB, 3 * HD)
+        attention, ((w_down,),) = reduce_tokens(
+            names, dot(mixed, w_out).astype(LOW), [sent[2]], both=False, name=f"reduce_one_{layer}"
+        )
+        residual_mid = residual + attention
+        scale_two, normed_two = norm_on(residual_mid, gains[layer, 1])
+        cargo = []
+        if layer == 0:
+            sent = weights_in(1)
+            cargo = sent[:1]
+        full_two, loads_two = gather_tokens(names, normed_two, cargo, name=f"gather_two_{layer}")
+        gate = dot(full_two, w_gate)
+        up = dot(full_two, w_up)
+        hidden = (gate * jax.nn.sigmoid(gate) * up).astype(LOW)
+        cargo = [GatherRows(slab_next, 0), GatherRows(out_weight[1], 1)] if layer == 0 else []
+        feed, loads = reduce_tokens(names, dot(hidden, w_down).astype(LOW), cargo, name=f"reduce_two_{layer}")
+        saved.append(
+            (
+                residual,
+                scale_one,
+                full_one,
+                queries,
+                keys,
+                values,
+                log_mass,
+                mixed,
+                residual_mid,
+                scale_two,
+                full_two,
+                gate,
+                up,
+                hidden,
+                (w_qkv, w_out, w_gate, w_up, w_down),
+            )
+        )
+        residual = residual_mid + feed
+        if layer == 0:
+            load = (loads[0][0], loads[1][0], loads_two[0])
+    states = residual.astype(LOW)
+
+    def own_part(full, dim):
+        size = full.shape[dim] // 4
+        return lax.dynamic_slice_in_dim(full, row_at * size, size, dim)
+
+    def settle(full, dim, slots):
+        return jnp.sum(slots.astype(F32), axis=0) + own_part(full, dim).astype(F32)
+
+    def settle_heads(tiles):
+        total = tiles[:, :, 0].astype(F32) + jnp.where(col_at >= 6, tiles[:, :, 1].astype(F32), 0.0)
+        weight = total[:, :, : D // 8].transpose(1, 2, 0, 3).reshape(D // 4, 2 * HD)
+        bias = lax.dynamic_slice_in_dim(total[:, 0, D // 8], row_at * (HD // 4), HD // 4, 1)
+        return weight, bias
+
+    grads = {}
+    gain_terms = [None] * LAYERS
+    waiting = None
+    for layer in reversed(range(LAYERS)):
+        (
+            residual_in,
+            scale_one,
+            full_one,
+            queries,
+            keys,
+            values,
+            log_mass,
+            mixed,
+            residual_mid,
+            scale_two,
+            full_two,
+            gate,
+            up,
+            hidden,
+            (w_qkv, w_out, w_gate, w_up, w_down),
+        ) = saved[layer]
+        if layer == LAYERS - 1:
+            grad_full = grad_full_last
+        else:
+            grad_full, loads = gather_tokens(
+                names,
+                grad.astype(LOW),
+                [ScatterRows(waiting[0], 0), ScatterRows(waiting[1], 1)],
+                name=f"gather_three_{layer}",
+            )
+            slab_sum = settle(waiting[0], 0, loads[0][0]).astype(LOW)
+            grads["out", layer + 1] = settle(waiting[1], 1, loads[1][0])
+        d_down = t_dot(hidden, grad_full).astype(LOW)
+        d_hidden = dot_t(grad_full, w_down)
+        squash = jax.nn.sigmoid(gate)
+        d_gate = (d_hidden * up * squash * (1.0 + gate * (1.0 - squash))).astype(LOW)
+        d_up = (d_hidden * gate * squash).astype(LOW)
+        d_normed = (dot_t(d_gate, w_gate) + dot_t(d_up, w_up)).astype(LOW)
+        cargo = [ScatterRows(d_down, 1)]
+        if layer < LAYERS - 1:
+            cargo.append(HeadsToOwners(slab_sum))
+        d_normed_two, loads = reduce_tokens(names, d_normed, cargo, name=f"reduce_three_{layer}")
+        if layer < LAYERS - 1:
+            grads["qkv", layer + 1] = settle_heads(loads[1][0])
+        grads["down", layer] = settle(d_down, 1, loads[0][0])
+        d_gate_w = t_dot(full_two, d_gate).astype(LOW)
+        d_up_w = t_dot(full_two, d_up).astype(LOW)
+        d_residual, d_gain_two = norm_back(d_normed_two, residual_mid, scale_two, gains[layer, 1])
+        grad = grad + d_residual
+        grad_own, loads = gather_tokens(
+            names, grad.astype(LOW), [ScatterRows(d_gate_w, 0)], both=False, name=f"gather_four_{layer}"
+        )
+        grads["gate", layer] = settle(d_gate_w, 0, loads[0][0])
+        d_out_w = t_dot(mixed, grad_own).astype(LOW)
+        d_mixed = dot_t(grad_own, w_out).astype(LOW).reshape(4 * QB, 3, HD).transpose(1, 0, 2)
+        masked = softmax_scores(queries, keys, mask)
+        probs = jnp.exp(masked - log_mass)
+        d_probs = jnp.einsum("htd,ud->htu", d_mixed, values, preferred_element_type=F32)
+        inner = jnp.sum(probs * d_probs, axis=-1, keepdims=True)
+        d_scores = (probs * (d_probs - inner)).astype(LOW)
+        d_queries = jnp.einsum("htu,ud->thd", d_scores, keys, preferred_element_type=F32) * HD ** (-0.5)
+        d_keys = jnp.einsum("htu,htd->ud", d_scores, queries, preferred_element_type=F32) * HD ** (-0.5)
+        d_values = jnp.einsum("htu,htd->ud", probs.astype(LOW), d_mixed, preferred_element_type=F32)
+        d_raw_q = turn_back(d_queries, own(cosine), own(sine)).astype(LOW).reshape(4, QB, 3 * HD)
+        mine = (jnp.arange(2) == core)[None, :, None, None]
+        d_raw_q = jnp.where(mine, d_raw_q[:, None], jnp.zeros((), LOW)).reshape(tok_row, 3 * HD)
+        d_raw_k = turn_back(d_keys, cosine[:, 0], sine[:, 0]).astype(LOW)
+        d_raw = jnp.concatenate([d_raw_q, d_raw_k, d_values.astype(LOW)], axis=1)
+        d_bias = jnp.sum(d_raw, axis=0, dtype=F32).astype(LOW)
+        d_qkv_w = t_dot(full_one, d_raw).astype(LOW).reshape(4, 2, D // 8, 5 * HD)
+        tail = jnp.broadcast_to(jnp.pad(d_bias[None], ((0, 15), (0, 0))), (4, 2, 16, 5 * HD))
+        d_slab = jnp.concatenate([d_qkv_w, tail], axis=2)
+        d_out_w = d_out_w.reshape(2, D // 8, D)
+
+        def half(full, dim, which):
+            return lax.dynamic_index_in_dim(full, which, dim, keepdims=False)
+
+        d_normed_one, loads = reduce_tokens(
+            names,
+            dot_t(d_raw, w_qkv).astype(LOW),
+            [ScatterRows(d_up_w, 0), Swap(half(d_slab, 1, 1 - core), half(d_out_w, 0, 1 - core))],
+            name=f"reduce_four_{layer}",
+        )
+        grads["up", layer] = settle(d_up_w, 0, loads[0][0])
+        slab_part = (half(d_slab, 1, core).astype(F32) + loads[1][0].astype(F32)).astype(LOW)
+        out_part = (half(d_out_w, 0, core).astype(F32) + loads[1][1].astype(F32)).astype(LOW)
+        waiting = (slab_part.reshape(4 * HALF, 5 * HD), out_part)
+        d_residual, d_gain_one = norm_back(d_normed_one, residual_in, scale_one, gains[layer, 0])
+        grad = grad + d_residual
+        gain_terms[layer] = jnp.stack([d_gain_one, d_gain_two])
+    leaving = jnp.concatenate([states, grad.astype(LOW)], axis=0).reshape(2 * QB, 8, D // 8).transpose(1, 0, 2)
+    gain_parts = jnp.pad(jnp.stack(gain_terms).reshape(2 * LAYERS, 8, D // 8), ((0, 8 - 2 * LAYERS), (0, 0), (0, 0)))
+    (left,), (gain_all,), (slots,), (out_slots,) = stages_call(
+        names,
+        [
+            [
+                Exchange(leaving),
+                Exchange(gain_parts.transpose(1, 0, 2), every_row=True),
+                ScatterRows(waiting[0], 0),
+                ScatterRows(waiting[1], 1),
+            ]
+        ],
+        name="close",
+    )
+    ((tiles,),) = stages_call(names, [[HeadsToOwners(settle(waiting[0], 0, slots).astype(LOW))]], name="close_heads")
+    grads["qkv", 0] = settle_heads(tiles)
+    grads["out", 0] = settle(waiting[1], 1, out_slots)
+    out_states = left[:, :QB].reshape(tok_row, D // 8).T
+    input_grad = left[:, QB:].reshape(tok_row, D // 8).T.astype(F32)
+    gain_grads = jnp.sum(gain_all, axis=(0, 1))[: 2 * LAYERS].reshape(LAYERS, 2, D // 8)
+
+    def both_layers(kind):
+        return jnp.stack([grads[kind, layer] for layer in range(LAYERS)])
+
+    heads = [jnp.stack([grads["qkv", layer][i] for layer in range(LAYERS)]) for i in range(2)]
+    return (
+        out_states,
+        input_grad,
+        gain_grads,
+        heads[0],
+        heads[1],
+        both_layers("out"),
+        both_layers("gate"),
+        both_layers("up"),
+        both_layers("down"),
+    )
+
+
 def solution(mesh):
     placed = (
         P("col", "row"),
@@ -340,8 +1338,9 @@
         P(None, "row", "col"),
         P(None, "col", "row"),
     )
+    on_lines = mesh.shape["row"] == 4 and mesh.shape["col"] == 8
     return jax.shard_map(
-        per_device,
+        per_device_line if on_lines else per_device,
         mesh=mesh,
         in_specs=placed,
         out_specs=(

time: 2300 us -> 1020 us (0.44)
  waiting for transfers between devices: 1620 us -> 0 us
  Pallas kernels: 0 us -> 619 us
  blocking collectives: 236 us -> 0 us
  matrix products: 220 us -> 157 us
  local copies, waits for them, and re-layouts: 97.7 us -> 138 us
  other arithmetic: 63.8 us -> 94.1 us
  starting transfers between devices: 25 us -> 0 us
    reduce_scatter x20 -> x0, waiting for transfers between devices: 1080 us -> none  [the longest x8 514 us: summed_rows(): lax.psum_scatter(make_term(jnp.int32(0), lax.axis_size('col') * rows), 'c...]
    pallas_call x0 -> x19, Pallas kernels: none -> 619 us  [the longest x16 537 us: carry_call(): results = list(call(*arrays, *(a for item in cargo for a in item.arrays)))]
    all_gather x16 -> x0, waiting for transfers between devices: 494 us -> none  [the longest x8 266 us: spread(): return lax.all_gather(values, 'col', axis=0, tiled=True)]
    psum x9 -> x0, blocking collectives: 114 us -> none  [the longest x8 107 us: feature_total(): return lax.psum(jnp.sum(values, axis=0), 'col')]
    all_to_all x4 -> x0, blocking collectives: 71.3 us -> none  [the longest x2 36.2 us: to_tokens(): lax.all_to_all(values, 'col', split_axis=0, concat_axis=1, tiled=True)]
    dot_general x42, matrix products: 220 us -> 157 us  [the longest x10 42.8 us: dot(): return jnp.dot(a, b, preferred_element_type=F32)]
    all_gather x6 -> x0, blocking collectives: 51.3 us -> none  [the longest x2 21.1 us: per_device(): lax.all_gather(qkv_weight[layer], 'row', axis=0, tiled=True)]
    unnamed x40 -> x0, waiting for transfers between devices: 27.6 us -> none
  transfers between devices with their start and end apart: 42 -> 0, of which waited for: 38 -> 0; matrix products, arithmetic and copies ran while one was open for 8% -> 0% of each run, Pallas kernels for 0% -> 0%
where the time goes in v1:
time: 1020 us; the launch traced here: 1010 us
  Pallas kernels  619 us (61%)
  matrix products  157 us (15%)
  local copies, waits for them, and re-layouts  138 us (14%)
  other arithmetic  94.1 us (9%)
    pallas_call x16, Pallas kernels, carry_call(): results = list(call(*arrays, *(a for item in cargo for a in item.arrays)))  537 us
    pallas_call x3, Pallas kernels, stages_call(): pl.pallas_call(kernel, out_shape=outs, in_specs=[ANY] * n_in, out_specs=[...  82.6 us
    unnamed x314, local copies, waits for them, and re-layouts  64.7 us
    dot_general x10, matrix products, dot(): return jnp.dot(a, b, preferred_element_type=F32)  42.8 us
    dot_general x10, matrix products, dot_t(): lax.dot_general(a, b, (((1,), (1,)), ((), ())), preferred_element_type=F32)  42.7 us
    dot_general x10, matrix products, t_dot(): lax.dot_general(a, b, (((0,), (0,)), ((), ())), preferred_element_type=F32)  42.3 us

profile of v1, /device:TPU:31, one launch (start us, length us, event | category | flops | bytes accessed | tf_op | source)
XLA Modules:
  0.0 1011.0 jit_solution(4548346818743070791)
XLA Ops:
  33.0 37.6 %open.1 = (bf16[208,640]{1,0:T(8,128)(2,1)}, bf16[832,640]{1,0:T(8,128)(2,1)S(1)}, bf16[192,1536]{1,0:T(8,128)(2,1)S(1)}, bf16[8,272,192]{2,1,0:T(8,128)(2,1)S(1...) custom-call(bf16[2,2,208,128]{3,2,1,0:T(8,128)(2,1)S(1)} %pad_maximum_fusion.17.refs_0_, ...), custom_call_target="tpu_custom_call" | custom-call | tf_op jit(solution)/shard_map/open/pallas_call | solution.py:668
  89.4 34.5 %gather_three_1.1 = (bf16[8,128,1536]{2,1,0:T(8,128)(2,1)S(1)}, bf16[1536,1120]{1,0:T(8,128)(2,1)S(1)}) custom-call(bf16[128,1536]{1,0:T(8,128)(2,1)S(1)} %copy.189.refs_0_, bf16[384,1120]{1,0:T(8,128)(2,1)S(1)} %bitcast.326), custom_call_target="tpu_custom_call" | custom-call | tf_op jit(solution)/shard_map/gather_three_1/pallas_call | solution.py:573
  127.5 34.3 %gather_one_0.1 = (bf16[8,128,1536]{2,1,0:T(8,128)(2,1)S(1)}, bf16[1536,1120]{1,0:T(8,128)(2,1)S(1)}) custom-call(bf16[128,1536]{1,0:T(8,128)(2,1)S(1)} %multiply_convert_fusion.11.refs_0_, bf16[384,1120]{1,0:T(8,128)(2,1)S(1)} %bitcast.327), custom_call_target="tpu_custom_call" | custom-call | tf_op jit(solution)/shard_map/gather_one_0/pallas_call | solution.py:573
  178.3 3.2 copy.259
  181.6 3.5 fusion.15
  193.5 31.0 %reduce_one_0.1 = (f32[128,1536]{1,0:T(8,128)S(1)}, bf16[1120,1536]{1,0:T(8,128)(2,1)S(1)}) custom-call(bf16[4,128,1536]{2,1,0:T(8,128)(2,1)S(1)} %bitcast.341, bf16[1120,384]{1,0:T(8,128)(2,1)S(1)} %copy-done.10), custom_call_target="tpu_custom_call" | custom-call | tf_op jit(solution)/shard_map/reduce_one_0/pallas_call | solution.py:573
  225.4 32.3 %gather_two_0.1 = (bf16[8,128,1536]{2,1,0:T(8,128)(2,1)S(1)}, bf16[1536,1120]{1,0:T(8,128)(2,1)S(1)}) custom-call(bf16[128,1536]{1,0:T(8,128)(2,1)S(1)} %multiply_convert_fusion.10.refs_0_, bf16[384,1120]{1,0:T(8,128)(2,1)S(1)} %bitcast.325), custom_call_target="tpu_custom_call" | custom-call | tf_op jit(solution)/shard_map/gather_two_0/pallas_call | solution.py:573
  259.5 3.8 fusion.85
  263.3 6.0 multiply_convert_fusion.7
  269.3 4.7 convolution_convert_fusion.9
  274.0 33.8 %reduce_two_0.1 = (f32[128,1536]{1,0:T(8,128)S(1)}, bf16[832,640]{1,0:T(8,128)(2,1)S(1)}, bf16[192,1536]{1,0:T(8,128)(2,1)S(1)}) custom-call(bf16[8,128,1536]{2,1,0:T(8,128)(2,1)S(1)} %bitcast.334, bf16[208,640]{1,0:T(8,128)(2,1)S(1)} %copy-done.32, bf16[192,384]{1,0:T(8,128)(2,1)S(1)} %copy-done.28), custom_call_target="tpu_custom_call" | custom-call | tf_op jit(solution)/shard_map/reduce_two_0/pallas_call | solution.py:573
  308.7 33.9 %gather_one_1.1 = (bf16[8,128,1536]{2,1,0:T(8,128)(2,1)S(1)}, bf16[1536,1120]{1,0:T(8,128)(2,1)S(1)}, bf16[832,640]{1,0:T(8,128)(2,1)S(1)}, bf16[192,1536]{1,0:T(8,128)(2,1)S(1)}) custom-call(bf16[128,1536]{1,0:T(8,128)(2,1)S(1)} %multiply_convert_fusion.9.refs_0_, bf16[384,1120]{1,0:T(8,128)(2,1)S(1)} %bitcast.324, ...), custom_call_target="tpu_custom_call" | custom-call | tf_op jit(solution)/shard_map/gather_one_1/pallas_call | solution.py:573
  357.0 3.2 copy.263
  366.5 3.5 fusion.17
  378.6 30.8 %reduce_one_1.1 = (f32[128,1536]{1,0:T(8,128)S(1)}, bf16[1120,1536]{1,0:T(8,128)(2,1)S(1)}) custom-call(bf16[4,128,1536]{2,1,0:T(8,128)(2,1)S(1)} %bitcast.342, bf16[1120,384]{1,0:T(8,128)(2,1)S(1)} %copy-done.9), custom_call_target="tpu_custom_call" | custom-call | tf_op jit(solution)/shard_map/reduce_one_1/pallas_call | solution.py:573
  409.8 32.4 %gather_two_1.1 = bf16[8,128,1536]{2,1,0:T(8,128)(2,1)S(1)} custom-call(bf16[128,1536]{1,0:T(8,128)(2,1)S(1)} %multiply_convert_fusion.8.refs_0_), custom_call_target="tpu_custom_call" | custom-call | tf_op jit(solution)/shard_map/gather_two_1/pallas_call | solution.py:573
  442.2 5.5 fusion.86
  447.6 5.3 fusion.87
  453.0 10.1 multiply_convert_fusion.6
  463.1 6.4 convolution_convert_fusion.8
  469.5 4.0 convolution_convert_fusion.5.refs_1_
  473.5 31.8 %reduce_two_1.1 = f32[128,1536]{1,0:T(8,128)S(1)} custom-call(bf16[8,128,1536]{2,1,0:T(8,128)(2,1)S(1)} %bitcast.337), custom_call_target="tpu_custom_call" | custom-call | tf_op jit(solution)/shard_map/reduce_two_1/pallas_call | solution.py:573
  505.3 6.3 fusion.88
  511.6 6.5 add_convert_fusion.1
  518.2 34.4 %reduce_three_1.1 = (f32[128,1536]{1,0:T(8,128)S(1)}, bf16[2,1120,384]{2,1,0:T(8,128)(2,1)S(1)}) custom-call(bf16[8,128,1536]{2,1,0:T(8,128)(2,1)S(1)} %bitcast.333, bf16[1120,1536]{1,0:T(8,128)(2,1)S(1)} %convolution_convert_fusion.5.refs_1_), custom_call_target="tpu_custom_call" | custom-call | tf_op jit(solution)/shard_map/reduce_three_1/pallas_call | solution.py:573
  556.2 4.5 convolution_convert_fusion.3.refs_1_
  560.8 4.6 convolution_convert_fusion.4.refs_1_
  565.4 31.5 %gather_four_1.1 = (bf16[4,128,1536]{2,1,0:T(8,128)(2,1)S(1)}, bf16[2,384,1120]{2,1,0:T(8,128)(2,1)S(1)}) custom-call(bf16[128,1536]{1,0:T(8,128)(2,1)S(1)} %get-tuple-element.157.refs_0_, bf16[1536,1120]{1,0:T(8,128)(2,1)S(1)} %convolution_convert_fusion.4.refs_1_), custom_call_target="tpu_custom_call" | custom-call | tf_op jit(solution)/shard_map/gather_four_1/pallas_call | solution.py:573
  605.9 3.3 convert_reduce_fusion.2
  609.2 4.0 multiply_reduce_fusion.1
  629.5 4.8 convolution_convert_fusion.11
  638.6 39.1 %reduce_four_1.1 = (f32[128,1536]{1,0:T(8,128)S(1)}, bf16[2,384,1120]{2,1,0:T(8,128)(2,1)S(1)}, bf16[4,208,640]{2,1,0:T(8,128)(2,1)S(1)}, bf16[192,1536]{1,0:T(8,128)(2,1)S(1)}) custom-call(bf16[8,128,1536]{2,1,0:T(8,128)(2,1)S(1)} %bitcast.336, bf16[1536,1120]{1,0:T(8,128)(2,1)S(1)} %convolution_convert_fusion.3.refs_1_, ...), custom_call_target="tpu_custom_call" | custom-call | tf_op jit(solution)/shard_map/reduce_four_1/pallas_call | solution.py:573
  682.6 32.9 %gather_three_0.1 = (bf16[8,128,1536]{2,1,0:T(8,128)(2,1)S(1)}, bf16[2,208,640]{2,1,0:T(8,128)(2,1)S(1)}, bf16[2,192,384]{2,1,0:T(8,128)(2,1)S(1)}) custom-call(bf16[128,1536]{1,0:T(8,128)(2,1)S(1)} %get-tuple-element.155.refs_0_, bf16[832,640]{1,0:T(8,128)(2,1)S(1)} %bitcast.321, bf16[192,1536]{1,0:T(8,128)(2,1)S(1)} %fusion.36.refs_2_), custom_call_target="tpu_custom_call" | custom-call | tf_op jit(solution)/shard_map/gather_three_0/pallas_call | solution.py:573
  715.6 7.9 multiply_convert_fusion.2
  723.4 4.0 convolution_convert_fusion.2.refs_1_
  728.4 4.3 fusion.89
  732.8 4.6 add_convert_fusion
  737.5 31.9 %reduce_three_0.1 = (f32[128,1536]{1,0:T(8,128)S(1)}, bf16[2,1120,384]{2,1,0:T(8,128)(2,1)S(1)}, bf16[2,2,2,208,128]{4,3,2,1,0:T(8,128)(2,1)S(1)}) custom-call(bf16[8,128,1536]{2,1,0:T(8,128)(2,1)S(1)} %bitcast.332, bf16[1120,1536]{1,0:T(8,128)(2,1)S(1)} %convolution_convert_fusion.2.refs_1_, bf16[208,640]{1,0:T(8,128)(2,1)S(1)} %add_convert_fusion.5.refs_2_), custom_call_target="tpu_custom_call" | custom-call | tf_op jit(solution)/shard_map/reduce_three_0/pallas_call | solution.py:573
  779.9 7.6 convolution_convert_fusion.refs_1_
  787.4 4.5 convolution_convert_fusion.1.refs_1_
  798.5 32.3 %gather_four_0.1 = (bf16[4,128,1536]{2,1,0:T(8,128)(2,1)S(1)}, bf16[2,384,1120]{2,1,0:T(8,128)(2,1)S(1)}) custom-call(bf16[128,1536]{1,0:T(8,128)(2,1)S(1)} %get-tuple-element.153.refs_0_, bf16[1536,1120]{1,0:T(8,128)(2,1)S(1)} %convolution_convert_fusion.1.refs_1_), custom_call_target="tpu_custom_call" | custom-call | tf_op jit(solution)/shard_map/gather_four_0/pallas_call | solution.py:573
  845.6 5.1 copy.237
  850.7 4.7 multiply_reduce_fusion
  855.4 3.6 multiply_convert_fusion
  873.8 4.8 convolution_convert_fusion.10
  883.1 39.7 %reduce_four_0.1 = (f32[128,1536]{1,0:T(8,128)S(1)}, bf16[2,384,1120]{2,1,0:T(8,128)(2,1)S(1)}, bf16[4,208,640]{2,1,0:T(8,128)(2,1)S(1)}, bf16[192,1536]{1,0:T(8,128)(2,1)S(1)}) custom-call(bf16[8,128,1536]{2,1,0:T(8,128)(2,1)S(1)} %bitcast.335, bf16[1536,1120]{1,0:T(8,128)(2,1)S(1)} %copy-done, bf16[4,208,640]{2,1,0:T(8,128)(2,1)S(1)} %fusion.40.refs_2_, ...), custom_call_target="tpu_custom_call" | custom-call | tf_op jit(solution)/shard_map/reduce_four_0/pallas_call | solution.py:573
  939.1 35.3 %close.1 = (bf16[8,256,192]{2,1,0:T(8,128)(2,1)S(1)}, f32[4,8,8,192]{3,2,1,0:T(8,128)S(1)}, bf16[2,208,640]{2,1,0:T(8,128)(2,1)S(1)}, bf16[2,192,384]{2,1,0:T(8,128)(2,1)S(1)}) custom-call(bf16[8,256,192]{2,1,0:T(8,128)(2,1)S(1)} %bitcast.323, f32[8,8,192]{2,1,0:T(8,128)S(1)} %copy-done.33, bf16[832,640]{1,0:T(8,128)(2,1)S(1)} %bitcast.320, ...), custom_call_target="tpu_custom_call" | custom-call | tf_op jit(solution)/shard_map/close/pallas_call | solution.py:668
  988.2 9.7 close_heads.1
  (519 shorter events, 244.2 us)
Async XLA Ops:
  75.0 9.3 copy-start.122
  75.5 8.9 copy-start.109
  75.5 149.8 %copy-start.111 = (f32[1536]{0:T(1024)}, f32[1536]{0:T(1024)S(1)}, u32[]{:S(2)}) copy-start(f32[1536]{0:T(1024)S(1)} %get-tuple-element.151) | copy-start | bytes 18436
  82.0 6.1 copy-start.23
  88.3 39.1 %copy-start.8 = (bf16[1,384,1120]{2,1,0:T(8,128)(2,1)S(1)}, bf16[1,384,1120]{2,1,0:T(8,128)(2,1)}, u32[]{:S(2)}) copy-start(bf16[1,384,1120]{2,1,0:T(8,128)(2,1)} %copy.256) | copy-start | bytes 2580484
  88.5 75.5 %copy-start.80 = (bf16[4,2,192,640]{3,2,1,0:T(8,128)(2,1)}, bf16[4,2,192,640]{3,2,1,0:T(8,128)(2,1)S(1)}, u32[]{:S(2)}) copy-start(bf16[4,2,192,640]{3,2,1,0:T(8,128)(2,1)S(1)} %pad_maximum_fusion.4) | copy-start | bytes 5898244
  192.1 32.3 %copy-start.128 = (bf16[128,3,512]{2,0,1:T(8,128)(2,1)}, bf16[128,3,512]{2,0,1:T(8,128)(2,1)S(1)}, u32[]{:S(2)}) copy-start(bf16[128,3,512]{2,0,1:T(8,128)(2,1)S(1)} %fusion.20) | copy-start | bytes 1179652
  192.2 32.3 %copy-start.55 = (f32[128,1536]{1,0:T(8,128)S(1)}, f32[128,1536]{1,0:T(8,128)}, u32[]{:S(2)}) copy-start(f32[128,1536]{1,0:T(8,128)} %copy.198) | copy-start | bytes 2359300
  224.5 44.8 %copy-start.45 = (bf16[1120,1536]{1,0:T(8,128)(2,1)}, bf16[1120,1536]{1,0:T(8,128)(2,1)S(1)}, u32[]{:S(2)}) copy-start(bf16[1120,1536]{1,0:T(8,128)(2,1)S(1)} %get-tuple-element.69) | copy-start | bytes 10321924
  224.5 35.0 %copy-start.36 = (bf16[1536,1120]{1,0:T(8,128)(2,1)S(1)}, bf16[1536,1120]{1,0:T(8,128)(2,1)}, u32[]{:S(2)}) copy-start(bf16[1536,1120]{1,0:T(8,128)(2,1)} %copy-done.35) | copy-start | bytes 10321924
  224.7 83.1 %copy-start.57 = (f32[128,1536]{1,0:T(8,128)}, f32[128,1536]{1,0:T(8,128)S(1)}, u32[]{:S(2)}) copy-start(f32[128,1536]{1,0:T(8,128)S(1)} %get-tuple-element.164) | copy-start | bytes 2359300
  225.3 38.0 %copy-start.118 = (f32[128]{0:T(128)}, f32[128]{0:T(128)S(1)}, u32[]{:S(2)}) copy-start(f32[128]{0:T(128)S(1)} %get-tuple-element.212) | copy-start | bytes 1540
  263.3 6.0 copy-start.132
  308.0 101.4 %copy-start.58 = (f32[128,1536]{1,0:T(8,128)}, f32[128,1536]{1,0:T(8,128)S(1)}, u32[]{:S(2)}) copy-start(f32[128,1536]{1,0:T(8,128)S(1)} %get-tuple-element.162) | copy-start | bytes 2359300
  308.6 35.3 %copy-start.120 = (f32[128]{0:T(128)}, f32[128]{0:T(128)S(1)}, u32[]{:S(2)}) copy-start(f32[128]{0:T(128)S(1)} %get-tuple-element.214) | copy-start | bytes 1540
  377.2 32.1 %copy-start.130 = (bf16[128,3,512]{2,0,1:T(8,128)(2,1)}, bf16[128,3,512]{2,0,1:T(8,128)(2,1)S(1)}, u32[]{:S(2)}) copy-start(bf16[128,3,512]{2,0,1:T(8,128)(2,1)S(1)} %fusion.19) | copy-start | bytes 1179652
  409.6 32.5 %copy-start.42 = (bf16[1536,1120]{1,0:T(8,128)(2,1)S(1)}, bf16[1536,1120]{1,0:T(8,128)(2,1)}, u32[]{:S(2)}) copy-start(bf16[1536,1120]{1,0:T(8,128)(2,1)} %copy-done.41) | copy-start | bytes 10321924
  442.2 5.5 copy-start.52
  447.6 5.3 copy-start.44
  463.0 6.4 copy-start.138
  473.4 44.8 %copy-start.4 = (bf16[1120,1536]{1,0:T(8,128)(2,1)}, bf16[1120,1536]{1,0:T(8,128)(2,1)S(1)}, u32[]{:S(2)}) copy-start(bf16[1120,1536]{1,0:T(8,128)(2,1)S(1)} %convolution_convert_fusion.5.refs_1_) | copy-start | bytes 10321924
  473.5 31.9 %copy-start.135 = (bf16[1024,1120]{0,1:T(8,128)(2,1)S(1)}, bf16[1024,1120]{0,1:T(8,128)(2,1)}, u32[]{:S(2)}) copy-start(bf16[1024,1120]{0,1:T(8,128)(2,1)} %get-tuple-element.168) | copy-start | bytes 6881284
  505.3 6.3 copy-start.140
  565.3 32.4 %copy-start.1 = (bf16[1536,1120]{1,0:T(8,128)(2,1)}, bf16[1536,1120]{1,0:T(8,128)(2,1)S(1)}, u32[]{:S(2)}) copy-start(bf16[1536,1120]{1,0:T(8,128)(2,1)S(1)} %convolution_convert_fusion.4.refs_1_) | copy-start | bytes 10321924
  565.4 31.5 %copy-start.104 = (bf16[192,1536]{1,0:T(8,128)(2,1)S(1)}, bf16[192,1536]{1,0:T(8,128)(2,1)}, u32[]{:S(2)}) copy-start(bf16[192,1536]{1,0:T(8,128)(2,1)} %get-tuple-element.185) | copy-start | bytes 1769476
  565.4 34.7 %slice-start.2 = ((s8[6291456]{0:T(1024)(128)(4,1)}), s8[2097152]{0:T(1024)(128)(4,1)S(1)}, s32[]{:S(2)}) async-start(s8[6291456]{0:T(1024)(128)(4,1)} %bitcast.361), calls=%async_computation.2 | async-start | bytes 4194304
  603.9 5.3 copy-start.86
  605.9 7.3 slice-start.4
  619.6 8.7 copy-start.116
  629.5 5.1 copy-start.83
  638.5 39.1 %copy-start.93 = (bf16[384,1536]{1,0:T(8,128)(2,1)S(1)}, bf16[384,1536]{1,0:T(8,128)(2,1)}, u32[]{:S(2)}) copy-start(bf16[384,1536]{1,0:T(8,128)(2,1)} %convolution_convert_fusion.15) | copy-start | bytes 3538948
  638.6 77.0 %slice-start.6 = ((s8[4587520]{0:T(1024)(128)(4,1)}), s8[4194304]{0:T(1024)(128)(4,1)S(1)}, s32[]{:S(2)}) async-start(s8[4587520]{0:T(1024)(128)(4,1)} %bitcast.430), calls=%async_computation.6 | async-start | bytes 8388608
  677.9 37.6 %slice-start.7 = ((s8[4587520]{0:T(1024)(128)(4,1)}), s8[393216]{0:T(1024)(128)(4,1)S(1)}, s32[]{:S(2)}) async-start(s8[4587520]{0:T(1024)(128)(4,1)} %bitcast.430), calls=%async_computation.7 | async-start | bytes 786432
  681.1 34.5 %copy-start.46 = (bf16[1120,1536]{1,0:T(8,128)(2,1)S(1)}, bf16[1120,1536]{1,0:T(8,128)(2,1)}, u32[]{:S(2)}) copy-start(bf16[1120,1536]{1,0:T(8,128)(2,1)} %copy-done.45) | copy-start | bytes 10321924
  715.5 7.9 copy-start.137
  723.4 5.0 copy-start.133
  723.4 5.0 copy-start.37
  727.4 10.0 copy-start.5
  771.5 5.5 copy-start.125
  779.9 7.6 copy-start.134
  792.0 6.5 copy-start.2
  796.5 37.5 %slice-start = ((s8[6291456]{0:T(1024)(128)(4,1)}), s8[2097152]{0:T(1024)(128)(4,1)S(1)}, s32[]{:S(2)}) async-start(s8[6291456]{0:T(1024)(128)(4,1)} %bitcast.359), calls=%async_computation | async-start | bytes 4194304
  798.5 32.3 %copy-start.99 = (bf16[192,1536]{1,0:T(8,128)(2,1)S(1)}, bf16[192,1536]{1,0:T(8,128)(2,1)}, u32[]{:S(2)}) copy-start(bf16[192,1536]{1,0:T(8,128)(2,1)} %get-tuple-element.186) | copy-start | bytes 1769476
  798.5 32.3 %copy-start.101 = (bf16[192,1536]{1,0:T(8,128)(2,1)S(1)}, bf16[192,1536]{1,0:T(8,128)(2,1)}, u32[]{:S(2)}) copy-start(bf16[192,1536]{1,0:T(8,128)(2,1)} %get-tuple-element.187) | copy-start | bytes 1769476
  863.9 8.7 copy-start.117
  873.8 5.1 copy-start.81
  883.1 39.7 %copy-start.92 = (bf16[384,1536]{1,0:T(8,128)(2,1)S(1)}, bf16[384,1536]{1,0:T(8,128)(2,1)}, u32[]{:S(2)}) copy-start(bf16[384,1536]{1,0:T(8,128)(2,1)} %convolution_convert_fusion.14) | copy-start | bytes 3538948
  985.9 12.1 %copy-start.124 = (f32[2,1,1,128]{3,2,1,0:T(1,128)S(1)}, f32[2,1,1,128]{3,2,1,0:T(1,128)}, u32[]{:S(2)}) copy-start(f32[2,1,1,128]{3,2,1,0:T(1,128)} %slice.271) | copy-start | bytes 3076
  (102 other events, 252.6 us)

commit v2 on v1

--- a/solution.py
+++ b/solution.py
@@ -51,7 +51,8 @@
         self.todo.append((wait, cond))
 
     def run(self):
-        for wait, cond in self.todo:
+        todo, self.todo = self.todo, []
+        for wait, cond in todo:
             if cond is None:
                 wait()
             else:
@@ -97,9 +98,10 @@
     outs = ()
     scratch = ()
     reach = "rows"
+    phase = 0
     slow = False
 
-    def middle(self, place, ins, outs, scratch, later):
+    def middle(self, place, ins, outs, scratch):
         pass
 
 
@@ -147,32 +149,32 @@
         ]
         return out, onward
 
+    def arrived(self, place, scratch, view, sem, row):
+        return remote(view, view, scratch[0].at[0], scratch[1].at[sem], (row, place.k))
+
     def start(self, place, ins, outs, scratch, later):
         (src,), (dst,), (_, _, keep_sem) = ins, outs, scratch
-        for copy in self.copies(place, ins, outs, scratch)[0]:
+        out, onward = self.copies(place, ins, outs, scratch)
+        for copy in out:
             copy.start()
         keep = pltpu.make_async_copy(src, part_of(dst, self.dim, place.r, self.size), keep_sem.at[0])
         keep.start()
         later.add(keep.wait)
-
-    def middle(self, place, ins, outs, scratch, later):
-        (src,), (dst,), (send, recv, _) = ins, outs, scratch
         x, y, d = place.rows()
         from_x, from_y, from_d = self.spots(dst, x), self.spots(dst, y), self.spots(dst, d)
-        block = self.halves(src)
-
-        def arrived(view, sem, device):
-            return remote(view, view, send.at[0], recv.at[sem], device)
-
-        out, onward = self.copies(place, ins, outs, scratch)
-        arrived(from_x[0], 0, (x, place.k)).wait_recv()
-        onward[0].start()
-        arrived(from_y[1], 3, (y, place.k)).wait_recv()
-        onward[1].start()
         for view, sem, row in ((from_x[1], 1, x), (from_y[0], 2, y), (from_d[0], 4, y), (from_d[1], 5, x)):
-            later.add(arrived(view, sem, (row, place.k)).wait_recv)
+            later.add(self.arrived(place, scratch, view, sem, row).wait_recv)
         for copy in (*out, *onward):
             later.add(copy.wait_send)
+
+    def middle(self, place, ins, outs, scratch):
+        (dst,) = outs
+        x, y, d = place.rows()
+        _, onward = self.copies(place, ins, outs, scratch)
+        self.arrived(place, scratch, self.spots(dst, x)[0], 0, x).wait_recv()
+        onward[0].start()
+        self.arrived(place, scratch, self.spots(dst, y)[1], 3, y).wait_recv()
+        onward[1].start()
 
 
 class ScatterRows(Cargo):
@@ -224,11 +226,15 @@
         return first, held, last
 
     def start(self, place, ins, outs, scratch, later):
-        first, held, _ = self.copies(place, ins, outs, scratch)
+        first, held, last = self.copies(place, ins, outs, scratch)
         for copy in (*first, *held):
             copy.start()
-
-    def middle(self, place, ins, outs, scratch, later):
+        for copy in (*first, *last):
+            later.add(copy.wait_send)
+        for copy in (*first[2:], *last):
+            later.add(copy.wait_recv)
+
+    def middle(self, place, ins, outs, scratch):
         via_x, via_y, own_x, own_y, sum_x, sum_y, *_ = scratch
         first, held, last = self.copies(place, ins, outs, scratch)
         held[0].wait()
@@ -239,10 +245,6 @@
         first[0].wait_recv()
         add_into(sum_y, [own_y, via_x])
         last[1].start()
-        for copy in (*first, *last):
-            later.add(copy.wait_send)
-        for copy in (*first[2:], *last):
-            later.add(copy.wait_recv)
 
 
 class Swap(Cargo):
@@ -448,7 +450,11 @@
             later.add(came.wait_recv)
 
 
-def reduce_line(place, part, out, from_p, from_r, from_l, held, sems, later, both, middle):
+def pair_copy(place, part, from_p, sems, j):
+    return remote(part.at[2 * j + 1 - place.c], from_p.at[j], sems[0].at[j], sems[1].at[j], place.at(place.z, 1 - place.c))
+
+
+def reduce_line(place, part, out, from_p, from_r, from_l, held, sems, later, both, middle, sent=False):
     send_p, recv_p, send, recv_r, recv_l = sems
     z, c = place.z, place.c
     right_at, left_at = place.at(jnp.minimum(z + 1, 3), c), place.at(jnp.maximum(z - 1, 0), c)
@@ -457,7 +463,7 @@
         return part.at[2 * j + c] if both else part.at[j]
 
     def partner(j):
-        return remote(part.at[2 * j + 1 - c], from_p.at[j], send_p.at[j], recv_p.at[j], place.at(z, 1 - c))
+        return pair_copy(place, part, from_p, sems, j)
 
     def moving(j, buffer, sem, device):
         return remote(held.at[j], buffer.at[j], send.at[j], sem.at[j], device)
@@ -465,7 +471,8 @@
     if both:
         for j in (3, 0, 2, 1):
             copy = partner(j)
-            copy.start()
+            if not sent:
+                copy.start()
             later.add(copy.wait_send)
 
     def terms(j):
@@ -538,39 +545,53 @@
         return taken
 
     ins = pop(n_in)
-    cargo_ins = [pop(len(item.arrays)) for item in cargo]
+    given = [pop(sum(not isinstance(a, From) for a in item.arrays)) for item in cargo]
     outs = pop(n_out)
-    cargo_outs = [pop(len(item.outs)) for item in cargo]
+    made = {item: pop(len(item.outs)) for item in cargo}
     scratch = pop(n_scratch)
-    cargo_scratch = [pop(len(item.scratch)) for item in cargo]
+    held = {item: pop(len(item.scratch)) for item in cargo}
+    taken = {
+        item: [made[a.item][a.at] if isinstance(a, From) else mine.pop(0) for a in item.arrays]
+        for item, mine in zip(cargo, given)
+    }
     place = Place()
     later = Later()
-    loads = list(zip(cargo, cargo_ins, cargo_outs, cargo_scratch))
+    owed = [Later(), Later()]
     greet(place, {reach, *(item.reach for item in cargo)})
-    for item, *theirs in loads:
-        item.start(place, *theirs, later)
-
-    def middle():
-        for item, *theirs in loads:
-            item.middle(place, *theirs, later)
-
-    body(place, ins, outs, scratch, later, middle)
+
+    def start(phase):
+        if phase == 1 and any(isinstance(a, From) for item in cargo for a in item.arrays):
+            owed[0].run()
+        for item in cargo:
+            if item.phase == phase:
+                item.start(place, taken[item], made[item], held[item], owed[phase])
+
+    def middle(phase=0):
+        for item in cargo:
+            if item.phase == phase:
+                item.middle(place, taken[item], made[item], held[item])
+
+    start(0)
+    body(place, ins, outs, scratch, later, middle, start)
     later.run()
-
-
-def carry_call(names, body, reach, arrays, in_specs, outs, out_specs, scratch, cargo, name=None):
+    owed[0].run()
+    owed[1].run()
+
+
+def carry_call(names, body, reach, arrays, in_specs, outs, out_specs, scratch, cargo, name=None, vmem=40):
+    given = [a for item in cargo for a in item.arrays if not isinstance(a, From)]
     call = pl.pallas_call(
         partial(carry_kernel, body, reach, len(arrays), len(outs), len(scratch), cargo),
         out_shape=[*outs, *(o for item in cargo for o in item.outs)],
-        in_specs=[*in_specs, *(ANY for item in cargo for _ in item.arrays)],
+        in_specs=[*in_specs, *(ANY for _ in given)],
         out_specs=[*out_specs, *(ANY for item in cargo for _ in item.outs)],
         scratch_shapes=[*scratch, *(s for item in cargo for s in item.scratch)],
         compiler_params=pltpu.CompilerParams(
-            collective_id=names.take(), has_side_effects=True, vmem_limit_bytes=40 * 2**20
+            collective_id=names.take(), has_side_effects=True, vmem_limit_bytes=vmem * 2**20
         ),
         name=name,
     )
-    results = list(call(*arrays, *(a for item in cargo for a in item.arrays)))
+    results = list(call(*arrays, *given))
     main = results[: len(outs)]
     rest = results[len(outs) :]
     loads = []
@@ -584,7 +605,7 @@
     tokens, width = block.shape
     blocks = 8 if both else 4
 
-    def body(place, ins, outs, scratch, later, middle):
+    def body(place, ins, outs, scratch, later, middle, start):
         gather_line(place, ins[0], outs[0], scratch, later, both, middle)
 
     (full,), loads = carry_call(
@@ -612,7 +633,7 @@
     blocks = 8 if both else 4
     tokens, width = part.shape[0] // blocks, part.shape[1]
 
-    def body(place, ins, outs, scratch, later, middle):
+    def body(place, ins, outs, scratch, later, middle, start):
         from_p, from_r, from_l, held, *sems = scratch
         reduce_line(place, ins[0], outs[0], from_p, from_r, from_l, held, sems, later, both, middle)
 
@@ -632,6 +653,169 @@
         name=name,
     )
     return total, loads
+
+
+class Gather:
+    scratch = (
+        pltpu.SemaphoreType.DMA((4,)),
+        pltpu.SemaphoreType.DMA((4,)),
+        pltpu.SemaphoreType.DMA((8,)),
+        pltpu.SemaphoreType.DMA((8,)),
+        pltpu.SemaphoreType.DMA((1,)),
+    )
+
+    def __init__(self, place, block, full, sems, both=True):
+        self.place, self.block, self.full, self.both = place, block, full, both
+        self.send_r, self.send_l, self.send_p, self.recv, self.keep = sems
+
+    def copies(self, src, zz, t, way):
+        z, c = self.place.z, self.place.c
+        spot, sem = self.full.at[2 * zz + c], self.recv.at[2 * zz + c]
+        right = remote(src, spot, self.send_r.at[t], sem, self.place.at(jnp.minimum(z + 1, 3), c))
+        left = remote(src, spot, self.send_l.at[t], sem, self.place.at(jnp.maximum(z - 1, 0), c))
+        partner = remote(src, spot, self.send_p.at[2 * t + way], sem, self.place.at(z, 1 - c))
+        return right, left, partner
+
+    def start(self, later):
+        z, c = self.place.z, self.place.c
+        right, left, partner = self.copies(self.block, z, 0, 0)
+        pl.when(z < 3)(right.start)
+        pl.when(z > 0)(left.start)
+        later.add(right.wait_send, z < 3)
+        later.add(left.wait_send, z > 0)
+        if self.both:
+            partner.start()
+            later.add(partner.wait_send)
+        keep = pltpu.make_async_copy(self.block, self.full.at[2 * z + c], self.keep.at[0])
+        keep.start()
+        keep.wait()
+        for t in range(1, 4):
+            for way in (0, 1):
+                zz, valid, onward, may, partner = self.step(t, way)
+                later.add(onward.wait_send, valid & may)
+                if self.both:
+                    later.add(partner.wait_send, valid)
+
+    def step(self, t, way):
+        z = self.place.z
+        there = z + (2 * way - 1) * t
+        zz = jnp.clip(there, 0, 3)
+        right, left, partner = self.copies(self.full.at[2 * zz + self.place.c], zz, t, way)
+        onward, may = (left, z > 0) if way else (right, z < 3)
+        return zz, (there >= 0) & (there <= 3), onward, may, partner
+
+    def pass_on(self, t):
+        for way in (0, 1):
+            _, valid, onward, may, partner = self.step(t, way)
+
+            @pl.when(valid)
+            def _(onward=onward, may=may, partner=partner):
+                onward.wait_recv()
+                pl.when(may)(onward.start)
+                if self.both:
+                    partner.start()
+
+    def chunk(self, p):
+        z, c = self.place.z, self.place.c
+        edge = (z == 0) | (z == 3)
+        t = jnp.where(edge, p, (p + 1) // 2)
+        pl.when((p >= 1) & (edge | (p != 2)))(lambda: self.pass_on(t))
+        second = jnp.where(z == 0, 1, z - 1)
+        third = jnp.where(z == 0, 2, jnp.where(z == 3, 1, z + 1))
+        fourth = jnp.where(z <= 1, 3, 0)
+        j = jnp.where(p == 0, z, jnp.where(p == 1, second, jnp.where(p == 2, third, fourth)))
+        if self.both:
+            spot = self.full.at[2 * j + 1 - c]
+            remote(spot, spot, self.send_p.at[0], self.recv.at[2 * j + 1 - c], self.place.at(z, 1 - c)).wait_recv()
+        return j
+
+
+def forward_feed(names, block, w_gate, w_up, w_down, cargo, name):
+    tokens, width = block.shape
+    inner = w_gate.shape[1]
+
+    def body(place, ins, outs, scratch, later, middle, start):
+        block_ref, gate_hbm, up_hbm, down_hbm = ins
+        total, full_out, gate_out, up_out = outs
+        n = len(Gather.scratch)
+        gather_sems, scratch = scratch[:n], scratch[n:]
+        full, part, gate_w, up_w, down_w, gates, ups, load_sem, keep_sem = scratch[:9]
+        from_p, from_r, from_l, held, *sems = scratch[9:]
+        gather = Gather(place, block_ref, full, gather_sems)
+        loads = [
+            pltpu.make_async_copy(src, dst, load_sem.at[i])
+            for i, (src, dst) in enumerate(((gate_hbm, gate_w), (up_hbm, up_w), (down_hbm, down_w)))
+        ]
+        for load in loads:
+            load.start()
+        gather.start(later)
+        for load in loads:
+            load.wait()
+
+        def keep(j):
+            rows = pl.ds(pl.multiple_of(2 * tokens * j, 2 * tokens), 2 * tokens)
+            return [
+                pltpu.make_async_copy(full.at[pl.ds(2 * j, 2)], full_out.at[pl.ds(2 * j, 2)], keep_sem.at[0, j]),
+                pltpu.make_async_copy(gates.at[rows, :], gate_out.at[rows, :], keep_sem.at[1, j]),
+                pltpu.make_async_copy(ups.at[rows, :], up_out.at[rows, :], keep_sem.at[2, j]),
+            ]
+
+        def step(p, carry):
+            j = gather.chunk(p)
+            pl.when(p == 2)(middle)
+            acts = full[pl.ds(2 * j, 2)].reshape(2 * tokens, width)
+            rows = pl.ds(pl.multiple_of(2 * tokens * j, 2 * tokens), 2 * tokens)
+            gate = jnp.dot(acts, gate_w[...], preferred_element_type=F32)
+            up = jnp.dot(acts, up_w[...], preferred_element_type=F32)
+            gates[rows, :] = gate.astype(LOW)
+            ups[rows, :] = up.astype(LOW)
+            hidden = (gate * jax.nn.sigmoid(gate) * up).astype(LOW)
+            sums = jnp.dot(hidden, down_w[...], preferred_element_type=F32).astype(LOW)
+            part[pl.ds(2 * j, 2)] = sums.reshape(2, tokens, width)
+            pair_copy(place, part, from_p, sems, j).start()
+            for copy in keep(j):
+                copy.start()
+            return carry
+
+        lax.fori_loop(0, 4, step, 0)
+        start(1)
+        reduce_line(place, part, total, from_p, from_r, from_l, held, sems, later, True, lambda: middle(1), sent=True)
+        for j in range(4):
+            for copy in keep(j):
+                copy.wait()
+
+    (total, full, gate, up), loads = carry_call(
+        names,
+        body,
+        "line",
+        [block, w_gate, w_up, w_down],
+        [ONCHIP, ANY, ANY, ANY],
+        [
+            jax.ShapeDtypeStruct((tokens, width), F32),
+            jax.ShapeDtypeStruct((8, tokens, width), LOW),
+            jax.ShapeDtypeStruct((8 * tokens, inner), LOW),
+            jax.ShapeDtypeStruct((8 * tokens, inner), LOW),
+        ],
+        [ONCHIP, ANY, ANY, ANY],
+        [
+            *Gather.scratch,
+            pltpu.VMEM((8, tokens, width), LOW),
+            pltpu.VMEM((8, tokens, width), LOW),
+            pltpu.VMEM(w_gate.shape, LOW),
+            pltpu.VMEM(w_up.shape, LOW),
+            pltpu.VMEM(w_down.shape, LOW),
+            pltpu.VMEM((8 * tokens, inner), LOW),
+            pltpu.VMEM((8 * tokens, inner), LOW),
+            pltpu.SemaphoreType.DMA((3,)),
+            pltpu.SemaphoreType.DMA((3, 4)),
+            *[pltpu.VMEM((4, tokens, width), LOW)] * 4,
+            *[pltpu.SemaphoreType.DMA((4,))] * 5,
+        ],
+        cargo,
+        name=name,
+        vmem=58,
+    )
+    return total, full.reshape(8 * tokens, width), gate, up, loads
 
 
 def stages_call(names, stages, name=None):
@@ -660,7 +844,7 @@
             for item, *theirs in begun:
                 item.start(place, *theirs)
             for item, *theirs in begun:
-                item.middle(place, *theirs)
+                item.middle(place, *theirs[:3])
             later.run()
         last.run()
 
@@ -1154,12 +1338,13 @@
         if layer == 0:
             sent = weights_in(1)
             cargo = sent[:1]
-        full_two, loads_two = gather_tokens(names, normed_two, cargo, name=f"gather_two_{layer}")
-        gate = dot(full_two, w_gate)
-        up = dot(full_two, w_up)
-        hidden = (gate * jax.nn.sigmoid(gate) * up).astype(LOW)
-        cargo = [GatherRows(slab_next, 0), GatherRows(out_weight[1], 1)] if layer == 0 else []
-        feed, loads = reduce_tokens(names, dot(hidden, w_down).astype(LOW), cargo, name=f"reduce_two_{layer}")
+        if layer == 0:
+            slab_rows, out_rows = GatherRows(slab_next, 0), GatherRows(out_weight[1], 1)
+            sent[0].phase = 1
+            cargo = [slab_rows, out_rows, sent[0]]
+        feed, full_two, gate, up, loads = forward_feed(
+            names, normed_two, w_gate, w_up, w_down, cargo, name=f"feed_{layer}"
+        )
         saved.append(
             (
                 residual,
@@ -1175,13 +1360,12 @@
                 full_two,
                 gate,
                 up,
-                hidden,
                 (w_qkv, w_out, w_gate, w_up, w_down),
             )
         )
         residual = residual_mid + feed
         if layer == 0:
-            load = (loads[0][0], loads[1][0], loads_two[0])
+            load = (loads[0][0], loads[1][0], loads[2])
     states = residual.astype(LOW)
 
     def own_part(full, dim):
@@ -1215,9 +1399,10 @@
             full_two,
             gate,
             up,
-            hidden,
             (w_qkv, w_out, w_gate, w_up, w_down),
         ) = saved[layer]
+        gate, up = gate.astype(F32), up.astype(F32)
+        hidden = (gate * jax.nn.sigmoid(gate) * up).astype(LOW)
         if layer == LAYERS - 1:
             grad_full = grad_full_last
         else:

time: 1020 us -> 997 us (0.977)
  matrix products: 157 us -> 142 us
    dot_general x10 -> x4, matrix products: 42.8 us -> 6.5 us  [dot(): return jnp.dot(a, b, preferred_element_type=F32)]
    dot_general x10, matrix products: 42.7 us -> 60.9 us  [dot_t(): lax.dot_general(a, b, (((1,), (1,)), ((), ())), preferred_element_type=F32)]
    unnamed x314 -> x376, local copies, waits for them, and re-layouts: 64.7 us -> 82.2 us
    pallas_call x16 -> x14, Pallas kernels: 537 us -> 537 us  [carry_call(): results = list(call(*arrays, *given))]
where the time goes in v2:
time: 997 us; the launch traced here: 990 us
  Pallas kernels  620 us (62%)
  matrix products  142 us (14%)
  local copies, waits for them, and re-layouts  139 us (14%)
  other arithmetic  85.5 us (9%)
    pallas_call x14, Pallas kernels, carry_call(): results = list(call(*arrays, *given))  537 us
    pallas_call x3, Pallas kernels, stages_call(): pl.pallas_call(kernel, out_shape=outs, in_specs=[ANY] * n_in, out_specs=[...  82.8 us
    unnamed x376, local copies, waits for them, and re-layouts  82.2 us
    dot_general x10, matrix products, dot_t(): lax.dot_general(a, b, (((1,), (1,)), ((), ())), preferred_element_type=F32)  60.9 us
    dot_general x10, matrix products, t_dot(): lax.dot_general(a, b, (((0,), (0,)), ((), ())), preferred_element_type=F32)  45.7 us

profile of v2, /device:TPU:31, one launch (start us, length us, event | category | flops | bytes accessed | tf_op | source)
XLA Modules:
  0.0 989.6 jit_solution(13411594394224926320)
XLA Ops:
  7.5 37.6 %open.1 = (bf16[208,640]{1,0:T(8,128)(2,1)}, bf16[832,640]{1,0:T(8,128)(2,1)S(1)}, bf16[192,1536]{1,0:T(8,128)(2,1)S(1)}, bf16[8,272,192]{2,1,0:T(8,128)(2,1)S(1...) custom-call(bf16[2,2,208,128]{3,2,1,0:T(8,128)(2,1)S(1)} %copy-done.39, ...), custom_call_target="tpu_custom_call" | custom-call | tf_op jit(solution)/shard_map/open/pallas_call | solution.py:852
  59.0 34.6 %gather_three_1.1 = (bf16[8,128,1536]{2,1,0:T(8,128)(2,1)S(1)}, bf16[1536,1120]{1,0:T(8,128)(2,1)S(1)}) custom-call(bf16[128,1536]{1,0:T(8,128)(2,1)S(1)} %copy.201.refs_0_, bf16[384,1120]{1,0:T(8,128)(2,1)S(1)} %bitcast.306), custom_call_target="tpu_custom_call" | custom-call | tf_op jit(solution)/shard_map/gather_three_1/pallas_call | solution.py:594
  95.3 3.9 fusion.104
  100.8 34.1 %gather_one_0.1 = (bf16[8,128,1536]{2,1,0:T(8,128)(2,1)S(1)}, bf16[1536,1120]{1,0:T(8,128)(2,1)S(1)}) custom-call(bf16[128,1536]{1,0:T(8,128)(2,1)S(1)} %multiply_convert_fusion.5.refs_0_, bf16[384,1120]{1,0:T(8,128)(2,1)S(1)} %bitcast.305), custom_call_target="tpu_custom_call" | custom-call | tf_op jit(solution)/shard_map/gather_one_0/pallas_call | solution.py:594
  150.2 3.2 neg.34
  160.3 3.7 fusion.39
  170.9 2.9 fusion.44
  176.0 31.0 %reduce_one_0.1 = (f32[128,1536]{1,0:T(8,128)S(1)}, bf16[1120,1536]{1,0:T(8,128)(2,1)S(1)}) custom-call(bf16[4,128,1536]{2,1,0:T(8,128)(2,1)S(1)} %bitcast.314, bf16[1120,384]{1,0:T(8,128)(2,1)S(1)} %get-tuple-element.186.refs_1_), custom_call_target="tpu_custom_call" | custom-call | tf_op jit(solution)/shard_map/reduce_one_0/pallas_call | solution.py:594
  212.6 66.9 %feed_0.1 = (f32[128,1536]{1,0:T(8,128)}, bf16[8,128,1536]{2,1,0:T(8,128)(2,1)}, bf16[1024,1120]{1,0:T(8,128)(2,1)}, bf16[1024,1120]{1,0:T(8,128)(2,1)}, bf16[83...) custom-call(bf16[128,1536]{1,0:T(8,128)(2,1)} %multiply_convert_fusion.4.refs_0_, ...), custom_call_target="tpu_custom_call" | custom-call | tf_op jit(solution)/shard_map/feed_0/pallas_call | solution.py:594
  286.1 33.4 %gather_one_1.1 = (bf16[8,128,1536]{2,1,0:T(8,128)(2,1)S(1)}, bf16[1536,1120]{1,0:T(8,128)(2,1)S(1)}, bf16[832,640]{1,0:T(8,128)(2,1)S(1)}, bf16[192,1536]{1,0:T(8,128)(2,1)S(1)}) custom-call(bf16[128,1536]{1,0:T(8,128)(2,1)S(1)} %copy-done.36, bf16[384,1120]{1,0:T(8,128)(2,1)S(1)} %bitcast.304, bf16[832,640]{1,0:T(8,128)(2,1)S(1)} %copy-done.7, ...), custom_call_target="tpu_custom_call" | custom-call | tf_op jit(solution)/shard_map/gather_one_1/pallas_call | solution.py:594
  327.5 3.2 copy.282
  332.6 3.2 neg.35
  337.3 3.0 copy.280
  340.3 3.5 fusion.41
  348.1 2.9 fusion.43
  352.2 29.9 %reduce_one_1.1 = (f32[128,1536]{1,0:T(8,128)S(1)}, bf16[1120,1536]{1,0:T(8,128)(2,1)S(1)}) custom-call(bf16[4,128,1536]{2,1,0:T(8,128)(2,1)S(1)} %bitcast.315, bf16[1120,384]{1,0:T(8,128)(2,1)S(1)} %get-tuple-element.185.refs_1_), custom_call_target="tpu_custom_call" | custom-call | tf_op jit(solution)/shard_map/reduce_one_1/pallas_call | solution.py:594
  384.9 63.5 %feed_1.1 = (f32[128,1536]{1,0:T(8,128)}, bf16[8,128,1536]{2,1,0:T(8,128)(2,1)}, bf16[1024,1120]{1,0:T(8,128)(2,1)}, bf16[1024,1120]{1,0:T(8,128)(2,1)}) custom-call(bf16[128,1536]{1,0:T(8,128)(2,1)} %multiply_convert_fusion.2.refs_0_, bf16[1536,1120]{1,0:T(8,128)(2,1)} %get-tuple-element.83.refs_1_, bf16[1536,1120]{1,0:T(8,128)(2,1)} %copy-done.13, ...), custom_call_target="tpu_custom_call" | custom-call | tf_op jit(solution)/shard_map/feed_1/pallas_call | solution.py:594
  448.4 10.6 %fusion.6 = (bf16[1024,1120]{1,0:T(8,128)(2,1)S(1)}, f32[1024,1120]{1,0:T(8,128)}) fusion(bf16[1024,1120]{1,0:T(8,128)(2,1)} %get-tuple-element.87, bf16[1024,1120]{1,0:T(8,128)(2,1)} %get-tuple-element.88, bf16[1024,1536]{1,0:T(8,128)(2,1)} %bitcast.318, bf16[1120,1536]{1,0:T(8,128)(2,1)S(1)} %copy-done.18), kind=kOutput, calls=%fused_computation.38 | convolution fusion | flops 3536977920 | bytes 18055168 | tf_op jit(solution)/shard_map/dot_general | solution.py:1199
  458.9 6.3 fusion.114
  465.3 9.2 add_convert_fusion.1
  474.6 5.5 convolution_convert_fusion.5.refs_1_
  480.1 38.6 %reduce_three_1.1 = (f32[128,1536]{1,0:T(8,128)S(1)}, bf16[2,1120,384]{2,1,0:T(8,128)(2,1)S(1)}) custom-call(bf16[8,128,1536]{2,1,0:T(8,128)(2,1)S(1)} %bitcast.308, bf16[1120,1536]{1,0:T(8,128)(2,1)S(1)} %convolution_convert_fusion.5.refs_1_), custom_call_target="tpu_custom_call" | custom-call | tf_op jit(solution)/shard_map/reduce_three_1/pallas_call | solution.py:594
  522.5 4.5 convolution_convert_fusion.4.refs_1_
  527.0 30.9 %gather_four_1.1 = (bf16[4,128,1536]{2,1,0:T(8,128)(2,1)S(1)}, bf16[2,384,1120]{2,1,0:T(8,128)(2,1)S(1)}) custom-call(bf16[128,1536]{1,0:T(8,128)(2,1)S(1)} %get-tuple-element.169.refs_0_, bf16[1536,1120]{1,0:T(8,128)(2,1)S(1)} %convolution_convert_fusion.4.refs_1_), custom_call_target="tpu_custom_call" | custom-call | tf_op jit(solution)/shard_map/gather_four_1/pallas_call | solution.py:594
  561.8 4.0 multiply_reduce_fusion.1
  574.6 3.1 broadcast_multiply_fusion.1
  583.4 5.4 convolution_convert_fusion.7
  588.8 7.4 convolution_convert_fusion.3.refs_1_
  597.8 4.9 convolution_convert_fusion.9
  606.1 38.0 %reduce_four_1.1 = (f32[128,1536]{1,0:T(8,128)S(1)}, bf16[2,384,1120]{2,1,0:T(8,128)(2,1)S(1)}, bf16[4,208,640]{2,1,0:T(8,128)(2,1)S(1)}, bf16[192,1536]{1,0:T(8,128)(2,1)S(1)}) custom-call(bf16[8,128,1536]{2,1,0:T(8,128)(2,1)S(1)} %bitcast.309, bf16[1536,1120]{1,0:T(8,128)(2,1)S(1)} %convolution_convert_fusion.3.refs_1_, ...), custom_call_target="tpu_custom_call" | custom-call | tf_op jit(solution)/shard_map/reduce_four_1/pallas_call | solution.py:594
  646.1 32.8 %gather_three_0.1 = (bf16[8,128,1536]{2,1,0:T(8,128)(2,1)S(1)}, bf16[2,208,640]{2,1,0:T(8,128)(2,1)S(1)}, bf16[2,192,384]{2,1,0:T(8,128)(2,1)S(1)}) custom-call(bf16[128,1536]{1,0:T(8,128)(2,1)S(1)} %get-tuple-element.167.refs_0_, bf16[832,640]{1,0:T(8,128)(2,1)S(1)} %bitcast.301, bf16[192,1536]{1,0:T(8,128)(2,1)S(1)} %fusion.60.refs_2_), custom_call_target="tpu_custom_call" | custom-call | tf_op jit(solution)/shard_map/gather_three_0/pallas_call | solution.py:594
  679.0 6.7 fusion.10
  685.8 6.3 fusion.115
  692.1 10.2 %add_convert_fusion = bf16[1024,1536]{1,0:T(8,128)(2,1)} fusion(f32[1024,1536]{1,0:T(8,128)} %fusion.115, bf16[1536,1120]{1,0:T(8,128)(2,1)S(1)} %copy-done.12, f32[1024,1120]{1,0:T(8,128)} %get-tuple-element.237, bf16[1024,1120]{1,0:T(8,128)(2,1)S(1)} %copy-done.160), kind=kOutput, calls=%fused_computation.17 | convolution fusion | flops 3534389248 | bytes 19759104 | tf_op jit(solution)/shard_map/dot_general | solution.py:1199
  702.3 6.7 convolution_convert_fusion.2.refs_1_
  715.0 31.9 %reduce_three_0.1 = (f32[128,1536]{1,0:T(8,128)S(1)}, bf16[2,1120,384]{2,1,0:T(8,128)(2,1)S(1)}, bf16[2,2,2,208,128]{4,3,2,1,0:T(8,128)(2,1)S(1)}) custom-call(bf16[8,128,1536]{2,1,0:T(8,128)(2,1)S(1)} %bitcast.307, bf16[1120,1536]{1,0:T(8,128)(2,1)S(1)} %copy-done.6, bf16[208,640]{1,0:T(8,128)(2,1)S(1)} %add_convert_fusion.5.refs_2_), custom_call_target="tpu_custom_call" | custom-call | tf_op jit(solution)/shard_map/reduce_three_0/pallas_call | solution.py:594
  750.5 4.9 convolution_convert_fusion.1.refs_1_
  755.4 32.4 %gather_four_0.1 = (bf16[4,128,1536]{2,1,0:T(8,128)(2,1)S(1)}, bf16[2,384,1120]{2,1,0:T(8,128)(2,1)S(1)}) custom-call(bf16[128,1536]{1,0:T(8,128)(2,1)S(1)} %get-tuple-element.165.refs_0_, bf16[1536,1120]{1,0:T(8,128)(2,1)S(1)} %convolution_convert_fusion.1.refs_1_), custom_call_target="tpu_custom_call" | custom-call | tf_op jit(solution)/shard_map/gather_four_0/pallas_call | solution.py:594
  794.0 4.7 multiply_reduce_fusion
  798.6 3.6 multiply_convert_fusion
  806.6 3.2 broadcast_multiply_fusion
  815.9 4.5 convolution_convert_fusion.6
  820.5 7.4 convolution_convert_fusion.refs_1_
  835.0 38.8 %reduce_four_0.1 = (f32[128,1536]{1,0:T(8,128)S(1)}, bf16[2,384,1120]{2,1,0:T(8,128)(2,1)S(1)}, bf16[4,208,640]{2,1,0:T(8,128)(2,1)S(1)}, bf16[192,1536]{1,0:T(8,128)(2,1)S(1)}) custom-call(bf16[8,128,1536]{2,1,0:T(8,128)(2,1)S(1)} %bitcast.310, bf16[1536,1120]{1,0:T(8,128)(2,1)S(1)} %convolution_convert_fusion.refs_1_, ...), custom_call_target="tpu_custom_call" | custom-call | tf_op jit(solution)/shard_map/reduce_four_0/pallas_call | solution.py:594
  887.6 35.4 %close.1 = (bf16[8,256,192]{2,1,0:T(8,128)(2,1)S(1)}, f32[4,8,8,192]{3,2,1,0:T(8,128)S(1)}, bf16[2,208,640]{2,1,0:T(8,128)(2,1)S(1)}, bf16[2,192,384]{2,1,0:T(8,128)(2,1)S(1)}) custom-call(bf16[8,256,192]{2,1,0:T(8,128)(2,1)S(1)} %bitcast.303, f32[8,8,192]{2,1,0:T(8,128)S(1)} %pad_bitcast_fusion.refs_1_, bf16[832,640]{1,0:T(8,128)(2,1)S(1)} %bitcast.299, ...), custom_call_target="tpu_custom_call" | custom-call | tf_op jit(solution)/shard_map/close/pallas_call | solution.py:852
  939.6 9.9 %close_heads.1 = bf16[2,2,2,208,128]{4,3,2,1,0:T(8,128)(2,1)S(1)} custom-call(bf16[208,640]{1,0:T(8,128)(2,1)S(1)} %add_convert_fusion.4.refs_0_), custom_call_target="tpu_custom_call" | custom-call | tf_op jit(solution)/shard_map/close_heads/pallas_call | solution.py:852
  967.4 5.3 copy.253
  978.7 5.2 copy.254
  (572 shorter events, 207.1 us)
Async XLA Ops:
  52.2 157.4 %copy-start.137 = (f32[1536]{0:T(1024)}, f32[1536]{0:T(1024)S(1)}, u32[]{:S(2)}) copy-start(f32[1536]{0:T(1024)S(1)} %get-tuple-element.163) | copy-start | bytes 18436
  159.0 408.5 %copy-start.88 = (f32[64,1024]{1,0:T(8,128)}, f32[64,1024]{1,0:T(8,128)S(1)}, u32[]{:S(2)}) copy-start(f32[64,1024]{1,0:T(8,128)S(1)} %get-tuple-element.213) | copy-start | bytes 786436
  175.8 33.0 %copy-start.70 = (f32[128,1536]{1,0:T(8,128)S(1)}, f32[128,1536]{1,0:T(8,128)}, u32[]{:S(2)}) copy-start(f32[128,1536]{1,0:T(8,128)} %copy-done.69) | copy-start | bytes 2359300
  176.0 34.5 %copy-start.96 = (bf16[1,384,1120]{1,2,0:T(8,128)(2,1)S(1)}, bf16[1,384,1120]{1,2,0:T(8,128)(2,1)}, u32[]{:S(2)}) copy-start(bf16[1,384,1120]{1,2,0:T(8,128)(2,1)} %get-tuple-element.189) | copy-start | bytes 2580484
  209.0 70.5 %copy-start.72 = (f32[128,1536]{1,0:T(8,128)}, f32[128,1536]{1,0:T(8,128)S(1)}, u32[]{:S(2)}) copy-start(f32[128,1536]{1,0:T(8,128)S(1)} %get-tuple-element.176) | copy-start | bytes 2359300
  209.6 69.9 %copy-start.146 = (f32[128]{0:T(128)}, f32[128]{0:T(128)S(1)}, u32[]{:S(2)}) copy-start(f32[128]{0:T(128)S(1)} %get-tuple-element.219) | copy-start | bytes 1540
  281.5 38.0 %copy-start.148 = (f32[128]{0:T(128)}, f32[128]{0:T(128)S(1)}, u32[]{:S(2)}) copy-start(f32[128]{0:T(128)S(1)} %get-tuple-element.221) | copy-start | bytes 1540
  351.1 32.7 %copy-start.75 = (f32[128,1536]{1,0:T(8,128)S(1)}, f32[128,1536]{1,0:T(8,128)}, u32[]{:S(2)}) copy-start(f32[128,1536]{1,0:T(8,128)} %copy-done.74) | copy-start | bytes 2359300
  384.9 63.5 %copy-start.18 = (bf16[1120,1536]{1,0:T(8,128)(2,1)S(1)}, bf16[1120,1536]{1,0:T(8,128)(2,1)}, u32[]{:S(2)}) copy-start(bf16[1120,1536]{1,0:T(8,128)(2,1)} %copy-done.17) | copy-start | bytes 10321924
  448.3 10.6 %copy-start.95 = (bf16[1536,1120]{1,0:T(8,128)(2,1)S(1)}, bf16[1536,1120]{1,0:T(8,128)(2,1)}, u32[]{:S(2)}) copy-start(bf16[1536,1120]{1,0:T(8,128)(2,1)} %get-tuple-element.83.refs_1_) | copy-start | bytes 10321924
  465.3 9.3 copy-start.58
  465.3 9.3 copy-start.165
  480.1 38.7 %copy-start.5 = (bf16[1120,1536]{1,0:T(8,128)(2,1)}, bf16[1120,1536]{1,0:T(8,128)(2,1)S(1)}, u32[]{:S(2)}) copy-start(bf16[1120,1536]{1,0:T(8,128)(2,1)S(1)} %convolution_convert_fusion.5.refs_1_) | copy-start | bytes 10321924
  480.1 39.5 %copy-start.122 = (f32[128,1536]{1,0:T(8,128)S(1)}, f32[128,1536]{1,0:T(8,128)}, u32[]{:S(2)}) copy-start(f32[128,1536]{1,0:T(8,128)} %get-tuple-element.86) | copy-start | bytes 2359300
  519.6 40.1 %slice-start.2 = ((s8[6291456]{0:T(1024)(128)(4,1)}), s8[2097152]{0:T(1024)(128)(4,1)S(1)}, s32[]{:S(2)}) async-start(s8[6291456]{0:T(1024)(128)(4,1)} %bitcast.330), calls=%async_computation.2 | async-start | bytes 4194304
  522.5 37.2 %slice-start.3 = ((s8[6291456]{0:T(1024)(128)(4,1)}), s8[4194304]{0:T(1024)(128)(4,1)S(1)}, s32[]{:S(2)}) async-start(s8[6291456]{0:T(1024)(128)(4,1)} %bitcast.330), calls=%async_computation.3 | async-start | bytes 8388608
  527.0 31.8 %copy-start = (bf16[1536,1120]{1,0:T(8,128)(2,1)}, bf16[1536,1120]{1,0:T(8,128)(2,1)S(1)}, u32[]{:S(2)}) copy-start(bf16[1536,1120]{1,0:T(8,128)(2,1)S(1)} %convolution_convert_fusion.4.refs_1_) | copy-start | bytes 10321924
  527.0 30.9 %copy-start.128 = (bf16[192,1536]{1,0:T(8,128)(2,1)S(1)}, bf16[192,1536]{1,0:T(8,128)(2,1)}, u32[]{:S(2)}) copy-start(bf16[192,1536]{1,0:T(8,128)(2,1)} %copy-done.127) | copy-start | bytes 1769476
  527.0 30.9 %copy-start.130 = (bf16[192,1536]{1,0:T(8,128)(2,1)S(1)}, bf16[192,1536]{1,0:T(8,128)(2,1)}, u32[]{:S(2)}) copy-start(bf16[192,1536]{1,0:T(8,128)(2,1)} %copy-done.129) | copy-start | bytes 1769476
  570.3 12.8 %copy-start.144 = (pred[1024]{0:T(1024)(128)(4,1)}, pred[1024]{0:T(1024)(128)(4,1)S(1)}, u32[]{:S(2)}) copy-start(pred[1024]{0:T(1024)(128)(4,1)S(1)} %broadcast_in_dim.154) | copy-start | bytes 3076
  606.1 38.0 %copy-start.76 = (f32[128,1536]{1,0:T(8,128)S(1)}, f32[128,1536]{1,0:T(8,128)}, u32[]{:S(2)}) copy-start(f32[128,1536]{1,0:T(8,128)} %copy-done.74) | copy-start | bytes 2359300
  606.1 38.0 %copy-start.149 = (f32[128]{0:T(128)S(1)}, f32[128]{0:T(128)}, u32[]{:S(2)}) copy-start(f32[128]{0:T(128)} %copy-done.148) | copy-start | bytes 1540
  606.1 38.2 %copy-start.98 = (f32[128,1536]{1,0:T(8,128)S(1)}, f32[128,1536]{1,0:T(8,128)}, u32[]{:S(2)}) copy-start(f32[128,1536]{1,0:T(8,128)} %get-tuple-element.170) | copy-start | bytes 2359300
  606.1 38.2 %copy-start.154 = (f32[128]{0:T(128)S(1)}, f32[128]{0:T(128)}, u32[]{:S(2)}) copy-start(f32[128]{0:T(128)} %get-tuple-element.220) | copy-start | bytes 1540
  644.4 34.6 %copy-start.162 = (bf16[1024,1120]{1,0:T(8,128)(2,1)S(1)}, bf16[1024,1120]{1,0:T(8,128)(2,1)}, u32[]{:S(2)}) copy-start(bf16[1024,1120]{1,0:T(8,128)(2,1)} %get-tuple-element.96) | copy-start | bytes 6881284
  645.6 33.4 %copy-start.160 = (bf16[1024,1120]{1,0:T(8,128)(2,1)S(1)}, bf16[1024,1120]{1,0:T(8,128)(2,1)}, u32[]{:S(2)}) copy-start(bf16[1024,1120]{1,0:T(8,128)(2,1)} %get-tuple-element.97) | copy-start | bytes 6881284
  645.9 39.8 %copy-start.4 = (bf16[4,208,640]{2,1,0:T(8,128)(2,1)}, bf16[4,208,640]{2,1,0:T(8,128)(2,1)S(1)}, u32[]{:S(2)}) copy-start(bf16[4,208,640]{2,1,0:T(8,128)(2,1)S(1)} %fusion.37) | copy-start | bytes 3194884
  645.9 33.1 %copy-start.16 = (bf16[1120,1536]{1,0:T(8,128)(2,1)S(1)}, bf16[1120,1536]{1,0:T(8,128)(2,1)}, u32[]{:S(2)}) copy-start(bf16[1120,1536]{1,0:T(8,128)(2,1)} %copy-done.15) | copy-start | bytes 10321924
  646.1 39.6 %copy-start.21 = (bf16[192,1536]{1,0:T(8,128)(2,1)}, bf16[192,1536]{1,0:T(8,128)(2,1)S(1)}, u32[]{:S(2)}) copy-start(bf16[192,1536]{1,0:T(8,128)(2,1)S(1)} %fusion.60.refs_2_) | copy-start | bytes 1769476
  714.9 32.8 %copy-start.73 = (f32[128,1536]{1,0:T(8,128)S(1)}, f32[128,1536]{1,0:T(8,128)}, u32[]{:S(2)}) copy-start(f32[128,1536]{1,0:T(8,128)} %copy-done.72) | copy-start | bytes 2359300
  714.9 32.8 %copy-start.138 = (f32[1536]{0:T(1024)S(1)}, f32[1536]{0:T(1024)}, u32[]{:S(2)}) copy-start(f32[1536]{0:T(1024)} %copy-done.137) | copy-start | bytes 18436
  714.9 32.8 %copy-start.147 = (f32[128]{0:T(128)S(1)}, f32[128]{0:T(128)}, u32[]{:S(2)}) copy-start(f32[128]{0:T(128)} %copy-done.146) | copy-start | bytes 1540
  714.9 33.6 %copy-start.101 = (f32[128,1536]{1,0:T(8,128)S(1)}, f32[128,1536]{1,0:T(8,128)}, u32[]{:S(2)}) copy-start(f32[128,1536]{1,0:T(8,128)} %get-tuple-element.168) | copy-start | bytes 2359300
  714.9 33.6 %copy-start.153 = (f32[128]{0:T(128)S(1)}, f32[128]{0:T(128)}, u32[]{:S(2)}) copy-start(f32[128]{0:T(128)} %get-tuple-element.218) | copy-start | bytes 1540
  714.9 34.8 %copy-start.172 = (bf16[1024,1120]{1,0:T(8,128)(2,1)S(1)}, bf16[1024,1120]{1,0:T(8,128)(2,1)}, u32[]{:S(2)}) copy-start(bf16[1024,1120]{1,0:T(8,128)(2,1)} %copy-done.171) | copy-start | bytes 6881284
  714.9 75.3 %slice-start = ((s8[6291456]{0:T(1024)(128)(4,1)}), s8[2097152]{0:T(1024)(128)(4,1)S(1)}, s32[]{:S(2)}) async-start(s8[6291456]{0:T(1024)(128)(4,1)} %bitcast.328), calls=%async_computation | async-start | bytes 4194304
  750.5 39.8 %slice-start.1 = ((s8[6291456]{0:T(1024)(128)(4,1)}), s8[4194304]{0:T(1024)(128)(4,1)S(1)}, s32[]{:S(2)}) async-start(s8[6291456]{0:T(1024)(128)(4,1)} %bitcast.328), calls=%async_computation.1 | async-start | bytes 8388608
  755.4 33.3 %copy-start.1 = (bf16[1536,1120]{1,0:T(8,128)(2,1)}, bf16[1536,1120]{1,0:T(8,128)(2,1)S(1)}, u32[]{:S(2)}) copy-start(bf16[1536,1120]{1,0:T(8,128)(2,1)S(1)} %convolution_convert_fusion.1.refs_1_) | copy-start | bytes 10321924
  755.4 32.4 %copy-start.124 = (bf16[192,1536]{1,0:T(8,128)(2,1)S(1)}, bf16[192,1536]{1,0:T(8,128)(2,1)}, u32[]{:S(2)}) copy-start(bf16[192,1536]{1,0:T(8,128)(2,1)} %copy-done.123) | copy-start | bytes 1769476
  755.4 32.4 %copy-start.126 = (bf16[192,1536]{1,0:T(8,128)(2,1)S(1)}, bf16[192,1536]{1,0:T(8,128)(2,1)}, u32[]{:S(2)}) copy-start(bf16[192,1536]{1,0:T(8,128)(2,1)} %copy-done.125) | copy-start | bytes 1769476
  820.4 7.8 copy-start.56
  835.0 38.9 %copy-start.71 = (f32[128,1536]{1,0:T(8,128)S(1)}, f32[128,1536]{1,0:T(8,128)}, u32[]{:S(2)}) copy-start(f32[128,1536]{1,0:T(8,128)} %copy-done.69) | copy-start | bytes 2359300
  835.0 38.9 %copy-start.136 = (f32[1536]{0:T(1024)S(1)}, f32[1536]{0:T(1024)}, u32[]{:S(2)}) copy-start(f32[1536]{0:T(1024)} %copy-done.135) | copy-start | bytes 18436
  835.0 38.9 %copy-start.151 = (f32[128]{0:T(128)S(1)}, f32[128]{0:T(128)}, u32[]{:S(2)}) copy-start(f32[128]{0:T(128)} %copy-done.150) | copy-start | bytes 1540
  835.0 39.7 %copy-start.100 = (f32[128,1536]{1,0:T(8,128)S(1)}, f32[128,1536]{1,0:T(8,128)}, u32[]{:S(2)}) copy-start(f32[128,1536]{1,0:T(8,128)} %get-tuple-element.166) | copy-start | bytes 2359300
  835.0 39.7 %copy-start.155 = (f32[128]{0:T(128)S(1)}, f32[128]{0:T(128)}, u32[]{:S(2)}) copy-start(f32[128]{0:T(128)} %get-tuple-element.216) | copy-start | bytes 1540
  887.4 36.7 %copy-start.3 = (bf16[4,208,640]{2,1,0:T(8,128)(2,1)}, bf16[4,208,640]{2,1,0:T(8,128)(2,1)S(1)}, u32[]{:S(2)}) copy-start(bf16[4,208,640]{2,1,0:T(8,128)(2,1)S(1)} %fusion.36) | copy-start | bytes 3194884
  887.6 36.5 %copy-start.22 = (bf16[192,1536]{1,0:T(8,128)(2,1)}, bf16[192,1536]{1,0:T(8,128)(2,1)S(1)}, u32[]{:S(2)}) copy-start(bf16[192,1536]{1,0:T(8,128)(2,1)S(1)} %fusion.59.refs_3_) | copy-start | bytes 1769476
  (133 other events, 377.4 us)

commit v3 on v2

--- a/solution.py
+++ b/solution.py
@@ -93,6 +93,12 @@
     pl.when(jnp.logical_not(edge))(lambda: pl.semaphore_wait(barrier, count + 2))
 
 
+class From:
+    def __init__(self, item, at=0):
+        self.item, self.at = item, at
+        self.shape, self.dtype = item.outs[at].shape, item.outs[at].dtype
+
+
 class Cargo:
     arrays = ()
     outs = ()
@@ -111,9 +117,11 @@
 
 
 class GatherRows(Cargo):
-    def __init__(self, block, dim):
-        self.dim = dim
+    def __init__(self, block, dim, layer=None, phase=0):
+        self.dim, self.layer, self.phase = dim, layer, phase
         self.arrays = (block,)
+        if layer is not None:
+            block = jax.ShapeDtypeStruct(block.shape[1:], block.dtype)
         full = list(block.shape)
         full[dim] *= 4
         self.size = block.shape[dim]
@@ -132,8 +140,11 @@
         first = pl.multiple_of(row * self.size, 16)
         return full.at[pl.ds(first, self.half), :], full.at[pl.ds(first + self.half, self.rest), :]
 
+    def source(self, ins):
+        return ins[0] if self.layer is None else ins[0].at[self.layer]
+
     def copies(self, place, ins, outs, scratch):
-        (src,), (dst,), (send, recv, _) = ins, outs, scratch
+        src, (dst,), (send, recv, _) = self.source(ins), outs, scratch
         x, y, d = place.rows()
         block, mine = self.halves(src), self.spots(dst, place.r)
         from_x, from_y = self.spots(dst, x), self.spots(dst, y)
@@ -153,7 +164,7 @@
         return remote(view, view, scratch[0].at[0], scratch[1].at[sem], (row, place.k))
 
     def start(self, place, ins, outs, scratch, later):
-        (src,), (dst,), (_, _, keep_sem) = ins, outs, scratch
+        src, (dst,), (_, _, keep_sem) = self.source(ins), outs, scratch
         out, onward = self.copies(place, ins, outs, scratch)
         for copy in out:
             copy.start()
@@ -178,8 +189,8 @@
 
 
 class ScatterRows(Cargo):
-    def __init__(self, grad, dim):
-        self.dim = dim
+    def __init__(self, grad, dim, phase=0):
+        self.dim, self.phase = dim, phase
         self.arrays = (grad,)
         part = list(grad.shape)
         part[dim] //= 4
@@ -250,8 +261,8 @@
 class Swap(Cargo):
     reach = "line"
 
-    def __init__(self, *arrays):
-        self.arrays = arrays
+    def __init__(self, *arrays, phase=0):
+        self.arrays, self.phase = arrays, phase
         self.outs = tuple(jax.ShapeDtypeStruct(a.shape, a.dtype) for a in arrays)
         self.scratch = (pltpu.SemaphoreType.DMA((len(arrays),)), pltpu.SemaphoreType.DMA((len(arrays),)))
 
@@ -273,39 +284,47 @@
 class HeadsToChips(Cargo):
     reach = "col"
 
-    def __init__(self, tiles):
-        self.arrays = (tiles,)
+    def __init__(self, weight, biases, layer):
+        self.layer = layer
+        self.arrays = (weight, biases)
         self.outs = (jax.ShapeDtypeStruct((HALF, 5 * HD), LOW),)
-        self.scratch = (pltpu.SemaphoreType.DMA((2, 2, 2)), pltpu.SemaphoreType.DMA((5,)))
+        self.scratch = (pltpu.SemaphoreType.DMA((2, 2, 2, 2)), pltpu.SemaphoreType.DMA((5, 2)))
 
     def start(self, place, ins, outs, scratch, later):
-        (tiles,), (slab,), (send, recv) = ins, outs, scratch
+        (weight, biases), (slab,), (send, recv) = ins, outs, scratch
         r, k, z, c = place.r, place.k, place.z, place.c
         query = k < 6
+        rows = D // 8
         for second in range(2):
             for i in range(2):
                 head = 2 * k + i
                 chip = jnp.where(query, head // 3, 2 * i + second)
                 t = jnp.where(query, head % 3, k - 3)
-                spot = slab.at[:, pl.ds(pl.multiple_of(t * HD, HD), HD)]
+                cut = pl.ds(pl.multiple_of(t * HD, HD), HD)
+                spots = slab.at[0:rows, cut], slab.at[rows:HALF, cut]
                 for core in range(2):
                     here = k == 2 * chip + core
                     away = jnp.logical_not(here)
                     if second == 1:
                         here, away = here & (k >= 6), away & (k >= 6)
-                    sem = send.at[i, second, core]
-                    copy = remote(tiles.at[i, core], spot, sem, recv.at[t], (r, 2 * chip + core))
-                    pl.when(away)(copy.start)
-                    later.add(copy.wait_send, away)
-                    keep = pltpu.make_async_copy(tiles.at[i, core], spot, sem)
-                    pl.when(here)(keep.start)
-                    later.add(keep.wait, here)
+                    views = (
+                        weight.at[self.layer, core * rows : (core + 1) * rows, i * HD : (i + 1) * HD],
+                        biases.at[self.layer, i],
+                    )
+                    for part in range(2):
+                        sem = send.at[i, second, core, part]
+                        copy = remote(views[part], spots[part], sem, recv.at[t, part], (r, 2 * chip + core))
+                        pl.when(away)(copy.start)
+                        later.add(copy.wait_send, away)
+                        keep = pltpu.make_async_copy(views[part], spots[part], sem)
+                        pl.when(here)(keep.start)
+                        later.add(keep.wait, here)
         for t in range(5):
             owner, _ = tile_owner(z, t)
-            came = remote(
-                tiles.at[0, 0], slab.at[:, t * HD : (t + 1) * HD], send.at[0, 0, 0], recv.at[t], (r, owner)
-            )
-            later.add(came.wait_recv, k != owner)
+            cut = slice(t * HD, (t + 1) * HD)
+            for part, spot in enumerate((slab.at[0:rows, cut], slab.at[rows:HALF, cut])):
+                came = remote(spot, spot, send.at[0, 0, 0, 0], recv.at[t, part], (r, owner))
+                later.add(came.wait_recv, k != owner)
 
 
 class HeadsToOwners(Cargo):
@@ -348,11 +367,12 @@
 
 
 class Exchange(Cargo):
-    def __init__(self, chunks, every_row=False):
+    def __init__(self, chunks, every_row=False, same=False):
         self.arrays = (chunks,)
+        self.same = same
         self.rows_too = every_row
         self.reach = "all" if every_row else "col"
-        lead = (4,) if every_row else ()
+        lead = (4,) if every_row else (8,) if same else ()
         self.outs = (jax.ShapeDtypeStruct((*lead, *chunks.shape), chunks.dtype),)
         self.scratch = (pltpu.SemaphoreType.DMA((4, 8)), pltpu.SemaphoreType.DMA((4, 8)))
 
@@ -367,12 +387,13 @@
                 theirs = dst.at[kk] if rr is None else dst.at[rr, kk]
                 at = 0 if rr is None else rr
                 my_at = 0 if rr is None else r
-                copy = remote(src.at[kk], mine, send.at[at, kk], recv.at[my_at, k], (to_row, kk))
+                part = src if self.same else src.at[kk]
+                copy = remote(part, mine, send.at[at, kk], recv.at[my_at, k], (to_row, kk))
                 pl.when(jnp.logical_not(here))(copy.start)
                 later.add(copy.wait_send, jnp.logical_not(here))
-                came = remote(src.at[kk], theirs, send.at[at, kk], recv.at[at, kk], (to_row, kk))
+                came = remote(part, theirs, send.at[at, kk], recv.at[at, kk], (to_row, kk))
                 later.add(came.wait_recv, jnp.logical_not(here))
-                keep = pltpu.make_async_copy(src.at[kk], mine, send.at[at, kk])
+                keep = pltpu.make_async_copy(part, mine, send.at[at, kk])
                 pl.when(here)(keep.start)
                 later.add(keep.wait, here)
 
@@ -391,70 +412,19 @@
     lax.fori_loop(0, rows // 16, step, 0)
 
 
-def gather_line(place, block, full, sems, later, both, middle):
-    send_r, send_l, send_p, recv, keep_sem = sems
-    z, c = place.z, place.c
-
-    def spot(zz, cc):
-        return full.at[2 * zz + cc] if both else full.at[zz]
-
-    def arrival(zz, cc):
-        return recv.at[2 * zz + cc]
-
-    def pass_on(src, zz, slot):
-        dst, sem = spot(zz, c), arrival(zz, c)
-
-        def go(send, device):
-            return remote(src, dst, send.at[slot], sem, device)
-
-        return (
-            go(send_r, place.at(jnp.minimum(z + 1, 3), c)),
-            go(send_l, place.at(jnp.maximum(z - 1, 0), c)),
-            go(send_p, place.at(z, 1 - c)),
-        )
-
-    right, left, partner = pass_on(block, z, 0)
-    pl.when(z < 3)(right.start)
-    pl.when(z > 0)(left.start)
-    later.add(right.wait_send, z < 3)
-    later.add(left.wait_send, z > 0)
-    if both:
-        partner.start()
-        later.add(partner.wait_send)
-    keep = pltpu.make_async_copy(block, spot(z, c), keep_sem.at[0])
-    keep.start()
-    later.add(keep.wait)
-    for t in range(1, 4):
-        if t == 2:
-            middle()
-        for way in (-1, 1):
-            there = z + way * t
-            valid = (there >= 0) & (there <= 3)
-            zz = jnp.clip(there, 0, 3)
-            right, left, partner = pass_on(spot(zz, c), zz, t if way == -1 else 3 + t)
-            onward, may = (right, z < 3) if way == -1 else (left, z > 0)
-
-            @pl.when(valid)
-            def _(onward=onward, may=may, partner=partner):
-                onward.wait_recv()
-                pl.when(may)(onward.start)
-                if both:
-                    partner.start()
-
-            later.add(onward.wait_send, valid & may)
-            if both:
-                later.add(partner.wait_send, valid)
-    if both:
-        for zz in range(4):
-            came = remote(block, spot(zz, 1 - c), send_p.at[0], arrival(zz, 1 - c), place.at(z, 1 - c))
-            later.add(came.wait_recv)
+def at_two(middle):
+    def between(s):
+        if s == 2:
+            middle(1)
+
+    return between
 
 
 def pair_copy(place, part, from_p, sems, j):
     return remote(part.at[2 * j + 1 - place.c], from_p.at[j], sems[0].at[j], sems[1].at[j], place.at(place.z, 1 - place.c))
 
 
-def reduce_line(place, part, out, from_p, from_r, from_l, held, sems, later, both, middle, sent=False):
+def reduce_line(place, part, out, from_p, from_r, from_l, held, sems, later, both, between, sent=False):
     send_p, recv_p, send, recv_r, recv_l = sems
     z, c = place.z, place.c
     right_at, left_at = place.at(jnp.minimum(z + 1, 3), c), place.at(jnp.maximum(z - 1, 0), c)
@@ -482,8 +452,8 @@
         return [own(j)]
 
     for s in range(3):
-        if s == 2:
-            middle()
+        if s:
+            between(s)
         for go_right in (True, False):
             if go_right:
                 j, valid, first = 3 - s + z, z <= s, z == 0
@@ -536,6 +506,15 @@
         return self.next - 1
 
 
+class Inner:
+    def __init__(self, shape, dtype=LOW):
+        self.shape, self.dtype = shape, dtype
+
+
+def given_arrays(item):
+    return [a for a in item.arrays if not isinstance(a, (From, Inner))]
+
+
 def carry_kernel(body, reach, n_in, n_out, n_scratch, cargo, *refs):
     refs = list(refs)
 
@@ -545,26 +524,31 @@
         return taken
 
     ins = pop(n_in)
-    given = [pop(sum(not isinstance(a, From) for a in item.arrays)) for item in cargo]
+    given = [pop(len(given_arrays(item))) for item in cargo]
     outs = pop(n_out)
     made = {item: pop(len(item.outs)) for item in cargo}
     scratch = pop(n_scratch)
     held = {item: pop(len(item.scratch)) for item in cargo}
     taken = {
-        item: [made[a.item][a.at] if isinstance(a, From) else mine.pop(0) for a in item.arrays]
+        item: [
+            made[a.item][a.at] if isinstance(a, From) else a if isinstance(a, Inner) else mine.pop(0)
+            for a in item.arrays
+        ]
         for item, mine in zip(cargo, given)
     }
     place = Place()
     later = Later()
-    owed = [Later(), Later()]
+    owed = [Later() for _ in range(4)]
     greet(place, {reach, *(item.reach for item in cargo)})
 
-    def start(phase):
-        if phase == 1 and any(isinstance(a, From) for item in cargo for a in item.arrays):
-            owed[0].run()
-        for item in cargo:
-            if item.phase == phase:
-                item.start(place, taken[item], made[item], held[item], owed[phase])
+    def start(phase, *inner):
+        inner = list(inner)
+        mine = [item for item in cargo if item.phase == phase]
+        for before in sorted({a.item.phase for item in mine for a in item.arrays if isinstance(a, From)}):
+            owed[before].run()
+        for item in mine:
+            taken[item] = [inner.pop(0) if isinstance(a, Inner) else a for a in taken[item]]
+            item.start(place, taken[item], made[item], held[item], owed[phase])
 
     def middle(phase=0):
         for item in cargo:
@@ -574,12 +558,12 @@
     start(0)
     body(place, ins, outs, scratch, later, middle, start)
     later.run()
-    owed[0].run()
-    owed[1].run()
+    for waits in owed:
+        waits.run()
 
 
 def carry_call(names, body, reach, arrays, in_specs, outs, out_specs, scratch, cargo, name=None, vmem=40):
-    given = [a for item in cargo for a in item.arrays if not isinstance(a, From)]
+    given = [a for item in cargo for a in given_arrays(item)]
     call = pl.pallas_call(
         partial(carry_kernel, body, reach, len(arrays), len(outs), len(scratch), cargo),
         out_shape=[*outs, *(o for item in cargo for o in item.outs)],
@@ -601,60 +585,6 @@
     return main, loads
 
 
-def gather_tokens(names, block, cargo, both=True, name=None):
-    tokens, width = block.shape
-    blocks = 8 if both else 4
-
-    def body(place, ins, outs, scratch, later, middle, start):
-        gather_line(place, ins[0], outs[0], scratch, later, both, middle)
-
-    (full,), loads = carry_call(
-        names,
-        body,
-        "line",
-        [block],
-        [ONCHIP],
-        [jax.ShapeDtypeStruct((blocks, tokens, width), block.dtype)],
-        [ANY],
-        [
-            pltpu.SemaphoreType.DMA((7,)),
-            pltpu.SemaphoreType.DMA((7,)),
-            pltpu.SemaphoreType.DMA((7,)),
-            pltpu.SemaphoreType.DMA((8,)),
-            pltpu.SemaphoreType.DMA((1,)),
-        ],
-        cargo,
-        name=name,
-    )
-    return full.reshape(blocks * tokens, width), loads
-
-
-def reduce_tokens(names, part, cargo, both=True, name=None):
-    blocks = 8 if both else 4
-    tokens, width = part.shape[0] // blocks, part.shape[1]
-
-    def body(place, ins, outs, scratch, later, middle, start):
-        from_p, from_r, from_l, held, *sems = scratch
-        reduce_line(place, ins[0], outs[0], from_p, from_r, from_l, held, sems, later, both, middle)
-
-    (total,), loads = carry_call(
-        names,
-        body,
-        "line",
-        [part.reshape(blocks, tokens, width)],
-        [ONCHIP],
-        [jax.ShapeDtypeStruct((tokens, width), F32)],
-        [ONCHIP],
-        [
-            *[pltpu.VMEM((4, tokens, width), LOW)] * 4,
-            *[pltpu.SemaphoreType.DMA((4,))] * 5,
-        ],
-        cargo,
-        name=name,
-    )
-    return total, loads
-
-
 class Gather:
     scratch = (
         pltpu.SemaphoreType.DMA((4,)),
@@ -668,9 +598,12 @@
         self.place, self.block, self.full, self.both = place, block, full, both
         self.send_r, self.send_l, self.send_p, self.recv, self.keep = sems
 
+    def spot(self, zz, c):
+        return self.full.at[2 * zz + c] if self.both else self.full.at[zz]
+
     def copies(self, src, zz, t, way):
         z, c = self.place.z, self.place.c
-        spot, sem = self.full.at[2 * zz + c], self.recv.at[2 * zz + c]
+        spot, sem = self.spot(zz, c), self.recv.at[2 * zz + c]
         right = remote(src, spot, self.send_r.at[t], sem, self.place.at(jnp.minimum(z + 1, 3), c))
         left = remote(src, spot, self.send_l.at[t], sem, self.place.at(jnp.maximum(z - 1, 0), c))
         partner = remote(src, spot, self.send_p.at[2 * t + way], sem, self.place.at(z, 1 - c))
@@ -686,7 +619,7 @@
         if self.both:
             partner.start()
             later.add(partner.wait_send)
-        keep = pltpu.make_async_copy(self.block, self.full.at[2 * z + c], self.keep.at[0])
+        keep = pltpu.make_async_copy(self.block, self.spot(z, c), self.keep.at[0])
         keep.start()
         keep.wait()
         for t in range(1, 4):
@@ -700,7 +633,7 @@
         z = self.place.z
         there = z + (2 * way - 1) * t
         zz = jnp.clip(there, 0, 3)
-        right, left, partner = self.copies(self.full.at[2 * zz + self.place.c], zz, t, way)
+        right, left, partner = self.copies(self.spot(zz, self.place.c), zz, t, way)
         onward, may = (left, z > 0) if way else (right, z < 3)
         return zz, (there >= 0) & (there <= 3), onward, may, partner
 
@@ -725,7 +658,7 @@
         fourth = jnp.where(z <= 1, 3, 0)
         j = jnp.where(p == 0, z, jnp.where(p == 1, second, jnp.where(p == 2, third, fourth)))
         if self.both:
-            spot = self.full.at[2 * j + 1 - c]
+            spot = self.spot(j, 1 - c)
             remote(spot, spot, self.send_p.at[0], self.recv.at[2 * j + 1 - c], self.place.at(z, 1 - c)).wait_recv()
         return j
 
@@ -779,7 +712,8 @@
 
         lax.fori_loop(0, 4, step, 0)
         start(1)
-        reduce_line(place, part, total, from_p, from_r, from_l, held, sems, later, True, lambda: middle(1), sent=True)
+        start(2)
+        reduce_line(place, part, total, from_p, from_r, from_l, held, sems, later, True, at_two(middle), sent=True)
         for j in range(4):
             for copy in keep(j):
                 copy.wait()
@@ -818,59 +752,427 @@
     return total, full.reshape(8 * tokens, width), gate, up, loads
 
 
-def stages_call(names, stages, name=None):
-    cargo = [item for stage in stages for item in stage]
-    arrays, outs, scratch = [], [], []
-    for item in cargo:
-        arrays += [a for a in item.arrays if not isinstance(a, From)]
-        outs += item.outs
-        scratch += item.scratch
-    n_in, n_out = len(arrays), len(outs)
-
-    def kernel(*refs):
-        ins, made, held = list(refs[:n_in]), list(refs[n_in : n_in + n_out]), list(refs[n_in + n_out :])
-        place = Place()
-        greet(place, {item.reach for item in cargo})
-        out_refs = {}
-        last = Later()
-        for stage in stages:
-            later = Later()
-            begun = []
-            for item in stage:
-                mine = [out_refs[a.item][a.at] if isinstance(a, From) else ins.pop(0) for a in item.arrays]
-                out_refs[item] = [made.pop(0) for _ in item.outs]
-                kept = [held.pop(0) for _ in item.scratch]
-                begun.append((item, mine, out_refs[item], kept, last if item.slow else later))
-            for item, *theirs in begun:
-                item.start(place, *theirs)
-            for item, *theirs in begun:
-                item.middle(place, *theirs[:3])
-            later.run()
-        last.run()
-
-    results = list(
-        pl.pallas_call(
-            kernel,
-            out_shape=outs,
-            in_specs=[ANY] * n_in,
-            out_specs=[ANY] * n_out,
-            scratch_shapes=scratch,
-            compiler_params=pltpu.CompilerParams(
-                collective_id=names.take(), has_side_effects=True, vmem_limit_bytes=40 * 2**20
-            ),
-            name=name,
-        )(*arrays)
-    )
-    loads = []
-    for item in cargo:
-        loads.append([results.pop(0) for _ in item.outs])
-    return loads
-
-
-class From:
-    def __init__(self, item, at=0):
-        self.item, self.at = item, at
-        self.shape, self.dtype = item.outs[at].shape, item.outs[at].dtype
+REDUCE_SEMS = [pltpu.SemaphoreType.DMA((4,))] * 5
+
+
+def reduce_scratch(tokens, width):
+    return [*[pltpu.VMEM((4, tokens, width), LOW)] * 4, *REDUCE_SEMS]
+
+
+def rows_of(first, count):
+    return pl.ds(pl.multiple_of(first, count), count)
+
+
+def copy_in(pairs, sem):
+    copies = [pltpu.make_async_copy(src, dst, sem.at[i]) for i, (src, dst) in enumerate(pairs)]
+    for copy in copies:
+        copy.start()
+    return copies
+
+
+def open_call(names, shard, cargo):
+    def body(place, ins, outs, scratch, later, middle, start):
+        gather = Gather(place, ins[0], outs[0], scratch)
+        gather.start(later)
+        start(1)
+        start(3)
+        gather.pass_on(1)
+        middle(1)
+        gather.pass_on(2)
+        start(2)
+        gather.pass_on(3)
+        middle(3)
+        for zz in range(4):
+            spot = gather.spot(zz, 1 - place.c)
+            recv = gather.recv.at[2 * zz + 1 - place.c]
+            later.add(remote(spot, spot, gather.send_p.at[0], recv, place.at(place.z, 1 - place.c)).wait_recv)
+
+    (full,), loads = carry_call(
+        names,
+        body,
+        "line",
+        [shard],
+        [ANY],
+        [jax.ShapeDtypeStruct((8, *shard.shape), shard.dtype)],
+        [ANY],
+        list(Gather.scratch),
+        cargo,
+        name="open",
+    )
+    return full, loads
+
+
+def close_call(names, cargo, name):
+    def body(place, ins, outs, scratch, later, middle, start):
+        middle(0)
+
+    return carry_call(names, body, "col", [], [], [], [], [], cargo, name=name)[1]
+
+
+def heads_of(ref, rows):
+    return jnp.concatenate([ref[rows, h * HD : (h + 1) * HD] for h in range(3)], axis=0)
+
+
+def block_probs(qkv, starts, b):
+    reach = QB + SEQ_MAX
+    first = jnp.maximum(b - SEQ_MAX // QB, 0) * QB
+    rows, window = rows_of(b * QB, QB), pl.ds(pl.multiple_of(first, QB), reach)
+    queries = heads_of(qkv, rows)
+    keys, values = qkv[window, 3 * HD : 4 * HD], qkv[window, 4 * HD : 5 * HD]
+    scores = (dot_t(queries, keys) * HD ** (-0.5)).reshape(3, QB, reach)
+    key_at = first + lax.broadcasted_iota(jnp.int32, (QB, reach), 1)
+    query_at = b * QB + lax.broadcasted_iota(jnp.int32, (QB, reach), 0)
+    allowed = (key_at >= starts[rows, :]) & (key_at <= query_at)
+    masked = jnp.where(allowed[None], scores, neg_fill)
+    lifted = jnp.exp(masked - jnp.max(masked, axis=-1, keepdims=True))
+    probs = lifted * (1.0 / jnp.sum(lifted, axis=-1, keepdims=True))
+    return queries, keys, values, probs, rows, window
+
+
+def roll_half(values):
+    return pltpu.roll(values, HD // 2, 1)
+
+
+def forward_heads(names, block, acts, w_qkv, bias, w_out, cosine, sine, starts, cargo, name):
+    tokens, width = QB, D
+    count = 8 * QB
+    apart = acts is not None
+
+    def body(place, ins, outs, scratch, later, middle, start):
+        ins = list(ins)
+        block_ref = ins.pop(0)
+        acts_hbm = ins.pop(0) if apart else None
+        qkv_hbm, bias_ref, out_hbm, cos_ref, sin_ref, starts_ref = ins
+        total, full_out, qkv_out, mixed_out = outs
+        scratch = list(scratch)
+        gather_sems = [scratch.pop(0) for _ in Gather.scratch]
+        full, acts_own, part, qkv_w, out_w, qkv, mixed, load_sem, keep_sem = scratch[:9]
+        from_p, from_r, from_l, held, *sems = scratch[9:]
+        pairs = [(qkv_hbm, qkv_w), (out_hbm, out_w)]
+        if apart:
+            pairs.append((acts_hbm, acts_own))
+        loads = copy_in(pairs, load_sem)
+        gather = Gather(place, block_ref, full, gather_sems)
+        gather.start(later)
+        for load in loads:
+            load.wait()
+
+        def keep(j):
+            return pltpu.make_async_copy(full.at[pl.ds(2 * j, 2)], full_out.at[pl.ds(2 * j, 2)], keep_sem.at[j])
+
+        def step(p, carry):
+            j = gather.chunk(p)
+            keep(j).start()
+            pl.when(p == 2)(middle)
+            rows = rows_of(j * 2 * QB, 2 * QB)
+            chunk = acts_own[rows, :] if apart else full[pl.ds(2 * j, 2)].reshape(2 * tokens, width)
+            raw = jnp.dot(chunk, qkv_w[...], preferred_element_type=F32) + bias_ref[...]
+            cos, sin = cos_ref[rows, :], sin_ref[rows, :]
+            for t in range(5):
+                head = raw[:, t * HD : (t + 1) * HD]
+                if t < 4:
+                    head = head * cos + roll_half(head) * sin
+                qkv[rows, t * HD : (t + 1) * HD] = head.astype(LOW)
+            return carry
+
+        lax.fori_loop(0, 4, step, 0)
+        start(1)
+
+        def attend(j, carry):
+            _, _, values, probs, _, _ = block_probs(qkv, starts_ref, 2 * j + place.c)
+            low = probs.astype(LOW).reshape(3 * QB, QB + SEQ_MAX)
+            heads = jnp.dot(low, values, preferred_element_type=F32).astype(LOW)
+            wide = jnp.concatenate([heads[h * QB : (h + 1) * QB] for h in range(3)], axis=1)
+            mixed[rows_of(j * QB, QB), :] = wide
+            part[j] = jnp.dot(wide, out_w[...], preferred_element_type=F32).astype(LOW)
+            return carry
+
+        lax.fori_loop(0, 4, attend, 0)
+        saves = copy_in([(qkv, qkv_out), (mixed, mixed_out)], load_sem)
+        reduce_line(place, part, total, from_p, from_r, from_l, held, sems, later, False, at_two(middle))
+        for copy in saves:
+            copy.wait()
+        for j in range(4):
+            keep(j).wait()
+
+    (total, full, qkv, mixed), loads = carry_call(
+        names,
+        body,
+        "line",
+        [block, *([acts] if apart else []), w_qkv, bias, w_out, cosine, sine, starts],
+        [ONCHIP, *([ANY] if apart else []), ANY, ONCHIP, ANY, ONCHIP, ONCHIP, ONCHIP],
+        [
+            jax.ShapeDtypeStruct((tokens, width), F32),
+            jax.ShapeDtypeStruct((8, *block.shape), LOW),
+            jax.ShapeDtypeStruct((count, 5 * HD), LOW),
+            jax.ShapeDtypeStruct((count // 2, 3 * HD), LOW),
+        ],
+        [ONCHIP, ANY, ANY, ANY],
+        [
+            *Gather.scratch,
+            pltpu.VMEM((8, *block.shape), LOW),
+            pltpu.VMEM((count, width) if apart else (16, 128), LOW),
+            pltpu.VMEM((4, tokens, width), LOW),
+            pltpu.VMEM(w_qkv.shape, LOW),
+            pltpu.VMEM(w_out.shape, LOW),
+            pltpu.VMEM((count, 5 * HD), LOW),
+            pltpu.VMEM((count // 2, 3 * HD), LOW),
+            pltpu.SemaphoreType.DMA((3,)),
+            pltpu.SemaphoreType.DMA((4,)),
+            *reduce_scratch(tokens, width),
+        ],
+        cargo,
+        name=name,
+        vmem=50,
+    )
+    return total, full, qkv, mixed, loads
+
+
+def backward_heads(names, block, acts, w_qkv, w_out, qkv, mixed, cosine, sine, starts, cargo, name):
+    tokens, width = QB, D
+    count = 8 * QB
+    reach = QB + SEQ_MAX
+
+    def body(place, ins, outs, scratch, later, middle, start):
+        block_ref, acts_hbm, qkv_hbm, out_hbm, saved_hbm, mixed_hbm, cos_ref, sin_ref, starts_ref = ins
+        total, slab_out, out_out = outs
+        scratch = list(scratch)
+        gather_sems = [scratch.pop(0) for _ in Gather.scratch]
+        full, part, qkv_w, out_w, qkv, mixed, acts_own, d_raw, d_keys, d_values = scratch[:10]
+        slab, d_out, slab_in, d_out_in, load_sem, swap_send, swap_recv = scratch[10:17]
+        from_p, from_r, from_l, held, *sems = scratch[17:]
+        pairs = [(qkv_hbm, qkv_w), (out_hbm, out_w), (saved_hbm, qkv), (mixed_hbm, mixed), (acts_hbm, acts_own)]
+        loads = copy_in(pairs, load_sem)
+        gather = Gather(place, block_ref, full, gather_sems, both=False)
+        gather.start(later)
+        d_keys[...] = jnp.zeros_like(d_keys)
+        d_values[...] = jnp.zeros_like(d_values)
+        for load in loads:
+            load.wait()
+
+        def step(p, carry):
+            j = gather.chunk(p)
+            pl.when(p == 2)(middle)
+            b = 2 * j + place.c
+            d_mixed = dot_t(full[j], out_w[...]).astype(LOW)
+            d_heads = jnp.concatenate([d_mixed[:, h * HD : (h + 1) * HD] for h in range(3)], axis=0)
+            queries, keys, values, probs, rows, window = block_probs(qkv, starts_ref, b)
+            d_probs = dot_t(d_heads, values).reshape(3, QB, reach)
+            inner = jnp.sum(probs * d_probs, axis=-1, keepdims=True)
+            d_scores = (probs * (d_probs - inner)).astype(LOW).reshape(3 * QB, reach)
+            d_queries = jnp.dot(d_scores, keys, preferred_element_type=F32) * HD ** (-0.5)
+            d_keys[window, :] += t_dot(d_scores, queries) * HD ** (-0.5)
+            d_values[window, :] += t_dot(probs.astype(LOW).reshape(3 * QB, reach), d_heads)
+            cos, sin = cos_ref[rows, :], sin_ref[rows, :]
+            for h in range(3):
+                head = d_queries[h * QB : (h + 1) * QB]
+                head = head * cos + roll_half(head * sin)
+                d_raw[rows, h * HD : (h + 1) * HD] = head.astype(LOW)
+            other = rows_of((2 * j + 1 - place.c) * QB, QB)
+            d_raw[other, 0 : 3 * HD] = jnp.zeros((QB, 3 * HD), LOW)
+            return carry
+
+        lax.fori_loop(0, 4, step, 0)
+        start(1)
+
+        def project(j, carry):
+            rows = rows_of(j * 2 * QB, 2 * QB)
+            head = d_keys[rows, :]
+            head = head * cos_ref[rows, :] + roll_half(head * sin_ref[rows, :])
+            d_raw[rows, 3 * HD : 4 * HD] = head.astype(LOW)
+            d_raw[rows, 4 * HD : 5 * HD] = d_values[rows, :].astype(LOW)
+            part[pl.ds(2 * j, 2)] = dot_t(d_raw[rows, :], qkv_w[...]).astype(LOW).reshape(2, tokens, width)
+            pair_copy(place, part, from_p, sems, j).start()
+            return carry
+
+        lax.fori_loop(0, 4, project, 0)
+
+        def swap():
+            to = place.at(place.z, 1 - place.c)
+            return [
+                remote(slab.at[1 - place.c], slab_in, swap_send.at[0], swap_recv.at[0], to),
+                remote(d_out.at[1 - place.c], d_out_in, swap_send.at[1], swap_recv.at[1], to),
+            ]
+
+        def between(s):
+            if s == 2:
+                middle(1)
+                for copy in swap():
+                    copy.start()
+                return
+
+            def weights(i, carry):
+                cut = pl.ds(pl.multiple_of(i * (D // 4), 128), D // 4)
+                grads = t_dot(acts_own[:, cut], d_raw[...]).astype(LOW)
+                slab[0, i, 0 : D // 8, :] = grads[: D // 8]
+                slab[1, i, 0 : D // 8, :] = grads[D // 8 :]
+                return carry
+
+            lax.fori_loop(0, 4, weights, 0)
+            sums = jnp.sum(d_raw[...].astype(F32), axis=0, keepdims=True)
+            first = lax.broadcasted_iota(jnp.int32, (16, 5 * HD), 0) == 0
+            tail = jnp.where(first, sums, 0.0).astype(LOW)
+            for half in range(2):
+                for i in range(4):
+                    slab[half, i, D // 8 :, :] = tail
+            grads = t_dot(mixed[...], full[...].reshape(4 * QB, D)).astype(LOW)
+            d_out[0] = grads[: D // 8]
+            d_out[1] = grads[D // 8 :]
+
+        reduce_line(place, part, total, from_p, from_r, from_l, held, sems, later, True, between, sent=True)
+        for copy in swap():
+            copy.wait()
+        for i in range(4):
+            add_into(slab_out.at[i], [slab.at[place.c, i], slab_in.at[i]])
+        add_into(out_out, [d_out.at[place.c], d_out_in])
+
+    (total, slab, d_out), loads = carry_call(
+        names,
+        body,
+        "line",
+        [block, acts, w_qkv, w_out, qkv, mixed, cosine, sine, starts],
+        [ONCHIP, ANY, ANY, ANY, ANY, ANY, ONCHIP, ONCHIP, ONCHIP],
+        [
+            jax.ShapeDtypeStruct((tokens, width), F32),
+            jax.ShapeDtypeStruct((4, HALF, 5 * HD), LOW),
+            jax.ShapeDtypeStruct((D // 8, D), LOW),
+        ],
+        [ONCHIP, ONCHIP, ONCHIP],
+        [
+            *Gather.scratch,
+            pltpu.VMEM((4, tokens, width), LOW),
+            pltpu.VMEM((8, tokens, width), LOW),
+            pltpu.VMEM(w_qkv.shape, LOW),
+            pltpu.VMEM(w_out.shape, LOW),
+            pltpu.VMEM((count, 5 * HD), LOW),
+            pltpu.VMEM((count // 2, 3 * HD), LOW),
+            pltpu.VMEM((count, width), LOW),
+            pltpu.VMEM((count, 5 * HD), LOW),
+            pltpu.VMEM((count, HD), F32),
+            pltpu.VMEM((count, HD), F32),
+            pltpu.VMEM((2, 4, HALF, 5 * HD), LOW),
+            pltpu.VMEM((2, D // 8, D), LOW),
+            pltpu.VMEM((4, HALF, 5 * HD), LOW),
+            pltpu.VMEM((D // 8, D), LOW),
+            pltpu.SemaphoreType.DMA((5,)),
+            pltpu.SemaphoreType.DMA((2,)),
+            pltpu.SemaphoreType.DMA((2,)),
+            *reduce_scratch(tokens, width),
+        ],
+        cargo,
+        name=name,
+        vmem=60,
+    )
+    return total, slab.reshape(4 * HALF, 5 * HD), d_out, loads
+
+
+def backward_feed(names, block, grads_all, acts, w_gate, w_up, w_down, gate, up, cargo, name):
+    tokens, width = QB, D
+    inner = w_gate.shape[1]
+    apart = grads_all is not None
+
+    def body(place, ins, outs, scratch, later, middle, start):
+        head_ref, acts_hbm, gate_hbm, up_hbm, down_hbm, gates_hbm, ups_hbm = ins
+        total, gate_out, up_out, down_out = outs
+        scratch = list(scratch)
+        gather_sems = [scratch.pop(0) for _ in Gather.scratch]
+        full, part, acts_own, gate_w, up_w, down_w, gates, ups, hiddens, load_sem, keep_sem = scratch[:11]
+        from_p, from_r, from_l, held, *sems = scratch[11:]
+        pairs = [(down_hbm, down_w), (gates_hbm, gates), (ups_hbm, ups), (gate_hbm, gate_w), (up_hbm, up_w)]
+        pairs.append((acts_hbm, acts_own))
+        if apart:
+            pairs.append((head_ref, full))
+        loads = copy_in(pairs, load_sem)
+        gather = None
+        if not apart:
+            gather = Gather(place, head_ref, full, gather_sems)
+            gather.start(later)
+        for load in loads:
+            load.wait()
+
+        def step(p, carry):
+            j = p if apart else gather.chunk(p)
+            pl.when(p == 2)(middle)
+            rows = rows_of(j * 2 * tokens, 2 * tokens)
+            grads = full[pl.ds(2 * j, 2)].reshape(2 * tokens, width)
+            d_hidden = dot_t(grads, down_w[...])
+            gate, up = gates[rows, :].astype(F32), ups[rows, :].astype(F32)
+            squash = jax.nn.sigmoid(gate)
+            lit = gate * squash
+            hiddens[rows, :] = (lit * up).astype(LOW)
+            d_gate = (d_hidden * up * squash * (1.0 + gate * (1.0 - squash))).astype(LOW)
+            d_up = (d_hidden * lit).astype(LOW)
+            gates[rows, :] = d_gate
+            ups[rows, :] = d_up
+            sums = dot_t(d_gate, gate_w[...]) + dot_t(d_up, up_w[...])
+            part[pl.ds(2 * j, 2)] = sums.astype(LOW).reshape(2, tokens, width)
+            pair_copy(place, part, from_p, sems, j).start()
+            return carry
+
+        lax.fori_loop(0, 4, step, 0)
+
+        def between(s):
+            if s == 1:
+                grads = full[...].reshape(8 * tokens, width)
+
+                def down(i, carry):
+                    cut = pl.ds(pl.multiple_of(i * 384, 128), 384)
+                    down_w[:, cut] = t_dot(hiddens[...], full[:, :, cut].reshape(8 * tokens, 384)).astype(LOW)
+                    return carry
+
+                lax.fori_loop(0, width // 384, down, 0)
+                start(1, down_w)
+                return
+
+            def rest(i, carry):
+                cut = pl.ds(pl.multiple_of(i * 384, 128), 384)
+                acts_cut = acts_own[:, cut]
+                rows = pl.ds(pl.multiple_of(i * 384, 128), 384)
+                gate_w[rows, :] = t_dot(acts_cut, gates[...]).astype(LOW)
+                up_w[rows, :] = t_dot(acts_cut, ups[...]).astype(LOW)
+                return carry
+
+            lax.fori_loop(0, width // 384, rest, 0)
+            middle(1)
+
+        reduce_line(place, part, total, from_p, from_r, from_l, held, sems, later, True, between, sent=True)
+        for copy in copy_in([(gate_w, gate_out), (up_w, up_out), (down_w, down_out)], keep_sem):
+            copy.wait()
+
+    head = grads_all.reshape(8, tokens, width) if apart else block
+    (total, d_gate, d_up, d_down), loads = carry_call(
+        names,
+        body,
+        "line",
+        [head, acts, w_gate, w_up, w_down, gate, up],
+        [ANY if apart else ONCHIP, ANY, ANY, ANY, ANY, ANY, ANY],
+        [
+            jax.ShapeDtypeStruct((tokens, width), F32),
+            jax.ShapeDtypeStruct(w_gate.shape, LOW),
+            jax.ShapeDtypeStruct(w_up.shape, LOW),
+            jax.ShapeDtypeStruct(w_down.shape, LOW),
+        ],
+        [ONCHIP, ANY, ANY, ANY],
+        [
+            *Gather.scratch,
+            pltpu.VMEM((8, tokens, width), LOW),
+            pltpu.VMEM((8, tokens, width), LOW),
+            pltpu.VMEM((8 * tokens, width), LOW),
+            pltpu.VMEM(w_gate.shape, LOW),
+            pltpu.VMEM(w_up.shape, LOW),
+            pltpu.VMEM(w_down.shape, LOW),
+            pltpu.VMEM((8 * tokens, inner), LOW),
+            pltpu.VMEM((8 * tokens, inner), LOW),
+            pltpu.VMEM((8 * tokens, inner), LOW),
+            pltpu.SemaphoreType.DMA((7,)),
+            pltpu.SemaphoreType.DMA((3,)),
+            *reduce_scratch(tokens, width),
+        ],
+        cargo,
+        name=name,
+        vmem=61,
+    )
+    return total, d_gate, d_up, d_down, loads
 
 
 eps_norm = 1e-06
@@ -1186,11 +1488,6 @@
     )
 
 
-def softmax_scores(queries, keys, mask):
-    scores = jnp.einsum("htd,ud->htu", queries, keys, preferred_element_type=F32) * HD ** (-0.5)
-    return jnp.where(mask[None], scores, neg_fill)
-
-
 def dot(a, b):
     return jnp.dot(a, b, preferred_element_type=F32)
 
@@ -1201,19 +1498,6 @@
 
 def t_dot(a, b):
     return lax.dot_general(a, b, (((0,), (0,)), ((), ())), preferred_element_type=F32)
-
-
-def turn(values, cosine, sine):
-    half = HD // 2
-    turned = jnp.concatenate([-values[..., half:], values[..., :half]], axis=-1)
-    return values * cosine + turned * sine
-
-
-def turn_back(grads, cosine, sine):
-    half = HD // 2
-    lifted = grads * sine
-    turned = jnp.concatenate([lifted[..., half:], -lifted[..., :half]], axis=-1)
-    return grads * cosine + turned
 
 
 def norm_on(residual, gain):
@@ -1246,102 +1530,79 @@
     row_at = lax.axis_index("row")
     col_at = lax.axis_index("col")
     core = col_at % 2
-    starts = row_starts(lengths[0], tok_row)
-    places = jnp.arange(tok_row, dtype=jnp.int32)
-    cosine, sine = rope_tables(places - starts)
-    cosine, sine = cosine.T[:, None], sine.T[:, None]
-
-    def own(values):
-        cut = values.reshape(4, 2, QB, *values.shape[1:])
-        return lax.dynamic_index_in_dim(cut, core, 1, keepdims=False).reshape(4 * QB, *values.shape[1:])
-
-    mask = (places[None, :] >= own(starts)[:, None]) & (places[None, :] <= own(places)[:, None])
-
-    def head_tiles(layer):
-        biases = jnp.zeros((2, 1, 16, HD), LOW)
-        biases = lax.dynamic_update_slice(biases, qkv_bias[layer][:, None, None], (0, 0, 0, row_at * (HD // 4)))
-        tiles = qkv_weight[layer].reshape(2, D // 8, 2, HD).transpose(2, 0, 1, 3)
-        return jnp.concatenate([tiles, jnp.broadcast_to(biases, (2, 2, 16, HD))], axis=2)
+
+    biases = jnp.zeros((LAYERS, 2, 16, HD), LOW)
+    biases = lax.dynamic_update_slice(biases, qkv_bias[:, :, None], (0, 0, 0, row_at * (HD // 4)))
+    gain_rows = jnp.pad(norm_gains.reshape(2 * LAYERS, D // 8), ((0, 16 - 2 * LAYERS), (0, 0)))
 
     def slab_of(mine, theirs, out_mine, out_theirs):
         first, second = jnp.where(core == 0, mine, theirs), jnp.where(core == 0, theirs, mine)
         both = jnp.stack([first.reshape(4, HALF, 5 * HD), second.reshape(4, HALF, 5 * HD)], axis=1)
         w_qkv = both[:, :, : D // 8].reshape(D, 5 * HD)
-        bias = jnp.sum(both[:, 0, D // 8].astype(F32), axis=0)
+        bias = jnp.sum(both[:, 0, D // 8].astype(F32), axis=0, keepdims=True)
         w_out = jnp.concatenate(
             [jnp.where(core == 0, out_mine, out_theirs), jnp.where(core == 0, out_theirs, out_mine)], axis=0
         )
         return w_qkv, bias, w_out
 
-    arrivals = jnp.concatenate(
-        [
-            hidden_states.T.reshape(8, QB, D // 8),
-            out_grad.T.reshape(8, QB, D // 8),
-            jnp.broadcast_to(
-                jnp.pad(norm_gains.reshape(2 * LAYERS, D // 8), ((0, 16 - 2 * LAYERS), (0, 0))), (8, 16, D // 8)
-            ),
-        ],
-        axis=1,
-    )
-    spread = Exchange(arrivals)
-    spread.slow = True
-    to_chips = [HeadsToChips(head_tiles(layer)) for layer in range(LAYERS)]
-    to_chips[1].slow = True
-    slab_rows, out_rows = GatherRows(From(to_chips[0]), 0), GatherRows(out_weight[0], 1)
-    swap = Swap(From(slab_rows), From(out_rows))
-    loads = stages_call(
-        names, [[to_chips[0]], [slab_rows, out_rows, spread, to_chips[1]], [swap]], name="open"
-    )
-    (_,), (mine,), (out_mine,), (came,), (slab_next,), (theirs, out_theirs) = loads
+    def rows_load(layer):
+        return (
+            GatherRows(gate_weight, 0, layer),
+            GatherRows(up_weight, 0, layer),
+            GatherRows(down_weight, 1, layer),
+        )
+
+    sent = rows_load(0)
+    to_chips = [HeadsToChips(qkv_weight, biases, layer) for layer in range(LAYERS)]
+    slab_rows, out_rows = GatherRows(From(to_chips[0]), 0, phase=1), GatherRows(out_weight, 1, 0, phase=1)
+    swap = Swap(From(slab_rows), From(out_rows), phase=2)
+    sent[0].phase = 3
+    states, loads = open_call(
+        names, hidden_states, [*to_chips, Exchange(gain_rows, same=True), slab_rows, out_rows, swap, sent[0]]
+    )
+    (_,), (slab_next,), (gains,), (mine,), (out_mine,), (theirs, out_theirs), (w_gate,) = loads
     load = (mine, theirs, out_mine, out_theirs)
-    came = came.transpose(1, 0, 2).reshape(2 * QB + 16, D)
-    residual = came[:QB].astype(F32)
-    grad = came[QB : 2 * QB].astype(F32)
-    gains = came[2 * QB : 2 * QB + 2 * LAYERS].astype(F32).reshape(LAYERS, 2, D)
-
-    def weights_in(layer):
-        return [GatherRows(gate_weight[layer], 0), GatherRows(up_weight[layer], 0), GatherRows(down_weight[layer], 1)]
-
-    sent = weights_in(0)
-    grad_full_last, ((w_gate,),) = gather_tokens(names, grad.astype(LOW), sent[:1], name="gather_three_1")
+    gains = gains[:, : 2 * LAYERS].transpose(1, 0, 2).reshape(LAYERS, 2, D).astype(F32)
+    starts = row_starts(lengths[0], tok_row)
+    cosine, sine = rope_tables(jnp.arange(tok_row, dtype=jnp.int32) - starts)
+    cosine, sine = cosine.T, sine.T * jnp.where(jnp.arange(HD) < HD // 2, -1.0, 1.0)[None]
+    starts = starts[:, None]
+
+    def own_block(transposed):
+        return lax.dynamic_slice_in_dim(transposed, col_at * QB, QB, 1).astype(F32).T
+
+    wide = states.reshape(D, tok_row)
+    residual = own_block(wide)
+    wide = wide.astype(F32)
+    scale_all = lax.rsqrt(jnp.mean(wide * wide, axis=0, keepdims=True) + eps_norm)
+    full_one = (wide * scale_all * gains[0, 0][:, None]).astype(LOW).T
+    scale_one, _ = norm_on(residual, gains[0, 0])
+
     saved = []
     for layer in range(LAYERS):
-        if layer == 1:
-            mine, out_mine, (w_gate,) = load
-        scale_one, normed_one = norm_on(residual, gains[layer, 0])
+        w_qkv, bias, w_out = slab_of(*load)
+        sent[1].phase, sent[2].phase = 0, 1
         if layer == 0:
-            normed_one, _ = lax.optimization_barrier((normed_one, grad_full_last))
-        cargo = [sent[1]] if layer == 0 else [sent[1], Swap(mine, out_mine)]
-        full_one, loads = gather_tokens(names, normed_one, cargo, name=f"gather_one_{layer}")
-        w_up = loads[0][0]
-        if layer == 1:
-            load = (mine, loads[1][0], out_mine, loads[1][1])
-        w_qkv, bias, w_out = slab_of(*load)
-        raw = (dot(full_one, w_qkv) + bias[None]).reshape(tok_row, 5, HD)
-        turned = jnp.concatenate([turn(raw[:, :4], cosine, sine), raw[:, 4:]], axis=1).astype(LOW)
-        queries = own(turned[:, :3]).transpose(1, 0, 2)
-        keys, values = turned[:, 3], turned[:, 4]
-        masked = softmax_scores(queries, keys, mask)
-        row_top = jnp.max(masked, axis=-1, keepdims=True)
-        lifted = jnp.exp(masked - row_top)
-        row_mass = jnp.sum(lifted, axis=-1, keepdims=True)
-        probs = (lifted / row_mass).astype(LOW)
-        log_mass = row_top + jnp.log(row_mass)
-        mixed = jnp.einsum("htu,ud->thd", probs, values, preferred_element_type=F32)
-        mixed = mixed.astype(LOW).reshape(4 * QB, 3 * HD)
-        attention, ((w_down,),) = reduce_tokens(
-            names, dot(mixed, w_out).astype(LOW), [sent[2]], both=False, name=f"reduce_one_{layer}"
-        )
+            attention, grads_wide, qkv, mixed, loads = forward_heads(
+                names, out_grad, full_one, w_qkv, bias, w_out, cosine, sine, starts, sent[1:], name="heads_0"
+            )
+            (w_up,), (w_down,) = loads
+            grads_wide = grads_wide.reshape(D, tok_row)
+        else:
+            scale_one, normed_one = norm_on(residual, gains[layer, 0])
+            attention, full_one, qkv, mixed, loads = forward_heads(
+                names, normed_one, None, w_qkv, bias, w_out, cosine, sine, starts, sent[1:], name="heads_1"
+            )
+            (w_up,), (w_down,) = loads
+            full_one = full_one.reshape(tok_row, D)
         residual_mid = residual + attention
         scale_two, normed_two = norm_on(residual_mid, gains[layer, 1])
         cargo = []
         if layer == 0:
-            sent = weights_in(1)
-            cargo = sent[:1]
-        if layer == 0:
-            slab_rows, out_rows = GatherRows(slab_next, 0), GatherRows(out_weight[1], 1)
+            sent = rows_load(1)
             sent[0].phase = 1
-            cargo = [slab_rows, out_rows, sent[0]]
+            slab_rows, out_rows = GatherRows(slab_next, 0), GatherRows(out_weight, 1, 1)
+            cargo = [slab_rows, out_rows, sent[0], Swap(From(slab_rows), From(out_rows), phase=2)]
         feed, full_two, gate, up, loads = forward_feed(
             names, normed_two, w_gate, w_up, w_down, cargo, name=f"feed_{layer}"
         )
@@ -1350,10 +1611,7 @@
                 residual,
                 scale_one,
                 full_one,
-                queries,
-                keys,
-                values,
-                log_mass,
+                qkv,
                 mixed,
                 residual_mid,
                 scale_two,
@@ -1365,7 +1623,8 @@
         )
         residual = residual_mid + feed
         if layer == 0:
-            load = (loads[0][0], loads[1][0], loads[2])
+            (mine,), (out_mine,), (w_gate,), (theirs, out_theirs) = loads
+            load = (mine, theirs, out_mine, out_theirs)
     states = residual.astype(LOW)
 
     def own_part(full, dim):
@@ -1383,16 +1642,14 @@
 
     grads = {}
     gain_terms = [None] * LAYERS
-    waiting = None
+    grad = own_block(grads_wide)
+    inner = w_gate.shape[1]
     for layer in reversed(range(LAYERS)):
         (
             residual_in,
             scale_one,
             full_one,
-            queries,
-            keys,
-            values,
-            log_mass,
+            qkv,
             mixed,
             residual_mid,
             scale_two,
@@ -1401,96 +1658,68 @@
             up,
             (w_qkv, w_out, w_gate, w_up, w_down),
         ) = saved[layer]
-        gate, up = gate.astype(F32), up.astype(F32)
-        hidden = (gate * jax.nn.sigmoid(gate) * up).astype(LOW)
-        if layer == LAYERS - 1:
-            grad_full = grad_full_last
-        else:
-            grad_full, loads = gather_tokens(
-                names,
-                grad.astype(LOW),
-                [ScatterRows(waiting[0], 0), ScatterRows(waiting[1], 1)],
-                name=f"gather_three_{layer}",
-            )
-            slab_sum = settle(waiting[0], 0, loads[0][0]).astype(LOW)
-            grads["out", layer + 1] = settle(waiting[1], 1, loads[1][0])
-        d_down = t_dot(hidden, grad_full).astype(LOW)
-        d_hidden = dot_t(grad_full, w_down)
-        squash = jax.nn.sigmoid(gate)
-        d_gate = (d_hidden * up * squash * (1.0 + gate * (1.0 - squash))).astype(LOW)
-        d_up = (d_hidden * gate * squash).astype(LOW)
-        d_normed = (dot_t(d_gate, w_gate) + dot_t(d_up, w_up)).astype(LOW)
-        cargo = [ScatterRows(d_down, 1)]
-        if layer < LAYERS - 1:
-            cargo.append(HeadsToOwners(slab_sum))
-        d_normed_two, loads = reduce_tokens(names, d_normed, cargo, name=f"reduce_three_{layer}")
-        if layer < LAYERS - 1:
-            grads["qkv", layer + 1] = settle_heads(loads[1][0])
-        grads["down", layer] = settle(d_down, 1, loads[0][0])
-        d_gate_w = t_dot(full_two, d_gate).astype(LOW)
-        d_up_w = t_dot(full_two, d_up).astype(LOW)
+        last = layer == LAYERS - 1
+        cargo = [] if last else [ScatterRows(slab, 0), ScatterRows(d_out_w, 1)]
+        cargo.append(ScatterRows(Inner((inner, D)), 1, phase=1))
+        d_normed_two, d_gate_w, d_up_w, d_down, loads = backward_feed(
+            names,
+            None if last else grad.astype(LOW),
+            grads_wide.T if last else None,
+            full_two,
+            w_gate,
+            w_up,
+            w_down,
+            gate,
+            up,
+            cargo,
+            name=f"back_feed_{layer}",
+        )
+        grads["down", layer] = settle(d_down, 1, loads[-1][0])
+        cargo = [ScatterRows(d_gate_w, 0), ScatterRows(d_up_w, 0, phase=1)]
+        if not last:
+            grads["out", layer + 1] = settle(d_out_w, 1, loads[1][0])
+            cargo.append(HeadsToOwners(settle(slab, 0, loads[0][0]).astype(LOW)))
         d_residual, d_gain_two = norm_back(d_normed_two, residual_mid, scale_two, gains[layer, 1])
         grad = grad + d_residual
-        grad_own, loads = gather_tokens(
-            names, grad.astype(LOW), [ScatterRows(d_gate_w, 0)], both=False, name=f"gather_four_{layer}"
+        d_normed_one, slab, d_out_w, loads = backward_heads(
+            names,
+            grad.astype(LOW),
+            full_one,
+            w_qkv,
+            w_out,
+            qkv,
+            mixed,
+            cosine,
+            sine,
+            starts,
+            cargo,
+            name=f"back_heads_{layer}",
         )
         grads["gate", layer] = settle(d_gate_w, 0, loads[0][0])
-        d_out_w = t_dot(mixed, grad_own).astype(LOW)
-        d_mixed = dot_t(grad_own, w_out).astype(LOW).reshape(4 * QB, 3, HD).transpose(1, 0, 2)
-        masked = softmax_scores(queries, keys, mask)
-        probs = jnp.exp(masked - log_mass)
-        d_probs = jnp.einsum("htd,ud->htu", d_mixed, values, preferred_element_type=F32)
-        inner = jnp.sum(probs * d_probs, axis=-1, keepdims=True)
-        d_scores = (probs * (d_probs - inner)).astype(LOW)
-        d_queries = jnp.einsum("htu,ud->thd", d_scores, keys, preferred_element_type=F32) * HD ** (-0.5)
-        d_keys = jnp.einsum("htu,htd->ud", d_scores, queries, preferred_element_type=F32) * HD ** (-0.5)
-        d_values = jnp.einsum("htu,htd->ud", probs.astype(LOW), d_mixed, preferred_element_type=F32)
-        d_raw_q = turn_back(d_queries, own(cosine), own(sine)).astype(LOW).reshape(4, QB, 3 * HD)
-        mine = (jnp.arange(2) == core)[None, :, None, None]
-        d_raw_q = jnp.where(mine, d_raw_q[:, None], jnp.zeros((), LOW)).reshape(tok_row, 3 * HD)
-        d_raw_k = turn_back(d_keys, cosine[:, 0], sine[:, 0]).astype(LOW)
-        d_raw = jnp.concatenate([d_raw_q, d_raw_k, d_values.astype(LOW)], axis=1)
-        d_bias = jnp.sum(d_raw, axis=0, dtype=F32).astype(LOW)
-        d_qkv_w = t_dot(full_one, d_raw).astype(LOW).reshape(4, 2, D // 8, 5 * HD)
-        tail = jnp.broadcast_to(jnp.pad(d_bias[None], ((0, 15), (0, 0))), (4, 2, 16, 5 * HD))
-        d_slab = jnp.concatenate([d_qkv_w, tail], axis=2)
-        d_out_w = d_out_w.reshape(2, D // 8, D)
-
-        def half(full, dim, which):
-            return lax.dynamic_index_in_dim(full, which, dim, keepdims=False)
-
-        d_normed_one, loads = reduce_tokens(
-            names,
-            dot_t(d_raw, w_qkv).astype(LOW),
-            [ScatterRows(d_up_w, 0), Swap(half(d_slab, 1, 1 - core), half(d_out_w, 0, 1 - core))],
-            name=f"reduce_four_{layer}",
-        )
-        grads["up", layer] = settle(d_up_w, 0, loads[0][0])
-        slab_part = (half(d_slab, 1, core).astype(F32) + loads[1][0].astype(F32)).astype(LOW)
-        out_part = (half(d_out_w, 0, core).astype(F32) + loads[1][1].astype(F32)).astype(LOW)
-        waiting = (slab_part.reshape(4 * HALF, 5 * HD), out_part)
+        grads["up", layer] = settle(d_up_w, 0, loads[1][0])
+        if not last:
+            grads["qkv", layer + 1] = settle_heads(loads[2][0])
         d_residual, d_gain_one = norm_back(d_normed_one, residual_in, scale_one, gains[layer, 0])
         grad = grad + d_residual
         gain_terms[layer] = jnp.stack([d_gain_one, d_gain_two])
-    leaving = jnp.concatenate([states, grad.astype(LOW)], axis=0).reshape(2 * QB, 8, D // 8).transpose(1, 0, 2)
+    leaving = jnp.concatenate([states.T, grad.astype(LOW).T], axis=1).reshape(8, D // 8, 2 * QB)
     gain_parts = jnp.pad(jnp.stack(gain_terms).reshape(2 * LAYERS, 8, D // 8), ((0, 8 - 2 * LAYERS), (0, 0), (0, 0)))
-    (left,), (gain_all,), (slots,), (out_slots,) = stages_call(
+    (left,), (gain_all,), (slots,), (out_slots,) = close_call(
         names,
         [
-            [
-                Exchange(leaving),
-                Exchange(gain_parts.transpose(1, 0, 2), every_row=True),
-                ScatterRows(waiting[0], 0),
-                ScatterRows(waiting[1], 1),
-            ]
+            Exchange(leaving),
+            Exchange(gain_parts.transpose(1, 0, 2), every_row=True),
+            ScatterRows(slab, 0),
+            ScatterRows(d_out_w, 1),
         ],
-        name="close",
-    )
-    ((tiles,),) = stages_call(names, [[HeadsToOwners(settle(waiting[0], 0, slots).astype(LOW))]], name="close_heads")
+        "close",
+    )
+    ((tiles,),) = close_call(names, [HeadsToOwners(settle(slab, 0, slots).astype(LOW))], "close_heads")
     grads["qkv", 0] = settle_heads(tiles)
-    grads["out", 0] = settle(waiting[1], 1, out_slots)
-    out_states = left[:, :QB].reshape(tok_row, D // 8).T
-    input_grad = left[:, QB:].reshape(tok_row, D // 8).T.astype(F32)
+    grads["out", 0] = settle(d_out_w, 1, out_slots)
+    left = left.transpose(1, 0, 2)
+    out_states = left[:, :, :QB].reshape(D // 8, tok_row)
+    input_grad = left[:, :, QB:].reshape(D // 8, tok_row).astype(F32)
     gain_grads = jnp.sum(gain_all, axis=(0, 1))[: 2 * LAYERS].reshape(LAYERS, 2, D // 8)
 
     def both_layers(kind):

time: 997 us -> 791 us (0.79)
  matrix products: 142 us -> 0 us
  local copies, waits for them, and re-layouts: 139 us -> 51.8 us
  Pallas kernels: 620 us -> 669 us
  other arithmetic: 85.5 us -> 58.8 us
    dot_general x36 -> x0, matrix products: 142 us -> none  [the longest x10 60.9 us: dot_t(): lax.dot_general(a, b, (((1,), (1,)), ((), ())), preferred_element_type=F32)]
    pallas_call x14 -> x11, Pallas kernels: 537 us -> 669 us  [carry_call(): results = list(call(*arrays, *given))]
    pallas_call x3 -> x0, Pallas kernels: 82.8 us -> none  [stages_call(): pl.pallas_call(kernel, out_shape=outs, in_specs=[ANY] * n_in, out_specs=[...]
    unnamed x376 -> x115, local copies, waits for them, and re-layouts: 82.2 us -> 33.4 us
    slice x12 -> x0, local copies, waits for them, and re-layouts: 14.7 us -> none  [the longest x1 3.91 us: weights_in(): up_weight[layer]]
    convert_element_type x15 -> x3, other arithmetic: 15.8 us -> 1.78 us  [the longest x1 1.71 us: per_device_line(): cargo.append(HeadsToOwners(settle(slab, 0, loads[0][0]).astype(LOW)))]
where the time goes in v3:
time: 791 us; the launch traced here: 782 us
  Pallas kernels  669 us (85%)
  other arithmetic  58.8 us (7%)
  local copies, waits for them, and re-layouts  51.8 us (7%)
    pallas_call x11, Pallas kernels, carry_call(): results = list(call(*arrays, *given))  669 us
    unnamed x115, local copies, waits for them, and re-layouts  33.4 us

profile of v3, /device:TPU:31, one launch (start us, length us, event | category | flops | bytes accessed | tf_op | source)
XLA Modules:
  0.0 781.9 jit_solution(5852025699181062900)
XLA Ops:
  4.7 1.9 multiply_sine_fusion
  7.0 2.9 copy.60.refs_7_.refs_6_
  9.9 4.1 copy.67.refs_8_.refs_7_
  17.0 57.6 %open.1 = (bf16[8,192,1024]{2,1,0:T(8,128)(2,1)S(1)}, bf16[208,640]{1,0:T(8,128)(2,1)}, bf16[208,640]{1,0:T(8,128)(2,1)S(1)}, bf16[8,16,192]{2,1,0:T(8,128)(2,1)...) custom-call(bf16[192,1024]{1,0:T(8,128)(2,1)S(1)} %copy-done.21, ...), custom_call_target="tpu_custom_call" | custom-call | tf_op jit(solution)/shard_map/open/pallas_call | solution.py:578
  74.6 1.7 copy-done.1
  76.4 1.7 copy-done.5
  82.5 2.7 multiply_reduce_fusion
  85.4 1.1 pad_maximum_fusion.5.refs_4_.refs_3_
  87.6 1.5 pad_maximum_fusion.4
  89.0 4.6 copy.61
  93.7 4.4 fusion.refs_1_
  98.1 74.0 %heads_0.1 = (f32[128,1536]{1,0:T(8,128)S(1)}, bf16[8,192,1024]{2,1,0:T(8,128)(2,1)}, bf16[1024,640]{1,0:T(8,128)(2,1)}, bf16[512,384]{1,0:T(8,128)(2,1)S(1)}, b...) custom-call(bf16[192,1024]{1,0:T(8,128)(2,1)S(1)} %copy-done.20, bf16[1024,1536]{1,0:T(8,128)(2,1)} %fusion.refs_1_, ...), custom_call_target="tpu_custom_call" | custom-call | tf_op jit(solution)/shard_map/heads_0/pallas_call | solution.py:578
  172.1 1.4 multiply_reduce_fusion.9
  177.4 4.6 copy.74
  182.0 69.5 %feed_0.1 = (f32[128,1536]{1,0:T(8,128)}, bf16[8,128,1536]{2,1,0:T(8,128)(2,1)}, bf16[1024,1120]{1,0:T(8,128)(2,1)}, bf16[1024,1120]{1,0:T(8,128)(2,1)}, bf16[83...) custom-call(bf16[128,1536]{1,0:T(8,128)(2,1)} %multiply_convert_fusi, ...), custom_call_target="tpu_custom_call" | custom-call | tf_op jit(solution)/shard_map/feed_0/pallas_call | solution.py:578
  251.6 1.4 multiply_reduce_fusion.8
  255.3 1.2 pad_maximum_fusion.6.refs_3_
  256.5 1.5 pad_maximum_fusion.3
  258.0 68.6 %heads_1.1 = (f32[128,1536]{1,0:T(8,128)S(1)}, bf16[8,128,1536]{2,1,0:T(8,128)(2,1)}, bf16[1024,640]{1,0:T(8,128)(2,1)}, bf16[512,384]{1,0:T(8,128)(2,1)S(1)}, b...) custom-call(bf16[128,1536]{1,0:T(8,128)(2,1)S(1)} %multiply_convert_fusion.2.refs_0_, bf16[1536,640]{1,0:T(8,128)(2,1)} %bitcast.124, ...), custom_call_target="tpu_custom_call" | custom-call | tf_op jit(solution)/shard_map/heads_1/pallas_call | solution.py:578
  328.3 62.9 %feed_1.1 = (f32[128,1536]{1,0:T(8,128)}, bf16[8,128,1536]{2,1,0:T(8,128)(2,1)}, bf16[1024,1120]{1,0:T(8,128)(2,1)}, bf16[1024,1120]{1,0:T(8,128)(2,1)}) custom-call(bf16[128,1536]{1,0:T(8,128)(2,1)} %multiply_convert_fusion.1.refs_0_, bf16[1536,1120]{1,0:T(8,128)(2,1)} %get-tuple-element.86.refs_1_.refs_2_, ...), custom_call_target="tpu_custom_call" | custom-call | tf_op jit(solution)/shard_map/feed_1/pallas_call | solution.py:578
  391.2 68.4 %back_feed_1.1 = (f32[128,1536]{1,0:T(8,128)}, bf16[1536,1120]{1,0:T(8,128)(2,1)}, bf16[1536,1120]{1,0:T(8,128)(2,1)}, bf16[1120,1536]{1,0:T(8,128)(2,1)}, bf16[2,1120,384]{2,1,0:T(8,128)(2,1)}) custom-call(bf16[8,128,1536]{2,1,0:T(8,128)(2,1)} %bitcast.126, bf16[1024,1536]{1,0:T(8,128)(2,1)} %bitcast.137, ...), custom_call_target="tpu_custom_call" | custom-call | tf_op jit(solution)/shard_map/back_feed_1/pallas_call | solution.py:578
  459.6 3.2 convert_reduce_fusion.4
  463.1 1.9 fusion.18
  465.0 72.5 %back_heads_1.1 = (f32[128,1536]{1,0:T(8,128)}, bf16[4,208,640]{2,1,0:T(8,128)(2,1)}, bf16[192,1536]{1,0:T(8,128)(2,1)}, bf16[2,384,1120]{2,1,0:T(8,128)(2,1)}, bf16[2,384,1120]{2,1,0:T(8,128)(2,1)}) custom-call(bf16[128,1536]{1,0:T(8,128)(2,1)} %get-tuple-element.172.refs_0_, bf16[1024,1536]{1,0:T(8,128)(2,1)} %bitcast.135, bf16[1536,640]{1,0:T(8,128)(2,1)} %bitcast.125, ...), custom_call_target="tpu_custom_call" | custom-call | tf_op jit(solution)/shard_map/back_heads_1/pallas_call | solution.py:578
  537.6 1.4 multiply_reduce_fusion.2
  539.1 1.1 fusion.17
  540.2 77.9 %back_feed_0.1 = (f32[128,1536]{1,0:T(8,128)}, bf16[1536,1120]{1,0:T(8,128)(2,1)}, bf16[1536,1120]{1,0:T(8,128)(2,1)}, bf16[1120,1536]{1,0:T(8,128)(2,1)}, bf16[...) custom-call(bf16[128,1536]{1,0:T(8,128)(2,1)} %get-tuple-element.170.refs_0_, ...), custom_call_target="tpu_custom_call" | custom-call | tf_op jit(solution)/shard_map/back_feed_0/pallas_call | solution.py:578
  618.1 1.2 convert_reduce_fusion.7
  619.4 1.7 add_convert_fusion.2.refs_11_
  621.3 1.0 fusion.16
  622.4 77.2 %back_heads_0.1 = (f32[128,1536]{1,0:T(8,128)}, bf16[4,208,640]{2,1,0:T(8,128)(2,1)}, bf16[192,1536]{1,0:T(8,128)(2,1)}, bf16[2,384,1120]{2,1,0:T(8,128)(2,1)}, ...) custom-call(bf16[128,1536]{1,0:T(8,128)(2,1)} %get-tuple-element.168.refs_0_, ...), custom_call_target="tpu_custom_call" | custom-call | tf_op jit(solution)/shard_map/back_heads_0/pallas_call | solution.py:578
  699.6 1.5 fusion.9
  701.1 1.6 fusion.12
  703.9 1.9 convert_reduce_fusion.8
  706.2 1.1 stack_reshape.23
  708.1 30.1 %close.1 = (bf16[8,192,256]{2,1,0:T(8,128)(2,1)S(1)}, f32[4,8,8,192]{3,2,1,0:T(8,128)S(1)}, bf16[2,208,640]{2,1,0:T(8,128)(2,1)S(1)}, bf16[2,192,384]{2,1,0:T(8,128)(2,1)S(1)}) custom-call(bf16[8,192,256]{2,1,0:T(8,128)(2,1)S(1)} %bitcast.118, f32[8,8,192]{2,1,0:T(8,128)S(1)} %copy-done.25, bf16[832,640]{1,0:T(8,128)(2,1)S(1)} %bitcast.119, ...), custom_call_target="tpu_custom_call" | custom-call | tf_op jit(solution)/shard_map/close/pallas_call | solution.py:578
  741.4 1.1 add_bitcast_fusion.8
  745.4 10.4 %close_heads.1 = bf16[2,2,2,208,128]{4,3,2,1,0:T(8,128)(2,1)S(1)} custom-call(bf16[208,640]{1,0:T(8,128)(2,1)S(1)} %add_convert_fusion.1.refs_0_), custom_call_target="tpu_custom_call" | custom-call | tf_op jit(solution)/shard_map/close_heads/pallas_call | solution.py:578
  758.5 1.2 copy-done.27
  759.7 1.7 add_bitcast_fusion.4
  761.4 2.0 pad_maximum_fusion.2
  763.9 1.2 copy-done.33
  765.4 3.0 add_bitcast_fusion.1
  768.7 1.2 copy-done.31
  770.2 2.9 add_bitcast_fusion
  773.3 2.9 copy.84
  776.3 2.2 pad_maximum_fusion
  778.5 2.9 copy.83
  (184 shorter events, 34.0 us)
Async XLA Ops:
  4.7 253.3 %copy-start.2 = (s32[1024,1]{1,0:T(8,128)}, s32[1024,1]{1,0:T(8,128)S(1)}, u32[]{:S(2)}) copy-start(s32[1024,1]{1,0:T(8,128)S(1)} %copy.66.refs_7_.refs_6_.refs_8_) | copy-start | bytes 12292
  6.8 251.2 %copy-start.4 = (f32[1024,128]{1,0:T(8,128)}, f32[1024,128]{1,0:T(8,128)S(1)}, u32[]{:S(2)}) copy-start(f32[1024,128]{1,0:T(8,128)S(1)} %fusion.10.refs_6_.refs_5_.refs_7_) | copy-start | bytes 1572868
  7.0 251.0 %copy-start.3 = (f32[1024,128]{1,0:T(8,128)}, f32[1024,128]{1,0:T(8,128)S(1)}, u32[]{:S(2)}) copy-start(f32[1024,128]{1,0:T(8,128)S(1)} %maximum_bitcast_fusion.refs_5_.refs_4_.refs_6_) | copy-start | bytes 1572868
  9.9 64.7 %copy-start = (bf16[2,384,1120]{2,1,0:T(8,128)(2,1)}, bf16[2,384,1120]{2,1,0:T(8,128)(2,1)S(1)}, u32[]{:S(2)}) copy-start(bf16[2,384,1120]{2,1,0:T(8,128)(2,1)S(1)} %copy.60.refs_7_.refs_6_) | copy-start | bytes 5160964
  14.0 1.0 copy-start.7
  15.0 1.0 copy-start.8
  16.0 1.0 copy-start.21
  74.6 1.8 copy-start.1
  76.4 1.7 copy-start.5
  78.1 1.0 copy-start.9
  79.0 1.0 copy-start.11
  82.3 2.9 copy-start.15
  82.3 2.9 copy-start.17
  85.2 168.3 %copy-start.44 = (f32[1536]{0:T(1024)}, f32[1536]{0:T(1024)S(1)}, u32[]{:S(2)}) copy-start(f32[1536]{0:T(1024)S(1)} %get-tuple-element.165) | copy-start | bytes 18436
  85.2 377.6 %copy-start.46 = (f32[1536]{0:T(1024)}, f32[1536]{0:T(1024)S(1)}, u32[]{:S(2)}) copy-start(f32[1536]{0:T(1024)S(1)} %get-tuple-element.164) | copy-start | bytes 18436
  85.3 1.7 copy-start.10
  85.4 2.0 copy-start.12
  93.7 4.4 copy-start.20
  172.0 1.4 copy-start.22
  174.0 8.1 %copy-start.47 = (f32[128]{0:T(128)}, f32[128]{0:T(128)S(1)}, u32[]{:S(2)}) copy-start(f32[128]{0:T(128)S(1)} %get-tuple-element.197) | copy-start | bytes 1540
  251.6 2.1 copy-start.41
  251.6 2.1 copy-start.42
  253.5 1.2 copy-start.38
  253.5 1.5 copy-start.39
  459.6 3.3 copy-start.28
  459.6 3.5 copy-start.36
  459.6 3.5 copy-start.40
  465.0 72.6 %copy-start.45 = (f32[1536]{0:T(1024)S(1)}, f32[1536]{0:T(1024)}, u32[]{:S(2)}) copy-start(f32[1536]{0:T(1024)} %copy-done.44) | copy-start | bytes 18436
  465.0 72.6 %copy-start.50 = (f32[128]{0:T(128)S(1)}, f32[128]{0:T(128)}, u32[]{:S(2)}) copy-start(f32[128]{0:T(128)} %copy-done.49) | copy-start | bytes 1540
  465.0 74.0 %copy-start.53 = (f32[128]{0:T(128)S(1)}, f32[128]{0:T(128)}, u32[]{:S(2)}) copy-start(f32[128]{0:T(128)} %get-tuple-element.198) | copy-start | bytes 1540
  537.6 1.5 copy-start.30
  618.1 3.0 copy-start.29
  618.1 3.0 copy-start.48
  618.1 3.2 copy-start.52
  622.4 77.3 %copy-start.51 = (f32[128]{0:T(128)S(1)}, f32[128]{0:T(128)}, u32[]{:S(2)}) copy-start(f32[128]{0:T(128)} %get-tuple-element.195) | copy-start | bytes 1540
  622.4 78.7 %copy-start.54 = (f32[128]{0:T(128)S(1)}, f32[128]{0:T(128)}, u32[]{:S(2)}) copy-start(f32[128]{0:T(128)} %get-tuple-element.194) | copy-start | bytes 1540
  702.8 3.0 copy-start.43
  703.9 3.4 copy-start.6
  703.9 3.4 copy-start.13
  707.2 0.8 copy-start.25
  743.3 2.0 copy-start.19
  755.8 1.4 copy-start.37
  756.0 2.3 copy-start.35
  758.2 1.5 copy-start.27
  761.4 2.2 copy-start.34
  763.6 1.5 copy-start.33
  765.3 3.1 copy-start.32
  768.4 1.5 copy-start.31
  (7 other events, 5.1 us)

commit v4 on v3

--- a/solution.py
+++ b/solution.py
@@ -19,6 +19,7 @@
 F32 = jnp.float32
 ANY = pl.BlockSpec(memory_space=pl.ANY)
 ONCHIP = pl.BlockSpec(memory_space=pltpu.VMEM)
+VMEM = 62 * 2**20
 HALF = 208
 
 
@@ -128,7 +129,12 @@
         self.half = block.shape[0] // 32 * 16
         self.rest = block.shape[0] - self.half
         self.outs = (jax.ShapeDtypeStruct(tuple(full), block.dtype),)
-        self.scratch = (pltpu.SemaphoreType.DMA((6,)), pltpu.SemaphoreType.DMA((6,)), pltpu.SemaphoreType.DMA((1,)))
+        self.scratch = (
+            pltpu.SemaphoreType.DMA((6,)),
+            pltpu.SemaphoreType.DMA((6,)),
+            pltpu.SemaphoreType.DMA((2,)),
+            pltpu.VMEM(block.shape, block.dtype),
+        )
 
     def halves(self, ref):
         return ref.at[0 : self.half, :], ref.at[self.half :, :]
@@ -144,7 +150,7 @@
         return ins[0] if self.layer is None else ins[0].at[self.layer]
 
     def copies(self, place, ins, outs, scratch):
-        src, (dst,), (send, recv, _) = self.source(ins), outs, scratch
+        src, (dst,), (send, recv, *_) = self.source(ins), outs, scratch
         x, y, d = place.rows()
         block, mine = self.halves(src), self.spots(dst, place.r)
         from_x, from_y = self.spots(dst, x), self.spots(dst, y)
@@ -160,17 +166,24 @@
         ]
         return out, onward
 
+    def keep(self, place, ins, outs, scratch):
+        *_, sem, buffer = scratch
+        return (
+            pltpu.make_async_copy(self.source(ins), buffer, sem.at[0]),
+            pltpu.make_async_copy(buffer, part_of(outs[0], self.dim, place.r, self.size), sem.at[1]),
+        )
+
     def arrived(self, place, scratch, view, sem, row):
         return remote(view, view, scratch[0].at[0], scratch[1].at[sem], (row, place.k))
 
     def start(self, place, ins, outs, scratch, later):
-        src, (dst,), (_, _, keep_sem) = self.source(ins), outs, scratch
+        (dst,) = outs
         out, onward = self.copies(place, ins, outs, scratch)
         for copy in out:
             copy.start()
-        keep = pltpu.make_async_copy(src, part_of(dst, self.dim, place.r, self.size), keep_sem.at[0])
-        keep.start()
-        later.add(keep.wait)
+        load, store = self.keep(place, ins, outs, scratch)
+        load.start()
+        later.add(store.wait)
         x, y, d = place.rows()
         from_x, from_y, from_d = self.spots(dst, x), self.spots(dst, y), self.spots(dst, d)
         for view, sem, row in ((from_x[1], 1, x), (from_y[0], 2, y), (from_d[0], 4, y), (from_d[1], 5, x)):
@@ -182,6 +195,9 @@
         (dst,) = outs
         x, y, d = place.rows()
         _, onward = self.copies(place, ins, outs, scratch)
+        load, store = self.keep(place, ins, outs, scratch)
+        load.wait()
+        store.start()
         self.arrived(place, scratch, self.spots(dst, x)[0], 0, x).wait_recv()
         onward[0].start()
         self.arrived(place, scratch, self.spots(dst, y)[1], 3, y).wait_recv()
@@ -288,10 +304,18 @@
         self.layer = layer
         self.arrays = (weight, biases)
         self.outs = (jax.ShapeDtypeStruct((HALF, 5 * HD), LOW),)
-        self.scratch = (pltpu.SemaphoreType.DMA((2, 2, 2, 2)), pltpu.SemaphoreType.DMA((5, 2)))
+        self.scratch = (
+            pltpu.SemaphoreType.DMA((2, 2, 2, 2)),
+            pltpu.SemaphoreType.DMA((5, 2)),
+            pltpu.VMEM(weight.shape[1:], weight.dtype),
+            pltpu.VMEM(biases.shape[1:], biases.dtype),
+            pltpu.SemaphoreType.DMA((2,)),
+        )
 
     def start(self, place, ins, outs, scratch, later):
-        (weight, biases), (slab,), (send, recv) = ins, outs, scratch
+        (slab,), (send, recv, weight, biases, load_sem) = outs, scratch
+        for load in copy_in([(ins[0].at[self.layer], weight), (ins[1].at[self.layer], biases)], load_sem):
+            load.wait()
         r, k, z, c = place.r, place.k, place.z, place.c
         query = k < 6
         rows = D // 8
@@ -308,8 +332,8 @@
                     if second == 1:
                         here, away = here & (k >= 6), away & (k >= 6)
                     views = (
-                        weight.at[self.layer, core * rows : (core + 1) * rows, i * HD : (i + 1) * HD],
-                        biases.at[self.layer, i],
+                        weight.at[core * rows : (core + 1) * rows, i * HD : (i + 1) * HD],
+                        biases.at[i],
                     )
                     for part in range(2):
                         sem = send.at[i, second, core, part]
@@ -412,89 +436,128 @@
     lax.fori_loop(0, rows // 16, step, 0)
 
 
-def at_two(middle):
-    def between(s):
-        if s == 2:
-            middle(1)
-
-    return between
-
-
-def pair_copy(place, part, from_p, sems, j):
-    return remote(part.at[2 * j + 1 - place.c], from_p.at[j], sems[0].at[j], sems[1].at[j], place.at(place.z, 1 - place.c))
-
-
-def reduce_line(place, part, out, from_p, from_r, from_l, held, sems, later, both, between, sent=False):
-    send_p, recv_p, send, recv_r, recv_l = sems
-    z, c = place.z, place.c
-    right_at, left_at = place.at(jnp.minimum(z + 1, 3), c), place.at(jnp.maximum(z - 1, 0), c)
-
-    def own(j):
-        return part.at[2 * j + c] if both else part.at[j]
-
-    def partner(j):
-        return pair_copy(place, part, from_p, sems, j)
-
-    def moving(j, buffer, sem, device):
-        return remote(held.at[j], buffer.at[j], send.at[j], sem.at[j], device)
-
-    if both:
-        for j in (3, 0, 2, 1):
-            copy = partner(j)
-            if not sent:
-                copy.start()
-            later.add(copy.wait_send)
-
-    def terms(j):
-        if both:
-            partner(j).wait_recv()
-            return [own(j), from_p.at[j]]
-        return [own(j)]
-
-    for s in range(3):
-        if s:
-            between(s)
-        for go_right in (True, False):
-            if go_right:
-                j, valid, first = 3 - s + z, z <= s, z == 0
-                buffer, sem, device = from_r, recv_r, right_at
-            else:
-                j, valid, first = s - 3 + z, z >= 3 - s, z == 3
-                buffer, sem, device = from_l, recv_l, left_at
-            j = jnp.clip(j, 0, 3)
-            copy = moving(j, buffer, sem, device)
-
-            @pl.when(valid & first)
-            def _(j=j, copy=copy):
-                add_into(held.at[j], terms(j))
-                copy.start()
-
-            @pl.when(valid & jnp.logical_not(first))
-            def _(j=j, copy=copy, buffer=buffer):
-                views = terms(j)
-                copy.wait_recv()
-                add_into(held.at[j], [*views, buffer.at[j]])
-                copy.start()
-
-            later.add(copy.wait_send, valid)
-    views = terms(z)
-    last_r, last_l = moving(z, from_r, recv_r, right_at), moving(z, from_l, recv_l, left_at)
-
-    @pl.when(z == 0)
-    def _():
-        last_l.wait_recv()
-        add_into(out, [*views, from_l.at[z]])
-
-    @pl.when(z == 3)
-    def _():
-        last_r.wait_recv()
-        add_into(out, [*views, from_r.at[z]])
-
-    @pl.when((z > 0) & (z < 3))
-    def _():
-        last_r.wait_recv()
-        last_l.wait_recv()
-        add_into(out, [*views, from_r.at[z], from_l.at[z]])
+SUB = 4
+
+
+class Reduce:
+    @staticmethod
+    def scratch(tokens, width):
+        return [
+            pltpu.VMEM((4, tokens, width), LOW),
+            pltpu.VMEM((2, 4, tokens, width), LOW),
+            pltpu.VMEM((4, tokens, width), LOW),
+            pltpu.SemaphoreType.DMA((4,)),
+            pltpu.SemaphoreType.DMA((4,)),
+            pltpu.SemaphoreType.DMA((4, SUB)),
+            pltpu.SemaphoreType.DMA((2, 4, SUB)),
+        ]
+
+    def __init__(self, place, part, out, scratch, both=True, far=False):
+        self.place, self.part, self.out, self.both, self.far = place, part, out, both, far
+        self.from_p, self.moved, self.held, self.send_p, self.recv_p, self.send, self.recv = scratch
+        z, c = place.z, place.c
+        self.edge = (z == 0) | (z == 3)
+        self.mid = jnp.logical_not(self.edge)
+        self.right, self.left = place.at(jnp.minimum(z + 1, 3), c), place.at(jnp.maximum(z - 1, 0), c)
+        self.size = part.shape[1] // SUB
+
+    def pair(self, j):
+        place = self.place
+        other = self.part.at[2 * j + 1 - place.c]
+        return remote(other, self.from_p.at[j], self.send_p.at[j], self.recv_p.at[j], place.at(place.z, 1 - place.c))
+
+    def piece(self, j, sub, way):
+        rows = pl.ds(sub * self.size, self.size)
+        column = jnp.where(way == 0, self.right[1], self.left[1])
+        return remote(
+            self.held.at[j, rows, :],
+            self.moved.at[way, j, rows, :],
+            self.send.at[j, sub],
+            self.recv.at[way, j, sub],
+            (self.place.r, column),
+        )
+
+    def terms(self, j):
+        if self.both:
+            return [self.part.at[2 * j + self.place.c], self.from_p.at[j]]
+        return [self.part.at[j]]
+
+    def made(self, j):
+        z = self.place.z
+        if self.both:
+            self.pair(j).start()
+
+        @pl.when(self.edge & (j != z))
+        def _():
+            if self.both:
+                self.pair(j).wait_recv()
+            add_into(self.held.at[j], self.terms(j))
+            for sub in range(SUB):
+                self.piece(j, sub, jnp.where(z == 0, 0, 1)).start()
+
+    def finish(self, later, between):
+        z = self.place.z
+        way = jnp.where(z == 1, 0, 1)
+        near, far, back = jnp.where(z == 1, 2, 1), jnp.where(z == 1, 3, 0), jnp.where(z == 1, 0, 3)
+        first, second = (far, near) if self.far else (near, far)
+
+        def step(j, sub, way):
+            copy = self.piece(j, sub, way)
+            copy.wait_recv()
+            rows = pl.ds(sub * self.size, self.size)
+            views = [view.at[rows, :] for view in (*self.terms(j), self.moved.at[way, j])]
+            add_into(self.held.at[j].at[rows, :], views)
+            copy.start()
+
+        for i in range(2 * SUB):
+            sub = i % SUB
+
+            @pl.when(self.mid)
+            def _(i=i, sub=sub):
+                if self.both and sub == 0:
+                    self.pair(first if i == 0 else second).wait_recv()
+                if i < SUB:
+                    step(first, sub, way)
+                    return
+                step(second, sub, way)
+                if self.both and sub == 0:
+                    self.pair(back).wait_recv()
+                step(back, sub, 1 - way)
+
+            between(i)
+        if self.both:
+            self.pair(z).wait_recv()
+
+        def came(way):
+            for sub in range(SUB):
+                self.piece(z, sub, way).wait_recv()
+
+        views = self.terms(z)
+
+        @pl.when(self.edge)
+        def _():
+            way = jnp.where(z == 0, 1, 0)
+            came(way)
+            add_into(self.out, [*views, self.moved.at[way, z]])
+
+        @pl.when(self.mid)
+        def _():
+            came(0)
+            came(1)
+            add_into(self.out, [*views, self.moved.at[0, z], self.moved.at[1, z]])
+
+        for j in range(4):
+            if self.both:
+                later.add(self.pair(j).wait_send)
+            for sub in range(SUB):
+                later.add(self.piece(j, sub, 0).wait_send, z != j)
+
+
+def far_first(place, p):
+    z = place.z
+    edge = jnp.where(z == 0, 3 - p, p)
+    mid = jnp.where(p == 0, jnp.where(z == 1, 3, 0), jnp.where(p == 1, jnp.where(z == 1, 2, 1), jnp.where(p == 2, jnp.where(z == 1, 0, 3), z)))
+    return jnp.where((z == 0) | (z == 3), edge, mid)
 
 
 class Names:
@@ -555,14 +618,13 @@
             if item.phase == phase:
                 item.middle(place, taken[item], made[item], held[item])
 
-    start(0)
     body(place, ins, outs, scratch, later, middle, start)
     later.run()
     for waits in owed:
         waits.run()
 
 
-def carry_call(names, body, reach, arrays, in_specs, outs, out_specs, scratch, cargo, name=None, vmem=40):
+def carry_call(names, body, reach, arrays, in_specs, outs, out_specs, scratch, cargo, name=None):
     given = [a for item in cargo for a in given_arrays(item)]
     call = pl.pallas_call(
         partial(carry_kernel, body, reach, len(arrays), len(outs), len(scratch), cargo),
@@ -571,7 +633,7 @@
         out_specs=[*out_specs, *(ANY for item in cargo for _ in item.outs)],
         scratch_shapes=[*scratch, *(s for item in cargo for s in item.scratch)],
         compiler_params=pltpu.CompilerParams(
-            collective_id=names.take(), has_side_effects=True, vmem_limit_bytes=vmem * 2**20
+            collective_id=names.take(), has_side_effects=True, vmem_limit_bytes=VMEM
         ),
         name=name,
     )
@@ -665,7 +727,7 @@
 
 def forward_feed(names, block, w_gate, w_up, w_down, cargo, name):
     tokens, width = block.shape
-    inner = w_gate.shape[1]
+    inner = w_gate.shape[0]
 
     def body(place, ins, outs, scratch, later, middle, start):
         block_ref, gate_hbm, up_hbm, down_hbm = ins
@@ -673,7 +735,7 @@
         n = len(Gather.scratch)
         gather_sems, scratch = scratch[:n], scratch[n:]
         full, part, gate_w, up_w, down_w, gates, ups, load_sem, keep_sem = scratch[:9]
-        from_p, from_r, from_l, held, *sems = scratch[9:]
+        reduce = Reduce(place, part, total, scratch[9:])
         gather = Gather(place, block_ref, full, gather_sems)
         loads = [
             pltpu.make_async_copy(src, dst, load_sem.at[i])
@@ -682,6 +744,8 @@
         for load in loads:
             load.start()
         gather.start(later)
+        start(0)
+        start(3)
         for load in loads:
             load.wait()
 
@@ -698,14 +762,14 @@
             pl.when(p == 2)(middle)
             acts = full[pl.ds(2 * j, 2)].reshape(2 * tokens, width)
             rows = pl.ds(pl.multiple_of(2 * tokens * j, 2 * tokens), 2 * tokens)
-            gate = jnp.dot(acts, gate_w[...], preferred_element_type=F32)
-            up = jnp.dot(acts, up_w[...], preferred_element_type=F32)
+            gate = dot_t(acts, gate_w[...])
+            up = dot_t(acts, up_w[...])
             gates[rows, :] = gate.astype(LOW)
             ups[rows, :] = up.astype(LOW)
             hidden = (gate * jax.nn.sigmoid(gate) * up).astype(LOW)
             sums = jnp.dot(hidden, down_w[...], preferred_element_type=F32).astype(LOW)
             part[pl.ds(2 * j, 2)] = sums.reshape(2, tokens, width)
-            pair_copy(place, part, from_p, sems, j).start()
+            reduce.made(j)
             for copy in keep(j):
                 copy.start()
             return carry
@@ -713,7 +777,7 @@
         lax.fori_loop(0, 4, step, 0)
         start(1)
         start(2)
-        reduce_line(place, part, total, from_p, from_r, from_l, held, sems, later, True, at_two(middle), sent=True)
+        reduce.finish(later, lambda i: middle(3) if i == 0 else None)
         for j in range(4):
             for copy in keep(j):
                 copy.wait()
@@ -742,21 +806,12 @@
             pltpu.VMEM((8 * tokens, inner), LOW),
             pltpu.SemaphoreType.DMA((3,)),
             pltpu.SemaphoreType.DMA((3, 4)),
-            *[pltpu.VMEM((4, tokens, width), LOW)] * 4,
-            *[pltpu.SemaphoreType.DMA((4,))] * 5,
+            *Reduce.scratch(tokens, width),
         ],
         cargo,
         name=name,
-        vmem=58,
     )
     return total, full.reshape(8 * tokens, width), gate, up, loads
-
-
-REDUCE_SEMS = [pltpu.SemaphoreType.DMA((4,))] * 5
-
-
-def reduce_scratch(tokens, width):
-    return [*[pltpu.VMEM((4, tokens, width), LOW)] * 4, *REDUCE_SEMS]
 
 
 def rows_of(first, count):
@@ -774,14 +829,15 @@
     def body(place, ins, outs, scratch, later, middle, start):
         gather = Gather(place, ins[0], outs[0], scratch)
         gather.start(later)
+        start(0)
+        start(3)
         start(1)
-        start(3)
         gather.pass_on(1)
         middle(1)
         gather.pass_on(2)
+        middle(3)
         start(2)
         gather.pass_on(3)
-        middle(3)
         for zz in range(4):
             spot = gather.spot(zz, 1 - place.c)
             recv = gather.recv.at[2 * zz + 1 - place.c]
@@ -804,6 +860,7 @@
 
 def close_call(names, cargo, name):
     def body(place, ins, outs, scratch, later, middle, start):
+        start(0)
         middle(0)
 
     return carry_call(names, body, "col", [], [], [], [], [], cargo, name=name)[1]
@@ -833,40 +890,53 @@
     return pltpu.roll(values, HD // 2, 1)
 
 
-def forward_heads(names, block, acts, w_qkv, bias, w_out, cosine, sine, starts, cargo, name):
+def forward_heads(names, block, wide, gain, w_qkv, bias, w_out, cosine, sine, starts, cargo, name):
     tokens, width = QB, D
     count = 8 * QB
-    apart = acts is not None
+    apart = wide is not None
 
     def body(place, ins, outs, scratch, later, middle, start):
         ins = list(ins)
         block_ref = ins.pop(0)
-        acts_hbm = ins.pop(0) if apart else None
+        if apart:
+            wide_hbm, gain_ref = ins.pop(0), ins.pop(0)
         qkv_hbm, bias_ref, out_hbm, cos_ref, sin_ref, starts_ref = ins
-        total, full_out, qkv_out, mixed_out = outs
+        total, full_out, qkv_out, mixed_out = outs[:4]
         scratch = list(scratch)
         gather_sems = [scratch.pop(0) for _ in Gather.scratch]
-        full, acts_own, part, qkv_w, out_w, qkv, mixed, load_sem, keep_sem = scratch[:9]
-        from_p, from_r, from_l, held, *sems = scratch[9:]
+        full, acts, flat, part, qkv_w, out_w, qkv, mixed, load_sem, keep_sem = scratch[:10]
+        reduce = Reduce(place, part, total, scratch[10:], both=False, far=True)
         pairs = [(qkv_hbm, qkv_w), (out_hbm, out_w)]
         if apart:
-            pairs.append((acts_hbm, acts_own))
+            pairs.append((wide_hbm, acts))
         loads = copy_in(pairs, load_sem)
         gather = Gather(place, block_ref, full, gather_sems)
         gather.start(later)
+        start(0)
+        start(3)
         for load in loads:
             load.wait()
 
         def keep(j):
+            if apart:
+                rows = rows_of(j * 2 * QB, 2 * QB)
+                return pltpu.make_async_copy(flat.at[rows, :], full_out.at[rows, :], keep_sem.at[j])
             return pltpu.make_async_copy(full.at[pl.ds(2 * j, 2)], full_out.at[pl.ds(2 * j, 2)], keep_sem.at[j])
 
         def step(p, carry):
             j = gather.chunk(p)
-            keep(j).start()
             pl.when(p == 2)(middle)
             rows = rows_of(j * 2 * QB, 2 * QB)
-            chunk = acts_own[rows, :] if apart else full[pl.ds(2 * j, 2)].reshape(2 * tokens, width)
-            raw = jnp.dot(chunk, qkv_w[...], preferred_element_type=F32) + bias_ref[...]
+            if apart:
+                chunk = acts[:, rows].astype(F32)
+                scale = lax.rsqrt(jnp.mean(chunk * chunk, axis=0, keepdims=True) + eps_norm)
+                chunk = (chunk * scale * gain_ref[...]).astype(LOW)
+                acts[:, rows] = chunk
+                raw = t_dot(chunk, qkv_w[...]) + bias_ref[...]
+            else:
+                keep(j).start()
+                raw = jnp.dot(full[pl.ds(2 * j, 2)].reshape(2 * tokens, width), qkv_w[...], preferred_element_type=F32)
+                raw = raw + bias_ref[...]
             cos, sin = cos_ref[rows, :], sin_ref[rows, :]
             for t in range(5):
                 head = raw[:, t * HD : (t + 1) * HD]
@@ -878,39 +948,66 @@
         lax.fori_loop(0, 4, step, 0)
         start(1)
 
-        def attend(j, carry):
+        def attend(p, carry):
+            j = far_first(place, p)
             _, _, values, probs, _, _ = block_probs(qkv, starts_ref, 2 * j + place.c)
             low = probs.astype(LOW).reshape(3 * QB, QB + SEQ_MAX)
             heads = jnp.dot(low, values, preferred_element_type=F32).astype(LOW)
-            wide = jnp.concatenate([heads[h * QB : (h + 1) * QB] for h in range(3)], axis=1)
-            mixed[rows_of(j * QB, QB), :] = wide
-            part[j] = jnp.dot(wide, out_w[...], preferred_element_type=F32).astype(LOW)
+            both = jnp.concatenate([heads[h * QB : (h + 1) * QB] for h in range(3)], axis=1)
+            mixed[rows_of(j * QB, QB), :] = both
+            part[j] = jnp.dot(both, out_w[...], preferred_element_type=F32).astype(LOW)
+            reduce.made(j)
             return carry
 
         lax.fori_loop(0, 4, attend, 0)
         saves = copy_in([(qkv, qkv_out), (mixed, mixed_out)], load_sem)
-        reduce_line(place, part, total, from_p, from_r, from_l, held, sems, later, False, at_two(middle))
+        if apart:
+            saves.append(pltpu.make_async_copy(acts, outs[4], load_sem.at[2]))
+            saves[-1].start()
+
+        def between(i):
+            if i == 0:
+                middle(3)
+            if not apart or i % 2:
+                return
+            j = i // 2
+
+            def turn(t, carry):
+                rows = rows_of(t * 2 * QB, 2 * QB)
+                piece = full[2 * j : 2 * j + 2, :, rows].reshape(D // 4, 2 * QB)
+                flat[rows, j * (D // 4) : (j + 1) * (D // 4)] = piece.T
+                return carry
+
+            lax.fori_loop(0, 4, turn, 0)
+
+        reduce.finish(later, between)
+        if apart:
+            for j in range(4):
+                keep(j).start()
         for copy in saves:
             copy.wait()
         for j in range(4):
             keep(j).wait()
 
-    (total, full, qkv, mixed), loads = carry_call(
+    gathered = (count, width) if apart else (8, tokens, width)
+    results, loads = carry_call(
         names,
         body,
         "line",
-        [block, *([acts] if apart else []), w_qkv, bias, w_out, cosine, sine, starts],
-        [ONCHIP, *([ANY] if apart else []), ANY, ONCHIP, ANY, ONCHIP, ONCHIP, ONCHIP],
+        [block, *([wide, gain] if apart else []), w_qkv, bias, w_out, cosine, sine, starts],
+        [ONCHIP, *([ANY, ONCHIP] if apart else []), ANY, ONCHIP, ANY, ONCHIP, ONCHIP, ONCHIP],
         [
             jax.ShapeDtypeStruct((tokens, width), F32),
-            jax.ShapeDtypeStruct((8, *block.shape), LOW),
+            jax.ShapeDtypeStruct(gathered, LOW),
             jax.ShapeDtypeStruct((count, 5 * HD), LOW),
             jax.ShapeDtypeStruct((count // 2, 3 * HD), LOW),
+            *([jax.ShapeDtypeStruct((width, count), LOW)] if apart else []),
         ],
-        [ONCHIP, ANY, ANY, ANY],
+        [ONCHIP, ANY, ANY, ANY, *([ANY] if apart else [])],
         [
             *Gather.scratch,
             pltpu.VMEM((8, *block.shape), LOW),
+            pltpu.VMEM((width, count) if apart else (16, 128), LOW),
             pltpu.VMEM((count, width) if apart else (16, 128), LOW),
             pltpu.VMEM((4, tokens, width), LOW),
             pltpu.VMEM(w_qkv.shape, LOW),
@@ -919,16 +1016,16 @@
             pltpu.VMEM((count // 2, 3 * HD), LOW),
             pltpu.SemaphoreType.DMA((3,)),
             pltpu.SemaphoreType.DMA((4,)),
-            *reduce_scratch(tokens, width),
+            *Reduce.scratch(tokens, width),
         ],
         cargo,
         name=name,
-        vmem=50,
     )
-    return total, full, qkv, mixed, loads
-
-
-def backward_heads(names, block, acts, w_qkv, w_out, qkv, mixed, cosine, sine, starts, cargo, name):
+    total, full, qkv, mixed = results[:4]
+    return total, full.reshape(count, width), qkv, mixed, results[4] if apart else None, loads
+
+
+def backward_heads(names, block, acts, turned, w_qkv, w_out, qkv, mixed, cosine, sine, starts, cargo, name):
     tokens, width = QB, D
     count = 8 * QB
     reach = QB + SEQ_MAX
@@ -940,11 +1037,13 @@
         gather_sems = [scratch.pop(0) for _ in Gather.scratch]
         full, part, qkv_w, out_w, qkv, mixed, acts_own, d_raw, d_keys, d_values = scratch[:10]
         slab, d_out, slab_in, d_out_in, load_sem, swap_send, swap_recv = scratch[10:17]
-        from_p, from_r, from_l, held, *sems = scratch[17:]
+        reduce = Reduce(place, part, total, scratch[17:], far=True)
         pairs = [(qkv_hbm, qkv_w), (out_hbm, out_w), (saved_hbm, qkv), (mixed_hbm, mixed), (acts_hbm, acts_own)]
         loads = copy_in(pairs, load_sem)
         gather = Gather(place, block_ref, full, gather_sems, both=False)
         gather.start(later)
+        start(0)
+        start(3)
         d_keys[...] = jnp.zeros_like(d_keys)
         d_values[...] = jnp.zeros_like(d_values)
         for load in loads:
@@ -975,14 +1074,15 @@
         lax.fori_loop(0, 4, step, 0)
         start(1)
 
-        def project(j, carry):
+        def project(p, carry):
+            j = far_first(place, p)
             rows = rows_of(j * 2 * QB, 2 * QB)
             head = d_keys[rows, :]
             head = head * cos_ref[rows, :] + roll_half(head * sin_ref[rows, :])
             d_raw[rows, 3 * HD : 4 * HD] = head.astype(LOW)
             d_raw[rows, 4 * HD : 5 * HD] = d_values[rows, :].astype(LOW)
             part[pl.ds(2 * j, 2)] = dot_t(d_raw[rows, :], qkv_w[...]).astype(LOW).reshape(2, tokens, width)
-            pair_copy(place, part, from_p, sems, j).start()
+            reduce.made(j)
             return carry
 
         lax.fori_loop(0, 4, project, 0)
@@ -994,32 +1094,31 @@
                 remote(d_out.at[1 - place.c], d_out_in, swap_send.at[1], swap_recv.at[1], to),
             ]
 
-        def between(s):
-            if s == 2:
-                middle(1)
+        def between(i):
+            if i < 4:
+                cut = slice(i * (D // 4), (i + 1) * (D // 4))
+                if turned:
+                    grads = jnp.dot(acts_own[cut, :], d_raw[...], preferred_element_type=F32).astype(LOW)
+                else:
+                    grads = t_dot(acts_own[:, cut], d_raw[...]).astype(LOW)
+                slab[0, i, 0 : D // 8, :] = grads[: D // 8]
+                slab[1, i, 0 : D // 8, :] = grads[D // 8 :]
+            elif i == 4:
+                sums = jnp.sum(d_raw[...].astype(F32), axis=0, keepdims=True)
+                first = lax.broadcasted_iota(jnp.int32, (16, 5 * HD), 0) == 0
+                tail = jnp.where(first, sums, 0.0).astype(LOW)
+                for half in range(2):
+                    for part_at in range(4):
+                        slab[half, part_at, D // 8 :, :] = tail
+                grads = t_dot(mixed[...], full[...].reshape(4 * QB, D)).astype(LOW)
+                d_out[0] = grads[: D // 8]
+                d_out[1] = grads[D // 8 :]
                 for copy in swap():
                     copy.start()
-                return
-
-            def weights(i, carry):
-                cut = pl.ds(pl.multiple_of(i * (D // 4), 128), D // 4)
-                grads = t_dot(acts_own[:, cut], d_raw[...]).astype(LOW)
-                slab[0, i, 0 : D // 8, :] = grads[: D // 8]
-                slab[1, i, 0 : D // 8, :] = grads[D // 8 :]
-                return carry
-
-            lax.fori_loop(0, 4, weights, 0)
-            sums = jnp.sum(d_raw[...].astype(F32), axis=0, keepdims=True)
-            first = lax.broadcasted_iota(jnp.int32, (16, 5 * HD), 0) == 0
-            tail = jnp.where(first, sums, 0.0).astype(LOW)
-            for half in range(2):
-                for i in range(4):
-                    slab[half, i, D // 8 :, :] = tail
-            grads = t_dot(mixed[...], full[...].reshape(4 * QB, D)).astype(LOW)
-            d_out[0] = grads[: D // 8]
-            d_out[1] = grads[D // 8 :]
-
-        reduce_line(place, part, total, from_p, from_r, from_l, held, sems, later, True, between, sent=True)
+            if i == 0:
+                middle(3)
+
+        reduce.finish(later, between)
         for copy in swap():
             copy.wait()
         for i in range(4):
@@ -1046,7 +1145,7 @@
             pltpu.VMEM(w_out.shape, LOW),
             pltpu.VMEM((count, 5 * HD), LOW),
             pltpu.VMEM((count // 2, 3 * HD), LOW),
-            pltpu.VMEM((count, width), LOW),
+            pltpu.VMEM(acts.shape, LOW),
             pltpu.VMEM((count, 5 * HD), LOW),
             pltpu.VMEM((count, HD), F32),
             pltpu.VMEM((count, HD), F32),
@@ -1057,18 +1156,48 @@
             pltpu.SemaphoreType.DMA((5,)),
             pltpu.SemaphoreType.DMA((2,)),
             pltpu.SemaphoreType.DMA((2,)),
-            *reduce_scratch(tokens, width),
+            *Reduce.scratch(tokens, width),
         ],
         cargo,
         name=name,
-        vmem=60,
     )
     return total, slab.reshape(4 * HALF, 5 * HD), d_out, loads
 
 
+def settle_rows(row, fulls, slots):
+    kinds, layers = len(fulls), len(fulls[0])
+    count, size = slots[0][0].shape[1:]
+    tile = count // 5
+
+    def kernel(row_ref, *refs):
+        ins, outs = refs[: 2 * kinds * layers], refs[2 * kinds * layers :]
+        for kind in range(kinds):
+            for layer in range(layers):
+                full, slot = ins[2 * (kind * layers + layer)], ins[2 * (kind * layers + layer) + 1]
+                outs[kind][layer] = full[...].astype(F32) + slot[0].astype(F32) + slot[1].astype(F32)
+
+    pairs = [pair for kind in range(kinds) for pair in zip(fulls[kind], slots[kind])]
+    return pl.pallas_call(
+        kernel,
+        out_shape=[jax.ShapeDtypeStruct((layers, count, size), F32)] * kinds,
+        grid_spec=pltpu.PrefetchScalarGridSpec(
+            num_scalar_prefetch=1,
+            grid=(count // tile,),
+            in_specs=[
+                pl.BlockSpec((tile, size), lambda i, row: (i, row[0])),
+                pl.BlockSpec((2, tile, size), lambda i, row: (0, i, 0)),
+            ]
+            * (kinds * layers),
+            out_specs=[pl.BlockSpec((layers, tile, size), lambda i, row: (0, i, 0))] * kinds,
+        ),
+        compiler_params=pltpu.CompilerParams(vmem_limit_bytes=VMEM),
+        name="settle",
+    )(row.reshape(1), *[array for pair in pairs for array in pair])
+
+
 def backward_feed(names, block, grads_all, acts, w_gate, w_up, w_down, gate, up, cargo, name):
     tokens, width = QB, D
-    inner = w_gate.shape[1]
+    inner = w_gate.shape[0]
     apart = grads_all is not None
 
     def body(place, ins, outs, scratch, later, middle, start):
@@ -1077,7 +1206,7 @@
         scratch = list(scratch)
         gather_sems = [scratch.pop(0) for _ in Gather.scratch]
         full, part, acts_own, gate_w, up_w, down_w, gates, ups, hiddens, load_sem, keep_sem = scratch[:11]
-        from_p, from_r, from_l, held, *sems = scratch[11:]
+        reduce = Reduce(place, part, total, scratch[11:], far=apart)
         pairs = [(down_hbm, down_w), (gates_hbm, gates), (ups_hbm, ups), (gate_hbm, gate_w), (up_hbm, up_w)]
         pairs.append((acts_hbm, acts_own))
         if apart:
@@ -1087,11 +1216,13 @@
         if not apart:
             gather = Gather(place, head_ref, full, gather_sems)
             gather.start(later)
+        start(0)
+        start(3)
         for load in loads:
             load.wait()
 
         def step(p, carry):
-            j = p if apart else gather.chunk(p)
+            j = far_first(place, p) if apart else gather.chunk(p)
             pl.when(p == 2)(middle)
             rows = rows_of(j * 2 * tokens, 2 * tokens)
             grads = full[pl.ds(2 * j, 2)].reshape(2 * tokens, width)
@@ -1104,38 +1235,48 @@
             d_up = (d_hidden * lit).astype(LOW)
             gates[rows, :] = d_gate
             ups[rows, :] = d_up
-            sums = dot_t(d_gate, gate_w[...]) + dot_t(d_up, up_w[...])
+            sums = dot(d_gate, gate_w[...]) + dot(d_up, up_w[...])
             part[pl.ds(2 * j, 2)] = sums.astype(LOW).reshape(2, tokens, width)
-            pair_copy(place, part, from_p, sems, j).start()
+            reduce.made(j)
             return carry
 
         lax.fori_loop(0, 4, step, 0)
 
-        def between(s):
-            if s == 1:
-                grads = full[...].reshape(8 * tokens, width)
-
-                def down(i, carry):
-                    cut = pl.ds(pl.multiple_of(i * 384, 128), 384)
-                    down_w[:, cut] = t_dot(hiddens[...], full[:, :, cut].reshape(8 * tokens, 384)).astype(LOW)
-                    return carry
-
-                lax.fori_loop(0, width // 384, down, 0)
+        def weights(dst, left, right, low, high):
+            def tile(i, carry):
+                cut = pl.ds(pl.multiple_of(i * 256, 256), 256)
+                dst[cut, :] = t_dot(left[:, cut], right()).astype(LOW)
+                return carry
+
+            whole = inner // 256
+            lax.fori_loop(low, min(high, whole), tile, 0)
+            if high > whole and inner % 256:
+                dst[whole * 256 :, :] = t_dot(left[:, whole * 256 :], right()).astype(LOW)
+
+        def grads_flat():
+            return full[...].reshape(8 * tokens, width)
+
+        def acts_flat():
+            return acts_own[...]
+
+        work = [
+            (down_w, hiddens, grads_flat, 0, 3),
+            (down_w, hiddens, grads_flat, 3, 5),
+            (gate_w, gates, acts_flat, 0, 3),
+            (gate_w, gates, acts_flat, 3, 5),
+            (up_w, ups, acts_flat, 0, 3),
+            (up_w, ups, acts_flat, 3, 5),
+        ]
+
+        def between(i):
+            if i < len(work):
+                weights(*work[i])
+            if i == 1:
                 start(1, down_w)
-                return
-
-            def rest(i, carry):
-                cut = pl.ds(pl.multiple_of(i * 384, 128), 384)
-                acts_cut = acts_own[:, cut]
-                rows = pl.ds(pl.multiple_of(i * 384, 128), 384)
-                gate_w[rows, :] = t_dot(acts_cut, gates[...]).astype(LOW)
-                up_w[rows, :] = t_dot(acts_cut, ups[...]).astype(LOW)
-                return carry
-
-            lax.fori_loop(0, width // 384, rest, 0)
-            middle(1)
-
-        reduce_line(place, part, total, from_p, from_r, from_l, held, sems, later, True, between, sent=True)
+            if i == 5:
+                middle(1)
+
+        reduce.finish(later, between)
         for copy in copy_in([(gate_w, gate_out), (up_w, up_out), (down_w, down_out)], keep_sem):
             copy.wait()
 
@@ -1166,11 +1307,10 @@
             pltpu.VMEM((8 * tokens, inner), LOW),
             pltpu.SemaphoreType.DMA((7,)),
             pltpu.SemaphoreType.DMA((3,)),
-            *reduce_scratch(tokens, width),
+            *Reduce.scratch(tokens, width),
         ],
         cargo,
         name=name,
-        vmem=61,
     )
     return total, d_gate, d_up, d_down, loads
 
@@ -1547,8 +1687,8 @@
 
     def rows_load(layer):
         return (
-            GatherRows(gate_weight, 0, layer),
-            GatherRows(up_weight, 0, layer),
+            GatherRows(gate_weight.swapaxes(1, 2), 1, layer),
+            GatherRows(up_weight.swapaxes(1, 2), 1, layer),
             GatherRows(down_weight, 1, layer),
         )
 
@@ -1568,39 +1708,31 @@
     cosine, sine = cosine.T, sine.T * jnp.where(jnp.arange(HD) < HD // 2, -1.0, 1.0)[None]
     starts = starts[:, None]
 
-    def own_block(transposed):
-        return lax.dynamic_slice_in_dim(transposed, col_at * QB, QB, 1).astype(F32).T
-
     wide = states.reshape(D, tok_row)
-    residual = own_block(wide)
-    wide = wide.astype(F32)
-    scale_all = lax.rsqrt(jnp.mean(wide * wide, axis=0, keepdims=True) + eps_norm)
-    full_one = (wide * scale_all * gains[0, 0][:, None]).astype(LOW).T
-    scale_one, _ = norm_on(residual, gains[0, 0])
+    residual = lax.dynamic_slice_in_dim(wide, col_at * QB, QB, 1).astype(F32).T
+
+    def own_rows(full):
+        return lax.dynamic_slice_in_dim(full, col_at * QB, QB, 0).astype(F32)
 
     saved = []
     for layer in range(LAYERS):
         w_qkv, bias, w_out = slab_of(*load)
-        sent[1].phase, sent[2].phase = 0, 1
+        sent[1].phase, sent[2].phase = 0, 3
+        scale_one, normed_one = norm_on(residual, gains[layer, 0])
+        fixed = (w_qkv, bias, w_out, cosine, sine, starts, sent[1:])
         if layer == 0:
-            attention, grads_wide, qkv, mixed, loads = forward_heads(
-                names, out_grad, full_one, w_qkv, bias, w_out, cosine, sine, starts, sent[1:], name="heads_0"
+            attention, grads_all, qkv, mixed, full_one, loads = forward_heads(
+                names, out_grad, wide, gains[0, 0][:, None], *fixed, name="heads_0"
             )
-            (w_up,), (w_down,) = loads
-            grads_wide = grads_wide.reshape(D, tok_row)
         else:
-            scale_one, normed_one = norm_on(residual, gains[layer, 0])
-            attention, full_one, qkv, mixed, loads = forward_heads(
-                names, normed_one, None, w_qkv, bias, w_out, cosine, sine, starts, sent[1:], name="heads_1"
-            )
-            (w_up,), (w_down,) = loads
-            full_one = full_one.reshape(tok_row, D)
+            attention, full_one, qkv, mixed, _, loads = forward_heads(names, normed_one, None, None, *fixed, name="heads_1")
+        (w_up,), (w_down,) = loads
         residual_mid = residual + attention
         scale_two, normed_two = norm_on(residual_mid, gains[layer, 1])
         cargo = []
         if layer == 0:
             sent = rows_load(1)
-            sent[0].phase = 1
+            sent[0].phase = 3
             slab_rows, out_rows = GatherRows(slab_next, 0), GatherRows(out_weight, 1, 1)
             cargo = [slab_rows, out_rows, sent[0], Swap(From(slab_rows), From(out_rows), phase=2)]
         feed, full_two, gate, up, loads = forward_feed(
@@ -1642,8 +1774,8 @@
 
     grads = {}
     gain_terms = [None] * LAYERS
-    grad = own_block(grads_wide)
-    inner = w_gate.shape[1]
+    grad = own_rows(grads_all)
+    inner = w_gate.shape[0]
     for layer in reversed(range(LAYERS)):
         (
             residual_in,
@@ -1664,7 +1796,7 @@
         d_normed_two, d_gate_w, d_up_w, d_down, loads = backward_feed(
             names,
             None if last else grad.astype(LOW),
-            grads_wide.T if last else None,
+            grads_all if last else None,
             full_two,
             w_gate,
             w_up,
@@ -1674,8 +1806,8 @@
             cargo,
             name=f"back_feed_{layer}",
         )
-        grads["down", layer] = settle(d_down, 1, loads[-1][0])
-        cargo = [ScatterRows(d_gate_w, 0), ScatterRows(d_up_w, 0, phase=1)]
+        grads["down", layer] = d_down, loads[-1][0]
+        cargo = [ScatterRows(d_gate_w, 1), ScatterRows(d_up_w, 1, phase=3)]
         if not last:
             grads["out", layer + 1] = settle(d_out_w, 1, loads[1][0])
             cargo.append(HeadsToOwners(settle(slab, 0, loads[0][0]).astype(LOW)))
@@ -1685,6 +1817,7 @@
             names,
             grad.astype(LOW),
             full_one,
+            layer == 0,
             w_qkv,
             w_out,
             qkv,
@@ -1695,8 +1828,8 @@
             cargo,
             name=f"back_heads_{layer}",
         )
-        grads["gate", layer] = settle(d_gate_w, 0, loads[0][0])
-        grads["up", layer] = settle(d_up_w, 0, loads[1][0])
+        grads["gate", layer] = d_gate_w, loads[0][0]
+        grads["up", layer] = d_up_w, loads[1][0]
         if not last:
             grads["qkv", layer + 1] = settle_heads(loads[2][0])
         d_residual, d_gain_one = norm_back(d_normed_one, residual_in, scale_one, gains[layer, 0])
@@ -1725,6 +1858,12 @@
     def both_layers(kind):
         return jnp.stack([grads[kind, layer] for layer in range(LAYERS)])
 
+    kinds = ("gate", "up", "down")
+    d_gate, d_up, d_down = settle_rows(
+        row_at,
+        [[grads[kind, layer][0] for layer in range(LAYERS)] for kind in kinds],
+        [[grads[kind, layer][1] for layer in range(LAYERS)] for kind in kinds],
+    )
     heads = [jnp.stack([grads["qkv", layer][i] for layer in range(LAYERS)]) for i in range(2)]
     return (
         out_states,
@@ -1733,9 +1872,9 @@
         heads[0],
         heads[1],
         both_layers("out"),
-        both_layers("gate"),
-        both_layers("up"),
-        both_layers("down"),
+        d_gate.swapaxes(1, 2),
+        d_up.swapaxes(1, 2),
+        d_down,
     )
 
 

time: 791 us -> 721 us (0.912)
  local copies, waits for them, and re-layouts: 51.8 us -> 15.6 us
  other arithmetic: 58.8 us -> 40.3 us
  Pallas kernels: 669 us -> 654 us
    unnamed x115 -> x43, local copies, waits for them, and re-layouts: 33.4 us -> 2.51 us
    pallas_call x11, Pallas kernels: 669 us -> 643 us  [carry_call(): results = list(call(*arrays, *given))]
    another operation x8 -> x2, other arithmetic: 14.1 us -> 1.94 us  [both_layers(): return jnp.stack([grads[kind, layer] for layer in range(LAYERS)])]
    pallas_call x0 -> x1, Pallas kernels: none -> 11.2 us  [settle_rows(): pl.pallas_call(kernel, out_shape=[jax.ShapeDtypeStruct((layers, count, si...]
where the time goes in v4:
time: 721 us; the launch traced here: 712 us
  Pallas kernels  654 us (91%)
  other arithmetic  40.3 us (6%)
  local copies, waits for them, and re-layouts  15.6 us (2%)
    pallas_call x11, Pallas kernels, carry_call(): results = list(call(*arrays, *given))  643 us

profile of v4, /device:TPU:31, one launch (start us, length us, event | category | flops | bytes accessed | tf_op | source)
XLA Modules:
  0.0 711.5 jit_solution(6515352239962259866)
XLA Ops:
  1.3 0.7 dynamic_update_slice.3.refs_2_.refs_4_
  2.1 0.7 reshape.196
  3.4 59.8 %open.1 = (bf16[8,192,1024]{2,1,0:T(8,128)(2,1)}, bf16[208,640]{1,0:T(8,128)(2,1)}, bf16[208,640]{1,0:T(8,128)(2,1)}, bf16[8,16,192]{2,1,0:T(8,128)(2,1)}, bf16[...) custom-call(bf16[192,1024]{1,0:T(8,128)(2,1)} %refs_0_.2, ...), custom_call_target="tpu_custom_call" | custom-call | tf_op jit(solution)/shard_map/open/pallas_call | solution.py:640
  63.2 1.3 broadcast_select_fusion.7
  64.5 1.1 pad_maximum_fusion.2.refs_5_.refs_3_
  66.7 1.5 pad_maximum_fusion.1
  68.8 0.8 convert_bitcast_fusion.1
  69.7 1.2 copy.50.refs_2_
  71.2 1.9 multiply_sine_fusion
  73.1 1.0 fusion.9.refs_7_.refs_5_
  74.1 1.0 maximum_bitcast_fusion.refs_6_.refs_4_
  75.1 1.0 copy.51.refs_8_.refs_6_
  76.1 63.4 %heads_0.1 = (f32[128,1536]{1,0:T(8,128)}, bf16[1024,1536]{1,0:T(8,128)(2,1)}, bf16[1024,640]{1,0:T(8,128)(2,1)}, bf16[512,384]{1,0:T(8,128)(2,1)}, bf16[1536,10...) custom-call(bf16[192,1024]{1,0:T(8,128)(2,1)} %refs_0_.3, bf16[1536,1024]{1,0:T(8,128)(2,1)} %bitcast.118, ...), custom_call_target="tpu_custom_call" | custom-call | tf_op jit(solution)/shard_map/heads_0/pallas_call | solution.py:640
  139.6 1.1 constant_dynamic-slice_fusion.2
  141.1 0.9 multiply_convert_fusion.2.refs_0_
  142.0 67.6 %feed_0.1 = (f32[128,1536]{1,0:T(8,128)}, bf16[8,128,1536]{2,1,0:T(8,128)(2,1)}, bf16[1024,1120]{1,0:T(8,128)(2,1)}, bf16[1024,1120]{1,0:T(8,128)(2,1)}, bf16[83...) custom-call(bf16[128,1536]{1,0:T(8,128)(2,1)} %multiply_convert_fusi, ...), custom_call_target="tpu_custom_call" | custom-call | tf_op jit(solution)/shard_map/feed_0/pallas_call | solution.py:640
  209.6 1.3 broadcast_select_fusion.5
  210.9 1.1 pad_maximum_fusion.3.refs_3_
  213.1 1.5 pad_maximum_fusion
  215.4 0.9 multiply_convert_fusion.1.refs_0_
  216.3 63.1 %heads_1.1 = (f32[128,1536]{1,0:T(8,128)}, bf16[8,128,1536]{2,1,0:T(8,128)(2,1)}, bf16[1024,640]{1,0:T(8,128)(2,1)}, bf16[512,384]{1,0:T(8,128)(2,1)}, bf16[1120...) custom-call(bf16[128,1536]{1,0:T(8,128)(2,1)} %multiply_convert_fusion.1.refs_0_, bf16[1536,640]{1,0:T(8,128)(2,1)} %bitcast.106, ...), custom_call_target="tpu_custom_call" | custom-call | tf_op jit(solution)/shard_map/heads_1/pallas_call | solution.py:640
  279.4 1.3 multiply_reduce_fusion.6
  281.6 0.9 multiply_convert_fusion.refs_0_
  282.5 59.7 %feed_1.1 = (f32[128,1536]{1,0:T(8,128)}, bf16[8,128,1536]{2,1,0:T(8,128)(2,1)}, bf16[1024,1120]{1,0:T(8,128)(2,1)}, bf16[1024,1120]{1,0:T(8,128)(2,1)}) custom-call(bf16[128,1536]{1,0:T(8,128)(2,1)} %multiply_convert_fusion.refs_0_, bf16[1120,1536]{1,0:T(8,128)(2,1)} %get-tuple-element.90.refs_1_.refs_2_, ...), custom_call_target="tpu_custom_call" | custom-call | tf_op jit(solution)/shard_map/feed_1/pallas_call | solution.py:640
  342.2 74.2 %back_feed_1.1 = (f32[128,1536]{1,0:T(8,128)}, bf16[1120,1536]{1,0:T(8,128)(2,1)}, bf16[1120,1536]{1,0:T(8,128)(2,1)}, bf16[1120,1536]{1,0:T(8,128)(2,1)}, bf16[2,1120,384]{2,1,0:T(8,128)(2,1)}) custom-call(bf16[8,128,1536]{2,1,0:T(8,128)(2,1)} %bitcast.120, bf16[1024,1536]{1,0:T(8,128)(2,1)} %bitcast.124, ...), custom_call_target="tpu_custom_call" | custom-call | tf_op jit(solution)/shard_map/back_feed_1/pallas_call | solution.py:640
  416.4 1.7 multiply_reduce_fusion
  418.3 2.8 fusion.17
  421.1 62.6 %back_heads_1.1 = (f32[128,1536]{1,0:T(8,128)}, bf16[4,208,640]{2,1,0:T(8,128)(2,1)}, bf16[192,1536]{1,0:T(8,128)(2,1)}, bf16[2,1120,384]{2,1,0:T(8,128)(2,1)}, bf16[2,1120,384]{2,1,0:T(8,128)(2,1)}) custom-call(bf16[128,1536]{1,0:T(8,128)(2,1)} %get-tuple-element.153.refs_0_, bf16[1024,1536]{1,0:T(8,128)(2,1)} %bitcast.121, bf16[1536,640]{1,0:T(8,128)(2,1)} %bitcast.107, ...), custom_call_target="tpu_custom_call" | custom-call | tf_op jit(solution)/shard_map/back_heads_1/pallas_call | solution.py:640
  483.7 1.5 multiply_reduce_fusion.1
  485.3 1.3 fusion.16
  486.6 79.3 %back_feed_0.1 = (f32[128,1536]{1,0:T(8,128)}, bf16[1120,1536]{1,0:T(8,128)(2,1)}, bf16[1120,1536]{1,0:T(8,128)(2,1)}, bf16[1120,1536]{1,0:T(8,128)(2,1)}, bf16[...) custom-call(bf16[128,1536]{1,0:T(8,128)(2,1)} %get-tuple-element.151.refs_0_, ...), custom_call_target="tpu_custom_call" | custom-call | tf_op jit(solution)/shard_map/back_feed_0/pallas_call | solution.py:640
  566.0 1.3 convert_reduce_fusion.1
  567.3 1.7 add_convert_fusion.2.refs_11_
  569.2 2.2 fusion.15
  571.4 71.2 %back_heads_0.1 = (f32[128,1536]{1,0:T(8,128)}, bf16[4,208,640]{2,1,0:T(8,128)(2,1)}, bf16[192,1536]{1,0:T(8,128)(2,1)}, bf16[2,1120,384]{2,1,0:T(8,128)(2,1)}, ...) custom-call(bf16[128,1536]{1,0:T(8,128)(2,1)} %get-tuple-element.149.refs_0_, ...), custom_call_target="tpu_custom_call" | custom-call | tf_op jit(solution)/shard_map/back_heads_0/pallas_call | solution.py:640
  642.6 11.2 %settle.1 = (f32[2,1120,384]{2,1,0:T(8,128)}, f32[2,1120,384]{2,1,0:T(8,128)}, f32[2,1120,384]{2,1,0:T(8,128)}) custom-call(s32[1]{0:T(128)} %bitcast.44.row_ref, bf16[1120,1536]{1,0:T(8,128)(2,1)} %get-tuple-element.114.refs_9_.refs_0_, bf16[2,1120,384]{2,1,0:T(8,128)(2,1)} %get-tuple-element.126.refs_1_, ...), custom_call_target="tpu_custom_call" | custom-call | tf_op jit(solution)/shard_map/settle/pallas_call | solution.py:1180
  655.3 1.0 pad_maximum_fusion.4
  656.4 1.2 copy.57
  657.6 31.9 %close.1 = (bf16[8,192,256]{2,1,0:T(8,128)(2,1)}, f32[4,8,8,192]{3,2,1,0:T(8,128)}, bf16[2,208,640]{2,1,0:T(8,128)(2,1)}, bf16[2,192,384]{2,1,0:T(8,128)(2,1)}) custom-call(bf16[8,192,256]{2,1,0:T(8,128)(2,1)} %bitcast.122, f32[8,8,192]{2,1,0:T(8,128)} %pad_bitcast_fusion.refs_1_, bf16[832,640]{1,0:T(8,128)(2,1)} %bitcast.127, ...), custom_call_target="tpu_custom_call" | custom-call | tf_op jit(solution)/shard_map/close/pallas_call | solution.py:640
  689.4 1.0 convert_reduce_fusion.3
  690.5 1.1 add_bitcast_fusion.2
  691.6 0.9 pad_maximum_fusion.6
  692.6 1.8 add_convert_fusion.1.refs_0_
  694.3 10.0 %close_heads.1 = bf16[2,2,2,208,128]{4,3,2,1,0:T(8,128)(2,1)} custom-call(bf16[208,640]{1,0:T(8,128)(2,1)} %add_convert_fusion.1.refs_0_), custom_call_target="tpu_custom_call" | custom-call | tf_op jit(solution)/shard_map/close_heads/pallas_call | solution.py:640
  704.3 1.1 add_bitcast_fusion.1
  707.5 0.9 pad_maximum_fusion.5
  708.6 1.0 copy.68
  709.6 0.9 copy.69
  (97 shorter events, 11.5 us)
Async XLA Ops:
  2.1 1.3 copy-start.19
  64.5 1.7 copy-start.10
  64.5 2.0 copy-start.11
  66.7 4.2 copy-start.20
  139.5 1.3 copy-start.13
  210.9 1.7 copy-start.8
  210.9 2.0 copy-start.9
  213.1 2.1 copy-start.12
  280.7 0.9 copy-start
  416.4 1.7 copy-start.1
  416.4 1.8 copy-start.7
  483.7 1.5 copy-start.5
  483.7 1.6 copy-start.6
  566.0 3.0 copy-start.4
  566.0 3.2 copy-start.3
  642.6 11.2 %copy-start.2 = (f32[128,1536]{1,0:T(8,128)S(1)}, f32[128,1536]{1,0:T(8,128)}, u32[]{:S(2)}) copy-start(f32[128,1536]{1,0:T(8,128)} %get-tuple-element.117) | copy-start | bytes 2359300
  657.6 32.9 %copy-start.17 = (bf16[2,192,384]{2,1,0:T(8,128)(2,1)S(1)}, bf16[2,192,384]{2,1,0:T(8,128)(2,1)}, u32[]{:S(2)}) copy-start(bf16[2,192,384]{2,1,0:T(8,128)(2,1)} %get-tuple-element.125) | copy-start | bytes 884740
  690.5 2.0 copy-start.15
  692.5 12.9 %copy-start.16 = (bf16[2,2,2,208,128]{4,3,2,1,0:T(8,128)(2,1)S(1)}, bf16[2,2,2,208,128]{4,3,2,1,0:T(8,128)(2,1)}, u32[]{:S(2)}) copy-start(bf16[2,2,2,208,128]{4,3,2,1,0:T(8,128)(2,1)} %get-tuple-element.123) | copy-start | bytes 1277956
  706.9 1.6 copy-start.14
  708.5 2.0 copy-start.18

commit v5 on v4

--- a/solution.py
+++ b/solution.py
@@ -146,6 +146,8 @@
         first = pl.multiple_of(row * self.size, 16)
         return full.at[pl.ds(first, self.half), :], full.at[pl.ds(first + self.half, self.rest), :]
 
+    split = False
+
     def source(self, ins):
         return ins[0] if self.layer is None else ins[0].at[self.layer]
 
@@ -179,7 +181,7 @@
     def start(self, place, ins, outs, scratch, later):
         (dst,) = outs
         out, onward = self.copies(place, ins, outs, scratch)
-        for copy in out:
+        for copy in out[:2] if self.split else out:
             copy.start()
         load, store = self.keep(place, ins, outs, scratch)
         load.start()
@@ -190,6 +192,10 @@
             later.add(self.arrived(place, scratch, view, sem, row).wait_recv)
         for copy in (*out, *onward):
             later.add(copy.wait_send)
+
+    def send_rest(self, place, ins, outs, scratch):
+        for copy in self.copies(place, ins, outs, scratch)[0][2:]:
+            copy.start()
 
     def middle(self, place, ins, outs, scratch):
         (dst,) = outs
@@ -437,6 +443,7 @@
 
 
 SUB = 4
+LAG = 2
 
 
 class Reduce:
@@ -509,22 +516,35 @@
             add_into(self.held.at[j].at[rows, :], views)
             copy.start()
 
-        for i in range(2 * SUB):
-            sub = i % SUB
-
-            @pl.when(self.mid)
-            def _(i=i, sub=sub):
-                if self.both and sub == 0:
-                    self.pair(first if i == 0 else second).wait_recv()
-                if i < SUB:
-                    step(first, sub, way)
-                    return
-                step(second, sub, way)
-                if self.both and sub == 0:
-                    self.pair(back).wait_recv()
-                step(back, sub, 1 - way)
-
-            between(i)
+        def pair_here(j):
+            if self.both:
+                self.pair(j).wait_recv()
+
+        def firsts(sub):
+            if sub == 0:
+                pair_here(first)
+            step(first, sub, way)
+
+        def seconds(sub):
+            if sub == 0:
+                pair_here(second)
+            step(second, sub, way)
+
+        def backs(sub):
+            if sub == 0:
+                pair_here(back)
+            step(back, sub, 1 - way)
+
+        for sub in range(SUB):
+            pl.when(self.mid)(partial(firsts, sub))
+            between(sub)
+        for sub in range(SUB):
+            pl.when(self.mid)(partial(seconds, sub))
+            if sub >= LAG:
+                pl.when(self.mid)(partial(backs, sub - LAG))
+            between(SUB + sub)
+        for sub in range(SUB - LAG, SUB):
+            pl.when(self.mid)(partial(backs, sub))
         if self.both:
             self.pair(z).wait_recv()
 
@@ -613,10 +633,10 @@
             taken[item] = [inner.pop(0) if isinstance(a, Inner) else a for a in taken[item]]
             item.start(place, taken[item], made[item], held[item], owed[phase])
 
-    def middle(phase=0):
+    def middle(phase=0, rest=False):
         for item in cargo:
             if item.phase == phase:
-                item.middle(place, taken[item], made[item], held[item])
+                (item.send_rest if rest else item.middle)(place, taken[item], made[item], held[item])
 
     body(place, ins, outs, scratch, later, middle, start)
     later.run()
@@ -649,93 +669,110 @@
 
 class Gather:
     scratch = (
-        pltpu.SemaphoreType.DMA((4,)),
-        pltpu.SemaphoreType.DMA((4,)),
-        pltpu.SemaphoreType.DMA((8,)),
-        pltpu.SemaphoreType.DMA((8,)),
+        pltpu.SemaphoreType.DMA((4, 2)),
+        pltpu.SemaphoreType.DMA((4, 2)),
+        pltpu.SemaphoreType.DMA((8, 2)),
+        pltpu.SemaphoreType.DMA((8, 2)),
         pltpu.SemaphoreType.DMA((1,)),
     )
 
     def __init__(self, place, block, full, sems, both=True):
         self.place, self.block, self.full, self.both = place, block, full, both
         self.send_r, self.send_l, self.send_p, self.recv, self.keep = sems
+        self.size = block.shape[0] // 2
 
     def spot(self, zz, c):
         return self.full.at[2 * zz + c] if self.both else self.full.at[zz]
 
-    def copies(self, src, zz, t, way):
+    def copies(self, src, zz, t, way, half):
         z, c = self.place.z, self.place.c
-        spot, sem = self.spot(zz, c), self.recv.at[2 * zz + c]
-        right = remote(src, spot, self.send_r.at[t], sem, self.place.at(jnp.minimum(z + 1, 3), c))
-        left = remote(src, spot, self.send_l.at[t], sem, self.place.at(jnp.maximum(z - 1, 0), c))
-        partner = remote(src, spot, self.send_p.at[2 * t + way], sem, self.place.at(z, 1 - c))
+        rows = pl.ds(half * self.size, self.size)
+        src, spot, sem = src.at[rows, :], self.spot(zz, c).at[rows, :], self.recv.at[2 * zz + c, half]
+        right = remote(src, spot, self.send_r.at[t, half], sem, self.place.at(jnp.minimum(z + 1, 3), c))
+        left = remote(src, spot, self.send_l.at[t, half], sem, self.place.at(jnp.maximum(z - 1, 0), c))
+        partner = remote(src, spot, self.send_p.at[2 * t + way, half], sem, self.place.at(z, 1 - c))
         return right, left, partner
 
     def start(self, later):
         z, c = self.place.z, self.place.c
-        right, left, partner = self.copies(self.block, z, 0, 0)
-        pl.when(z < 3)(right.start)
-        pl.when(z > 0)(left.start)
-        later.add(right.wait_send, z < 3)
-        later.add(left.wait_send, z > 0)
-        if self.both:
-            partner.start()
-            later.add(partner.wait_send)
+        for half in range(2):
+            right, left, partner = self.copies(self.block, z, 0, 0, half)
+            pl.when(z < 3)(right.start)
+            pl.when(z > 0)(left.start)
+            later.add(right.wait_send, z < 3)
+            later.add(left.wait_send, z > 0)
+            if self.both:
+                partner.start()
+                later.add(partner.wait_send)
         keep = pltpu.make_async_copy(self.block, self.spot(z, c), self.keep.at[0])
         keep.start()
         keep.wait()
         for t in range(1, 4):
             for way in (0, 1):
-                zz, valid, onward, may, partner = self.step(t, way)
-                later.add(onward.wait_send, valid & may)
-                if self.both:
-                    later.add(partner.wait_send, valid)
-
-    def step(self, t, way):
+                for half in range(2):
+                    valid, onward, may, partner = self.step(t, way, half)
+                    later.add(onward.wait_send, valid & may)
+                    if self.both:
+                        later.add(partner.wait_send, valid)
+
+    def step(self, t, way, half):
         z = self.place.z
         there = z + (2 * way - 1) * t
         zz = jnp.clip(there, 0, 3)
-        right, left, partner = self.copies(self.spot(zz, self.place.c), zz, t, way)
+        right, left, partner = self.copies(self.spot(zz, self.place.c), zz, t, way, half)
         onward, may = (left, z > 0) if way else (right, z < 3)
-        return zz, (there >= 0) & (there <= 3), onward, may, partner
+        return (there >= 0) & (there <= 3), onward, may, partner
 
     def pass_on(self, t):
-        for way in (0, 1):
-            _, valid, onward, may, partner = self.step(t, way)
-
-            @pl.when(valid)
-            def _(onward=onward, may=may, partner=partner):
-                onward.wait_recv()
-                pl.when(may)(onward.start)
-                if self.both:
-                    partner.start()
+        for half in range(2):
+            for way in (0, 1):
+                valid, onward, may, partner = self.step(t, way, half)
+
+                @pl.when(valid)
+                def _(onward=onward, may=may, partner=partner):
+                    onward.wait_recv()
+                    pl.when(may)(onward.start)
+                    if self.both:
+                        partner.start()
+
+    def from_partner(self, zz):
+        c = self.place.c
+        for half in range(2):
+            spot = self.spot(zz, 1 - c).at[pl.ds(half * self.size, self.size), :]
+            recv = self.recv.at[2 * zz + 1 - c, half]
+            yield remote(spot, spot, self.send_p.at[0, half], recv, self.place.at(self.place.z, 1 - c)).wait_recv
+
+    def order(self, p):
+        z = self.place.z
+        second = jnp.where(z == 0, 1, z - 1)
+        third = jnp.where(z == 0, 2, jnp.where(z == 3, 1, z + 1))
+        fourth = jnp.where(z <= 1, 3, 0)
+        return jnp.where(p == 0, z, jnp.where(p == 1, second, jnp.where(p == 2, third, fourth)))
 
     def chunk(self, p):
-        z, c = self.place.z, self.place.c
+        z = self.place.z
         edge = (z == 0) | (z == 3)
         t = jnp.where(edge, p, (p + 1) // 2)
         pl.when((p >= 1) & (edge | (p != 2)))(lambda: self.pass_on(t))
-        second = jnp.where(z == 0, 1, z - 1)
-        third = jnp.where(z == 0, 2, jnp.where(z == 3, 1, z + 1))
-        fourth = jnp.where(z <= 1, 3, 0)
-        j = jnp.where(p == 0, z, jnp.where(p == 1, second, jnp.where(p == 2, third, fourth)))
+        j = self.order(p)
         if self.both:
-            spot = self.spot(j, 1 - c)
-            remote(spot, spot, self.send_p.at[0], self.recv.at[2 * j + 1 - c], self.place.at(z, 1 - c)).wait_recv()
+            for wait in self.from_partner(j):
+                wait()
         return j
 
 
-def forward_feed(names, block, w_gate, w_up, w_down, cargo, name):
+def forward_feed(names, block, residual, gain, w_gate, w_up, w_down, cargo, name):
     tokens, width = block.shape
     inner = w_gate.shape[0]
+    normed = gain is not None
 
     def body(place, ins, outs, scratch, later, middle, start):
-        block_ref, gate_hbm, up_hbm, down_hbm = ins
-        total, full_out, gate_out, up_out = outs
+        block_ref, residual_ref, gain_ref, gate_hbm, up_hbm, down_hbm = ins
+        states_out, normed_out, full_out, gate_out, up_out = outs
         n = len(Gather.scratch)
         gather_sems, scratch = scratch[:n], scratch[n:]
-        full, part, gate_w, up_w, down_w, gates, ups, load_sem, keep_sem = scratch[:9]
-        reduce = Reduce(place, part, total, scratch[9:])
+        full, part, gate_w, up_w, down_w, gates, ups, load_sem, keep_sem, total = scratch[:10]
+        reduce = Reduce(place, part, total, scratch[10:])
         gather = Gather(place, block_ref, full, gather_sems)
         loads = [
             pltpu.make_async_copy(src, dst, load_sem.at[i])
@@ -778,23 +815,25 @@
         start(1)
         start(2)
         reduce.finish(later, lambda i: middle(3) if i == 0 else None)
+        after_forward(total, residual_ref, gain_ref if normed else None, states_out, normed_out)
         for j in range(4):
             for copy in keep(j):
                 copy.wait()
 
-    (total, full, gate, up), loads = carry_call(
+    (states, low, full, gate, up), loads = carry_call(
         names,
         body,
         "line",
-        [block, w_gate, w_up, w_down],
-        [ONCHIP, ANY, ANY, ANY],
+        [block, residual, gain if normed else jnp.ones((1, width), F32), w_gate, w_up, w_down],
+        [ONCHIP, ONCHIP, ONCHIP, ANY, ANY, ANY],
         [
             jax.ShapeDtypeStruct((tokens, width), F32),
+            jax.ShapeDtypeStruct((tokens, width), LOW),
             jax.ShapeDtypeStruct((8, tokens, width), LOW),
             jax.ShapeDtypeStruct((8 * tokens, inner), LOW),
             jax.ShapeDtypeStruct((8 * tokens, inner), LOW),
         ],
-        [ONCHIP, ANY, ANY, ANY],
+        [ONCHIP, ONCHIP, ANY, ANY, ANY],
         [
             *Gather.scratch,
             pltpu.VMEM((8, tokens, width), LOW),
@@ -806,12 +845,13 @@
             pltpu.VMEM((8 * tokens, inner), LOW),
             pltpu.SemaphoreType.DMA((3,)),
             pltpu.SemaphoreType.DMA((3, 4)),
+            pltpu.VMEM((tokens, width), F32),
             *Reduce.scratch(tokens, width),
         ],
         cargo,
         name=name,
     )
-    return total, full.reshape(8 * tokens, width), gate, up, loads
+    return states, low, full.reshape(8 * tokens, width), gate, up, loads
 
 
 def rows_of(first, count):
@@ -832,6 +872,7 @@
         start(0)
         start(3)
         start(1)
+        middle(3, rest=True)
         gather.pass_on(1)
         middle(1)
         gather.pass_on(2)
@@ -839,9 +880,8 @@
         start(2)
         gather.pass_on(3)
         for zz in range(4):
-            spot = gather.spot(zz, 1 - place.c)
-            recv = gather.recv.at[2 * zz + 1 - place.c]
-            later.add(remote(spot, spot, gather.send_p.at[0], recv, place.at(place.z, 1 - place.c)).wait_recv)
+            for wait in gather.from_partner(zz):
+                later.add(wait)
 
     (full,), loads = carry_call(
         names,
@@ -864,6 +904,79 @@
         middle(0)
 
     return carry_call(names, body, "col", [], [], [], [], [], cargo, name=name)[1]
+
+
+def after_forward(sums, residual, gain, states, normed):
+    def step(i, carry):
+        rows = rows_of(i * 16, 16)
+        now = residual[rows, :] + sums[rows, :]
+        states[rows, :] = now
+        if gain is not None:
+            now = now * lax.rsqrt(jnp.mean(now * now, axis=1, keepdims=True) + eps_norm) * gain[...]
+        normed[rows, :] = now.astype(LOW)
+        return carry
+
+    lax.fori_loop(0, sums.shape[0] // 16, step, 0)
+
+
+def after_backward(sums, grad, residual, gain, grad_out, low_out, gain_out):
+    def step(i, total):
+        rows = rows_of(i * 16, 16)
+        d_normed, now = sums[rows, :], residual[rows, :]
+        scale = lax.rsqrt(jnp.mean(now * now, axis=1, keepdims=True) + eps_norm)
+        weighted = d_normed * gain[...]
+        inner = jnp.sum(weighted * now, axis=1, keepdims=True)
+        out = grad[rows, :] + (weighted * scale - now * (scale * scale * scale) * inner / D)
+        grad_out[rows, :] = out
+        low_out[rows, :] = out.astype(LOW)
+        return total + jnp.sum(d_normed * now * scale, axis=0, keepdims=True)
+
+    gain_out[...] = lax.fori_loop(0, sums.shape[0] // 16, step, jnp.zeros((1, D), F32))
+
+
+class Slab:
+    scratch = (
+        pltpu.VMEM((D, 5 * HD), LOW),
+        pltpu.VMEM((3 * HD, D), LOW),
+        pltpu.VMEM((4, 16, 5 * HD), LOW),
+        pltpu.SemaphoreType.DMA((2, 5)),
+        pltpu.SemaphoreType.DMA((4,)),
+    )
+
+    def __init__(self, place, refs, scratch):
+        self.place = place
+        self.mine, self.theirs, self.out_mine, self.out_theirs = refs
+        self.qkv, self.out, self.tails, self.sems, self.tail_sems = scratch
+
+    def copies(self, half, mine):
+        source, out = (self.mine, self.out_mine) if mine else (self.theirs, self.out_theirs)
+        sem = self.sems.at[half]
+        rows = D // 8
+        for row in range(4):
+            spot = self.qkv.at[(2 * row + half) * rows : (2 * row + half + 1) * rows, :]
+            yield pltpu.make_async_copy(source.at[row * HALF : row * HALF + rows, :], spot, sem.at[row])
+        yield pltpu.make_async_copy(out, self.out.at[half * rows : (half + 1) * rows, :], sem.at[4])
+        if half == 0:
+            for row in range(4):
+                tail = source.at[row * HALF + rows : (row + 1) * HALF, :]
+                yield pltpu.make_async_copy(tail, self.tails.at[row], self.tail_sems.at[row])
+
+    def start(self):
+        for half in range(2):
+            for mine in (True, False):
+
+                @pl.when((self.place.c == half) == mine)
+                def _(half=half, mine=mine):
+                    for copy in self.copies(half, mine):
+                        copy.start()
+
+    def wait(self):
+        for half in range(2):
+            for copy in self.copies(half, True):
+                copy.wait()
+
+    def bias(self):
+        return jnp.sum(self.tails[:, 0, :].astype(F32), axis=0, keepdims=True)
 
 
 def heads_of(ref, rows):
@@ -890,7 +1003,7 @@
     return pltpu.roll(values, HD // 2, 1)
 
 
-def forward_heads(names, block, wide, gain, w_qkv, bias, w_out, cosine, sine, starts, cargo, name):
+def forward_heads(names, block, wide, gain, residual, gain_two, slab, cosine, sine, starts, cargo, name):
     tokens, width = QB, D
     count = 8 * QB
     apart = wide is not None
@@ -900,22 +1013,23 @@
         block_ref = ins.pop(0)
         if apart:
             wide_hbm, gain_ref = ins.pop(0), ins.pop(0)
-        qkv_hbm, bias_ref, out_hbm, cos_ref, sin_ref, starts_ref = ins
-        total, full_out, qkv_out, mixed_out = outs[:4]
+        residual_ref, two_ref, cos_ref, sin_ref, starts_ref, *slab_refs = ins
+        states_out, normed_out, full_out, qkv_out, mixed_out = outs[:5]
         scratch = list(scratch)
         gather_sems = [scratch.pop(0) for _ in Gather.scratch]
-        full, acts, flat, part, qkv_w, out_w, qkv, mixed, load_sem, keep_sem = scratch[:10]
-        reduce = Reduce(place, part, total, scratch[10:], both=False, far=True)
-        pairs = [(qkv_hbm, qkv_w), (out_hbm, out_w)]
-        if apart:
-            pairs.append((wide_hbm, acts))
-        loads = copy_in(pairs, load_sem)
+        weights = Slab(place, slab_refs, [scratch.pop(0) for _ in Slab.scratch])
+        full, acts, flat, part, qkv, mixed, load_sem, keep_sem, total = scratch[:9]
+        reduce = Reduce(place, part, total, scratch[9:], both=False, far=True)
+        weights.start()
+        loads = copy_in([(wide_hbm, acts)] if apart else [], load_sem)
         gather = Gather(place, block_ref, full, gather_sems)
         gather.start(later)
         start(0)
         start(3)
         for load in loads:
             load.wait()
+        weights.wait()
+        bias = weights.bias()
 
         def keep(j):
             if apart:
@@ -924,19 +1038,22 @@
             return pltpu.make_async_copy(full.at[pl.ds(2 * j, 2)], full_out.at[pl.ds(2 * j, 2)], keep_sem.at[j])
 
         def step(p, carry):
-            j = gather.chunk(p)
-            pl.when(p == 2)(middle)
+            if apart:
+                j = gather.order(p)
+            else:
+                j = gather.chunk(p)
+                pl.when(p == 2)(middle)
             rows = rows_of(j * 2 * QB, 2 * QB)
             if apart:
                 chunk = acts[:, rows].astype(F32)
                 scale = lax.rsqrt(jnp.mean(chunk * chunk, axis=0, keepdims=True) + eps_norm)
                 chunk = (chunk * scale * gain_ref[...]).astype(LOW)
                 acts[:, rows] = chunk
-                raw = t_dot(chunk, qkv_w[...]) + bias_ref[...]
+                raw = t_dot(chunk, weights.qkv[...]) + bias
             else:
                 keep(j).start()
-                raw = jnp.dot(full[pl.ds(2 * j, 2)].reshape(2 * tokens, width), qkv_w[...], preferred_element_type=F32)
-                raw = raw + bias_ref[...]
+                raw = jnp.dot(full[pl.ds(2 * j, 2)].reshape(2 * tokens, width), weights.qkv[...], preferred_element_type=F32)
+                raw = raw + bias
             cos, sin = cos_ref[rows, :], sin_ref[rows, :]
             for t in range(5):
                 head = raw[:, t * HD : (t + 1) * HD]
@@ -955,35 +1072,44 @@
             heads = jnp.dot(low, values, preferred_element_type=F32).astype(LOW)
             both = jnp.concatenate([heads[h * QB : (h + 1) * QB] for h in range(3)], axis=1)
             mixed[rows_of(j * QB, QB), :] = both
-            part[j] = jnp.dot(both, out_w[...], preferred_element_type=F32).astype(LOW)
+            part[j] = jnp.dot(both, weights.out[...], preferred_element_type=F32).astype(LOW)
             reduce.made(j)
             return carry
 
         lax.fori_loop(0, 4, attend, 0)
         saves = copy_in([(qkv, qkv_out), (mixed, mixed_out)], load_sem)
         if apart:
-            saves.append(pltpu.make_async_copy(acts, outs[4], load_sem.at[2]))
+            saves.append(pltpu.make_async_copy(acts, outs[5], load_sem.at[2]))
             saves[-1].start()
 
         def between(i):
-            if i == 0:
+            if not apart:
+                if i == 0:
+                    middle(3)
+                return
+            if i in (0, SUB, 2 * SUB - 1):
+                gather.pass_on(1 + (i + 1) // SUB)
+            if i == SUB:
+                middle(0)
+            if i == 2 * SUB - 1:
                 middle(3)
-            if not apart or i % 2:
-                return
-            j = i // 2
+
+        reduce.finish(later, between)
+        after_forward(total, residual_ref, two_ref, states_out, normed_out)
+        if apart:
+            for zz in range(4):
+                for wait in gather.from_partner(zz):
+                    wait()
 
             def turn(t, carry):
                 rows = rows_of(t * 2 * QB, 2 * QB)
-                piece = full[2 * j : 2 * j + 2, :, rows].reshape(D // 4, 2 * QB)
-                flat[rows, j * (D // 4) : (j + 1) * (D // 4)] = piece.T
+                for j in range(4):
+                    piece = full[2 * j : 2 * j + 2, :, rows].reshape(D // 4, 2 * QB)
+                    flat[rows, j * (D // 4) : (j + 1) * (D // 4)] = piece.T
+                keep(t).start()
                 return carry
 
             lax.fori_loop(0, 4, turn, 0)
-
-        reduce.finish(later, between)
-        if apart:
-            for j in range(4):
-                keep(j).start()
         for copy in saves:
             copy.wait()
         for j in range(4):
@@ -994,52 +1120,55 @@
         names,
         body,
         "line",
-        [block, *([wide, gain] if apart else []), w_qkv, bias, w_out, cosine, sine, starts],
-        [ONCHIP, *([ANY, ONCHIP] if apart else []), ANY, ONCHIP, ANY, ONCHIP, ONCHIP, ONCHIP],
+        [block, *([wide, gain] if apart else []), residual, gain_two, cosine, sine, starts, *slab],
+        [ONCHIP, *([ANY, ONCHIP] if apart else []), *[ONCHIP] * 5, *[ANY] * 4],
         [
             jax.ShapeDtypeStruct((tokens, width), F32),
+            jax.ShapeDtypeStruct((tokens, width), LOW),
             jax.ShapeDtypeStruct(gathered, LOW),
             jax.ShapeDtypeStruct((count, 5 * HD), LOW),
             jax.ShapeDtypeStruct((count // 2, 3 * HD), LOW),
             *([jax.ShapeDtypeStruct((width, count), LOW)] if apart else []),
         ],
-        [ONCHIP, ANY, ANY, ANY, *([ANY] if apart else [])],
+        [ONCHIP, ONCHIP, ANY, ANY, ANY, *([ANY] if apart else [])],
         [
             *Gather.scratch,
+            *Slab.scratch,
             pltpu.VMEM((8, *block.shape), LOW),
             pltpu.VMEM((width, count) if apart else (16, 128), LOW),
             pltpu.VMEM((count, width) if apart else (16, 128), LOW),
             pltpu.VMEM((4, tokens, width), LOW),
-            pltpu.VMEM(w_qkv.shape, LOW),
-            pltpu.VMEM(w_out.shape, LOW),
             pltpu.VMEM((count, 5 * HD), LOW),
             pltpu.VMEM((count // 2, 3 * HD), LOW),
             pltpu.SemaphoreType.DMA((3,)),
             pltpu.SemaphoreType.DMA((4,)),
+            pltpu.VMEM((tokens, width), F32),
             *Reduce.scratch(tokens, width),
         ],
         cargo,
         name=name,
     )
-    total, full, qkv, mixed = results[:4]
-    return total, full.reshape(count, width), qkv, mixed, results[4] if apart else None, loads
-
-
-def backward_heads(names, block, acts, turned, w_qkv, w_out, qkv, mixed, cosine, sine, starts, cargo, name):
+    states, low, full, qkv, mixed = results[:5]
+    return states, low, full.reshape(count, width), qkv, mixed, results[5] if apart else None, loads
+
+
+def backward_heads(names, block, grad, residual, gain, acts, turned, slab, qkv, mixed, cosine, sine, starts, cargo, name):
     tokens, width = QB, D
     count = 8 * QB
     reach = QB + SEQ_MAX
 
     def body(place, ins, outs, scratch, later, middle, start):
-        block_ref, acts_hbm, qkv_hbm, out_hbm, saved_hbm, mixed_hbm, cos_ref, sin_ref, starts_ref = ins
-        total, slab_out, out_out = outs
+        block_ref, grad_ref, residual_ref, gain_ref, acts_hbm, saved_hbm, mixed_hbm = ins[:7]
+        cos_ref, sin_ref, starts_ref, *slab_refs = ins[7:]
+        grad_out, low_out, gain_out, slab_out, out_out = outs
         scratch = list(scratch)
         gather_sems = [scratch.pop(0) for _ in Gather.scratch]
-        full, part, qkv_w, out_w, qkv, mixed, acts_own, d_raw, d_keys, d_values = scratch[:10]
-        slab, d_out, slab_in, d_out_in, load_sem, swap_send, swap_recv = scratch[10:17]
-        reduce = Reduce(place, part, total, scratch[17:], far=True)
-        pairs = [(qkv_hbm, qkv_w), (out_hbm, out_w), (saved_hbm, qkv), (mixed_hbm, mixed), (acts_hbm, acts_own)]
-        loads = copy_in(pairs, load_sem)
+        weights = Slab(place, slab_refs, [scratch.pop(0) for _ in Slab.scratch])
+        full, part, qkv, mixed, acts_own, d_raw, d_keys, d_values = scratch[:8]
+        slab, d_out, slab_in, d_out_in, load_sem, swap_send, swap_recv, total = scratch[8:16]
+        reduce = Reduce(place, part, total, scratch[16:], far=True)
+        weights.start()
+        loads = copy_in([(saved_hbm, qkv), (mixed_hbm, mixed), (acts_hbm, acts_own)], load_sem)
         gather = Gather(place, block_ref, full, gather_sems, both=False)
         gather.start(later)
         start(0)
@@ -1048,12 +1177,13 @@
         d_values[...] = jnp.zeros_like(d_values)
         for load in loads:
             load.wait()
+        weights.wait()
 
         def step(p, carry):
             j = gather.chunk(p)
             pl.when(p == 2)(middle)
             b = 2 * j + place.c
-            d_mixed = dot_t(full[j], out_w[...]).astype(LOW)
+            d_mixed = dot_t(full[j], weights.out[...]).astype(LOW)
             d_heads = jnp.concatenate([d_mixed[:, h * HD : (h + 1) * HD] for h in range(3)], axis=0)
             queries, keys, values, probs, rows, window = block_probs(qkv, starts_ref, b)
             d_probs = dot_t(d_heads, values).reshape(3, QB, reach)
@@ -1081,7 +1211,7 @@
             head = head * cos_ref[rows, :] + roll_half(head * sin_ref[rows, :])
             d_raw[rows, 3 * HD : 4 * HD] = head.astype(LOW)
             d_raw[rows, 4 * HD : 5 * HD] = d_values[rows, :].astype(LOW)
-            part[pl.ds(2 * j, 2)] = dot_t(d_raw[rows, :], qkv_w[...]).astype(LOW).reshape(2, tokens, width)
+            part[pl.ds(2 * j, 2)] = dot_t(d_raw[rows, :], weights.qkv[...]).astype(LOW).reshape(2, tokens, width)
             reduce.made(j)
             return carry
 
@@ -1119,30 +1249,32 @@
                 middle(3)
 
         reduce.finish(later, between)
+        after_backward(total, grad_ref, residual_ref, gain_ref, grad_out, low_out, gain_out)
         for copy in swap():
             copy.wait()
         for i in range(4):
             add_into(slab_out.at[i], [slab.at[place.c, i], slab_in.at[i]])
         add_into(out_out, [d_out.at[place.c], d_out_in])
 
-    (total, slab, d_out), loads = carry_call(
+    (grad, low, d_gain, d_slab, d_out), loads = carry_call(
         names,
         body,
         "line",
-        [block, acts, w_qkv, w_out, qkv, mixed, cosine, sine, starts],
-        [ONCHIP, ANY, ANY, ANY, ANY, ANY, ONCHIP, ONCHIP, ONCHIP],
+        [block, grad, residual, gain, acts, qkv, mixed, cosine, sine, starts, *slab],
+        [*[ONCHIP] * 4, *[ANY] * 3, *[ONCHIP] * 3, *[ANY] * 4],
         [
             jax.ShapeDtypeStruct((tokens, width), F32),
+            jax.ShapeDtypeStruct((tokens, width), LOW),
+            jax.ShapeDtypeStruct((1, width), F32),
             jax.ShapeDtypeStruct((4, HALF, 5 * HD), LOW),
             jax.ShapeDtypeStruct((D // 8, D), LOW),
         ],
-        [ONCHIP, ONCHIP, ONCHIP],
+        [ONCHIP] * 5,
         [
             *Gather.scratch,
+            *Slab.scratch,
             pltpu.VMEM((4, tokens, width), LOW),
             pltpu.VMEM((8, tokens, width), LOW),
-            pltpu.VMEM(w_qkv.shape, LOW),
-            pltpu.VMEM(w_out.shape, LOW),
             pltpu.VMEM((count, 5 * HD), LOW),
             pltpu.VMEM((count // 2, 3 * HD), LOW),
             pltpu.VMEM(acts.shape, LOW),
@@ -1153,15 +1285,16 @@
             pltpu.VMEM((2, D // 8, D), LOW),
             pltpu.VMEM((4, HALF, 5 * HD), LOW),
             pltpu.VMEM((D // 8, D), LOW),
-            pltpu.SemaphoreType.DMA((5,)),
+            pltpu.SemaphoreType.DMA((3,)),
             pltpu.SemaphoreType.DMA((2,)),
             pltpu.SemaphoreType.DMA((2,)),
+            pltpu.VMEM((tokens, width), F32),
             *Reduce.scratch(tokens, width),
         ],
         cargo,
         name=name,
     )
-    return total, slab.reshape(4 * HALF, 5 * HD), d_out, loads
+    return grad, low, d_gain, d_slab.reshape(4 * HALF, 5 * HD), d_out, loads
 
 
 def settle_rows(row, fulls, slots):
@@ -1195,22 +1328,42 @@
     )(row.reshape(1), *[array for pair in pairs for array in pair])
 
 
-def backward_feed(names, block, grads_all, acts, w_gate, w_up, w_down, gate, up, cargo, name):
+def backward_feed(names, block, grads_all, grad, residual, gain, acts, w_gate, w_up, w_down, gate, up, cargo, name):
     tokens, width = QB, D
     inner = w_gate.shape[0]
     apart = grads_all is not None
 
     def body(place, ins, outs, scratch, later, middle, start):
-        head_ref, acts_hbm, gate_hbm, up_hbm, down_hbm, gates_hbm, ups_hbm = ins
-        total, gate_out, up_out, down_out = outs
+        head_ref, grad_ref, residual_ref, gain_ref, acts_hbm, gate_hbm, up_hbm, down_hbm, gates_hbm, ups_hbm = ins
+        grad_out, low_out, gain_out, gate_out, up_out, down_out = outs
         scratch = list(scratch)
         gather_sems = [scratch.pop(0) for _ in Gather.scratch]
-        full, part, acts_own, gate_w, up_w, down_w, gates, ups, hiddens, load_sem, keep_sem = scratch[:11]
-        reduce = Reduce(place, part, total, scratch[11:], far=apart)
-        pairs = [(down_hbm, down_w), (gates_hbm, gates), (ups_hbm, ups), (gate_hbm, gate_w), (up_hbm, up_w)]
-        pairs.append((acts_hbm, acts_own))
+        full, part, acts_own, gate_w, up_w, down_w, gates, ups, hiddens, load_sem, keep_sem, total, d_down = scratch[:13]
+        reduce = Reduce(place, part, total, scratch[13:], far=apart)
+        if not apart:
+            d_down = down_w
+        def weights(dst, left, right, low, high):
+            def tile(i, carry):
+                cut = pl.ds(pl.multiple_of(i * 256, 256), 256)
+                dst[cut, :] = t_dot(left[:, cut], right()).astype(LOW)
+                return carry
+
+            whole = inner // 256
+            lax.fori_loop(low, min(high, whole), tile, 0)
+            if high > whole and inner % 256:
+                dst[whole * 256 :, :] = t_dot(left[:, whole * 256 :], right()).astype(LOW)
+
+        def grads_flat():
+            return full[...].reshape(8 * tokens, width)
+
+        def acts_flat():
+            return acts_own[...]
+
+        pairs = [(gates_hbm, gates), (ups_hbm, ups)]
         if apart:
             pairs.append((head_ref, full))
+        early = len(pairs)
+        pairs += [(down_hbm, down_w), (gate_hbm, gate_w), (up_hbm, up_w), (acts_hbm, acts_own)]
         loads = copy_in(pairs, load_sem)
         gather = None
         if not apart:
@@ -1218,7 +1371,26 @@
             gather.start(later)
         start(0)
         start(3)
-        for load in loads:
+        for load in loads[:early]:
+            load.wait()
+
+        def lit(rows):
+            gate, up = gates[rows, :].astype(F32), ups[rows, :].astype(F32)
+            squash = jax.nn.sigmoid(gate)
+            glow = gate * squash
+            hiddens[rows, :] = (glow * up).astype(LOW)
+            return gate, up, squash, glow
+
+        if apart:
+
+            def light(i, carry):
+                lit(rows_of(i * tokens, tokens))
+                return carry
+
+            lax.fori_loop(0, 8, light, 0)
+            weights(d_down, hiddens, grads_flat, 0, 5)
+            start(1, d_down)
+        for load in loads[early:]:
             load.wait()
 
         def step(p, carry):
@@ -1227,12 +1399,9 @@
             rows = rows_of(j * 2 * tokens, 2 * tokens)
             grads = full[pl.ds(2 * j, 2)].reshape(2 * tokens, width)
             d_hidden = dot_t(grads, down_w[...])
-            gate, up = gates[rows, :].astype(F32), ups[rows, :].astype(F32)
-            squash = jax.nn.sigmoid(gate)
-            lit = gate * squash
-            hiddens[rows, :] = (lit * up).astype(LOW)
+            gate, up, squash, glow = lit(rows)
             d_gate = (d_hidden * up * squash * (1.0 + gate * (1.0 - squash))).astype(LOW)
-            d_up = (d_hidden * lit).astype(LOW)
+            d_up = (d_hidden * glow).astype(LOW)
             gates[rows, :] = d_gate
             ups[rows, :] = d_up
             sums = dot(d_gate, gate_w[...]) + dot(d_up, up_w[...])
@@ -1242,58 +1411,44 @@
 
         lax.fori_loop(0, 4, step, 0)
 
-        def weights(dst, left, right, low, high):
-            def tile(i, carry):
-                cut = pl.ds(pl.multiple_of(i * 256, 256), 256)
-                dst[cut, :] = t_dot(left[:, cut], right()).astype(LOW)
-                return carry
-
-            whole = inner // 256
-            lax.fori_loop(low, min(high, whole), tile, 0)
-            if high > whole and inner % 256:
-                dst[whole * 256 :, :] = t_dot(left[:, whole * 256 :], right()).astype(LOW)
-
-        def grads_flat():
-            return full[...].reshape(8 * tokens, width)
-
-        def acts_flat():
-            return acts_own[...]
-
         work = [
-            (down_w, hiddens, grads_flat, 0, 3),
-            (down_w, hiddens, grads_flat, 3, 5),
             (gate_w, gates, acts_flat, 0, 3),
             (gate_w, gates, acts_flat, 3, 5),
             (up_w, ups, acts_flat, 0, 3),
             (up_w, ups, acts_flat, 3, 5),
         ]
+        if not apart:
+            weights(d_down, hiddens, grads_flat, 0, 5)
+            start(1, d_down)
 
         def between(i):
+            if apart and i == 0 or not apart and i == 5:
+                middle(1)
             if i < len(work):
                 weights(*work[i])
-            if i == 1:
-                start(1, down_w)
-            if i == 5:
-                middle(1)
 
         reduce.finish(later, between)
-        for copy in copy_in([(gate_w, gate_out), (up_w, up_out), (down_w, down_out)], keep_sem):
+        saves = copy_in([(gate_w, gate_out), (up_w, up_out), (d_down, down_out)], keep_sem)
+        after_backward(total, grad_ref, residual_ref, gain_ref, grad_out, low_out, gain_out)
+        for copy in saves:
             copy.wait()
 
     head = grads_all.reshape(8, tokens, width) if apart else block
-    (total, d_gate, d_up, d_down), loads = carry_call(
+    (grad, low, d_gain, d_gate, d_up, d_down), loads = carry_call(
         names,
         body,
         "line",
-        [head, acts, w_gate, w_up, w_down, gate, up],
-        [ANY if apart else ONCHIP, ANY, ANY, ANY, ANY, ANY, ANY],
+        [head, grad, residual, gain, acts, w_gate, w_up, w_down, gate, up],
+        [ANY if apart else ONCHIP, ONCHIP, ONCHIP, ONCHIP, ANY, ANY, ANY, ANY, ANY, ANY],
         [
             jax.ShapeDtypeStruct((tokens, width), F32),
+            jax.ShapeDtypeStruct((tokens, width), LOW),
+            jax.ShapeDtypeStruct((1, width), F32),
             jax.ShapeDtypeStruct(w_gate.shape, LOW),
             jax.ShapeDtypeStruct(w_up.shape, LOW),
             jax.ShapeDtypeStruct(w_down.shape, LOW),
         ],
-        [ONCHIP, ANY, ANY, ANY],
+        [ONCHIP, ONCHIP, ONCHIP, ANY, ANY, ANY],
         [
             *Gather.scratch,
             pltpu.VMEM((8, tokens, width), LOW),
@@ -1307,12 +1462,14 @@
             pltpu.VMEM((8 * tokens, inner), LOW),
             pltpu.SemaphoreType.DMA((7,)),
             pltpu.SemaphoreType.DMA((3,)),
+            pltpu.VMEM((tokens, width), F32),
+            pltpu.VMEM(w_down.shape if apart else (16, 128), LOW),
             *Reduce.scratch(tokens, width),
         ],
         cargo,
         name=name,
     )
-    return total, d_gate, d_up, d_down, loads
+    return grad, low, d_gain, d_gate, d_up, d_down, loads
 
 
 eps_norm = 1e-06
@@ -1640,19 +1797,6 @@
     return lax.dot_general(a, b, (((0,), (0,)), ((), ())), preferred_element_type=F32)
 
 
-def norm_on(residual, gain):
-    scale = lax.rsqrt(jnp.mean(residual * residual, axis=1, keepdims=True) + eps_norm)
-    return scale, (residual * scale * gain[None, :]).astype(LOW)
-
-
-def norm_back(d_normed, residual, scale, gain):
-    weighted = d_normed * gain[None, :]
-    inner = jnp.sum(weighted * residual, axis=1, keepdims=True)
-    d_residual = weighted * scale - residual * (scale * scale * scale) * inner / D
-    d_gain = jnp.sum(d_normed * residual * scale, axis=0)
-    return d_residual, d_gain
-
-
 def per_device_line(
     hidden_states,
     out_grad,
@@ -1675,16 +1819,6 @@
     biases = lax.dynamic_update_slice(biases, qkv_bias[:, :, None], (0, 0, 0, row_at * (HD // 4)))
     gain_rows = jnp.pad(norm_gains.reshape(2 * LAYERS, D // 8), ((0, 16 - 2 * LAYERS), (0, 0)))
 
-    def slab_of(mine, theirs, out_mine, out_theirs):
-        first, second = jnp.where(core == 0, mine, theirs), jnp.where(core == 0, theirs, mine)
-        both = jnp.stack([first.reshape(4, HALF, 5 * HD), second.reshape(4, HALF, 5 * HD)], axis=1)
-        w_qkv = both[:, :, : D // 8].reshape(D, 5 * HD)
-        bias = jnp.sum(both[:, 0, D // 8].astype(F32), axis=0, keepdims=True)
-        w_out = jnp.concatenate(
-            [jnp.where(core == 0, out_mine, out_theirs), jnp.where(core == 0, out_theirs, out_mine)], axis=0
-        )
-        return w_qkv, bias, w_out
-
     def rows_load(layer):
         return (
             GatherRows(gate_weight.swapaxes(1, 2), 1, layer),
@@ -1696,7 +1830,7 @@
     to_chips = [HeadsToChips(qkv_weight, biases, layer) for layer in range(LAYERS)]
     slab_rows, out_rows = GatherRows(From(to_chips[0]), 0, phase=1), GatherRows(out_weight, 1, 0, phase=1)
     swap = Swap(From(slab_rows), From(out_rows), phase=2)
-    sent[0].phase = 3
+    sent[0].phase, sent[0].split = 3, True
     states, loads = open_call(
         names, hidden_states, [*to_chips, Exchange(gain_rows, same=True), slab_rows, out_rows, swap, sent[0]]
     )
@@ -1714,50 +1848,38 @@
     def own_rows(full):
         return lax.dynamic_slice_in_dim(full, col_at * QB, QB, 0).astype(F32)
 
+    def gain_of(layer, which):
+        return gains[layer, which][None]
+
     saved = []
+    normed = None
     for layer in range(LAYERS):
-        w_qkv, bias, w_out = slab_of(*load)
+        slab = load
         sent[1].phase, sent[2].phase = 0, 3
-        scale_one, normed_one = norm_on(residual, gains[layer, 0])
-        fixed = (w_qkv, bias, w_out, cosine, sine, starts, sent[1:])
+        fixed = (residual, gain_of(layer, 1), slab, cosine, sine, starts, sent[1:])
         if layer == 0:
-            attention, grads_all, qkv, mixed, full_one, loads = forward_heads(
+            mid, normed, grads_all, qkv, mixed, full_one, loads = forward_heads(
                 names, out_grad, wide, gains[0, 0][:, None], *fixed, name="heads_0"
             )
         else:
-            attention, full_one, qkv, mixed, _, loads = forward_heads(names, normed_one, None, None, *fixed, name="heads_1")
+            mid, normed, full_one, qkv, mixed, _, loads = forward_heads(names, normed, None, None, *fixed, name="heads_1")
         (w_up,), (w_down,) = loads
-        residual_mid = residual + attention
-        scale_two, normed_two = norm_on(residual_mid, gains[layer, 1])
         cargo = []
         if layer == 0:
             sent = rows_load(1)
             sent[0].phase = 3
             slab_rows, out_rows = GatherRows(slab_next, 0), GatherRows(out_weight, 1, 1)
             cargo = [slab_rows, out_rows, sent[0], Swap(From(slab_rows), From(out_rows), phase=2)]
-        feed, full_two, gate, up, loads = forward_feed(
-            names, normed_two, w_gate, w_up, w_down, cargo, name=f"feed_{layer}"
+        following = gain_of(layer + 1, 0) if layer + 1 < LAYERS else None
+        states, normed, full_two, gate, up, loads = forward_feed(
+            names, normed, mid, following, w_gate, w_up, w_down, cargo, name=f"feed_{layer}"
         )
-        saved.append(
-            (
-                residual,
-                scale_one,
-                full_one,
-                qkv,
-                mixed,
-                residual_mid,
-                scale_two,
-                full_two,
-                gate,
-                up,
-                (w_qkv, w_out, w_gate, w_up, w_down),
-            )
-        )
-        residual = residual_mid + feed
+        saved.append((residual, full_one, slab, qkv, mixed, mid, full_two, gate, up, (w_gate, w_up, w_down)))
+        residual = states
         if layer == 0:
             (mine,), (out_mine,), (w_gate,), (theirs, out_theirs) = loads
             load = (mine, theirs, out_mine, out_theirs)
-    states = residual.astype(LOW)
+    states = normed
 
     def own_part(full, dim):
         size = full.shape[dim] // 4
@@ -1774,80 +1896,67 @@
 
     grads = {}
     gain_terms = [None] * LAYERS
-    grad = own_rows(grads_all)
+    grad, low = own_rows(grads_all), None
     inner = w_gate.shape[0]
+    owners = []
     for layer in reversed(range(LAYERS)):
-        (
-            residual_in,
-            scale_one,
-            full_one,
-            qkv,
-            mixed,
-            residual_mid,
-            scale_two,
+        residual_in, full_one, slab, qkv, mixed, mid, full_two, gate, up, feed_weights = saved[layer]
+        last = layer == LAYERS - 1
+        cargo = [] if last else [ScatterRows(d_slab, 0), ScatterRows(d_out_w, 1)]
+        cargo.append(ScatterRows(Inner((inner, D)), 1, phase=1))
+        grad, low, d_gain_two, d_gate_w, d_up_w, d_down, loads = backward_feed(
+            names,
+            low,
+            grads_all if last else None,
+            grad,
+            mid,
+            gain_of(layer, 1),
             full_two,
-            gate,
-            up,
-            (w_qkv, w_out, w_gate, w_up, w_down),
-        ) = saved[layer]
-        last = layer == LAYERS - 1
-        cargo = [] if last else [ScatterRows(slab, 0), ScatterRows(d_out_w, 1)]
-        cargo.append(ScatterRows(Inner((inner, D)), 1, phase=1))
-        d_normed_two, d_gate_w, d_up_w, d_down, loads = backward_feed(
-            names,
-            None if last else grad.astype(LOW),
-            grads_all if last else None,
-            full_two,
-            w_gate,
-            w_up,
-            w_down,
+            *feed_weights,
             gate,
             up,
             cargo,
             name=f"back_feed_{layer}",
         )
         grads["down", layer] = d_down, loads[-1][0]
-        cargo = [ScatterRows(d_gate_w, 1), ScatterRows(d_up_w, 1, phase=3)]
         if not last:
             grads["out", layer + 1] = settle(d_out_w, 1, loads[1][0])
-            cargo.append(HeadsToOwners(settle(slab, 0, loads[0][0]).astype(LOW)))
-        d_residual, d_gain_two = norm_back(d_normed_two, residual_mid, scale_two, gains[layer, 1])
-        grad = grad + d_residual
-        d_normed_one, slab, d_out_w, loads = backward_heads(
+            owners.append(HeadsToOwners(settle(d_slab, 0, loads[0][0]).astype(LOW)))
+        grad, low, d_gain_one, d_slab, d_out_w, loads = backward_heads(
             names,
-            grad.astype(LOW),
+            low,
+            grad,
+            residual_in,
+            gain_of(layer, 0),
             full_one,
             layer == 0,
-            w_qkv,
-            w_out,
+            slab,
             qkv,
             mixed,
             cosine,
             sine,
             starts,
-            cargo,
+            [ScatterRows(d_gate_w, 1), ScatterRows(d_up_w, 1, phase=3)],
             name=f"back_heads_{layer}",
         )
         grads["gate", layer] = d_gate_w, loads[0][0]
         grads["up", layer] = d_up_w, loads[1][0]
-        if not last:
-            grads["qkv", layer + 1] = settle_heads(loads[2][0])
-        d_residual, d_gain_one = norm_back(d_normed_one, residual_in, scale_one, gains[layer, 0])
-        grad = grad + d_residual
-        gain_terms[layer] = jnp.stack([d_gain_one, d_gain_two])
-    leaving = jnp.concatenate([states.T, grad.astype(LOW).T], axis=1).reshape(8, D // 8, 2 * QB)
+        gain_terms[layer] = jnp.concatenate([d_gain_one, d_gain_two], axis=0)
+    leaving = jnp.concatenate([states, low], axis=0).T.reshape(8, D // 8, 2 * QB)
     gain_parts = jnp.pad(jnp.stack(gain_terms).reshape(2 * LAYERS, 8, D // 8), ((0, 8 - 2 * LAYERS), (0, 0), (0, 0)))
-    (left,), (gain_all,), (slots,), (out_slots,) = close_call(
+    (left,), (gain_all,), (slots,), (out_slots,), (tiles,) = close_call(
         names,
         [
             Exchange(leaving),
             Exchange(gain_parts.transpose(1, 0, 2), every_row=True),
-            ScatterRows(slab, 0),
+            ScatterRows(d_slab, 0),
             ScatterRows(d_out_w, 1),
+            *owners,
         ],
         "close",
     )
-    ((tiles,),) = close_call(names, [HeadsToOwners(settle(slab, 0, slots).astype(LOW))], "close_heads")
+    grads["qkv", 1] = settle_heads(tiles)
+    ((tiles,),) = close_call(names, [HeadsToOwners(settle(d_slab, 0, slots).astype(LOW))], "close_heads")
     grads["qkv", 0] = settle_heads(tiles)
     grads["out", 0] = settle(d_out_w, 1, out_slots)
     left = left.transpose(1, 0, 2)

time: 721 us -> 672 us (0.932)
  Pallas kernels: 654 us -> 630 us
  other arithmetic: 40.3 us -> 17.4 us
    pallas_call x11, Pallas kernels: 643 us -> 619 us  [carry_call(): results = list(call(*arrays, *given))]
where the time goes in v5:
time: 672 us; the launch traced here: 662 us
  Pallas kernels  630 us (94%)
  other arithmetic  17.4 us (3%)
  local copies, waits for them, and re-layouts  13.2 us (2%)
    pallas_call x11, Pallas kernels, carry_call(): results = list(call(*arrays, *given))  619 us

profile of v5, /device:TPU:31, one launch (start us, length us, event | category | flops | bytes accessed | tf_op | source)
XLA Modules:
  0.0 662.3 jit_solution(3877558326138647642)
XLA Ops:
  0.6 0.7 copy.37
  1.3 0.7 dynamic_update_slice.3.refs_2_.refs_4_
  2.1 0.7 reshape.124
  2.8 0.6 pad.8.refs_5_
  3.4 63.3 %open.1 = (bf16[8,192,1024]{2,1,0:T(8,128)(2,1)}, bf16[208,640]{1,0:T(8,128)(2,1)}, bf16[208,640]{1,0:T(8,128)(2,1)}, bf16[8,16,192]{2,1,0:T(8,128)(2,1)}, bf16[...) custom-call(bf16[192,1024]{1,0:T(8,128)(2,1)} %refs_0_.2, ...), custom_call_target="tpu_custom_call" | custom-call | tf_op jit(solution)/shard_map/open/pallas_call | solution.py:660
  66.7 1.0 constant_dynamic-slice_fusion.2
  67.7 0.2 copy.51
  67.9 1.0 convert_bitcast_fusion.1.refs_3_.refs_2_
  68.9 0.8 convert_bitcast_fusion.2
  69.6 0.1 reshape.140
  69.7 0.6 slice_bitcast_fusion.6
  70.4 1.2 copy.40.refs_2_
  71.5 0.2 reduce-window.7
  71.8 1.9 multiply_sine_fusion
  73.7 1.0 fusion.refs_6_.refs_4_.refs_8_
  74.7 1.0 maximum_bitcast_fusion.1.refs_5_.refs_3_.refs_7_
  75.7 1.0 copy.41.refs_7_.refs_5_.refs_9_
  76.8 65.7 %heads_0.1 = (f32[128,1536]{1,0:T(8,128)}, bf16[128,1536]{1,0:T(8,128)(2,1)}, bf16[1024,1536]{1,0:T(8,128)(2,1)}, bf16[1024,640]{1,0:T(8,128)(2,1)}, bf16[512,38...) custom-call(bf16[192,1024]{1,0:T(8,128)(2,1)} %refs_0_.3, ...), custom_call_target="tpu_custom_call" | custom-call | tf_op jit(solution)/shard_map/heads_0/pallas_call | solution.py:660
  142.5 60.8 %feed_0.1 = (f32[128,1536]{1,0:T(8,128)}, bf16[128,1536]{1,0:T(8,128)(2,1)}, bf16[8,128,1536]{2,1,0:T(8,128)(2,1)}, bf16[1024,1120]{1,0:T(8,128)(2,1)}, bf16[102...) custom-call(bf16[128,1536]{1,0:T(8,128)(2,1)} %get-tuple-element.89., ...), custom_call_target="tpu_custom_call" | custom-call | tf_op jit(solution)/shard_map/feed_0/pallas_call | solution.py:660
  203.3 63.7 %heads_1.1 = (f32[128,1536]{1,0:T(8,128)}, bf16[128,1536]{1,0:T(8,128)(2,1)}, bf16[8,128,1536]{2,1,0:T(8,128)(2,1)}, bf16[1024,640]{1,0:T(8,128)(2,1)}, bf16[512...) custom-call(bf16[128,1536]{1,0:T(8,128)(2,1)} %get-tuple-element.95.refs_0_, ...), custom_call_target="tpu_custom_call" | custom-call | tf_op jit(solution)/shard_map/heads_1/pallas_call | solution.py:660
  267.1 0.6 broadcast_in_dim.49.refs_2_
  267.7 57.6 %feed_1.1 = (f32[128,1536]{1,0:T(8,128)}, bf16[128,1536]{1,0:T(8,128)(2,1)}, bf16[8,128,1536]{2,1,0:T(8,128)(2,1)}, bf16[1024,1120]{1,0:T(8,128)(2,1)}, bf16[1024,1120]{1,0:T(8,128)(2,1)}) custom-call(bf16[128,1536]{1,0:T(8,128)(2,1)} %get-tuple-element.101.refs_0_, f32[128,1536]{1,0:T(8,128)} %get-tuple-element.102.refs_1_.refs_2_, ...), custom_call_target="tpu_custom_call" | custom-call | tf_op jit(solution)/shard_map/feed_1/pallas_call | solution.py:660
  325.3 2.0 dynamic-slice_convert_fusion.refs_1_
  327.2 53.9 %back_feed_1.1 = (f32[128,1536]{1,0:T(8,128)}, bf16[128,1536]{1,0:T(8,128)(2,1)}, f32[1,1536]{1,0:T(1,128)}, bf16[1120,1536]{1,0:T(8,128)(2,1)}, bf16[1120,1536]...) custom-call(bf16[8,128,1536]{2,1,0:T(8,128)(2,1)} %bitcast.75, ...), custom_call_target="tpu_custom_call" | custom-call | tf_op jit(solution)/shard_map/back_feed_1/pallas_call | solution.py:660
  381.1 68.4 %back_heads_1.1 = (f32[128,1536]{1,0:T(8,128)}, bf16[128,1536]{1,0:T(8,128)(2,1)}, f32[1,1536]{1,0:T(1,128)}, bf16[4,208,640]{2,1,0:T(8,128)(2,1)}, bf16[192,153...) custom-call(bf16[128,1536]{1,0:T(8,128)(2,1)} %get-tuple-element.111.refs_0_, ...), custom_call_target="tpu_custom_call" | custom-call | tf_op jit(solution)/shard_map/back_heads_1/pallas_call | solution.py:660
  449.5 76.4 %back_feed_0.1 = (f32[128,1536]{1,0:T(8,128)}, bf16[128,1536]{1,0:T(8,128)(2,1)}, f32[1,1536]{1,0:T(1,128)}, bf16[1120,1536]{1,0:T(8,128)(2,1)}, bf16[1120,1536]...) custom-call(bf16[128,1536]{1,0:T(8,128)(2,1)} %get-tuple-element.118, ...), custom_call_target="tpu_custom_call" | custom-call | tf_op jit(solution)/shard_map/back_feed_0/pallas_call | solution.py:660
  526.0 65.7 %back_heads_0.1 = (f32[128,1536]{1,0:T(8,128)}, bf16[128,1536]{1,0:T(8,128)(2,1)}, f32[1,1536]{1,0:T(1,128)}, bf16[4,208,640]{2,1,0:T(8,128)(2,1)}, bf16[192,153...) custom-call(bf16[128,1536]{1,0:T(8,128)(2,1)} %get-tuple-element.125.refs_0_, ...), custom_call_target="tpu_custom_call" | custom-call | tf_op jit(solution)/shard_map/back_heads_0/pallas_call | solution.py:660
  591.7 11.2 %settle.1 = (f32[2,1120,384]{2,1,0:T(8,128)}, f32[2,1120,384]{2,1,0:T(8,128)}, f32[2,1120,384]{2,1,0:T(8,128)}) custom-call(s32[1]{0:T(128)} %bitcast.37.row_ref, bf16[1120,1536]{1,0:T(8,128)(2,1)} %get-tuple-element.130.refs_14_.refs_0_, bf16[2,1120,384]{2,1,0:T(8,128)(2,1)} %get-tuple-element.146.refs_1_, ...), custom_call_target="tpu_custom_call" | custom-call | tf_op jit(solution)/shard_map/settle/pallas_call | solution.py:1313
  603.1 1.8 add_convert_fusion.1.refs_4_
  605.0 0.6 pad_bitcast_fusion.refs_1_
  605.7 1.2 copy.45
  606.9 33.6 %close.1 = (bf16[8,192,256]{2,1,0:T(8,128)(2,1)}, f32[4,8,8,192]{3,2,1,0:T(8,128)}, bf16[2,208,640]{2,1,0:T(8,128)(2,1)}, bf16[2,192,384]{2,1,0:T(8,128)(2,1)}, bf16[2,2,2,208,128]{4,3,2,1,0:T(8,128)(2,1)}) custom-call(bf16[8,192,256]{2,1,0:T(8,128)(2,1)} %bitcast.79, f32[8,8,192]{2,1,0:T(8,128)} %pad_bitcast_fusion.refs_1_, bf16[832,640]{1,0:T(8,128)(2,1)} %bitcast.84, ...), custom_call_target="tpu_custom_call" | custom-call | tf_op jit(solution)/shard_map/close/pallas_call | solution.py:660
  640.5 1.1 convert_reduce_fusion.3
  641.7 1.0 add_bitcast_fusion.2
  642.7 0.9 pad_maximum_fusion.1
  643.6 1.7 add_convert_fusion.refs_0_
  645.4 9.7 %close_heads.1 = bf16[2,2,2,208,128]{4,3,2,1,0:T(8,128)(2,1)} custom-call(bf16[208,640]{1,0:T(8,128)(2,1)} %add_convert_fusion.refs_0_), custom_call_target="tpu_custom_call" | custom-call | tf_op jit(solution)/shard_map/close_heads/pallas_call | solution.py:660
  655.1 1.1 add_bitcast_fusion.1
  656.4 0.6 pad_maximum_fusion.3
  657.0 0.3 copy.49
  657.3 0.3 stack_reshape.6
  657.7 0.3 copy.50
  658.0 0.3 stack_reshape.7
  658.3 0.9 pad_maximum_fusion
  659.2 0.1 convert_bitcast_fusion
  659.4 1.0 copy.56
  660.3 0.9 copy.57
  661.2 0.6 reshape.138
  (52 shorter events, 0.8 us)
Async XLA Ops:
  2.1 1.3 copy-start.8
  66.7 4.9 copy-start.13
  591.7 11.3 %copy-start.1 = (bf16[2,208,640]{2,1,0:T(8,128)(2,1)S(1)}, bf16[2,208,640]{2,1,0:T(8,128)(2,1)}, u32[]{:S(2)}) copy-start(bf16[2,208,640]{2,1,0:T(8,128)(2,1)} %get-tuple-element.139) | copy-start | bytes 1597444
  591.7 13.1 %copy-start.11 = (f32[1,1536]{1,0:T(1,128)S(1)}, f32[1,1536]{1,0:T(1,128)}, u32[]{:S(2)}) copy-start(f32[1,1536]{1,0:T(1,128)} %get-tuple-element.134) | copy-start | bytes 18436
  591.7 13.1 %copy-start.12 = (f32[1,1536]{1,0:T(1,128)S(1)}, f32[1,1536]{1,0:T(1,128)}, u32[]{:S(2)}) copy-start(f32[1,1536]{1,0:T(1,128)} %get-tuple-element.133) | copy-start | bytes 18436
  591.7 13.2 %copy-start.9 = (f32[1,1536]{1,0:T(1,128)S(1)}, f32[1,1536]{1,0:T(1,128)}, u32[]{:S(2)}) copy-start(f32[1,1536]{1,0:T(1,128)} %get-tuple-element.136) | copy-start | bytes 18436
  591.7 13.2 %copy-start.10 = (f32[1,1536]{1,0:T(1,128)S(1)}, f32[1,1536]{1,0:T(1,128)}, u32[]{:S(2)}) copy-start(f32[1,1536]{1,0:T(1,128)} %get-tuple-element.135) | copy-start | bytes 18436
  603.0 2.7 copy-start.4
  603.0 2.7 copy-start.5
  605.7 35.9 %copy-start.6 = (bf16[2,192,384]{2,1,0:T(8,128)(2,1)S(1)}, bf16[2,192,384]{2,1,0:T(8,128)(2,1)}, u32[]{:S(2)}) copy-start(bf16[2,192,384]{2,1,0:T(8,128)(2,1)} %get-tuple-element.145) | copy-start | bytes 884740
  640.5 3.1 copy-start.2
  642.7 13.5 %copy-start.3 = (bf16[2,2,2,208,128]{4,3,2,1,0:T(8,128)(2,1)S(1)}, bf16[2,2,2,208,128]{4,3,2,1,0:T(8,128)(2,1)}, u32[]{:S(2)}) copy-start(bf16[2,2,2,208,128]{4,3,2,1,0:T(8,128)(2,1)} %get-tuple-element.143) | copy-start | bytes 1277956
  657.3 1.9 copy-start
  659.2 2.0 copy-start.7

commit v6 on v5

--- a/solution.py
+++ b/solution.py
@@ -146,8 +146,6 @@
         first = pl.multiple_of(row * self.size, 16)
         return full.at[pl.ds(first, self.half), :], full.at[pl.ds(first + self.half, self.rest), :]
 
-    split = False
-
     def source(self, ins):
         return ins[0] if self.layer is None else ins[0].at[self.layer]
 
@@ -181,7 +179,7 @@
     def start(self, place, ins, outs, scratch, later):
         (dst,) = outs
         out, onward = self.copies(place, ins, outs, scratch)
-        for copy in out[:2] if self.split else out:
+        for copy in out:
             copy.start()
         load, store = self.keep(place, ins, outs, scratch)
         load.start()
@@ -192,10 +190,6 @@
             later.add(self.arrived(place, scratch, view, sem, row).wait_recv)
         for copy in (*out, *onward):
             later.add(copy.wait_send)
-
-    def send_rest(self, place, ins, outs, scratch):
-        for copy in self.copies(place, ins, outs, scratch)[0][2:]:
-            copy.start()
 
     def middle(self, place, ins, outs, scratch):
         (dst,) = outs
@@ -258,7 +252,11 @@
         ]
         return first, held, last
 
+    tell = None
+
     def start(self, place, ins, outs, scratch, later):
+        if self.tell is not None:
+            self.tell[0] = lambda: outs[0]
         first, held, last = self.copies(place, ins, outs, scratch)
         for copy in (*first, *held):
             copy.start()
@@ -308,6 +306,7 @@
 
     def __init__(self, weight, biases, layer):
         self.layer = layer
+        self.phase = 0 if layer == 0 else 3
         self.arrays = (weight, biases)
         self.outs = (jax.ShapeDtypeStruct((HALF, 5 * HD), LOW),)
         self.scratch = (
@@ -400,6 +399,7 @@
     def __init__(self, chunks, every_row=False, same=False):
         self.arrays = (chunks,)
         self.same = same
+        self.phase = 3
         self.rows_too = every_row
         self.reach = "all" if every_row else "col"
         lead = (4,) if every_row else (8,) if same else ()
@@ -474,7 +474,7 @@
         return remote(other, self.from_p.at[j], self.send_p.at[j], self.recv_p.at[j], place.at(place.z, 1 - place.c))
 
     def piece(self, j, sub, way):
-        rows = pl.ds(sub * self.size, self.size)
+        rows = rows_of(sub * self.size, self.size)
         column = jnp.where(way == 0, self.right[1], self.left[1])
         return remote(
             self.held.at[j, rows, :],
@@ -502,49 +502,42 @@
             for sub in range(SUB):
                 self.piece(j, sub, jnp.where(z == 0, 0, 1)).start()
 
-    def finish(self, later, between):
+    def finish(self, later, early=None, late=None):
         z = self.place.z
         way = jnp.where(z == 1, 0, 1)
         near, far, back = jnp.where(z == 1, 2, 1), jnp.where(z == 1, 3, 0), jnp.where(z == 1, 0, 3)
         first, second = (far, near) if self.far else (near, far)
 
         def step(j, sub, way):
+            if self.both:
+                pl.when(sub == 0)(lambda: self.pair(j).wait_recv())
             copy = self.piece(j, sub, way)
             copy.wait_recv()
-            rows = pl.ds(sub * self.size, self.size)
+            rows = rows_of(sub * self.size, self.size)
             views = [view.at[rows, :] for view in (*self.terms(j), self.moved.at[way, j])]
             add_into(self.held.at[j].at[rows, :], views)
             copy.start()
 
-        def pair_here(j):
-            if self.both:
-                self.pair(j).wait_recv()
-
-        def firsts(sub):
-            if sub == 0:
-                pair_here(first)
-            step(first, sub, way)
-
-        def seconds(sub):
-            if sub == 0:
-                pair_here(second)
-            step(second, sub, way)
-
-        def backs(sub):
-            if sub == 0:
-                pair_here(back)
-            step(back, sub, 1 - way)
-
-        for sub in range(SUB):
-            pl.when(self.mid)(partial(firsts, sub))
-            between(sub)
-        for sub in range(SUB):
-            pl.when(self.mid)(partial(seconds, sub))
-            if sub >= LAG:
-                pl.when(self.mid)(partial(backs, sub - LAG))
-            between(SUB + sub)
-        for sub in range(SUB - LAG, SUB):
-            pl.when(self.mid)(partial(backs, sub))
+        def one(sub, carry):
+            pl.when(self.mid)(lambda: step(first, sub, way))
+            if early is not None:
+                early(sub)
+            return carry
+
+        def two(sub, carry):
+            pl.when(self.mid)(lambda: step(second, sub, way))
+            pl.when(self.mid & (sub >= LAG))(lambda: step(back, sub - LAG, 1 - way))
+            if late is not None:
+                late(sub)
+            return carry
+
+        def three(sub, carry):
+            pl.when(self.mid)(lambda: step(back, sub, 1 - way))
+            return carry
+
+        lax.fori_loop(0, SUB, one, 0)
+        lax.fori_loop(0, SUB, two, 0)
+        lax.fori_loop(SUB - LAG, SUB, three, 0)
         if self.both:
             self.pair(z).wait_recv()
 
@@ -633,10 +626,12 @@
             taken[item] = [inner.pop(0) if isinstance(a, Inner) else a for a in taken[item]]
             item.start(place, taken[item], made[item], held[item], owed[phase])
 
-    def middle(phase=0, rest=False):
+    start.wait = lambda phase: owed[phase].run()
+
+    def middle(phase=0):
         for item in cargo:
             if item.phase == phase:
-                (item.send_rest if rest else item.middle)(place, taken[item], made[item], held[item])
+                item.middle(place, taken[item], made[item], held[item])
 
     body(place, ins, outs, scratch, later, middle, start)
     later.run()
@@ -761,6 +756,16 @@
         return j
 
 
+def tiles(count, work, size=256):
+    def tile(i, carry):
+        work(rows_of(i * size, size))
+        return carry
+
+    lax.fori_loop(0, count // size, tile, 0)
+    if count % size:
+        work(pl.ds(count // size * size, count % size))
+
+
 def forward_feed(names, block, residual, gain, w_gate, w_up, w_down, cargo, name):
     tokens, width = block.shape
     inner = w_gate.shape[0]
@@ -771,8 +776,8 @@
         states_out, normed_out, full_out, gate_out, up_out = outs
         n = len(Gather.scratch)
         gather_sems, scratch = scratch[:n], scratch[n:]
-        full, part, gate_w, up_w, down_w, gates, ups, load_sem, keep_sem, total = scratch[:10]
-        reduce = Reduce(place, part, total, scratch[10:])
+        full, part, gate_w, up_w, down_w, gates, ups, load_sem, keep_sem, total, hidden = scratch[:11]
+        reduce = Reduce(place, part, total, scratch[11:])
         gather = Gather(place, block_ref, full, gather_sems)
         loads = [
             pltpu.make_async_copy(src, dst, load_sem.at[i])
@@ -799,13 +804,21 @@
             pl.when(p == 2)(middle)
             acts = full[pl.ds(2 * j, 2)].reshape(2 * tokens, width)
             rows = pl.ds(pl.multiple_of(2 * tokens * j, 2 * tokens), 2 * tokens)
-            gate = dot_t(acts, gate_w[...])
-            up = dot_t(acts, up_w[...])
-            gates[rows, :] = gate.astype(LOW)
-            ups[rows, :] = up.astype(LOW)
-            hidden = (gate * jax.nn.sigmoid(gate) * up).astype(LOW)
-            sums = jnp.dot(hidden, down_w[...], preferred_element_type=F32).astype(LOW)
-            part[pl.ds(2 * j, 2)] = sums.reshape(2, tokens, width)
+
+            def columns(cut):
+                gate = dot_t(acts, gate_w[cut, :])
+                up = dot_t(acts, up_w[cut, :])
+                gates[rows, cut] = gate.astype(LOW)
+                ups[rows, cut] = up.astype(LOW)
+                hidden[:, cut] = (gate * jax.nn.sigmoid(gate) * up).astype(LOW)
+
+            tiles(inner, columns, 512)
+
+            def outputs(cut):
+                sums = dot(hidden[...], down_w[:, cut]).astype(LOW)
+                part[pl.ds(2 * j, 2), :, cut] = sums.reshape(2, tokens, cut.size)
+
+            tiles(width, outputs, 768)
             reduce.made(j)
             for copy in keep(j):
                 copy.start()
@@ -814,7 +827,7 @@
         lax.fori_loop(0, 4, step, 0)
         start(1)
         start(2)
-        reduce.finish(later, lambda i: middle(3) if i == 0 else None)
+        reduce.finish(later, early=lambda i: pl.when(i == 0)(lambda: middle(3)))
         after_forward(total, residual_ref, gain_ref if normed else None, states_out, normed_out)
         for j in range(4):
             for copy in keep(j):
@@ -846,6 +859,7 @@
             pltpu.SemaphoreType.DMA((3,)),
             pltpu.SemaphoreType.DMA((3, 4)),
             pltpu.VMEM((tokens, width), F32),
+            pltpu.VMEM((2 * tokens, inner), LOW),
             *Reduce.scratch(tokens, width),
         ],
         cargo,
@@ -868,11 +882,10 @@
 def open_call(names, shard, cargo):
     def body(place, ins, outs, scratch, later, middle, start):
         gather = Gather(place, ins[0], outs[0], scratch)
+        start(0)
         gather.start(later)
-        start(0)
         start(3)
         start(1)
-        middle(3, rest=True)
         gather.pass_on(1)
         middle(1)
         gather.pass_on(2)
@@ -898,12 +911,46 @@
     return full, loads
 
 
-def close_call(names, cargo, name):
+def close_call(names, slab, cargo):
     def body(place, ins, outs, scratch, later, middle, start):
+        slab_ref = ins[0]
+        own, came, total, sem = scratch
         start(0)
+        start(3)
         middle(0)
-
-    return carry_call(names, body, "col", [], [], [], [], [], cargo, name=name)[1]
+        middle(3)
+        load = pltpu.make_async_copy(slab_ref.at[rows_of(place.r * HALF, HALF), :], own, sem.at[0])
+        load.start()
+        start.wait(0)
+        fetch = pltpu.make_async_copy(cargo_refs[0](), came, sem.at[1])
+        fetch.start()
+        load.wait()
+        fetch.wait()
+        add_into(total, [own, came.at[0], came.at[1]])
+        start(1, total)
+
+    cargo_refs = [None]
+    rows, owners = ScatterRows(slab, 0), HeadsToOwners(Inner((HALF, 5 * HD)))
+    owners.phase = 1
+    rows.tell = cargo_refs
+    _, loads = carry_call(
+        names,
+        body,
+        "col",
+        [slab],
+        [ANY],
+        [],
+        [],
+        [
+            pltpu.VMEM((HALF, 5 * HD), LOW),
+            pltpu.VMEM((2, HALF, 5 * HD), LOW),
+            pltpu.VMEM((HALF, 5 * HD), LOW),
+            pltpu.SemaphoreType.DMA((2,)),
+        ],
+        [rows, owners, *cargo],
+        name="close",
+    )
+    return loads[1][0], loads[2:]
 
 
 def after_forward(sums, residual, gain, states, normed):
@@ -983,20 +1030,22 @@
     return jnp.concatenate([ref[rows, h * HD : (h + 1) * HD] for h in range(3)], axis=0)
 
 
-def block_probs(qkv, starts, b):
+def block_window(b):
+    first = jnp.maximum(b - SEQ_MAX // QB, 0) * QB
+    return rows_of(b * QB, QB), pl.ds(pl.multiple_of(first, QB), QB + SEQ_MAX), first
+
+
+def block_probs(queries, keys, starts, b):
     reach = QB + SEQ_MAX
-    first = jnp.maximum(b - SEQ_MAX // QB, 0) * QB
-    rows, window = rows_of(b * QB, QB), pl.ds(pl.multiple_of(first, QB), reach)
-    queries = heads_of(qkv, rows)
-    keys, values = qkv[window, 3 * HD : 4 * HD], qkv[window, 4 * HD : 5 * HD]
-    scores = (dot_t(queries, keys) * HD ** (-0.5)).reshape(3, QB, reach)
+    rows, _, first = block_window(b)
+    scores = (dot_t(queries, keys) * HD ** (-0.5)).reshape(-1, QB, reach)
     key_at = first + lax.broadcasted_iota(jnp.int32, (QB, reach), 1)
     query_at = b * QB + lax.broadcasted_iota(jnp.int32, (QB, reach), 0)
     allowed = (key_at >= starts[rows, :]) & (key_at <= query_at)
     masked = jnp.where(allowed[None], scores, neg_fill)
     lifted = jnp.exp(masked - jnp.max(masked, axis=-1, keepdims=True))
     probs = lifted * (1.0 / jnp.sum(lifted, axis=-1, keepdims=True))
-    return queries, keys, values, probs, rows, window
+    return probs.reshape(-1, reach)
 
 
 def roll_half(values):
@@ -1067,9 +1116,10 @@
 
         def attend(p, carry):
             j = far_first(place, p)
-            _, _, values, probs, _, _ = block_probs(qkv, starts_ref, 2 * j + place.c)
-            low = probs.astype(LOW).reshape(3 * QB, QB + SEQ_MAX)
-            heads = jnp.dot(low, values, preferred_element_type=F32).astype(LOW)
+            b = 2 * j + place.c
+            rows, window, _ = block_window(b)
+            probs = block_probs(heads_of(qkv, rows), qkv[window, 3 * HD : 4 * HD], starts_ref, b)
+            heads = dot(probs.astype(LOW), qkv[window, 4 * HD : 5 * HD]).astype(LOW)
             both = jnp.concatenate([heads[h * QB : (h + 1) * QB] for h in range(3)], axis=1)
             mixed[rows_of(j * QB, QB), :] = both
             part[j] = jnp.dot(both, weights.out[...], preferred_element_type=F32).astype(LOW)
@@ -1082,19 +1132,26 @@
             saves.append(pltpu.make_async_copy(acts, outs[5], load_sem.at[2]))
             saves[-1].start()
 
-        def between(i):
-            if not apart:
-                if i == 0:
+        def early(i):
+            if apart:
+                pl.when(i == 0)(lambda: gather.pass_on(1))
+            else:
+                pl.when(i == 0)(lambda: middle(3))
+
+        def late(i):
+            if apart:
+
+                @pl.when(i == 0)
+                def _():
+                    gather.pass_on(2)
+                    middle(0)
+
+                @pl.when(i == SUB - 1)
+                def _():
+                    gather.pass_on(3)
                     middle(3)
-                return
-            if i in (0, SUB, 2 * SUB - 1):
-                gather.pass_on(1 + (i + 1) // SUB)
-            if i == SUB:
-                middle(0)
-            if i == 2 * SUB - 1:
-                middle(3)
-
-        reduce.finish(later, between)
+
+        reduce.finish(later, early, late)
         after_forward(total, residual_ref, two_ref, states_out, normed_out)
         if apart:
             for zz in range(4):
@@ -1165,8 +1222,8 @@
         gather_sems = [scratch.pop(0) for _ in Gather.scratch]
         weights = Slab(place, slab_refs, [scratch.pop(0) for _ in Slab.scratch])
         full, part, qkv, mixed, acts_own, d_raw, d_keys, d_values = scratch[:8]
-        slab, d_out, slab_in, d_out_in, load_sem, swap_send, swap_recv, total = scratch[8:16]
-        reduce = Reduce(place, part, total, scratch[16:], far=True)
+        slab, d_out, slab_in, d_out_in, load_sem, swap_send, swap_recv, total, d_mixed = scratch[8:17]
+        reduce = Reduce(place, part, total, scratch[17:], far=True)
         weights.start()
         loads = copy_in([(saved_hbm, qkv), (mixed_hbm, mixed), (acts_hbm, acts_own)], load_sem)
         gather = Gather(place, block_ref, full, gather_sems, both=False)
@@ -1183,20 +1240,25 @@
             j = gather.chunk(p)
             pl.when(p == 2)(middle)
             b = 2 * j + place.c
-            d_mixed = dot_t(full[j], weights.out[...]).astype(LOW)
-            d_heads = jnp.concatenate([d_mixed[:, h * HD : (h + 1) * HD] for h in range(3)], axis=0)
-            queries, keys, values, probs, rows, window = block_probs(qkv, starts_ref, b)
-            d_probs = dot_t(d_heads, values).reshape(3, QB, reach)
-            inner = jnp.sum(probs * d_probs, axis=-1, keepdims=True)
-            d_scores = (probs * (d_probs - inner)).astype(LOW).reshape(3 * QB, reach)
-            d_queries = jnp.dot(d_scores, keys, preferred_element_type=F32) * HD ** (-0.5)
-            d_keys[window, :] += t_dot(d_scores, queries) * HD ** (-0.5)
-            d_values[window, :] += t_dot(probs.astype(LOW).reshape(3 * QB, reach), d_heads)
-            cos, sin = cos_ref[rows, :], sin_ref[rows, :]
-            for h in range(3):
-                head = d_queries[h * QB : (h + 1) * QB]
-                head = head * cos + roll_half(head * sin)
-                d_raw[rows, h * HD : (h + 1) * HD] = head.astype(LOW)
+            d_mixed[...] = dot_t(full[j], weights.out[...]).astype(LOW)
+            rows, window, _ = block_window(b)
+
+            def head(h, carry):
+                cut = rows_of(h * HD, HD)
+                queries, d_head = qkv[rows, cut], d_mixed[:, cut]
+                keys, values = qkv[window, 3 * HD : 4 * HD], qkv[window, 4 * HD : 5 * HD]
+                probs = block_probs(queries, keys, starts_ref, b)
+                d_probs = dot_t(d_head, values)
+                inner = jnp.sum(probs * d_probs, axis=-1, keepdims=True)
+                d_scores = (probs * (d_probs - inner)).astype(LOW)
+                d_queries = dot(d_scores, keys) * HD ** (-0.5)
+                d_keys[window, :] += t_dot(d_scores, queries) * HD ** (-0.5)
+                d_values[window, :] += t_dot(probs.astype(LOW), d_head)
+                turned_back = d_queries * cos_ref[rows, :] + roll_half(d_queries * sin_ref[rows, :])
+                d_raw[rows, cut] = turned_back.astype(LOW)
+                return carry
+
+            lax.fori_loop(0, 3, head, 0)
             other = rows_of((2 * j + 1 - place.c) * QB, QB)
             d_raw[other, 0 : 3 * HD] = jnp.zeros((QB, 3 * HD), LOW)
             return carry
@@ -1224,16 +1286,19 @@
                 remote(d_out.at[1 - place.c], d_out_in, swap_send.at[1], swap_recv.at[1], to),
             ]
 
-        def between(i):
-            if i < 4:
-                cut = slice(i * (D // 4), (i + 1) * (D // 4))
-                if turned:
-                    grads = jnp.dot(acts_own[cut, :], d_raw[...], preferred_element_type=F32).astype(LOW)
-                else:
-                    grads = t_dot(acts_own[:, cut], d_raw[...]).astype(LOW)
-                slab[0, i, 0 : D // 8, :] = grads[: D // 8]
-                slab[1, i, 0 : D // 8, :] = grads[D // 8 :]
-            elif i == 4:
+        def early(i):
+            cut = rows_of(i * (D // 4), D // 4)
+            if turned:
+                grads = dot(acts_own[cut, :], d_raw[...]).astype(LOW)
+            else:
+                grads = t_dot(acts_own[:, cut], d_raw[...]).astype(LOW)
+            slab[0, i, 0 : D // 8, :] = grads[: D // 8]
+            slab[1, i, 0 : D // 8, :] = grads[D // 8 :]
+            pl.when(i == 0)(lambda: middle(3))
+
+        def late(i):
+            @pl.when(i == 0)
+            def _():
                 sums = jnp.sum(d_raw[...].astype(F32), axis=0, keepdims=True)
                 first = lax.broadcasted_iota(jnp.int32, (16, 5 * HD), 0) == 0
                 tail = jnp.where(first, sums, 0.0).astype(LOW)
@@ -1245,10 +1310,8 @@
                 d_out[1] = grads[D // 8 :]
                 for copy in swap():
                     copy.start()
-            if i == 0:
-                middle(3)
-
-        reduce.finish(later, between)
+
+        reduce.finish(later, early, late)
         after_backward(total, grad_ref, residual_ref, gain_ref, grad_out, low_out, gain_out)
         for copy in swap():
             copy.wait()
@@ -1289,6 +1352,7 @@
             pltpu.SemaphoreType.DMA((2,)),
             pltpu.SemaphoreType.DMA((2,)),
             pltpu.VMEM((tokens, width), F32),
+            pltpu.VMEM((QB, 3 * HD), LOW),
             *Reduce.scratch(tokens, width),
         ],
         cargo,
@@ -1338,20 +1402,13 @@
         grad_out, low_out, gain_out, gate_out, up_out, down_out = outs
         scratch = list(scratch)
         gather_sems = [scratch.pop(0) for _ in Gather.scratch]
-        full, part, acts_own, gate_w, up_w, down_w, gates, ups, hiddens, load_sem, keep_sem, total, d_down = scratch[:13]
-        reduce = Reduce(place, part, total, scratch[13:], far=apart)
+        full, part, acts_own, pair_w, down_w, pair, hiddens, load_sem, keep_sem, total, d_down = scratch[:11]
+        gate_w, up_w, gates, ups = pair_w.at[0], pair_w.at[1], pair.at[0], pair.at[1]
+        reduce = Reduce(place, part, total, scratch[11:], far=apart)
         if not apart:
             d_down = down_w
-        def weights(dst, left, right, low, high):
-            def tile(i, carry):
-                cut = pl.ds(pl.multiple_of(i * 256, 256), 256)
-                dst[cut, :] = t_dot(left[:, cut], right()).astype(LOW)
-                return carry
-
-            whole = inner // 256
-            lax.fori_loop(low, min(high, whole), tile, 0)
-            if high > whole and inner % 256:
-                dst[whole * 256 :, :] = t_dot(left[:, whole * 256 :], right()).astype(LOW)
+        def weights(dst, left, right, cut):
+            dst[cut, :] = t_dot(left[:, cut], right()).astype(LOW)
 
         def grads_flat():
             return full[...].reshape(8 * tokens, width)
@@ -1374,21 +1431,21 @@
         for load in loads[:early]:
             load.wait()
 
-        def lit(rows):
-            gate, up = gates[rows, :].astype(F32), ups[rows, :].astype(F32)
+        def lit(rows, cut):
+            gate, up = gates[rows, cut].astype(F32), ups[rows, cut].astype(F32)
             squash = jax.nn.sigmoid(gate)
             glow = gate * squash
-            hiddens[rows, :] = (glow * up).astype(LOW)
+            hiddens[rows, cut] = (glow * up).astype(LOW)
             return gate, up, squash, glow
 
         if apart:
 
             def light(i, carry):
-                lit(rows_of(i * tokens, tokens))
+                lit(rows_of(i * tokens, tokens), slice(None))
                 return carry
 
             lax.fori_loop(0, 8, light, 0)
-            weights(d_down, hiddens, grads_flat, 0, 5)
+            tiles(inner, partial(weights, d_down, hiddens, grads_flat))
             start(1, d_down)
         for load in loads[early:]:
             load.wait()
@@ -1398,36 +1455,50 @@
             pl.when(p == 2)(middle)
             rows = rows_of(j * 2 * tokens, 2 * tokens)
             grads = full[pl.ds(2 * j, 2)].reshape(2 * tokens, width)
-            d_hidden = dot_t(grads, down_w[...])
-            gate, up, squash, glow = lit(rows)
-            d_gate = (d_hidden * up * squash * (1.0 + gate * (1.0 - squash))).astype(LOW)
-            d_up = (d_hidden * glow).astype(LOW)
-            gates[rows, :] = d_gate
-            ups[rows, :] = d_up
-            sums = dot(d_gate, gate_w[...]) + dot(d_up, up_w[...])
-            part[pl.ds(2 * j, 2)] = sums.astype(LOW).reshape(2, tokens, width)
+
+            def columns(cut):
+                d_hidden = dot_t(grads, down_w[cut, :])
+                gate, up, squash, glow = lit(rows, cut)
+                gates[rows, cut] = (d_hidden * up * squash * (1.0 + gate * (1.0 - squash))).astype(LOW)
+                ups[rows, cut] = (d_hidden * glow).astype(LOW)
+
+            tiles(inner, columns)
+
+            def outputs(cut):
+                sums = dot(gates[rows, :], gate_w[:, cut]) + dot(ups[rows, :], up_w[:, cut])
+                part[pl.ds(2 * j, 2), :, cut] = sums.astype(LOW).reshape(2, tokens, cut.size)
+
+            tiles(width, outputs, 512)
             reduce.made(j)
             return carry
 
         lax.fori_loop(0, 4, step, 0)
 
-        work = [
-            (gate_w, gates, acts_flat, 0, 3),
-            (gate_w, gates, acts_flat, 3, 5),
-            (up_w, ups, acts_flat, 0, 3),
-            (up_w, ups, acts_flat, 3, 5),
-        ]
         if not apart:
-            weights(d_down, hiddens, grads_flat, 0, 5)
+            tiles(inner, partial(weights, d_down, hiddens, grads_flat))
             start(1, d_down)
 
-        def between(i):
-            if apart and i == 0 or not apart and i == 5:
-                middle(1)
-            if i < len(work):
-                weights(*work[i])
-
-        reduce.finish(later, between)
+        def both_rows(cut):
+            def kind(k, carry):
+                weights(pair_w.at[k], pair.at[k], acts_flat, cut)
+                return carry
+
+            lax.fori_loop(0, 2, kind, 0)
+
+        def early(i):
+            if apart:
+                pl.when(i == 0)(lambda: middle(1))
+            both_rows(rows_of(i * 256, 256))
+
+        def late(i):
+            @pl.when(i == 0)
+            def _():
+                if inner > 256 * SUB:
+                    both_rows(pl.ds(256 * SUB, inner - 256 * SUB))
+                if not apart:
+                    middle(1)
+
+        reduce.finish(later, early, late)
         saves = copy_in([(gate_w, gate_out), (up_w, up_out), (d_down, down_out)], keep_sem)
         after_backward(total, grad_ref, residual_ref, gain_ref, grad_out, low_out, gain_out)
         for copy in saves:
@@ -1454,11 +1525,9 @@
             pltpu.VMEM((8, tokens, width), LOW),
             pltpu.VMEM((8, tokens, width), LOW),
             pltpu.VMEM((8 * tokens, width), LOW),
-            pltpu.VMEM(w_gate.shape, LOW),
-            pltpu.VMEM(w_up.shape, LOW),
+            pltpu.VMEM((2, *w_gate.shape), LOW),
             pltpu.VMEM(w_down.shape, LOW),
-            pltpu.VMEM((8 * tokens, inner), LOW),
-            pltpu.VMEM((8 * tokens, inner), LOW),
+            pltpu.VMEM((2, 8 * tokens, inner), LOW),
             pltpu.VMEM((8 * tokens, inner), LOW),
             pltpu.SemaphoreType.DMA((7,)),
             pltpu.SemaphoreType.DMA((3,)),
@@ -1797,6 +1866,32 @@
     return lax.dot_general(a, b, (((0,), (0,)), ((), ())), preferred_element_type=F32)
 
 
+def line_tables(sizes, count):
+    fine = 32
+    freq = rope_base ** (-(jnp.arange(HD // 2, dtype=F32) * (2.0 / HD)))
+    firsts = jnp.cumsum(sizes) - sizes
+    places = jnp.arange(count, dtype=jnp.int32)[:, None]
+    inside = (places >= firsts[None]) & (places < (firsts + sizes)[None])
+    starts = jnp.sum(jnp.where(inside, firsts[None], 0), axis=1, keepdims=True)
+    points = jnp.concatenate([jnp.arange(count // fine) * fine, jnp.arange(fine), -firsts])
+    angles = points.astype(F32)[:, None] * freq[None]
+    cosines, sines = jnp.cos(angles), jnp.sin(angles)
+
+    def add(one, two):
+        return one[0] * two[0] - one[1] * two[1], one[1] * two[0] + one[0] * two[1]
+
+    def pick(low, high):
+        return cosines[low:high], sines[low:high]
+
+    coarse = count // fine
+    upper = [part[:, None] for part in pick(0, coarse)]
+    lower = [part[None] for part in pick(coarse, coarse + fine)]
+    at = [part.reshape(count, HD // 2) for part in add(upper, lower)]
+    shift = [jnp.sum(jnp.where(inside[:, :, None], part[None], 0.0), axis=1) for part in pick(coarse + fine, None)]
+    cosine, sine = add(at, shift)
+    return starts, jnp.concatenate([cosine, cosine], axis=1), jnp.concatenate([-sine, sine], axis=1)
+
+
 def per_device_line(
     hidden_states,
     out_grad,
@@ -1830,17 +1925,14 @@
     to_chips = [HeadsToChips(qkv_weight, biases, layer) for layer in range(LAYERS)]
     slab_rows, out_rows = GatherRows(From(to_chips[0]), 0, phase=1), GatherRows(out_weight, 1, 0, phase=1)
     swap = Swap(From(slab_rows), From(out_rows), phase=2)
-    sent[0].phase, sent[0].split = 3, True
+    sent[0].phase = 3
     states, loads = open_call(
         names, hidden_states, [*to_chips, Exchange(gain_rows, same=True), slab_rows, out_rows, swap, sent[0]]
     )
     (_,), (slab_next,), (gains,), (mine,), (out_mine,), (theirs, out_theirs), (w_gate,) = loads
     load = (mine, theirs, out_mine, out_theirs)
     gains = gains[:, : 2 * LAYERS].transpose(1, 0, 2).reshape(LAYERS, 2, D).astype(F32)
-    starts = row_starts(lengths[0], tok_row)
-    cosine, sine = rope_tables(jnp.arange(tok_row, dtype=jnp.int32) - starts)
-    cosine, sine = cosine.T, sine.T * jnp.where(jnp.arange(HD) < HD // 2, -1.0, 1.0)[None]
-    starts = starts[:, None]
+    starts, cosine, sine = line_tables(lengths[0], tok_row)
 
     wide = states.reshape(D, tok_row)
     residual = lax.dynamic_slice_in_dim(wide, col_at * QB, QB, 1).astype(F32).T
@@ -1902,7 +1994,10 @@
     for layer in reversed(range(LAYERS)):
         residual_in, full_one, slab, qkv, mixed, mid, full_two, gate, up, feed_weights = saved[layer]
         last = layer == LAYERS - 1
-        cargo = [] if last else [ScatterRows(d_slab, 0), ScatterRows(d_out_w, 1)]
+        if last:
+            cargo = [Exchange(states.T.reshape(8, D // 8, QB))]
+        else:
+            cargo = [ScatterRows(d_slab, 0), ScatterRows(d_out_w, 1)]
         cargo.append(ScatterRows(Inner((inner, D)), 1, phase=1))
         grad, low, d_gain_two, d_gate_w, d_up_w, d_down, loads = backward_feed(
             names,
@@ -1919,7 +2014,9 @@
             name=f"back_feed_{layer}",
         )
         grads["down", layer] = d_down, loads[-1][0]
-        if not last:
+        if last:
+            out_states = loads[0][0]
+        else:
             grads["out", layer + 1] = settle(d_out_w, 1, loads[1][0])
             owners.append(HeadsToOwners(settle(d_slab, 0, loads[0][0]).astype(LOW)))
         grad, low, d_gain_one, d_slab, d_out_w, loads = backward_heads(
@@ -1942,26 +2039,24 @@
         grads["gate", layer] = d_gate_w, loads[0][0]
         grads["up", layer] = d_up_w, loads[1][0]
         gain_terms[layer] = jnp.concatenate([d_gain_one, d_gain_two], axis=0)
-    leaving = jnp.concatenate([states, low], axis=0).T.reshape(8, D // 8, 2 * QB)
     gain_parts = jnp.pad(jnp.stack(gain_terms).reshape(2 * LAYERS, 8, D // 8), ((0, 8 - 2 * LAYERS), (0, 0), (0, 0)))
-    (left,), (gain_all,), (slots,), (out_slots,), (tiles,) = close_call(
+    for owner in owners:
+        owner.phase = 3
+    tiles, ((left,), (gain_all,), (out_slots,), (tiles_next,)) = close_call(
         names,
+        d_slab,
         [
-            Exchange(leaving),
+            Exchange(low.T.reshape(8, D // 8, QB)),
             Exchange(gain_parts.transpose(1, 0, 2), every_row=True),
-            ScatterRows(d_slab, 0),
-            ScatterRows(d_out_w, 1),
+            ScatterRows(d_out_w, 1, phase=3),
             *owners,
         ],
-        "close",
     )
-    grads["qkv", 1] = settle_heads(tiles)
-    ((tiles,),) = close_call(names, [HeadsToOwners(settle(d_slab, 0, slots).astype(LOW))], "close_heads")
+    grads["qkv", 1] = settle_heads(tiles_next)
     grads["qkv", 0] = settle_heads(tiles)
     grads["out", 0] = settle(d_out_w, 1, out_slots)
-    left = left.transpose(1, 0, 2)
-    out_states = left[:, :, :QB].reshape(D // 8, tok_row)
-    input_grad = left[:, :, QB:].reshape(D // 8, tok_row).astype(F32)
+    out_states = out_states.transpose(1, 0, 2).reshape(D // 8, tok_row)
+    input_grad = left.transpose(1, 0, 2).reshape(D // 8, tok_row).astype(F32)
     gain_grads = jnp.sum(gain_all, axis=(0, 1))[: 2 * LAYERS].reshape(LAYERS, 2, D // 8)
 
     def both_layers(kind):

time: 672 us -> 662 us (0.985)
  Pallas kernels: 630 us -> 622 us
    pallas_call x11 -> x10, Pallas kernels: 619 us -> 611 us  [carry_call(): results = list(call(*arrays, *given))]
where the time goes in v6:
time: 662 us; the launch traced here: 653 us
  Pallas kernels  622 us (94%)
  other arithmetic  16.4 us (2%)
  local copies, waits for them, and re-layouts  13 us (2%)
    pallas_call x10, Pallas kernels, carry_call(): results = list(call(*arrays, *given))  611 us

profile of v6, /device:TPU:31, one launch (start us, length us, event | category | flops | bytes accessed | tf_op | source)
XLA Modules:
  0.0 652.8 jit_solution(8314425320711897325)
XLA Ops:
  0.6 0.8 reduce-window.4
  1.5 0.7 fusion.4
  2.2 0.2 multiply_sine_fusion
  2.5 0.2 multiply_subtract_fusion
  2.6 0.7 fusion.3
  3.4 0.3 select_reduce_fusion.1
  3.7 0.2 copy.42
  3.9 0.2 copy.43
  4.2 1.0 pad_maximum_fusion.3.refs_6_.refs_4_.refs_8_
  5.2 1.0 pad_maximum_fusion.2.refs_5_.refs_3_.refs_7_
  6.2 0.7 dynamic_update_slice.3.refs_2_.refs_4_
  7.0 0.6 pad.8.refs_5_
  7.6 60.0 %open.1 = (bf16[8,192,1024]{2,1,0:T(8,128)(2,1)}, bf16[208,640]{1,0:T(8,128)(2,1)}, bf16[208,640]{1,0:T(8,128)(2,1)}, bf16[8,16,192]{2,1,0:T(8,128)(2,1)}, bf16[...) custom-call(bf16[192,1024]{1,0:T(8,128)(2,1)} %refs_0_.2, ...), custom_call_target="tpu_custom_call" | custom-call | tf_op jit(solution)/shard_map/open/pallas_call | solution.py:655
  67.7 1.0 constant_dynamic-slice_fusion.2
  68.7 0.2 copy.58
  68.9 1.0 convert_bitcast_fusion.1.refs_3_.refs_2_
  69.8 0.8 convert_bitcast_fusion.2
  70.7 0.6 slice_bitcast_fusion.5
  71.3 1.2 copy.46.refs_2_
  72.6 1.0 copy.47.refs_7_.refs_5_.refs_9_
  73.6 63.0 %heads_0.1 = (f32[128,1536]{1,0:T(8,128)}, bf16[128,1536]{1,0:T(8,128)(2,1)}, bf16[1024,1536]{1,0:T(8,128)(2,1)}, bf16[1024,640]{1,0:T(8,128)(2,1)}, bf16[512,38...) custom-call(bf16[192,1024]{1,0:T(8,128)(2,1)} %refs_0_.3, ...), custom_call_target="tpu_custom_call" | custom-call | tf_op jit(solution)/shard_map/heads_0/pallas_call | solution.py:655
  136.6 62.3 %feed_0.1 = (f32[128,1536]{1,0:T(8,128)}, bf16[128,1536]{1,0:T(8,128)(2,1)}, bf16[8,128,1536]{2,1,0:T(8,128)(2,1)}, bf16[1024,1120]{1,0:T(8,128)(2,1)}, bf16[102...) custom-call(bf16[128,1536]{1,0:T(8,128)(2,1)} %get-tuple-element.91., ...), custom_call_target="tpu_custom_call" | custom-call | tf_op jit(solution)/shard_map/feed_0/pallas_call | solution.py:655
  198.9 63.2 %heads_1.1 = (f32[128,1536]{1,0:T(8,128)}, bf16[128,1536]{1,0:T(8,128)(2,1)}, bf16[8,128,1536]{2,1,0:T(8,128)(2,1)}, bf16[1024,640]{1,0:T(8,128)(2,1)}, bf16[512...) custom-call(bf16[128,1536]{1,0:T(8,128)(2,1)} %get-tuple-element.97.refs_0_, ...), custom_call_target="tpu_custom_call" | custom-call | tf_op jit(solution)/shard_map/heads_1/pallas_call | solution.py:655
  262.2 0.6 broadcast_in_dim.78.refs_2_
  262.8 59.7 %feed_1.1 = (f32[128,1536]{1,0:T(8,128)}, bf16[128,1536]{1,0:T(8,128)(2,1)}, bf16[8,128,1536]{2,1,0:T(8,128)(2,1)}, bf16[1024,1120]{1,0:T(8,128)(2,1)}, bf16[1024,1120]{1,0:T(8,128)(2,1)}) custom-call(bf16[128,1536]{1,0:T(8,128)(2,1)} %get-tuple-element.104.refs_0_, f32[128,1536]{1,0:T(8,128)} %get-tuple-element.103.refs_1_.refs_2_, ...), custom_call_target="tpu_custom_call" | custom-call | tf_op jit(solution)/shard_map/feed_1/pallas_call | solution.py:655
  322.5 1.9 copy.49
  324.4 2.0 dynamic-slice_convert_fusion.refs_1_
  326.4 58.6 %back_feed_1.1 = (f32[128,1536]{1,0:T(8,128)}, bf16[128,1536]{1,0:T(8,128)(2,1)}, f32[1,1536]{1,0:T(1,128)}, bf16[1120,1536]{1,0:T(8,128)(2,1)}, bf16[1120,1536]...) custom-call(bf16[8,128,1536]{2,1,0:T(8,128)(2,1)} %bitcast.99, ...), custom_call_target="tpu_custom_call" | custom-call | tf_op jit(solution)/shard_map/back_feed_1/pallas_call | solution.py:655
  385.0 66.9 %back_heads_1.1 = (f32[128,1536]{1,0:T(8,128)}, bf16[128,1536]{1,0:T(8,128)(2,1)}, f32[1,1536]{1,0:T(1,128)}, bf16[4,208,640]{2,1,0:T(8,128)(2,1)}, bf16[192,153...) custom-call(bf16[128,1536]{1,0:T(8,128)(2,1)} %get-tuple-element.113.refs_0_, ...), custom_call_target="tpu_custom_call" | custom-call | tf_op jit(solution)/shard_map/back_heads_1/pallas_call | solution.py:655
  451.8 77.6 %back_feed_0.1 = (f32[128,1536]{1,0:T(8,128)}, bf16[128,1536]{1,0:T(8,128)(2,1)}, f32[1,1536]{1,0:T(1,128)}, bf16[1120,1536]{1,0:T(8,128)(2,1)}, bf16[1120,1536]...) custom-call(bf16[128,1536]{1,0:T(8,128)(2,1)} %get-tuple-element.120, ...), custom_call_target="tpu_custom_call" | custom-call | tf_op jit(solution)/shard_map/back_feed_0/pallas_call | solution.py:655
  529.4 67.3 %back_heads_0.1 = (f32[128,1536]{1,0:T(8,128)}, bf16[128,1536]{1,0:T(8,128)(2,1)}, f32[1,1536]{1,0:T(1,128)}, bf16[4,208,640]{2,1,0:T(8,128)(2,1)}, bf16[192,153...) custom-call(bf16[128,1536]{1,0:T(8,128)(2,1)} %get-tuple-element.127.refs_0_, ...), custom_call_target="tpu_custom_call" | custom-call | tf_op jit(solution)/shard_map/back_heads_0/pallas_call | solution.py:655
  596.8 11.3 %settle.1 = (f32[2,1120,384]{2,1,0:T(8,128)}, f32[2,1120,384]{2,1,0:T(8,128)}, f32[2,1120,384]{2,1,0:T(8,128)}) custom-call(s32[1]{0:T(128)} %bitcast.42.row_ref, bf16[1120,1536]{1,0:T(8,128)(2,1)} %get-tuple-element.132.refs_14_.refs_0_, bf16[2,1120,384]{2,1,0:T(8,128)(2,1)} %get-tuple-element.148.refs_1_, ...), custom_call_target="tpu_custom_call" | custom-call | tf_op jit(solution)/shard_map/settle/pallas_call | solution.py:1377
  608.2 1.8 add_convert_fusion.refs_5_
  610.1 0.6 pad_bitcast_fusion.refs_3_
  610.8 0.9 copy.53
  611.7 32.0 %close.1 = (bf16[2,208,640]{2,1,0:T(8,128)(2,1)}, bf16[2,2,2,208,128]{4,3,2,1,0:T(8,128)(2,1)}, bf16[8,192,128]{2,1,0:T(8,128)(2,1)}, f32[4,8,8,192]{3,2,1,0:T(8...) custom-call(bf16[832,640]{1,0:T(8,128)(2,1)} %bitcast.97, bf16[832,640]{1,0:T(8,128)(2,1)} %bitcast.98, ...), custom_call_target="tpu_custom_call" | custom-call | tf_op jit(solution)/shard_map/close/pallas_call | solution.py:655
  643.7 1.1 convert_reduce_fusion.2
  644.9 1.0 add_bitcast_fusion.2
  645.9 0.9 pad_maximum_fusion.1
  647.0 0.6 pad_maximum_fusion.5
  647.6 0.3 copy.56
  648.0 0.3 stack_reshape.6
  648.3 0.3 copy.57
  648.6 0.3 stack_reshape.7
  648.9 0.9 pad_maximum_fusion
  649.9 1.0 copy_bitcast_fusion
  650.9 0.6 reshape.193
  651.5 0.8 copy_bitcast_fusion.1
  (62 shorter events, 1.1 us)
Async XLA Ops:
  4.1 2.2 copy-start.14
  4.1 2.9 copy-start.13
  7.0 0.6 copy-start.8
  596.7 11.4 %copy-start = (bf16[2,208,640]{2,1,0:T(8,128)(2,1)S(1)}, bf16[2,208,640]{2,1,0:T(8,128)(2,1)}, u32[]{:S(2)}) copy-start(bf16[2,208,640]{2,1,0:T(8,128)(2,1)} %get-tuple-element.141) | copy-start | bytes 1597444
  596.7 13.2 %copy-start.11 = (f32[1,1536]{1,0:T(1,128)S(1)}, f32[1,1536]{1,0:T(1,128)}, u32[]{:S(2)}) copy-start(f32[1,1536]{1,0:T(1,128)} %get-tuple-element.137) | copy-start | bytes 18436
  596.7 13.2 %copy-start.12 = (f32[1,1536]{1,0:T(1,128)S(1)}, f32[1,1536]{1,0:T(1,128)}, u32[]{:S(2)}) copy-start(f32[1,1536]{1,0:T(1,128)} %get-tuple-element.136) | copy-start | bytes 18436
  596.7 13.2 %copy-start.9 = (f32[1,1536]{1,0:T(1,128)S(1)}, f32[1,1536]{1,0:T(1,128)}, u32[]{:S(2)}) copy-start(f32[1,1536]{1,0:T(1,128)} %get-tuple-element.139) | copy-start | bytes 18436
  596.7 13.2 %copy-start.10 = (f32[1,1536]{1,0:T(1,128)S(1)}, f32[1,1536]{1,0:T(1,128)}, u32[]{:S(2)}) copy-start(f32[1,1536]{1,0:T(1,128)} %get-tuple-element.138) | copy-start | bytes 18436
  596.7 14.0 %copy-start.4 = (bf16[128,1536]{1,0:T(8,128)(2,1)S(1)}, bf16[128,1536]{1,0:T(8,128)(2,1)}, u32[]{:S(2)}) copy-start(bf16[128,1536]{1,0:T(8,128)(2,1)} %get-tuple-element.135) | copy-start | bytes 1179652
  608.2 36.6 %copy-start.6 = (bf16[2,192,384]{2,1,0:T(8,128)(2,1)S(1)}, bf16[2,192,384]{2,1,0:T(8,128)(2,1)}, u32[]{:S(2)}) copy-start(bf16[2,192,384]{2,1,0:T(8,128)(2,1)} %get-tuple-element.147) | copy-start | bytes 884740
  643.7 3.1 copy-start.2
  643.7 3.1 copy-start.1
  647.6 2.3 copy-start.5
  647.9 2.9 copy-start.7
  647.9 3.6 copy-start.3

commit v7 on v6

--- a/solution.py
+++ b/solution.py
@@ -812,13 +812,13 @@
                 ups[rows, cut] = up.astype(LOW)
                 hidden[:, cut] = (gate * jax.nn.sigmoid(gate) * up).astype(LOW)
 
-            tiles(inner, columns, 512)
+            tiles(inner, columns)
 
             def outputs(cut):
                 sums = dot(hidden[...], down_w[:, cut]).astype(LOW)
                 part[pl.ds(2 * j, 2), :, cut] = sums.reshape(2, tokens, cut.size)
 
-            tiles(width, outputs, 768)
+            tiles(width, outputs, 512)
             reduce.made(j)
             for copy in keep(j):
                 copy.start()
@@ -1026,6 +1026,79 @@
         return jnp.sum(self.tails[:, 0, :].astype(F32), axis=0, keepdims=True)
 
 
+def after_forward(sums, residual, gain, states, normed):
+    def step(i, carry):
+        rows = rows_of(i * 16, 16)
+        now = residual[rows, :] + sums[rows, :]
+        states[rows, :] = now
+        if gain is not None:
+            now = now * lax.rsqrt(jnp.mean(now * now, axis=1, keepdims=True) + eps_norm) * gain[...]
+        normed[rows, :] = now.astype(LOW)
+        return carry
+
+    lax.fori_loop(0, sums.shape[0] // 16, step, 0)
+
+
+def after_backward(sums, grad, residual, gain, grad_out, low_out, gain_out):
+    def step(i, total):
+        rows = rows_of(i * 16, 16)
+        d_normed, now = sums[rows, :], residual[rows, :]
+        scale = lax.rsqrt(jnp.mean(now * now, axis=1, keepdims=True) + eps_norm)
+        weighted = d_normed * gain[...]
+        inner = jnp.sum(weighted * now, axis=1, keepdims=True)
+        out = grad[rows, :] + (weighted * scale - now * (scale * scale * scale) * inner / D)
+        grad_out[rows, :] = out
+        low_out[rows, :] = out.astype(LOW)
+        return total + jnp.sum(d_normed * now * scale, axis=0, keepdims=True)
+
+    gain_out[...] = lax.fori_loop(0, sums.shape[0] // 16, step, jnp.zeros((1, D), F32))
+
+
+class Slab:
+    scratch = (
+        pltpu.VMEM((D, 5 * HD), LOW),
+        pltpu.VMEM((3 * HD, D), LOW),
+        pltpu.VMEM((4, 16, 5 * HD), LOW),
+        pltpu.SemaphoreType.DMA((2, 5)),
+        pltpu.SemaphoreType.DMA((4,)),
+    )
+
+    def __init__(self, place, refs, scratch):
+        self.place = place
+        self.mine, self.theirs, self.out_mine, self.out_theirs = refs
+        self.qkv, self.out, self.tails, self.sems, self.tail_sems = scratch
+
+    def copies(self, half, mine):
+        source, out = (self.mine, self.out_mine) if mine else (self.theirs, self.out_theirs)
+        sem = self.sems.at[half]
+        rows = D // 8
+        for row in range(4):
+            spot = self.qkv.at[(2 * row + half) * rows : (2 * row + half + 1) * rows, :]
+            yield pltpu.make_async_copy(source.at[row * HALF : row * HALF + rows, :], spot, sem.at[row])
+        yield pltpu.make_async_copy(out, self.out.at[half * rows : (half + 1) * rows, :], sem.at[4])
+        if half == 0:
+            for row in range(4):
+                tail = source.at[row * HALF + rows : (row + 1) * HALF, :]
+                yield pltpu.make_async_copy(tail, self.tails.at[row], self.tail_sems.at[row])
+
+    def start(self):
+        for half in range(2):
+            for mine in (True, False):
+
+                @pl.when((self.place.c == half) == mine)
+                def _(half=half, mine=mine):
+                    for copy in self.copies(half, mine):
+                        copy.start()
+
+    def wait(self):
+        for half in range(2):
+            for copy in self.copies(half, True):
+                copy.wait()
+
+    def bias(self):
+        return jnp.sum(self.tails[:, 0, :].astype(F32), axis=0, keepdims=True)
+
+
 def heads_of(ref, rows):
     return jnp.concatenate([ref[rows, h * HD : (h + 1) * HD] for h in range(3)], axis=0)
 
@@ -1118,11 +1191,16 @@
             j = far_first(place, p)
             b = 2 * j + place.c
             rows, window, _ = block_window(b)
-            probs = block_probs(heads_of(qkv, rows), qkv[window, 3 * HD : 4 * HD], starts_ref, b)
-            heads = dot(probs.astype(LOW), qkv[window, 4 * HD : 5 * HD]).astype(LOW)
-            both = jnp.concatenate([heads[h * QB : (h + 1) * QB] for h in range(3)], axis=1)
-            mixed[rows_of(j * QB, QB), :] = both
-            part[j] = jnp.dot(both, weights.out[...], preferred_element_type=F32).astype(LOW)
+            mine = rows_of(j * QB, QB)
+
+            def head(h, carry):
+                cut = rows_of(h * HD, HD)
+                probs = block_probs(qkv[rows, cut], qkv[window, 3 * HD : 4 * HD], starts_ref, b)
+                mixed[mine, cut] = dot(probs.astype(LOW), qkv[window, 4 * HD : 5 * HD]).astype(LOW)
+                return carry
+
+            lax.fori_loop(0, 3, head, 0)
+            part[j] = dot(mixed[mine, :], weights.out[...]).astype(LOW)
             reduce.made(j)
             return carry
 
@@ -1160,9 +1238,12 @@
 
             def turn(t, carry):
                 rows = rows_of(t * 2 * QB, 2 * QB)
-                for j in range(4):
-                    piece = full[2 * j : 2 * j + 2, :, rows].reshape(D // 4, 2 * QB)
-                    flat[rows, j * (D // 4) : (j + 1) * (D // 4)] = piece.T
+
+                def piece(j, carry):
+                    flat[rows, rows_of(j * (D // 4), D // 4)] = full[pl.ds(2 * j, 2), :, rows].reshape(D // 4, 2 * QB).T
+                    return carry
+
+                lax.fori_loop(0, 4, piece, 0)
                 keep(t).start()
                 return carry
 

time: 662 us -> 658 us (level); the launches traced: 653 us -> 656 us
  no operation moved by 1% of the time
where the time goes in v7:
time: 658 us; the launch traced here: 656 us
  Pallas kernels  626 us (95%)
  other arithmetic  16.4 us (2%)
  local copies, waits for them, and re-layouts  13 us (2%)
    pallas_call x10, Pallas kernels, carry_call(): results = list(call(*arrays, *given))  615 us

profile of v7, /device:TPU:31, one launch (start us, length us, event | category | flops | bytes accessed | tf_op | source)
XLA Modules:
  0.0 656.4 jit_solution(11106565877744266684)
XLA Ops:
  0.6 0.8 reduce-window.4
  1.5 0.7 fusion.4
  2.2 0.2 multiply_sine_fusion
  2.5 0.2 multiply_subtract_fusion
  2.6 0.7 fusion.3
  3.4 0.3 select_reduce_fusion.1
  3.7 0.2 copy.42
  3.9 0.2 copy.43
  4.2 1.0 pad_maximum_fusion.3.refs_6_.refs_4_.refs_8_
  5.2 1.0 pad_maximum_fusion.2.refs_5_.refs_3_.refs_7_
  6.2 0.7 dynamic_update_slice.3.refs_2_.refs_4_
  7.0 0.6 pad.8.refs_5_
  7.6 60.0 %open.1 = (bf16[8,192,1024]{2,1,0:T(8,128)(2,1)}, bf16[208,640]{1,0:T(8,128)(2,1)}, bf16[208,640]{1,0:T(8,128)(2,1)}, bf16[8,16,192]{2,1,0:T(8,128)(2,1)}, bf16[...) custom-call(bf16[192,1024]{1,0:T(8,128)(2,1)} %refs_0_.2, ...), custom_call_target="tpu_custom_call" | custom-call | tf_op jit(solution)/shard_map/open/pallas_call | solution.py:655
  67.7 1.0 constant_dynamic-slice_fusion.2
  68.7 0.2 copy.58
  68.9 1.0 convert_bitcast_fusion.1.refs_3_.refs_2_
  69.8 0.8 convert_bitcast_fusion.2
  70.7 0.6 slice_bitcast_fusion.5
  71.3 1.2 copy.46.refs_2_
  72.6 1.0 copy.47.refs_7_.refs_5_.refs_9_
  73.6 63.0 %heads_0.1 = (f32[128,1536]{1,0:T(8,128)}, bf16[128,1536]{1,0:T(8,128)(2,1)}, bf16[1024,1536]{1,0:T(8,128)(2,1)}, bf16[1024,640]{1,0:T(8,128)(2,1)}, bf16[512,38...) custom-call(bf16[192,1024]{1,0:T(8,128)(2,1)} %refs_0_.3, ...), custom_call_target="tpu_custom_call" | custom-call | tf_op jit(solution)/shard_map/heads_0/pallas_call | solution.py:655
  136.6 63.8 %feed_0.1 = (f32[128,1536]{1,0:T(8,128)}, bf16[128,1536]{1,0:T(8,128)(2,1)}, bf16[8,128,1536]{2,1,0:T(8,128)(2,1)}, bf16[1024,1120]{1,0:T(8,128)(2,1)}, bf16[102...) custom-call(bf16[128,1536]{1,0:T(8,128)(2,1)} %get-tuple-element.91., ...), custom_call_target="tpu_custom_call" | custom-call | tf_op jit(solution)/shard_map/feed_0/pallas_call | solution.py:655
  200.4 64.0 %heads_1.1 = (f32[128,1536]{1,0:T(8,128)}, bf16[128,1536]{1,0:T(8,128)(2,1)}, bf16[8,128,1536]{2,1,0:T(8,128)(2,1)}, bf16[1024,640]{1,0:T(8,128)(2,1)}, bf16[512...) custom-call(bf16[128,1536]{1,0:T(8,128)(2,1)} %get-tuple-element.97.refs_0_, ...), custom_call_target="tpu_custom_call" | custom-call | tf_op jit(solution)/shard_map/heads_1/pallas_call | solution.py:655
  264.4 0.6 broadcast_in_dim.78.refs_2_
  265.0 61.5 %feed_1.1 = (f32[128,1536]{1,0:T(8,128)}, bf16[128,1536]{1,0:T(8,128)(2,1)}, bf16[8,128,1536]{2,1,0:T(8,128)(2,1)}, bf16[1024,1120]{1,0:T(8,128)(2,1)}, bf16[1024,1120]{1,0:T(8,128)(2,1)}) custom-call(bf16[128,1536]{1,0:T(8,128)(2,1)} %get-tuple-element.104.refs_0_, f32[128,1536]{1,0:T(8,128)} %get-tuple-element.103.refs_1_.refs_2_, ...), custom_call_target="tpu_custom_call" | custom-call | tf_op jit(solution)/shard_map/feed_1/pallas_call | solution.py:655
  326.5 1.9 copy.49
  328.4 2.0 dynamic-slice_convert_fusion.refs_1_
  330.4 58.6 %back_feed_1.1 = (f32[128,1536]{1,0:T(8,128)}, bf16[128,1536]{1,0:T(8,128)(2,1)}, f32[1,1536]{1,0:T(1,128)}, bf16[1120,1536]{1,0:T(8,128)(2,1)}, bf16[1120,1536]...) custom-call(bf16[8,128,1536]{2,1,0:T(8,128)(2,1)} %bitcast.99, ...), custom_call_target="tpu_custom_call" | custom-call | tf_op jit(solution)/shard_map/back_feed_1/pallas_call | solution.py:655
  389.0 66.9 %back_heads_1.1 = (f32[128,1536]{1,0:T(8,128)}, bf16[128,1536]{1,0:T(8,128)(2,1)}, f32[1,1536]{1,0:T(1,128)}, bf16[4,208,640]{2,1,0:T(8,128)(2,1)}, bf16[192,153...) custom-call(bf16[128,1536]{1,0:T(8,128)(2,1)} %get-tuple-element.113.refs_0_, ...), custom_call_target="tpu_custom_call" | custom-call | tf_op jit(solution)/shard_map/back_heads_1/pallas_call | solution.py:655
  455.9 78.4 %back_feed_0.1 = (f32[128,1536]{1,0:T(8,128)}, bf16[128,1536]{1,0:T(8,128)(2,1)}, f32[1,1536]{1,0:T(1,128)}, bf16[1120,1536]{1,0:T(8,128)(2,1)}, bf16[1120,1536]...) custom-call(bf16[128,1536]{1,0:T(8,128)(2,1)} %get-tuple-element.120, ...), custom_call_target="tpu_custom_call" | custom-call | tf_op jit(solution)/shard_map/back_feed_0/pallas_call | solution.py:655
  534.3 66.6 %back_heads_0.1 = (f32[128,1536]{1,0:T(8,128)}, bf16[128,1536]{1,0:T(8,128)(2,1)}, f32[1,1536]{1,0:T(1,128)}, bf16[4,208,640]{2,1,0:T(8,128)(2,1)}, bf16[192,153...) custom-call(bf16[128,1536]{1,0:T(8,128)(2,1)} %get-tuple-element.127.refs_0_, ...), custom_call_target="tpu_custom_call" | custom-call | tf_op jit(solution)/shard_map/back_heads_0/pallas_call | solution.py:655
  601.0 11.3 %settle.1 = (f32[2,1120,384]{2,1,0:T(8,128)}, f32[2,1120,384]{2,1,0:T(8,128)}, f32[2,1120,384]{2,1,0:T(8,128)}) custom-call(s32[1]{0:T(128)} %bitcast.42.row_ref, bf16[1120,1536]{1,0:T(8,128)(2,1)} %get-tuple-element.132.refs_14_.refs_0_, bf16[2,1120,384]{2,1,0:T(8,128)(2,1)} %get-tuple-element.148.refs_1_, ...), custom_call_target="tpu_custom_call" | custom-call | tf_op jit(solution)/shard_map/settle/pallas_call | solution.py:1458
  612.5 1.8 add_convert_fusion.refs_5_
  614.4 0.6 pad_bitcast_fusion.refs_3_
  615.1 0.9 copy.53
  616.0 31.8 %close.1 = (bf16[2,208,640]{2,1,0:T(8,128)(2,1)}, bf16[2,2,2,208,128]{4,3,2,1,0:T(8,128)(2,1)}, bf16[8,192,128]{2,1,0:T(8,128)(2,1)}, f32[4,8,8,192]{3,2,1,0:T(8...) custom-call(bf16[832,640]{1,0:T(8,128)(2,1)} %bitcast.97, bf16[832,640]{1,0:T(8,128)(2,1)} %bitcast.98, ...), custom_call_target="tpu_custom_call" | custom-call | tf_op jit(solution)/shard_map/close/pallas_call | solution.py:655
  647.8 1.1 convert_reduce_fusion.2
  649.0 1.0 add_bitcast_fusion.2
  650.0 0.9 pad_maximum_fusion.1
  651.1 0.6 pad_maximum_fusion.5
  651.7 0.3 copy.56
  652.1 0.3 stack_reshape.6
  652.4 0.3 copy.57
  652.7 0.3 stack_reshape.7
  653.0 0.9 pad_maximum_fusion
  654.0 1.0 copy_bitcast_fusion
  655.0 0.6 reshape.193
  655.6 0.8 copy_bitcast_fusion.1
  (62 shorter events, 1.1 us)
Async XLA Ops:
  4.1 2.2 copy-start.14
  4.1 2.9 copy-start.13
  7.0 0.6 copy-start.8
  601.0 11.4 %copy-start = (bf16[2,208,640]{2,1,0:T(8,128)(2,1)S(1)}, bf16[2,208,640]{2,1,0:T(8,128)(2,1)}, u32[]{:S(2)}) copy-start(bf16[2,208,640]{2,1,0:T(8,128)(2,1)} %get-tuple-element.141) | copy-start | bytes 1597444
  601.0 13.2 %copy-start.11 = (f32[1,1536]{1,0:T(1,128)S(1)}, f32[1,1536]{1,0:T(1,128)}, u32[]{:S(2)}) copy-start(f32[1,1536]{1,0:T(1,128)} %get-tuple-element.137) | copy-start | bytes 18436
  601.0 13.2 %copy-start.12 = (f32[1,1536]{1,0:T(1,128)S(1)}, f32[1,1536]{1,0:T(1,128)}, u32[]{:S(2)}) copy-start(f32[1,1536]{1,0:T(1,128)} %get-tuple-element.136) | copy-start | bytes 18436
  601.0 13.2 %copy-start.9 = (f32[1,1536]{1,0:T(1,128)S(1)}, f32[1,1536]{1,0:T(1,128)}, u32[]{:S(2)}) copy-start(f32[1,1536]{1,0:T(1,128)} %get-tuple-element.139) | copy-start | bytes 18436
  601.0 13.2 %copy-start.10 = (f32[1,1536]{1,0:T(1,128)S(1)}, f32[1,1536]{1,0:T(1,128)}, u32[]{:S(2)}) copy-start(f32[1,1536]{1,0:T(1,128)} %get-tuple-element.138) | copy-start | bytes 18436
  601.0 14.0 %copy-start.4 = (bf16[128,1536]{1,0:T(8,128)(2,1)S(1)}, bf16[128,1536]{1,0:T(8,128)(2,1)}, u32[]{:S(2)}) copy-start(bf16[128,1536]{1,0:T(8,128)(2,1)} %get-tuple-element.135) | copy-start | bytes 1179652
  612.5 36.5 %copy-start.6 = (bf16[2,192,384]{2,1,0:T(8,128)(2,1)S(1)}, bf16[2,192,384]{2,1,0:T(8,128)(2,1)}, u32[]{:S(2)}) copy-start(bf16[2,192,384]{2,1,0:T(8,128)(2,1)} %get-tuple-element.147) | copy-start | bytes 884740
  647.8 3.1 copy-start.2
  647.8 3.1 copy-start.1
  651.7 2.3 copy-start.5
  652.0 2.9 copy-start.7
  652.0 3.6 copy-start.3
